TPU v7x, 32 devices: a whole 2x2x4 slice. The times are simulated.
32 devices in a mesh: leaf: 8 (over z, x), blk: 4 (over y, core).
Axes of the slice: x: 2, y: 2, z: 4, core: 2. Of those that a mesh axis runs over, the one named last changes fastest.
Arguments:
- desc_panel: bfloat16 [256, 384, 128], P(('leaf', 'blk')), may hold values from -18 to 18
- row_map: int32 [256, 3], P(('leaf', 'blk')), may hold values from 0 to 55, as said below
- anc_order: int32 [8], replicated, may hold values from 0 to 7, as said below
- anc_below: int32 [8, 12], replicated, may hold values from 32 to 55, as said below
- anc_panel: float32 [8, 4, 4, 128, 512], P('leaf', None, 'blk'), may hold values from -6 to 27, as said below
Outputs:
- chol_panel: float32 [8, 4, 4, 128, 512], P('leaf', None, 'blk')
Inputs may be any that keep to these rules, and one draw needn't show every extreme that they name: `row_map`: entry 0 of each row is a column block of one ancestor; the other entries are distinct entries of that ancestor's row of anc_below. Over the descendants of one device, entry 0 names the column blocks of any one ancestor at most 2 times, and of some ancestor exactly 2 times. `anc_order`: each leaf index holds a different column range. `anc_below`: each row holds 12 distinct indices. `anc_panel`: the leading 512 rows of each ancestor's panel are symmetric, and the leading block of S stays positive definite.
All inputs are finite; a program needn't handle non-finite values.
Results may differ from a plain program's by a relative error of at most 0.0003.
Values may be sent and summed in bfloat16 or wider, within the bound.
No kernel may reach another device: no remote copies, remote signals or barrier semaphores. Data moves between devices by JAX's collectives and lax.ppermute only.
A program may use at most 192 MiB of HBM per device.

v0:
```python
import jax
import jax.numpy as jnp
from jax import lax
from jax.experimental import pallas as pl
from jax.experimental.pallas import tpu as pltpu
from jax.sharding import PartitionSpec as P


SLOTS = 2
CODES = 4
CODE_ROWS = 16
PANEL = 8
SPLIT = 2
DIRECT = 8
HIGHEST = lax.Precision.HIGHEST


def repeat(count, body, unroll_to=16):
    if count <= unroll_to:
        for index in range(count):
            body(index)
    else:
        lax.fori_loop(0, count, lambda index, carry: (body(index), carry)[1], 0)


def spaces(count, space):
    return [pl.BlockSpec(memory_space=space)] * count


def pack_kernel(cb, nb, direct, row_map, anc_order, anc_below, panel, *refs):
    leaves = anc_order.shape[0]
    block_count, desc_count = row_map.shape
    rows = panel.shape[1] // block_count
    outs = refs[: leaves if direct else 1]
    tail_out, inverse, used, chosen, codes, tail_sem = refs[len(outs):]
    me = lax.axis_index("leaf")

    def clear(leaf):
        inverse[anc_order[leaf]] = leaf
        used[leaf] = 0
        for slot in range(SLOTS):
            chosen[leaf * SLOTS + slot] = -1
            codes[(leaf * SLOTS + slot) * CODES] = cb
            for r in range(1, CODES):
                codes[(leaf * SLOTS + slot) * CODES + r] = nb

    repeat(leaves, clear)

    def assign(desc):
        head = row_map[0, desc]
        leaf = inverse[lax.div(head, cb)]
        taken = used[leaf]
        used[leaf] = taken + 1
        place = leaf * SLOTS + taken
        chosen[place] = desc
        codes[place * CODES] = head - anc_order[leaf] * cb
        for r in range(1, block_count):
            target = row_map[r, desc]
            found = jnp.int32(nb)
            for q in range(anc_below.shape[1]):
                found = jnp.where(anc_below[leaf, q] == target, q, found)
            codes[place * CODES + r] = found

    repeat(desc_count, assign)

    def dest(index):
        return jnp.bitwise_xor(me, index) if direct else index

    def tail_copy(index, slot):
        leaf = dest(index)
        desc = chosen[leaf * SLOTS + slot]
        tail_rows = (block_count - 1) * rows
        return desc, pltpu.make_async_copy(
            panel.at[jnp.maximum(desc, 0), pl.ds(rows, tail_rows)],
            tail_out.at[leaf, pl.ds(slot * tail_rows, tail_rows)],
            tail_sem.at[index, slot],
        )

    def start(index):
        for slot in range(SLOTS):
            desc, copy = tail_copy(index, slot)

            @pl.when(desc >= 0)
            def _():
                copy.start()

    repeat(leaves, start)

    def write_head(index):
        leaf = dest(index)
        row = lax.broadcasted_iota(jnp.int32, (CODE_ROWS, 128), 0)
        values = jnp.zeros((CODE_ROWS, 128), jnp.int32)
        for entry in range(SLOTS * CODES):
            values = jnp.where(row == entry, codes[leaf * SLOTS * CODES + entry], values)
        values = values.astype(jnp.float32).astype(panel.dtype)
        for slot in range(SLOTS):
            desc = jnp.maximum(chosen[leaf * SLOTS + slot], 0)
            block = panel[desc, pl.ds(0, rows)]
            if direct:
                outs[index][pl.ds(slot * rows, rows)] = block
            else:
                outs[0][index, pl.ds(slot * rows, rows)] = block
        if direct:
            outs[index][pl.ds(SLOTS * rows, CODE_ROWS)] = values
        else:
            outs[0][index, pl.ds(SLOTS * rows, CODE_ROWS)] = values

    repeat(leaves, write_head)

    def finish(index):
        for slot in range(SLOTS):
            desc, copy = tail_copy(index, slot)

            @pl.when(desc >= 0)
            def _():
                copy.wait()

    repeat(leaves, finish)


def pack(desc_panel, row_map, anc_order, anc_below, cb, direct):
    leaves = anc_order.shape[0]
    block_count = row_map.shape[1]
    rows = desc_panel.shape[1] // block_count
    width = desc_panel.shape[2]
    head_rows = SLOTS * rows + CODE_ROWS
    dtype = desc_panel.dtype
    if direct:
        heads = [jax.ShapeDtypeStruct((head_rows, width), dtype)] * leaves
    else:
        heads = [jax.ShapeDtypeStruct((leaves, head_rows, width), dtype)]
    tails = jax.ShapeDtypeStruct((leaves, SLOTS * (block_count - 1) * rows, width), dtype)
    nb = anc_below.shape[1]

    def body(*refs):
        pack_kernel(cb, nb, direct, *refs)

    return pl.pallas_call(
        body,
        name="pack",
        out_shape=heads + [tails],
        in_specs=spaces(3, pltpu.SMEM) + spaces(1, pltpu.VMEM),
        out_specs=spaces(len(heads), pltpu.VMEM) + spaces(1, pl.ANY),
        scratch_shapes=[
            pltpu.SMEM((leaves,), jnp.int32),
            pltpu.SMEM((leaves,), jnp.int32),
            pltpu.SMEM((leaves * SLOTS,), jnp.int32),
            pltpu.SMEM((leaves * SLOTS * CODES,), jnp.int32),
            pltpu.SemaphoreType.DMA((leaves, SLOTS)),
        ],
    )(row_map.T, anc_order, anc_below, desc_panel)


def diagonal_kernel(cb, leaves, *refs):
    heads = refs[:-4]
    out, codes, left, right = refs[-4:]
    direct = len(heads) > 1
    rows = out.shape[1]
    group = min(leaves, 8)

    def load(index, start, size):
        if direct:
            return heads[index][pl.ds(start, size)]
        return heads[0][index, pl.ds(start, size)]

    lane = lax.broadcasted_iota(jnp.int32, (1, rows), 1)

    def step(base):
        for offset in range(group):
            marks = load(base + offset, SLOTS * rows, CODE_ROWS).astype(jnp.float32)
            packed = jnp.zeros((1, rows), jnp.float32)
            for entry in range(SLOTS * CODES):
                packed = jnp.where(lane == entry, marks[entry:entry + 1], packed)
            codes[pl.ds(base + offset, 1)] = packed.astype(jnp.int32)
            for slot in range(SLOTS):
                block = load(base + offset, slot * rows, rows)
                lanes = pl.ds((offset * SLOTS + slot) * rows, rows)
                code = jnp.broadcast_to(marks[slot * CODES:slot * CODES + 1], (rows, rows))
                code = code.astype(block.dtype)
                zero = jnp.zeros_like(block)
                right[:, lanes] = jnp.where(code < cb, block, zero)
                for c in range(cb):
                    left[c * rows:(c + 1) * rows, lanes] = jnp.where(code == c, block, zero)
        return lax.dot_general(
            left[...], right[...], (((1,), (1,)), ((), ())), preferred_element_type=jnp.float32
        )

    if leaves == group:
        out[...] = step(0).reshape(out.shape)
    else:
        out[...] = jnp.zeros_like(out)

        def accumulate(index, carry):
            out[...] += step(index * group).reshape(out.shape)
            return carry

        lax.fori_loop(0, leaves // group, accumulate, 0)


def diagonal_update(heads, cb, leaves, rows):
    group = min(leaves, 8)

    def body(*refs):
        diagonal_kernel(cb, leaves, *refs)

    return pl.pallas_call(
        body,
        name="diagonal",
        out_shape=[
            jax.ShapeDtypeStruct((cb * rows, rows), jnp.float32),
            jax.ShapeDtypeStruct((leaves, rows), jnp.int32),
        ],
        in_specs=spaces(len(heads), pltpu.VMEM),
        out_specs=spaces(2, pltpu.VMEM),
        scratch_shapes=[
            pltpu.VMEM((cb * rows, group * SLOTS * rows), heads[0].dtype),
            pltpu.VMEM((rows, group * SLOTS * rows), heads[0].dtype),
        ],
        cost_estimate=pl.CostEstimate(flops=2000000000, bytes_accessed=1000000, transcendentals=0),
    )(*heads)


def below_kernel(cb, blk_count, per, leaves, count, codes, tails, *refs):
    heads = refs[:count]
    outs = refs[count:count + blk_count]
    acc, products, sems = refs[count + blk_count:]
    direct = count > 1
    me_leaf = lax.axis_index("leaf")
    me_blk = lax.axis_index("blk")
    rows = acc.shape[1]
    group = min(leaves, 8)
    tail_rows = tails.shape[1] // SLOTS
    extra = tail_rows // rows
    trash = blk_count * cb * per

    def zero(index, carry):
        acc[pl.ds(index * cb, cb)] = jnp.zeros((cb, rows, rows), jnp.float32)
        return carry

    lax.fori_loop(0, blk_count * per, zero, 0)

    def step(base):
        for offset in range(group):
            index = base + offset
            source = jnp.bitwise_xor(me_leaf, index) if direct else index
            for slot in range(SLOTS):
                if direct:
                    head = heads[index][pl.ds(slot * rows, rows)]
                else:
                    head = heads[0][index, pl.ds(slot * rows, rows)]
                tail = tails[source, pl.ds(slot * tail_rows, tail_rows)]
                products[offset * SLOTS + slot] = lax.dot_general(
                    tail, head, (((1,), (1,)), ((), ())), preferred_element_type=jnp.float32
                )
        for offset in range(group):
            for slot in range(SLOTS):
                column = codes[base + offset, slot * CODES]
                for r in range(extra):
                    position = codes[base + offset, slot * CODES + 1 + r]
                    relative = jnp.bitwise_xor(lax.rem(position, blk_count), me_blk)
                    place = (relative * cb + column) * per + lax.div(position, blk_count)
                    place = jnp.where(column < cb, place, trash)
                    acc[place] += products[offset * SLOTS + slot, pl.ds(r * rows, rows)]

    if leaves == group:
        step(0)
    else:
        lax.fori_loop(0, leaves // group, lambda index, carry: (step(index * group), carry)[1], 0)
    transfers = [
        pltpu.make_async_copy(acc.at[pl.ds(x * cb * per, cb * per)], outs[x], sems.at[x])
        for x in range(blk_count)
    ]
    for transfer in reversed(transfers):
        transfer.start()
    for transfer in transfers:
        transfer.wait()


def below_update(heads, tails, codes, cb, blk_count, per, leaves, rows):
    group = min(leaves, 8)
    blocks = blk_count * cb * per

    def body(*refs):
        below_kernel(cb, blk_count, per, leaves, len(heads), *refs)

    return pl.pallas_call(
        body,
        name="below",
        out_shape=[jax.ShapeDtypeStruct((cb * per, rows, rows), jnp.float32)] * blk_count,
        in_specs=spaces(1, pltpu.SMEM) + spaces(1 + len(heads), pltpu.VMEM),
        out_specs=spaces(blk_count, pl.ANY),
        scratch_shapes=[
            pltpu.VMEM((blocks + 1, rows, rows), jnp.float32),
            pltpu.VMEM((group * SLOTS, tails.shape[1] // SLOTS, rows), jnp.float32),
            pltpu.SemaphoreType.DMA((blk_count,)),
        ],
        cost_estimate=pl.CostEstimate(flops=2000000000, bytes_accessed=4000000, transcendentals=0),
    )(codes, tails, *heads)


def factor_block(work, rows):
    lane = lax.broadcasted_iota(jnp.int32, (1, rows), 1)
    sub = lax.broadcasted_iota(jnp.int32, (PANEL, 1), 0)
    segments = 4
    size = rows // segments

    for segment in range(segments):
        top = segment * size

        def panel(index, carry):
            base = pl.multiple_of(top + index * PANEL, PANEL)
            strip = work[pl.ds(base, PANEL), :]
            picks = [(lane == base + k) for k in range(PANEL)]
            corner = [
                jnp.sum(jnp.where(picks[k], strip[:, :rows], 0.0), axis=1, keepdims=True)
                for k in range(PANEL)
            ]
            scales = []
            for k in range(PANEL):
                scale = lax.rsqrt(corner[k][k:k + 1])
                scales.append(scale)
                row = strip[k:k + 1] * scale
                low = jnp.where(sub > k, corner[k] * scale, 0.0)
                strip = jnp.where(sub == k, row, strip - low * row)
                for m in range(k, PANEL):
                    entry = corner[m][k:k + 1] * scale
                    corner[m] = jnp.where(sub == k, entry, corner[m] - low * entry)
            full = work[pl.ds(top, rows - top), :rows]
            work[pl.ds(base, PANEL), :] = strip
            rest = lax.broadcasted_iota(jnp.int32, (rows - top, 1), 0) + top >= base + PANEL
            total = jnp.zeros((rows - top, 2 * rows), jnp.float32)
            for k in reversed(range(PANEL)):
                solved = strip[k:k + 1] * scales[k]
                strip = strip - jnp.where(sub < k, corner[k], 0.0) * solved
                column = jnp.sum(jnp.where(picks[k], full, 0.0), axis=1, keepdims=True)
                total = total + jnp.where(rest, column, 0.0) * solved
            work[pl.ds(top, rows - top), :] -= total
            return carry

        lax.fori_loop(0, size // PANEL, panel, 0)


def eliminate(schur, inverses, work, block, cb, rows):
    eye = lax.broadcasted_iota(jnp.int32, (rows, rows), 0) == lax.broadcasted_iota(
        jnp.int32, (rows, rows), 1
    )
    upper = lax.broadcasted_iota(jnp.int32, (rows, rows), 0) <= lax.broadcasted_iota(
        jnp.int32, (rows, rows), 1
    )
    here = block * rows
    work[:, :rows] = schur[block, :, here:here + rows]
    work[:, rows:] = eye.astype(jnp.float32)
    factor_block(work, rows)
    schur[block, :, here:here + rows] = jnp.where(upper, work[:, :rows], 0.0)
    inverse = work[:, rows:]
    inverses[block] = inverse
    if block + 1 < cb:
        after = here + rows
        strip = lax.dot_general(
            inverse, schur[block, :, after:], (((1,), (0,)), ((), ())),
            precision=HIGHEST, preferred_element_type=jnp.float32,
        )
        schur[block, :, after:] = strip
        for other in range(block + 1, cb):
            offset = (other - block - 1) * rows
            schur[other, :, other * rows:] -= lax.dot_general(
                strip[:, offset:offset + rows], strip[:, offset:], (((0,), (0,)), ((), ())),
                precision=HIGHEST, preferred_element_type=jnp.float32,
            )


def first_factor(own_sum, other_sum, strips, cb, rows):
    blk_count = len(strips)

    def body(own_ref, other_ref, *refs):
        strip_refs = refs[:blk_count]
        schur, inverses, work = refs[blk_count:]
        me = lax.axis_index("blk")
        for x in range(blk_count):
            schur[jnp.bitwise_xor(me, x)] = strip_refs[x][...]
        for c in range(cb):
            part = slice(c * rows, (c + 1) * rows)
            schur[c, :, part] -= own_ref[part] + other_ref[part]
        for block in range(cb // SPLIT):
            eliminate(schur, inverses, work, block, cb, rows)

    return pl.pallas_call(
        body,
        name="factor_first",
        out_shape=[
            jax.ShapeDtypeStruct((cb, rows, cb * rows), jnp.float32),
            jax.ShapeDtypeStruct((cb, rows, rows), jnp.float32),
        ],
        in_specs=spaces(2 + blk_count, pltpu.VMEM),
        out_specs=spaces(2, pltpu.VMEM),
        scratch_shapes=[pltpu.VMEM((rows, 2 * rows), jnp.float32)],
        cost_estimate=pl.CostEstimate(flops=10000000000, bytes_accessed=2000000, transcendentals=0),
    )(own_sum, other_sum, *strips)


def last_factor(schur_in, inverses_in, cb, rows):
    width = cb * rows

    def body(schur_ref, inverses_ref, whole, lower, schur, inverses, work):
        me = lax.axis_index("blk")
        schur[...] = schur_ref[...]
        for block in range(cb // SPLIT):
            inverses[block] = inverses_ref[block]
        for block in range(cb // SPLIT, cb):
            eliminate(schur, inverses, work, block, cb, rows)
        for k in range(cb):
            piece = jnp.where(k <= me, schur[k, :, pl.ds(pl.multiple_of(me * rows, rows), rows)], 0.0)
            lower[:, k * rows:(k + 1) * rows] = piece.T
        whole[...] = jnp.zeros_like(whole)
        for i in range(cb):
            whole[i * rows:(i + 1) * rows, i * rows:(i + 1) * rows] = inverses[i]
            if i:
                done = slice(0, i * rows)
                total = jnp.zeros((rows, i * rows), jnp.float32)
                for k in range(i):
                    total = total + lax.dot_general(
                        schur[k, :, i * rows:(i + 1) * rows],
                        whole[k * rows:(k + 1) * rows, done],
                        (((0,), (0,)), ((), ())),
                        precision=HIGHEST, preferred_element_type=jnp.float32,
                    )
                whole[i * rows:(i + 1) * rows, done] = -lax.dot_general(
                    inverses[i], total, (((1,), (0,)), ((), ())),
                    precision=HIGHEST, preferred_element_type=jnp.float32,
                )

    return pl.pallas_call(
        body,
        name="factor_last",
        out_shape=[
            jax.ShapeDtypeStruct((width, width), jnp.float32),
            jax.ShapeDtypeStruct((rows, width), jnp.float32),
        ],
        in_specs=spaces(2, pltpu.VMEM),
        out_specs=spaces(2, pltpu.VMEM),
        scratch_shapes=[
            pltpu.VMEM((cb, rows, width), jnp.float32),
            pltpu.VMEM((cb, rows, rows), jnp.float32),
            pltpu.VMEM((rows, 2 * rows), jnp.float32),
        ],
        cost_estimate=pl.CostEstimate(flops=12000000000, bytes_accessed=2000000, transcendentals=0),
    )(schur_in, inverses_in)


def solve_rows(panel, kept, from_core, from_far, whole, lower, cb, per, rows):
    width = cb * rows

    def body(panel_ref, kept_ref, core_ref, far_ref, whole_ref, lower_ref, out):
        out[0] = lower_ref[...]
        parts = []
        for c in range(cb):
            block = slice(c * per, (c + 1) * per)
            original = panel_ref[1:, :, c * rows:(c + 1) * rows]
            update = kept_ref[block] + core_ref[block] + far_ref[block]
            parts.append((original - update).reshape(per * rows, rows))
        step = 2
        for j in range(0, cb, step):
            left = jnp.concatenate(parts[:j + step], axis=1)
            span = slice(j * rows, (j + step) * rows)
            value = lax.dot_general(
                left, whole_ref[span, :(j + step) * rows], (((1,), (1,)), ((), ())),
                precision=HIGHEST, preferred_element_type=jnp.float32,
            )
            out[1:, :, span] = value.reshape(per, rows, step * rows)

    return pl.pallas_call(
        body,
        name="solve",
        out_shape=jax.ShapeDtypeStruct((per + 1, rows, width), jnp.float32),
        in_specs=spaces(6, pltpu.VMEM),
        out_specs=pl.BlockSpec(memory_space=pltpu.VMEM),
        cost_estimate=pl.CostEstimate(flops=2000000000, bytes_accessed=5000000, transcendentals=0),
    )(panel, kept, from_core, from_far, whole, lower)


def shards(desc_panel, row_map, anc_order, anc_below, anc_panel):
    leaves = lax.axis_size("leaf")
    blk_count = lax.axis_size("blk")
    rows = anc_panel.shape[3]
    width = anc_panel.shape[4]
    cb = width // rows
    per = anc_below.shape[1] // blk_count
    assert cb == blk_count == 4 and desc_panel.shape[2] == rows
    direct = leaves <= DIRECT and leaves & (leaves - 1) == 0
    near = [(i, i ^ 1) for i in range(blk_count)]
    far = [(i, i ^ 2) for i in range(blk_count)]

    *heads, tails = pack(desc_panel, row_map, anc_order, anc_below, cb, direct)
    if direct:
        heads = [heads[0]] + [
            lax.ppermute(heads[k], "leaf", [(i, i ^ k) for i in range(leaves)])
            for k in range(1, leaves)
        ]
    else:
        heads = [lax.all_to_all(heads[0], "leaf", split_axis=0, concat_axis=0, tiled=True)]
    tails = lax.all_to_all(tails, "leaf", split_axis=0, concat_axis=0, tiled=True)

    panel = anc_panel.reshape(per + 1, rows, width)
    strip = panel[0]
    strip_far = lax.ppermute(strip, "blk", far)
    strip_near = lax.ppermute(strip, "blk", near)
    strip_both = lax.ppermute(strip_far, "blk", near)
    strips = [strip, strip_near, strip_far, strip_both]

    diagonal, codes = diagonal_update(heads, cb, leaves, rows)
    diagonal_near = lax.ppermute(diagonal, "blk", near)
    diagonal = diagonal + diagonal_near
    diagonal_far = lax.ppermute(diagonal, "blk", far)
    schur, inverses = first_factor(diagonal, diagonal_far, strips, cb, rows)

    kept, for_near, for_far, for_both = below_update(
        heads, tails, codes, cb, blk_count, per, leaves, rows
    )
    for_both = lax.ppermute(for_both, "blk", near)
    from_near = lax.ppermute(for_near, "blk", near)
    onward = for_far + for_both
    from_far = lax.ppermute(onward, "blk", far)
    whole, lower = last_factor(schur, inverses, cb, rows)
    out = solve_rows(panel, kept, from_near, from_far, whole, lower, cb, per, rows)
    return out.reshape(anc_panel.shape)


def solution(mesh):
    in_specs = (
        P(("leaf", "blk"), None, None),
        P(("leaf", "blk"), None),
        P(),
        P(),
        P("leaf", None, "blk", None, None),
    )
    out_specs = P("leaf", None, "blk", None, None)

    return jax.shard_map(shards, mesh=mesh, in_specs=in_specs, out_specs=out_specs, check_vma=False)
```

profile of v0, /device:TPU:0, one launch (start us, length us, event | category | flops | bytes accessed | tf_op | source)
XLA Modules:
  0.0 98.7 jit_solution(17965097134470394566)
XLA Ops:
  0.0 3.2 %pack.1 = (bf16[272,128]{1,0:T(8,128)(2,1)}, bf16[272,128]{1,0:T(8,128)(2,1)}, bf16[272,128]{1,0:T(8,128)(2,1)}, bf16[272,128]{1,0:T(8,128)(2,1)}, bf16[272,128]...) custom-call(s32[3,8]{1,0:T(4,128)} %bitcast.8, ...), custom_call_target="tpu_custom_call" | custom-call | tf_op jit(solution)/shard_map/pack/pallas_call | solution.py:138
  3.3 7.4 %all-to-all-start = ((bf16[8,512,128]{2,1,0:T(8,128)(2,1)}), bf16[8,512,128]{2,1,0:T(8,128)(2,1)S(1)}, u32[]{:S(2)}, u32[]{:S(2)}) async-start(bf16[8,512,128]{2,1,0:T(8,128)(2,1)} %get-tuple-element.33), calls=%async_computation | async-start | bytes 2097152 | tf_op jit(solution)/shard_map/all_to_all | solution.py:501
  10.7 2.0 %collective-permute-start = (bf16[272,128]{1,0:T(8,128)(2,1)S(1)}, bf16[272,128]{1,0:T(8,128)(2,1)S(1)}, u32[]{:S(2)}, u32[]{:S(2)}) collective-permute-start(bf16[272,128]{1,0:T(8,128)(2,1)S(1)} %copy-done.20), channel_id=1, source_target_pairs={{0,4},{4,0},{8,12},{12,8},{16,20},{20,16},{24,28},{28,24},{1,5},{5... | collective-permute-start | bytes 208904 | tf_op jit(solution)/shard_map/ppermute | solution.py:496
  12.7 1.5 %collective-permute-start.1 = (bf16[272,128]{1,0:T(8,128)(2,1)S(1)}, bf16[272,128]{1,0:T(8,128)(2,1)S(1)}, u32[]{:S(2)}, u32[]{:S(2)}) collective-permute-start(bf16[272,128]{1,0:T(8,128)(2,1)S(1)} %copy-done.19), channel_id=1, source_target_pairs={{0,8},{4,12},{8,0},{12,4},{16,24},{20,28},{24,16},{28,20},{1,9},{5... | collective-permute-start | bytes 208904 | tf_op jit(solution)/shard_map/ppermute | solution.py:496
  14.2 0.1 collective-permute-start.2
  14.3 2.8 %collective-permute-start.3 = (bf16[272,128]{1,0:T(8,128)(2,1)S(1)}, bf16[272,128]{1,0:T(8,128)(2,1)S(1)}, u32[]{:S(2)}, u32[]{:S(2)}) collective-permute-start(bf16[272,128]{1,0:T(8,128)(2,1)S(1)} %copy-done.17), channel_id=1, source_target_pairs={{0,16},{4,20},{8,24},{12,28},{16,0},{20,4},{24,8},{28,12},{1,17},{... | collective-permute-start | bytes 208904 | tf_op jit(solution)/shard_map/ppermute | solution.py:496
  17.1 1.5 %collective-permute-start.4 = (bf16[272,128]{1,0:T(8,128)(2,1)S(1)}, bf16[272,128]{1,0:T(8,128)(2,1)S(1)}, u32[]{:S(2)}, u32[]{:S(2)}) collective-permute-start(bf16[272,128]{1,0:T(8,128)(2,1)S(1)} %copy-done.16), channel_id=1, source_target_pairs={{0,20},{4,16},{8,28},{12,24},{16,4},{20,0},{24,12},{28,8},{1,21},{... | collective-permute-start | bytes 208904 | tf_op jit(solution)/shard_map/ppermute | solution.py:496
  18.6 2.7 %collective-permute-done.refs_1_.refs_3_ = bf16[272,128]{1,0:T(8,128)(2,1)S(1)} collective-permute-done((bf16[272,128]{1,0:T(8,128)(2,1)S(1)}, bf16[272,128]{1,0:T(8,128)(2,1)S(1)}, u32[]{:S(2)}, u32[]{:S(2)}) %collective-permute-start) | collective-permute-done | bytes 69664 | tf_op jit(solution)/shard_map/ppermute | solution.py:496
  21.3 2.7 %collective-permute-start.5 = (bf16[272,128]{1,0:T(8,128)(2,1)S(1)}, bf16[272,128]{1,0:T(8,128)(2,1)S(1)}, u32[]{:S(2)}, u32[]{:S(2)}) collective-permute-start(bf16[272,128]{1,0:T(8,128)(2,1)S(1)} %copy-done.15), channel_id=1, source_target_pairs={{0,24},{4,28},{8,16},{12,20},{16,8},{20,12},{24,0},{28,4},{1,25},{... | collective-permute-start | bytes 208904 | tf_op jit(solution)/shard_map/ppermute | solution.py:496
  24.0 6.4 %collective-permute-done.1.refs_2_.refs_4_ = bf16[272,128]{1,0:T(8,128)(2,1)S(1)} collective-permute-done((bf16[272,128]{1,0:T(8,128)(2,1)S(1)}, bf16[272,128]{1,0:T(8,128)(2,1)S(1)}, u32[]{:S(2)}, u32[]{:S(2)}) %collective-permute-start.1) | collective-permute-done | bytes 69664 | tf_op jit(solution)/shard_map/ppermute | solution.py:496
  30.5 4.6 %collective-permute-start.6 = (bf16[272,128]{1,0:T(8,128)(2,1)S(1)}, bf16[272,128]{1,0:T(8,128)(2,1)S(1)}, u32[]{:S(2)}, u32[]{:S(2)}) collective-permute-start(bf16[272,128]{1,0:T(8,128)(2,1)S(1)} %copy-done.14), channel_id=1, source_target_pairs={{0,28},{4,24},{8,20},{12,16},{16,12},{20,8},{24,4},{28,0},{1,29},{... | collective-permute-start | bytes 208904 | tf_op jit(solution)/shard_map/ppermute | solution.py:496
  35.0 1.0 slice_bitcast_fusion.refs_0_
  36.1 1.6 %collective-permute-start.13 = (f32[128,512]{1,0:T(8,128)S(1)}, f32[128,512]{1,0:T(8,128)S(1)}, u32[]{:S(2)}, u32[]{:S(2)}) collective-permute-start(f32[128,512]{1,0:T(8,128)S(1)} %slice_bitcast_fusion.refs_0_), channel_id=1, source_target_pairs={{0,2},{1,3},{2,0},{3,1},{4,6},{5,7},{6,4},{7,5},{8,10},{9,11},{10,... | collective-permute-start | bytes 786440 | tf_op jit(solution)/shard_map/ppermute | solution.py:505
  37.6 7.6 %collective-permute-done.3.refs_4_.refs_6_ = bf16[272,128]{1,0:T(8,128)(2,1)S(1)} collective-permute-done((bf16[272,128]{1,0:T(8,128)(2,1)S(1)}, bf16[272,128]{1,0:T(8,128)(2,1)S(1)}, u32[]{:S(2)}, u32[]{:S(2)}) %collective-permute-start.3) | collective-permute-done | bytes 69664 | tf_op jit(solution)/shard_map/ppermute | solution.py:496
  45.3 2.0 %collective-permute-done.4.refs_5_.refs_7_ = bf16[272,128]{1,0:T(8,128)(2,1)S(1)} collective-permute-done((bf16[272,128]{1,0:T(8,128)(2,1)S(1)}, bf16[272,128]{1,0:T(8,128)(2,1)S(1)}, u32[]{:S(2)}, u32[]{:S(2)}) %collective-permute-start.4) | collective-permute-done | bytes 69664 | tf_op jit(solution)/shard_map/ppermute | solution.py:496
  47.3 0.6 copy-done.11
  48.0 2.6 %diagonal.1 = (f32[512,128]{1,0:T(8,128)}, s32[8,128]{1,0:T(8,128)}) custom-call(bf16[272,128]{1,0:T(8,128)(2,1)} %get-tuple-element.24.refs_0_.refs_2_, bf16[272,128]{1,0:T(8,128)(2,1)} %copy-done.7, bf16[272,128]{1,0:T(8,128)(2,1)} %copy-done.8, bf16[272,128]{1,0:T(8,128)(2,1)} %copy-done.9, bf16[272,128]{1,0:T(8,128)(2,1)} %copy-done.10, ...), custom_call_target="tpu_custom_call" | custom-call | flops 2000000000 | bytes 1000000 | tf_op jit(solution)/shard_map/diagonal/pallas_call | solution.py:206
  50.6 0.5 collective-permute-start.12
  51.1 0.1 collective-permute-start.14
  51.2 1.1 %collective-permute-done.10 = f32[512,128]{1,0:T(8,128)S(1)} collective-permute-done((f32[512,128]{1,0:T(8,128)}, f32[512,128]{1,0:T(8,128)S(1)}, u32[]{:S(2)}, u32[]{:S(2)}) %collective-permute-start.10) | collective-permute-done | bytes 262176 | tf_op jit(solution)/shard_map/ppermute | solution.py:511
  52.3 1.0 %add.7.own_ref = f32[512,128]{1,0:T(8,128)S(1)} add(f32[512,128]{1,0:T(8,128)} %get-tuple-element.38, f32[512,128]{1,0:T(8,128)S(1)} %collective-permute-done.10) | non-fusion elementwise | flops 65536 | bytes 786432 | tf_op jit(solution)/shard_map/add | solution.py:512
  53.3 1.6 %collective-permute-start.11 = (f32[512,128]{1,0:T(8,128)S(1)}, f32[512,128]{1,0:T(8,128)}, u32[]{:S(2)}, u32[]{:S(2)}) collective-permute-start(f32[512,128]{1,0:T(8,128)S(1)} %add.7.own_ref), channel_id=1, source_target_pairs={{0,2},{1,3},{2,0},{3,1},{4,6},{5,7},{6,4},{7,5},{8,10},{9,11},{10,... | collective-permute-start | bytes 786440 | tf_op jit(solution)/shard_map/ppermute | solution.py:513
  54.9 1.0 copy-done
  55.9 3.7 %below.1 = (f32[12,128,128]{2,1,0:T(8,128)}, f32[12,128,128]{2,1,0:T(8,128)}, f32[12,128,128]{2,1,0:T(8,128)}, f32[12,128,128]{2,1,0:T(8,128)}) custom-call(s32[8,128]{1,0:T(8,128)} %get-tuple-element.32.refs_0_, bf16[8,512,128]{2,1,0:T(8,128)(2,1)} %copy-done, bf16[272,128]{1,0:T(8,128)(2,1)} %get-tuple-element.24.refs_0_.refs_2_, ...), custom_call_target="tpu_custom_call" | custom-call | flops 2000000000 | bytes 4000000 | tf_op jit(solution)/shard_map/below/pallas_call | solution.py:286
  59.7 2.1 %collective-permute-done.11.other_ref = f32[512,128]{1,0:T(8,128)} collective-permute-done((f32[512,128]{1,0:T(8,128)S(1)}, f32[512,128]{1,0:T(8,128)}, u32[]{:S(2)}, u32[]{:S(2)}) %collective-permute-start.11) | collective-permute-done | bytes 262176 | tf_op jit(solution)/shard_map/ppermute | solution.py:513
  61.8 11.4 %factor_first.1 = (f32[4,128,512]{2,1,0:T(8,128)}, f32[4,128,128]{2,1,0:T(8,128)}) custom-call(f32[512,128]{1,0:T(8,128)} %copy-done.2, f32[512,128]{1,0:T(8,128)} %collective-permute-done.11.other_ref, f32[128,512]{1,0:T(8,128)} %copy-done.3, f32[128,512]{1,0:T(8,128)} %collective-permute-done.12.refs_1_, f32[128,512]{1,0:T(8,128)} %copy-done.6, ...), custom_call_target="tpu_custom_call" | custom-call | flops 10000000000 | bytes 2000000 | tf_op jit(solution)/shard_map/factor_first/pallas_call | solution.py:387
  73.3 0.1 add.6
  73.4 1.6 %collective-permute-start.9 = (f32[12,128,128]{2,1,0:T(8,128)S(1)}, f32[12,128,128]{2,1,0:T(8,128)S(1)}, u32[]{:S(2)}, u32[]{:S(2)}) collective-permute-start(f32[12,128,128]{2,1,0:T(8,128)S(1)} %add.6), channel_id=1, source_target_pairs={{0,2},{1,3},{2,0},{3,1},{4,6},{5,7},{6,4},{7,5},{8,10},{9,11},{10,... | collective-permute-start | bytes 2359304 | tf_op jit(solution)/shard_map/ppermute | solution.py:522
  75.0 12.7 %factor_last.1 = (f32[512,512]{1,0:T(8,128)}, f32[128,512]{1,0:T(8,128)}) custom-call(f32[4,128,512]{2,1,0:T(8,128)} %get-tuple-element.39.schur_ref, f32[4,128,128]{2,1,0:T(8,128)} %get-tuple-element.40.inverses_ref), custom_call_target="tpu_custom_call" | custom-call | flops 12000000000 | bytes 2000000 | tf_op jit(solution)/shard_map/factor_last/pallas_call | solution.py:432
  87.7 5.7 %collective-permute-done.9.far_ref = f32[12,128,128]{2,1,0:T(8,128)S(1)} collective-permute-done((f32[12,128,128]{2,1,0:T(8,128)S(1)}, f32[12,128,128]{2,1,0:T(8,128)S(1)}, u32[]{:S(2)}, u32[]{:S(2)}) %collective-permute-start.9) | collective-permute-done | bytes 786464 | tf_op jit(solution)/shard_map/ppermute | solution.py:522
  93.4 0.9 copy-done.5
  94.3 4.4 %solve.1 = f32[4,128,512]{2,1,0:T(8,128)} custom-call(f32[4,128,512]{2,1,0:T(8,128)} %bitcast.7, f32[12,128,128]{2,1,0:T(8,128)} %get-tuple-element.34.kept_ref, f32[12,128,128]{2,1,0:T(8,128)} %collective-permute-done.7.core_ref, f32[12,128,128]{2,1,0:T(8,128)} %copy-done.5, f32[512,512]{1,0:T(8,128)} %get-tuple-element.41.whole_ref, ...), custom_call_target="tpu_custom_call" | custom-call | flops 2000000000 | bytes 5000000 | tf_op jit(solution)/shard_map/solve/pallas_call | solution.py:471
  (51 shorter events, 0.2 us)
Async XLA Ops:
  3.2 7.5 %copy-start.20 = (bf16[272,128]{1,0:T(8,128)(2,1)S(1)}, bf16[272,128]{1,0:T(8,128)(2,1)}, u32[]{:S(2)}) copy-start(bf16[272,128]{1,0:T(8,128)(2,1)} %get-tuple-element.25) | copy-start | bytes 208900
  3.2 9.5 %copy-start.19 = (bf16[272,128]{1,0:T(8,128)(2,1)S(1)}, bf16[272,128]{1,0:T(8,128)(2,1)}, u32[]{:S(2)}) copy-start(bf16[272,128]{1,0:T(8,128)(2,1)} %get-tuple-element.26) | copy-start | bytes 208900
  3.2 11.0 %copy-start.18 = (bf16[272,128]{1,0:T(8,128)(2,1)S(1)}, bf16[272,128]{1,0:T(8,128)(2,1)}, u32[]{:S(2)}) copy-start(bf16[272,128]{1,0:T(8,128)(2,1)} %get-tuple-element.27) | copy-start | bytes 208900
  3.2 11.0 %copy-start.17 = (bf16[272,128]{1,0:T(8,128)(2,1)S(1)}, bf16[272,128]{1,0:T(8,128)(2,1)}, u32[]{:S(2)}) copy-start(bf16[272,128]{1,0:T(8,128)(2,1)} %get-tuple-element.28) | copy-start | bytes 208900
  3.2 13.9 %copy-start.16 = (bf16[272,128]{1,0:T(8,128)(2,1)S(1)}, bf16[272,128]{1,0:T(8,128)(2,1)}, u32[]{:S(2)}) copy-start(bf16[272,128]{1,0:T(8,128)(2,1)} %get-tuple-element.29) | copy-start | bytes 208900
  3.2 18.1 %copy-start.15 = (bf16[272,128]{1,0:T(8,128)(2,1)S(1)}, bf16[272,128]{1,0:T(8,128)(2,1)}, u32[]{:S(2)}) copy-start(bf16[272,128]{1,0:T(8,128)(2,1)} %get-tuple-element.30) | copy-start | bytes 208900
  3.3 27.2 %copy-start.14 = (bf16[272,128]{1,0:T(8,128)(2,1)S(1)}, bf16[272,128]{1,0:T(8,128)(2,1)}, u32[]{:S(2)}) copy-start(bf16[272,128]{1,0:T(8,128)(2,1)} %get-tuple-element.31) | copy-start | bytes 208900
  3.3 51.6 %all-to-all-start = ((bf16[8,512,128]{2,1,0:T(8,128)(2,1)}), bf16[8,512,128]{2,1,0:T(8,128)(2,1)S(1)}, u32[]{:S(2)}, u32[]{:S(2)}) async-start(bf16[8,512,128]{2,1,0:T(8,128)(2,1)} %get-tuple-element.33), calls=%async_computation | async-start | bytes 2097152 | tf_op jit(solution)/shard_map/all_to_all | solution.py:501
  10.7 10.6 %collective-permute-start = (bf16[272,128]{1,0:T(8,128)(2,1)S(1)}, bf16[272,128]{1,0:T(8,128)(2,1)S(1)}, u32[]{:S(2)}, u32[]{:S(2)}) collective-permute-start(bf16[272,128]{1,0:T(8,128)(2,1)S(1)} %copy-done.20), channel_id=1, source_target_pairs={{0,4},{4,0},{8,12},{12,8},{16,20},{20,16},{24,28},{28,24},{1,5},{5... | collective-permute-start | bytes 208904 | tf_op jit(solution)/shard_map/ppermute | solution.py:496
  12.7 17.7 %collective-permute-start.1 = (bf16[272,128]{1,0:T(8,128)(2,1)S(1)}, bf16[272,128]{1,0:T(8,128)(2,1)S(1)}, u32[]{:S(2)}, u32[]{:S(2)}) collective-permute-start(bf16[272,128]{1,0:T(8,128)(2,1)S(1)} %copy-done.19), channel_id=1, source_target_pairs={{0,8},{4,12},{8,0},{12,4},{16,24},{20,28},{24,16},{28,20},{1,9},{5... | collective-permute-start | bytes 208904 | tf_op jit(solution)/shard_map/ppermute | solution.py:496
  14.2 21.9 %collective-permute-start.2 = (bf16[272,128]{1,0:T(8,128)(2,1)S(1)}, bf16[272,128]{1,0:T(8,128)(2,1)S(1)}, u32[]{:S(2)}, u32[]{:S(2)}) collective-permute-start(bf16[272,128]{1,0:T(8,128)(2,1)S(1)} %copy-done.18), channel_id=1, source_target_pairs={{0,12},{4,8},{8,4},{12,0},{16,28},{20,24},{24,20},{28,16},{1,13},{... | collective-permute-start | bytes 208904 | tf_op jit(solution)/shard_map/ppermute | solution.py:496
  14.3 31.0 %collective-permute-start.3 = (bf16[272,128]{1,0:T(8,128)(2,1)S(1)}, bf16[272,128]{1,0:T(8,128)(2,1)S(1)}, u32[]{:S(2)}, u32[]{:S(2)}) collective-permute-start(bf16[272,128]{1,0:T(8,128)(2,1)S(1)} %copy-done.17), channel_id=1, source_target_pairs={{0,16},{4,20},{8,24},{12,28},{16,0},{20,4},{24,8},{28,12},{1,17},{... | collective-permute-start | bytes 208904 | tf_op jit(solution)/shard_map/ppermute | solution.py:496
  17.1 30.2 %collective-permute-start.4 = (bf16[272,128]{1,0:T(8,128)(2,1)S(1)}, bf16[272,128]{1,0:T(8,128)(2,1)S(1)}, u32[]{:S(2)}, u32[]{:S(2)}) collective-permute-start(bf16[272,128]{1,0:T(8,128)(2,1)S(1)} %copy-done.16), channel_id=1, source_target_pairs={{0,20},{4,16},{8,28},{12,24},{16,4},{20,0},{24,12},{28,8},{1,21},{... | collective-permute-start | bytes 208904 | tf_op jit(solution)/shard_map/ppermute | solution.py:496
  21.3 14.7 %copy-start.7 = (bf16[272,128]{1,0:T(8,128)(2,1)}, bf16[272,128]{1,0:T(8,128)(2,1)S(1)}, u32[]{:S(2)}) copy-start(bf16[272,128]{1,0:T(8,128)(2,1)S(1)} %collective-permute-done.refs_1_.refs_3_) | copy-start | bytes 208900
  21.3 26.0 %collective-permute-start.5 = (bf16[272,128]{1,0:T(8,128)(2,1)S(1)}, bf16[272,128]{1,0:T(8,128)(2,1)S(1)}, u32[]{:S(2)}, u32[]{:S(2)}) collective-permute-start(bf16[272,128]{1,0:T(8,128)(2,1)S(1)} %copy-done.15), channel_id=1, source_target_pairs={{0,24},{4,28},{8,16},{12,20},{16,8},{20,12},{24,0},{28,4},{1,25},{... | collective-permute-start | bytes 208904 | tf_op jit(solution)/shard_map/ppermute | solution.py:496
  30.4 5.6 %copy-start.8 = (bf16[272,128]{1,0:T(8,128)(2,1)}, bf16[272,128]{1,0:T(8,128)(2,1)S(1)}, u32[]{:S(2)}) copy-start(bf16[272,128]{1,0:T(8,128)(2,1)S(1)} %collective-permute-done.1.refs_2_.refs_4_) | copy-start | bytes 208900
  30.5 16.8 %collective-permute-start.6 = (bf16[272,128]{1,0:T(8,128)(2,1)S(1)}, bf16[272,128]{1,0:T(8,128)(2,1)S(1)}, u32[]{:S(2)}, u32[]{:S(2)}) collective-permute-start(bf16[272,128]{1,0:T(8,128)(2,1)S(1)} %copy-done.14), channel_id=1, source_target_pairs={{0,28},{4,24},{8,20},{12,16},{16,12},{20,8},{24,4},{28,0},{1,29},{... | collective-permute-start | bytes 208904 | tf_op jit(solution)/shard_map/ppermute | solution.py:496
  36.0 14.5 %copy-start.3 = (f32[128,512]{1,0:T(8,128)}, f32[128,512]{1,0:T(8,128)S(1)}, u32[]{:S(2)}) copy-start(f32[128,512]{1,0:T(8,128)S(1)} %slice_bitcast_fusion.refs_0_) | copy-start | bytes 786436
  36.0 11.2 %copy-start.9 = (bf16[272,128]{1,0:T(8,128)(2,1)}, bf16[272,128]{1,0:T(8,128)(2,1)S(1)}, u32[]{:S(2)}) copy-start(bf16[272,128]{1,0:T(8,128)(2,1)S(1)} %collective-permute-done.2.refs_3_.refs_5_) | copy-start | bytes 208900
  36.1 15.0 %collective-permute-start.13 = (f32[128,512]{1,0:T(8,128)S(1)}, f32[128,512]{1,0:T(8,128)S(1)}, u32[]{:S(2)}, u32[]{:S(2)}) collective-permute-start(f32[128,512]{1,0:T(8,128)S(1)} %slice_bitcast_fusion.refs_0_), channel_id=1, source_target_pairs={{0,2},{1,3},{2,0},{3,1},{4,6},{5,7},{6,4},{7,5},{8,10},{9,11},{10,... | collective-permute-start | bytes 786440 | tf_op jit(solution)/shard_map/ppermute | solution.py:505
  45.3 2.0 %copy-start.10 = (bf16[272,128]{1,0:T(8,128)(2,1)}, bf16[272,128]{1,0:T(8,128)(2,1)S(1)}, u32[]{:S(2)}) copy-start(bf16[272,128]{1,0:T(8,128)(2,1)S(1)} %collective-permute-done.3.refs_4_.refs_6_) | copy-start | bytes 208900
  50.6 1.7 %collective-permute-start.10 = (f32[512,128]{1,0:T(8,128)}, f32[512,128]{1,0:T(8,128)S(1)}, u32[]{:S(2)}, u32[]{:S(2)}) collective-permute-start(f32[512,128]{1,0:T(8,128)} %get-tuple-element.38), channel_id=1, source_target_pairs={{0,1},{1,0},{2,3},{3,2},{4,5},{5,4},{6,7},{7,6},{8,9},{9,8},{10,11... | collective-permute-start | bytes 786440 | tf_op jit(solution)/shard_map/ppermute | solution.py:511
  50.6 9.2 %collective-permute-start.12 = (f32[128,512]{1,0:T(8,128)S(1)}, f32[128,512]{1,0:T(8,128)}, u32[]{:S(2)}, u32[]{:S(2)}) collective-permute-start(f32[128,512]{1,0:T(8,128)S(1)} %slice_bitcast_fusion.refs_0_), channel_id=1, source_target_pairs={{0,1},{1,0},{2,3},{3,2},{4,5},{5,4},{6,7},{7,6},{8,9},{9,8},{10,11... | collective-permute-start | bytes 786440 | tf_op jit(solution)/shard_map/ppermute | solution.py:506
  51.1 2.2 %copy-start.6 = (f32[128,512]{1,0:T(8,128)}, f32[128,512]{1,0:T(8,128)S(1)}, u32[]{:S(2)}) copy-start(f32[128,512]{1,0:T(8,128)S(1)} %collective-permute-done.13.refs_2_) | copy-start | bytes 786436
  51.1 8.7 %collective-permute-start.14 = (f32[128,512]{1,0:T(8,128)S(1)}, f32[128,512]{1,0:T(8,128)}, u32[]{:S(2)}, u32[]{:S(2)}) collective-permute-start(f32[128,512]{1,0:T(8,128)S(1)} %collective-permute-done.13.refs_2_), channel_id=1, source_target_pairs={{0,1},{1,0},{2,3},{3,2},{4,5},{5,4},{6,7},{7,6},{8,9},{9,8},{10,11... | collective-permute-start | bytes 786440 | tf_op jit(solution)/shard_map/ppermute | solution.py:507
  53.3 6.3 %copy-start.2 = (f32[512,128]{1,0:T(8,128)}, f32[512,128]{1,0:T(8,128)S(1)}, u32[]{:S(2)}) copy-start(f32[512,128]{1,0:T(8,128)S(1)} %add.7.own_ref) | copy-start | bytes 786436
  53.3 8.5 %collective-permute-start.11 = (f32[512,128]{1,0:T(8,128)S(1)}, f32[512,128]{1,0:T(8,128)}, u32[]{:S(2)}, u32[]{:S(2)}) collective-permute-start(f32[512,128]{1,0:T(8,128)S(1)} %add.7.own_ref), channel_id=1, source_target_pairs={{0,2},{1,3},{2,0},{3,1},{4,6},{5,7},{6,4},{7,5},{8,10},{9,11},{10,... | collective-permute-start | bytes 786440 | tf_op jit(solution)/shard_map/ppermute | solution.py:513
  59.6 13.7 %copy-start.4 = (f32[12,128,128]{2,1,0:T(8,128)S(1)}, f32[12,128,128]{2,1,0:T(8,128)}, u32[]{:S(2)}) copy-start(f32[12,128,128]{2,1,0:T(8,128)} %get-tuple-element.35) | copy-start | bytes 2359300
  59.6 13.7 %copy-start.1 = (f32[12,128,128]{2,1,0:T(8,128)S(1)}, f32[12,128,128]{2,1,0:T(8,128)}, u32[]{:S(2)}) copy-start(f32[12,128,128]{2,1,0:T(8,128)} %get-tuple-element.36) | copy-start | bytes 2359300
  59.6 13.6 %collective-permute-start.8 = (f32[12,128,128]{2,1,0:T(8,128)}, f32[12,128,128]{2,1,0:T(8,128)S(1)}, u32[]{:S(2)}, u32[]{:S(2)}) collective-permute-start(f32[12,128,128]{2,1,0:T(8,128)} %get-tuple-element.37), channel_id=1, source_target_pairs={{0,1},{1,0},{2,3},{3,2},{4,5},{5,4},{6,7},{7,6},{8,9},{9,8},{10,11... | collective-permute-start | bytes 2359304 | tf_op jit(solution)/shard_map/ppermute | solution.py:519
  73.3 14.4 %collective-permute-start.7 = (f32[12,128,128]{2,1,0:T(8,128)S(1)}, f32[12,128,128]{2,1,0:T(8,128)}, u32[]{:S(2)}, u32[]{:S(2)}) collective-permute-start(f32[12,128,128]{2,1,0:T(8,128)S(1)} %copy-done.4), channel_id=1, source_target_pairs={{0,1},{1,0},{2,3},{3,2},{4,5},{5,4},{6,7},{7,6},{8,9},{9,8},{10,11... | collective-permute-start | bytes 2359304 | tf_op jit(solution)/shard_map/ppermute | solution.py:520
  73.4 20.0 %collective-permute-start.9 = (f32[12,128,128]{2,1,0:T(8,128)S(1)}, f32[12,128,128]{2,1,0:T(8,128)S(1)}, u32[]{:S(2)}, u32[]{:S(2)}) collective-permute-start(f32[12,128,128]{2,1,0:T(8,128)S(1)} %add.6), channel_id=1, source_target_pairs={{0,2},{1,3},{2,0},{3,1},{4,6},{5,7},{6,4},{7,5},{8,10},{9,11},{10,... | collective-permute-start | bytes 2359304 | tf_op jit(solution)/shard_map/ppermute | solution.py:522
  (5 other events, 3.8 us)
where the time goes:
time: 99.1 us; the launch traced here: 98.7 us
  Pallas kernels  38.1 us (38%)
  starting transfers between devices  28 us (28%)
  waiting for transfers between devices  27.7 us (28%)
  local copies, waits for them, and re-layouts  3.56 us (4%)
  other arithmetic  1.08 us (1%)
    ppermute x7, waiting for transfers between devices, shards(): lax.ppermute(heads[k], 'leaf', [(i, i ^ k) for i in range(leaves)])  18.8 us
    ppermute x7, starting transfers between devices, shards(): lax.ppermute(heads[k], 'leaf', [(i, i ^ k) for i in range(leaves)])  15.2 us
    pallas_call x1, Pallas kernels, last_factor(): pl.pallas_call(body, name='factor_last', out_shape=[jax.ShapeDtypeStruct(...  12.7 us
    pallas_call x1, Pallas kernels, first_factor(): pl.pallas_call(body, name='factor_first', out_shape=[jax.ShapeDtypeStruct...  11.4 us
    all_to_all x1, starting transfers between devices, shards(): lax.all_to_all(tails, 'leaf', split_axis=0, concat_axis=0, tiled=True)  7.42 us
    ppermute x1, waiting for transfers between devices, shards(): from_far = lax.ppermute(onward, 'blk', far)  5.72 us
    pallas_call x1, Pallas kernels, solve_rows(): pl.pallas_call(body, name='solve', out_shape=jax.ShapeDtypeStruct((per +...  4.43 us
    pallas_call x1, Pallas kernels, below_update(): pl.pallas_call(body, name='below', out_shape=[jax.ShapeDtypeStruct((cb *...  3.74 us
  transfers between devices with their start and end apart: 16, of which 7 were waited for; matrix products, arithmetic and copies ran while one was open for 2% of the time, Pallas kernels for 31%

commit v1 on v0

--- a/solution.py
+++ b/solution.py
@@ -11,6 +11,7 @@
 CODE_ROWS = 16
 PANEL = 8
 SPLIT = 2
+HALVES = 2
 DIRECT = 8
 HIGHEST = lax.Precision.HIGHEST
 
@@ -220,10 +221,10 @@
     )(*heads)
 
 
-def below_kernel(cb, blk_count, per, leaves, count, codes, tails, *refs):
+def below_kernel(cb, blk_count, per, leaves, count, codes, tails_hbm, *refs):
     heads = refs[:count]
-    outs = refs[count:count + blk_count]
-    acc, products, sems = refs[count + blk_count:]
+    outs = refs[count:count + blk_count * HALVES]
+    acc, products, tails, sems = refs[count + blk_count * HALVES:]
     direct = count > 1
     me_leaf = lax.axis_index("leaf")
     me_blk = lax.axis_index("blk")
@@ -231,24 +232,32 @@
     group = min(leaves, 8)
     tail_rows = tails.shape[1] // SLOTS
     extra = tail_rows // rows
-    trash = blk_count * cb * per
-
-    def zero(index, carry):
-        acc[pl.ds(index * cb, cb)] = jnp.zeros((cb, rows, rows), jnp.float32)
-        return carry
-
-    lax.fori_loop(0, blk_count * per, zero, 0)
+    blocks = blk_count * cb * per
+
+    def source(index):
+        return jnp.bitwise_xor(me_leaf, index) if direct else index
+
+    def fetch(index, slot):
+        return pltpu.make_async_copy(tails_hbm.at[source(index)], tails.at[slot], sems.at[slot])
 
     def step(base):
         for offset in range(group):
+            fetch(base + offset, offset).start()
+
+        @pl.when(base == 0)
+        def _():
+            for first in range(0, blocks, cb):
+                acc[pl.ds(first, cb)] = jnp.zeros((cb, rows, rows), jnp.float32)
+
+        for offset in range(group):
             index = base + offset
-            source = jnp.bitwise_xor(me_leaf, index) if direct else index
+            fetch(index, offset).wait()
             for slot in range(SLOTS):
                 if direct:
                     head = heads[index][pl.ds(slot * rows, rows)]
                 else:
                     head = heads[0][index, pl.ds(slot * rows, rows)]
-                tail = tails[source, pl.ds(slot * tail_rows, tail_rows)]
+                tail = tails[offset, pl.ds(slot * tail_rows, tail_rows)]
                 products[offset * SLOTS + slot] = lax.dot_general(
                     tail, head, (((1,), (1,)), ((), ())), preferred_element_type=jnp.float32
                 )
@@ -259,26 +268,22 @@
                     position = codes[base + offset, slot * CODES + 1 + r]
                     relative = jnp.bitwise_xor(lax.rem(position, blk_count), me_blk)
                     place = (relative * cb + column) * per + lax.div(position, blk_count)
-                    place = jnp.where(column < cb, place, trash)
+                    place = jnp.where(column < cb, place, blocks)
                     acc[place] += products[offset * SLOTS + slot, pl.ds(r * rows, rows)]
 
     if leaves == group:
         step(0)
     else:
         lax.fori_loop(0, leaves // group, lambda index, carry: (step(index * group), carry)[1], 0)
-    transfers = [
-        pltpu.make_async_copy(acc.at[pl.ds(x * cb * per, cb * per)], outs[x], sems.at[x])
-        for x in range(blk_count)
-    ]
-    for transfer in reversed(transfers):
-        transfer.start()
-    for transfer in transfers:
-        transfer.wait()
+    size = cb * per // HALVES
+    for part, out in enumerate(outs):
+        out[...] = acc[pl.ds(part * size, size)]
 
 
 def below_update(heads, tails, codes, cb, blk_count, per, leaves, rows):
     group = min(leaves, 8)
     blocks = blk_count * cb * per
+    outs = blk_count * HALVES
 
     def body(*refs):
         below_kernel(cb, blk_count, per, leaves, len(heads), *refs)
@@ -286,13 +291,14 @@
     return pl.pallas_call(
         body,
         name="below",
-        out_shape=[jax.ShapeDtypeStruct((cb * per, rows, rows), jnp.float32)] * blk_count,
-        in_specs=spaces(1, pltpu.SMEM) + spaces(1 + len(heads), pltpu.VMEM),
-        out_specs=spaces(blk_count, pl.ANY),
+        out_shape=[jax.ShapeDtypeStruct((cb * per // HALVES, rows, rows), jnp.float32)] * outs,
+        in_specs=spaces(1, pltpu.SMEM) + spaces(1, pl.ANY) + spaces(len(heads), pltpu.VMEM),
+        out_specs=spaces(outs, pltpu.VMEM),
         scratch_shapes=[
             pltpu.VMEM((blocks + 1, rows, rows), jnp.float32),
             pltpu.VMEM((group * SLOTS, tails.shape[1] // SLOTS, rows), jnp.float32),
-            pltpu.SemaphoreType.DMA((blk_count,)),
+            pltpu.VMEM((group,) + tails.shape[1:], tails.dtype),
+            pltpu.SemaphoreType.DMA((group,)),
         ],
         cost_estimate=pl.CostEstimate(flops=2000000000, bytes_accessed=4000000, transcendentals=0),
     )(codes, tails, *heads)
@@ -447,35 +453,77 @@
     )(schur_in, inverses_in)
 
 
-def solve_rows(panel, kept, from_core, from_far, whole, lower, cb, per, rows):
+def solve_dot(left, right):
+    return lax.dot_general(
+        left, right, (((1,), (1,)), ((), ())),
+        precision=HIGHEST, preferred_element_type=jnp.float32,
+    )
+
+
+def remaining(panel_ref, update_refs, half, cb, per, rows):
+    parts = []
+    for c in range(cb // HALVES):
+        column = (half * (cb // HALVES) + c) * rows
+        block = slice(c * per, (c + 1) * per)
+        update = update_refs[0][block]
+        for ref in update_refs[1:]:
+            update = update + ref[block]
+        original = panel_ref[1:, :, column:column + rows]
+        parts.append((original - update).reshape(per * rows, rows))
+    return jnp.concatenate(parts, axis=1)
+
+
+def solve_left(panel, updates, whole, lower, cb, per, rows):
     width = cb * rows
-
-    def body(panel_ref, kept_ref, core_ref, far_ref, whole_ref, lower_ref, out):
+    half = width // HALVES
+
+    def body(panel_ref, *refs):
+        updates_ref = refs[:len(updates)]
+        whole_ref, lower_ref, out, carried = refs[len(updates):]
+        left = remaining(panel_ref, updates_ref, 0, cb, per, rows)
         out[0] = lower_ref[...]
-        parts = []
-        for c in range(cb):
-            block = slice(c * per, (c + 1) * per)
-            original = panel_ref[1:, :, c * rows:(c + 1) * rows]
-            update = kept_ref[block] + core_ref[block] + far_ref[block]
-            parts.append((original - update).reshape(per * rows, rows))
-        step = 2
-        for j in range(0, cb, step):
-            left = jnp.concatenate(parts[:j + step], axis=1)
-            span = slice(j * rows, (j + step) * rows)
-            value = lax.dot_general(
-                left, whole_ref[span, :(j + step) * rows], (((1,), (1,)), ((), ())),
-                precision=HIGHEST, preferred_element_type=jnp.float32,
-            )
-            out[1:, :, span] = value.reshape(per, rows, step * rows)
-
-    return pl.pallas_call(
-        body,
-        name="solve",
+        out[1:, :, :half] = solve_dot(left, whole_ref[:half, :half]).reshape(per, rows, half)
+        carried[...] = solve_dot(left, whole_ref[half:, :half])
+
+    return pl.pallas_call(
+        body,
+        name="solve_left",
+        out_shape=[
+            jax.ShapeDtypeStruct((per + 1, rows, width), jnp.float32),
+            jax.ShapeDtypeStruct((per * rows, half), jnp.float32),
+        ],
+        in_specs=spaces(3 + len(updates), pltpu.VMEM),
+        out_specs=spaces(2, pltpu.VMEM),
+        cost_estimate=pl.CostEstimate(flops=2000000000, bytes_accessed=5000000, transcendentals=0),
+    )(panel, *updates, whole, lower)
+
+
+def solve_right(panel, updates, whole, carried, out, cb, per, rows):
+    width = cb * rows
+    half = width // HALVES
+
+    def body(panel_ref, *refs):
+        updates_ref = refs[:len(updates)]
+        whole_ref, carried_ref, _, result, stage, sem = refs[len(updates):]
+        left = remaining(panel_ref, updates_ref, 1, cb, per, rows)
+        value = carried_ref[...] + solve_dot(left, whole_ref[half:, half:])
+        stage[...] = value.reshape(per, rows, half)
+        copy = pltpu.make_async_copy(
+            stage, result.at[pl.ds(1, per), :, pl.ds(half, half)], sem
+        )
+        copy.start()
+        copy.wait()
+
+    return pl.pallas_call(
+        body,
+        name="solve_right",
         out_shape=jax.ShapeDtypeStruct((per + 1, rows, width), jnp.float32),
-        in_specs=spaces(6, pltpu.VMEM),
-        out_specs=pl.BlockSpec(memory_space=pltpu.VMEM),
+        in_specs=spaces(3 + len(updates), pltpu.VMEM) + spaces(1, pl.ANY),
+        out_specs=pl.BlockSpec(memory_space=pl.ANY),
+        scratch_shapes=[pltpu.VMEM((per, rows, half), jnp.float32), pltpu.SemaphoreType.DMA(())],
+        input_output_aliases={3 + len(updates): 0},
         cost_estimate=pl.CostEstimate(flops=2000000000, bytes_accessed=5000000, transcendentals=0),
-    )(panel, kept, from_core, from_far, whole, lower)
+    )(panel, *updates, whole, carried, out)
 
 
 def shards(desc_panel, row_map, anc_order, anc_below, anc_panel):
@@ -513,15 +561,21 @@
     diagonal_far = lax.ppermute(diagonal, "blk", far)
     schur, inverses = first_factor(diagonal, diagonal_far, strips, cb, rows)
 
-    kept, for_near, for_far, for_both = below_update(
-        heads, tails, codes, cb, blk_count, per, leaves, rows
+    partials = below_update(heads, tails, codes, cb, blk_count, per, leaves, rows)
+    kept, for_near, for_far, for_both = (
+        partials[HALVES * x:HALVES * (x + 1)] for x in range(blk_count)
     )
-    for_both = lax.ppermute(for_both, "blk", near)
-    from_near = lax.ppermute(for_near, "blk", near)
-    onward = for_far + for_both
-    from_far = lax.ppermute(onward, "blk", far)
+    from_near = []
+    from_far = []
+    for half in range(HALVES):
+        passed = lax.ppermute(for_both[half], "blk", near)
+        from_far.append(lax.ppermute(for_far[half] + passed, "blk", far))
+    for half in range(HALVES):
+        from_near.append(lax.ppermute(for_near[half], "blk", near))
     whole, lower = last_factor(schur, inverses, cb, rows)
-    out = solve_rows(panel, kept, from_near, from_far, whole, lower, cb, per, rows)
+    updates = [[kept[half], from_near[half], from_far[half]] for half in range(HALVES)]
+    out, carried = solve_left(panel, updates[0], whole, lower, cb, per, rows)
+    out = solve_right(panel, updates[1], whole, carried, out, cb, per, rows)
     return out.reshape(anc_panel.shape)
 
 

time: 99.1 us -> 99.9 us (level)
  waiting for transfers between devices: 27.7 us -> 19.9 us
  Pallas kernels: 38.1 us -> 42.5 us
  local copies, waits for them, and re-layouts: 3.56 us -> 6.25 us
  starting transfers between devices: 28 us -> 29.2 us
    ppermute x3 -> x6, waiting for transfers between devices: 5.73 us -> 0.02 us  [the longest x2 0.01 us: shards(): passed = lax.ppermute(for_both[half], 'blk', near)]
    pallas_call x1 -> x2, Pallas kernels: 4.43 us -> 7.16 us  [the longest x1 3.9 us: solve_left(): pl.pallas_call(body, name='solve_left', out_shape=[jax.ShapeDtypeStruct((...]
    unnamed x42 -> x58, local copies, waits for them, and re-layouts: 2.59 us -> 5.29 us
    ppermute x1, waiting for transfers between devices: 2.09 us -> 0.01 us  [shards(): diagonal_far = lax.ppermute(diagonal, 'blk', far)]
    pallas_call x1, Pallas kernels: 3.74 us -> 5.44 us  [below_update(): pl.pallas_call(body, name='below', out_shape=[jax.ShapeDtypeStruct((cb *...]
    ppermute x3 -> x6, starting transfers between devices: 1.65 us -> 2.86 us  [the longest x2 1.81 us: shards(): from_far.append(lax.ppermute(for_far[half] + passed, 'blk', far))]
  transfers between devices with their start and end apart: 16 -> 19, of which waited for: 7 -> 5; matrix products, arithmetic and copies ran while one was open for 2% -> 2% of each run, Pallas kernels for 31% -> 36%
where the time goes in v1:
time: 99.9 us; the launch traced here: 99.3 us
  Pallas kernels  42.5 us (43%)
  starting transfers between devices  29.2 us (29%)
  waiting for transfers between devices  19.9 us (20%)
  local copies, waits for them, and re-layouts  6.25 us (6%)
  other arithmetic  1.09 us (1%)
    ppermute x7, waiting for transfers between devices, shards(): lax.ppermute(heads[k], 'leaf', [(i, i ^ k) for i in range(leaves)])  18.8 us
    ppermute x7, starting transfers between devices, shards(): lax.ppermute(heads[k], 'leaf', [(i, i ^ k) for i in range(leaves)])  15.2 us
    pallas_call x1, Pallas kernels, last_factor(): pl.pallas_call(body, name='factor_last', out_shape=[jax.ShapeDtypeStruct(...  12.7 us
    pallas_call x1, Pallas kernels, first_factor(): pl.pallas_call(body, name='factor_first', out_shape=[jax.ShapeDtypeStruct...  11.4 us
    all_to_all x1, starting transfers between devices, shards(): lax.all_to_all(tails, 'leaf', split_axis=0, concat_axis=0, tiled=True)  7.42 us
    pallas_call x1, Pallas kernels, below_update(): pl.pallas_call(body, name='below', out_shape=[jax.ShapeDtypeStruct((cb *...  5.44 us
    unnamed x58, local copies, waits for them, and re-layouts  5.29 us
    pallas_call x1, Pallas kernels, solve_left(): pl.pallas_call(body, name='solve_left', out_shape=[jax.ShapeDtypeStruct((...  3.9 us
  transfers between devices with their start and end apart: 19, of which 5 were waited for; matrix products, arithmetic and copies ran while one was open for 2% of the time, Pallas kernels for 36%

profile of v1, /device:TPU:0, one launch (start us, length us, event | category | flops | bytes accessed | tf_op | source)
XLA Modules:
  0.0 99.3 jit_solution(8959321077623977617)
XLA Ops:
  0.0 3.2 %pack.1 = (bf16[272,128]{1,0:T(8,128)(2,1)}, bf16[272,128]{1,0:T(8,128)(2,1)}, bf16[272,128]{1,0:T(8,128)(2,1)}, bf16[272,128]{1,0:T(8,128)(2,1)}, bf16[272,128]...) custom-call(s32[3,8]{1,0:T(4,128)} %bitcast.9, ...), custom_call_target="tpu_custom_call" | custom-call | tf_op jit(solution)/shard_map/pack/pallas_call | solution.py:139
  3.3 7.4 %all-to-all-start = ((bf16[8,512,128]{2,1,0:T(8,128)(2,1)}), bf16[8,512,128]{2,1,0:T(8,128)(2,1)S(1)}, u32[]{:S(2)}, u32[]{:S(2)}) async-start(bf16[8,512,128]{2,1,0:T(8,128)(2,1)} %get-tuple-element.39), calls=%async_computation | async-start | bytes 2097152 | tf_op jit(solution)/shard_map/all_to_all | solution.py:549
  10.7 2.0 %collective-permute-start = (bf16[272,128]{1,0:T(8,128)(2,1)S(1)}, bf16[272,128]{1,0:T(8,128)(2,1)S(1)}, u32[]{:S(2)}, u32[]{:S(2)}) collective-permute-start(bf16[272,128]{1,0:T(8,128)(2,1)S(1)} %copy-done.28), channel_id=1, source_target_pairs={{0,4},{4,0},{8,12},{12,8},{16,20},{20,16},{24,28},{28,24},{1,5},{5... | collective-permute-start | bytes 208904 | tf_op jit(solution)/shard_map/ppermute | solution.py:544
  12.7 1.5 %collective-permute-start.1 = (bf16[272,128]{1,0:T(8,128)(2,1)S(1)}, bf16[272,128]{1,0:T(8,128)(2,1)S(1)}, u32[]{:S(2)}, u32[]{:S(2)}) collective-permute-start(bf16[272,128]{1,0:T(8,128)(2,1)S(1)} %copy-done.27), channel_id=1, source_target_pairs={{0,8},{4,12},{8,0},{12,4},{16,24},{20,28},{24,16},{28,20},{1,9},{5... | collective-permute-start | bytes 208904 | tf_op jit(solution)/shard_map/ppermute | solution.py:544
  14.3 2.8 %collective-permute-start.3 = (bf16[272,128]{1,0:T(8,128)(2,1)S(1)}, bf16[272,128]{1,0:T(8,128)(2,1)S(1)}, u32[]{:S(2)}, u32[]{:S(2)}) collective-permute-start(bf16[272,128]{1,0:T(8,128)(2,1)S(1)} %copy-done.25), channel_id=1, source_target_pairs={{0,16},{4,20},{8,24},{12,28},{16,0},{20,4},{24,8},{28,12},{1,17},{... | collective-permute-start | bytes 208904 | tf_op jit(solution)/shard_map/ppermute | solution.py:544
  17.1 1.5 %collective-permute-start.4 = (bf16[272,128]{1,0:T(8,128)(2,1)S(1)}, bf16[272,128]{1,0:T(8,128)(2,1)S(1)}, u32[]{:S(2)}, u32[]{:S(2)}) collective-permute-start(bf16[272,128]{1,0:T(8,128)(2,1)S(1)} %copy-done.24), channel_id=1, source_target_pairs={{0,20},{4,16},{8,28},{12,24},{16,4},{20,0},{24,12},{28,8},{1,21},{... | collective-permute-start | bytes 208904 | tf_op jit(solution)/shard_map/ppermute | solution.py:544
  18.6 2.7 %collective-permute-done.refs_1_.refs_3_ = bf16[272,128]{1,0:T(8,128)(2,1)S(1)} collective-permute-done((bf16[272,128]{1,0:T(8,128)(2,1)S(1)}, bf16[272,128]{1,0:T(8,128)(2,1)S(1)}, u32[]{:S(2)}, u32[]{:S(2)}) %collective-permute-start) | collective-permute-done | bytes 69664 | tf_op jit(solution)/shard_map/ppermute | solution.py:544
  21.3 2.7 %collective-permute-start.5 = (bf16[272,128]{1,0:T(8,128)(2,1)S(1)}, bf16[272,128]{1,0:T(8,128)(2,1)S(1)}, u32[]{:S(2)}, u32[]{:S(2)}) collective-permute-start(bf16[272,128]{1,0:T(8,128)(2,1)S(1)} %copy-done.23), channel_id=1, source_target_pairs={{0,24},{4,28},{8,16},{12,20},{16,8},{20,12},{24,0},{28,4},{1,25},{... | collective-permute-start | bytes 208904 | tf_op jit(solution)/shard_map/ppermute | solution.py:544
  24.1 6.4 %collective-permute-done.1.refs_2_.refs_4_ = bf16[272,128]{1,0:T(8,128)(2,1)S(1)} collective-permute-done((bf16[272,128]{1,0:T(8,128)(2,1)S(1)}, bf16[272,128]{1,0:T(8,128)(2,1)S(1)}, u32[]{:S(2)}, u32[]{:S(2)}) %collective-permute-start.1) | collective-permute-done | bytes 69664 | tf_op jit(solution)/shard_map/ppermute | solution.py:544
  30.5 4.6 %collective-permute-start.6 = (bf16[272,128]{1,0:T(8,128)(2,1)S(1)}, bf16[272,128]{1,0:T(8,128)(2,1)S(1)}, u32[]{:S(2)}, u32[]{:S(2)}) collective-permute-start(bf16[272,128]{1,0:T(8,128)(2,1)S(1)} %copy-done.22), channel_id=1, source_target_pairs={{0,28},{4,24},{8,20},{12,16},{16,12},{20,8},{24,4},{28,0},{1,29},{... | collective-permute-start | bytes 208904 | tf_op jit(solution)/shard_map/ppermute | solution.py:544
  35.1 1.0 slice_bitcast_fusion.refs_0_
  36.1 1.6 %collective-permute-start.13 = (f32[128,512]{1,0:T(8,128)S(1)}, f32[128,512]{1,0:T(8,128)S(1)}, u32[]{:S(2)}, u32[]{:S(2)}) collective-permute-start(f32[128,512]{1,0:T(8,128)S(1)} %slice_bitcast_fusion.refs_0_), channel_id=1, source_target_pairs={{0,2},{1,3},{2,0},{3,1},{4,6},{5,7},{6,4},{7,5},{8,10},{9,11},{10,... | collective-permute-start | bytes 786440 | tf_op jit(solution)/shard_map/ppermute | solution.py:553
  37.7 7.6 %collective-permute-done.3.refs_4_.refs_6_ = bf16[272,128]{1,0:T(8,128)(2,1)S(1)} collective-permute-done((bf16[272,128]{1,0:T(8,128)(2,1)S(1)}, bf16[272,128]{1,0:T(8,128)(2,1)S(1)}, u32[]{:S(2)}, u32[]{:S(2)}) %collective-permute-start.3) | collective-permute-done | bytes 69664 | tf_op jit(solution)/shard_map/ppermute | solution.py:544
  45.3 2.0 %collective-permute-done.4.refs_5_.refs_7_ = bf16[272,128]{1,0:T(8,128)(2,1)S(1)} collective-permute-done((bf16[272,128]{1,0:T(8,128)(2,1)S(1)}, bf16[272,128]{1,0:T(8,128)(2,1)S(1)}, u32[]{:S(2)}, u32[]{:S(2)}) %collective-permute-start.4) | collective-permute-done | bytes 69664 | tf_op jit(solution)/shard_map/ppermute | solution.py:544
  47.3 0.6 copy-done.19
  48.0 2.6 %diagonal.1 = (f32[512,128]{1,0:T(8,128)}, s32[8,128]{1,0:T(8,128)}) custom-call(bf16[272,128]{1,0:T(8,128)(2,1)} %get-tuple-element.30.refs_0_.refs_2_, bf16[272,128]{1,0:T(8,128)(2,1)} %copy-done.15, bf16[272,128]{1,0:T(8,128)(2,1)} %copy-done.16, bf16[272,128]{1,0:T(8,128)(2,1)} %copy-done.17, bf16[272,128]{1,0:T(8,128)(2,1)} %copy-done.18, ...), custom_call_target="tpu_custom_call" | custom-call | flops 2000000000 | bytes 1000000 | tf_op jit(solution)/shard_map/diagonal/pallas_call | solution.py:207
  50.6 0.5 collective-permute-start.12
  51.2 1.1 %collective-permute-done.10 = f32[512,128]{1,0:T(8,128)S(1)} collective-permute-done((f32[512,128]{1,0:T(8,128)}, f32[512,128]{1,0:T(8,128)S(1)}, u32[]{:S(2)}, u32[]{:S(2)}) %collective-permute-start.10) | collective-permute-done | bytes 262176 | tf_op jit(solution)/shard_map/ppermute | solution.py:559
  52.3 1.0 add.10.own_ref
  53.3 1.6 %collective-permute-start.11 = (f32[512,128]{1,0:T(8,128)S(1)}, f32[512,128]{1,0:T(8,128)S(1)}, u32[]{:S(2)}, u32[]{:S(2)}) collective-permute-start(f32[512,128]{1,0:T(8,128)S(1)} %add.10.own_ref), channel_id=1, source_target_pairs={{0,2},{1,3},{2,0},{3,1},{4,6},{5,7},{6,4},{7,5},{8,10},{9,11},{10,... | collective-permute-start | bytes 786440 | tf_op jit(solution)/shard_map/ppermute | solution.py:561
  54.9 1.0 copy-done
  55.9 5.4 %below.1 = (f32[6,128,128]{2,1,0:T(8,128)}, f32[6,128,128]{2,1,0:T(8,128)}, f32[6,128,128]{2,1,0:T(8,128)}, f32[6,128,128]{2,1,0:T(8,128)}, f32[6,128,128]{2,1,0...) custom-call(s32[8,128]{1,0:T(8,128)} %get-tuple-element.38.refs_0_, ...), custom_call_target="tpu_custom_call" | custom-call | flops 2000000000 | bytes 4000000 | tf_op jit(solution)/shard_map/below/pallas_call | solution.py:291
  61.9 0.7 copy-done.12
  62.7 0.7 copy-done.14
  63.4 11.4 %factor_first.1 = (f32[4,128,512]{2,1,0:T(8,128)}, f32[4,128,128]{2,1,0:T(8,128)}) custom-call(f32[512,128]{1,0:T(8,128)} %copy-done.3, f32[512,128]{1,0:T(8,128)} %copy-done.14, f32[128,512]{1,0:T(8,128)} %copy-done.4, f32[128,512]{1,0:T(8,128)} %copy-done.12, f32[128,512]{1,0:T(8,128)} %copy-done.11, f32[128,512]{1,0:T(8,128)} %copy-done.13), custom_call_target="tpu_custom_call" | custom-call | flops 10000000000 | bytes 2000000 | tf_op jit(solution)/shard_map/factor_first/pallas_call | solution.py:393
  75.5 0.6 collective-permute-start.17
  76.5 1.2 %collective-permute-start.9 = (f32[6,128,128]{2,1,0:T(8,128)S(1)}, f32[6,128,128]{2,1,0:T(8,128)S(1)}, u32[]{:S(2)}, u32[]{:S(2)}) collective-permute-start(f32[6,128,128]{2,1,0:T(8,128)S(1)} %add.9), channel_id=1, source_target_pairs={{0,2},{1,3},{2,0},{3,1},{4,6},{5,7},{6,4},{7,5},{8,10},{9,11},{10,... | collective-permute-start | bytes 1179656 | tf_op jit(solution)/shard_map/ppermute | solution.py:572
  77.7 12.7 %factor_last.1 = (f32[512,512]{1,0:T(8,128)}, f32[128,512]{1,0:T(8,128)}) custom-call(f32[4,128,512]{2,1,0:T(8,128)} %get-tuple-element.45.schur_ref, f32[4,128,128]{2,1,0:T(8,128)} %get-tuple-element.46.inverses_ref), custom_call_target="tpu_custom_call" | custom-call | flops 12000000000 | bytes 2000000 | tf_op jit(solution)/shard_map/factor_last/pallas_call | solution.py:438
  90.4 0.7 copy-done.8
  91.2 3.9 %solve_left.1 = (f32[4,128,512]{2,1,0:T(8,128)}, f32[384,256]{1,0:T(8,128)}) custom-call(f32[4,128,512]{2,1,0:T(8,128)} %bitcast.7, f32[6,128,128]{2,1,0:T(8,128)} %get-tuple-element.48.refs_0_, f32[6,128,128]{2,1,0:T(8,128)} %copy-done.8, f32[6,128,128]{2,1,0:T(8,128)} %copy-done.10, f32[512,512]{1,0:T(8,128)} %get-tuple-element.47.refs_3_, ...), custom_call_target="tpu_custom_call" | custom-call | flops 2000000000 | bytes 5000000 | tf_op jit(solution)/shard_map/solve_left/pallas_call | solution.py:488
  95.2 0.7 copy-done.7
  96.1 3.3 %solve_right.1 = f32[4,128,512]{2,1,0:T(8,128)} custom-call(f32[4,128,512]{2,1,0:T(8,128)} %bitcast.8, f32[6,128,128]{2,1,0:T(8,128)} %get-tuple-element.40.refs_0_, f32[6,128,128]{2,1,0:T(8,128)} %copy-done.7, f32[6,128,128]{2,1,0:T(8,128)} %copy-done.9, f32[512,512]{1,0:T(8,128)} %get-tuple-element.47.refs_3_, ...), custom_call_target="tpu_custom_call", output_to_operand_aliasing={{}: (6, {})} | custom-call | flops 2000000000 | bytes 5000000 | tf_op jit(solution)/shard_map/solve_right/pallas_call | solution.py:517
  (75 shorter events, 2.2 us)
Async XLA Ops:
  3.2 9.5 %copy-start.27 = (bf16[272,128]{1,0:T(8,128)(2,1)S(1)}, bf16[272,128]{1,0:T(8,128)(2,1)}, u32[]{:S(2)}) copy-start(bf16[272,128]{1,0:T(8,128)(2,1)} %get-tuple-element.32) | copy-start | bytes 208900
  3.2 11.0 %copy-start.26 = (bf16[272,128]{1,0:T(8,128)(2,1)S(1)}, bf16[272,128]{1,0:T(8,128)(2,1)}, u32[]{:S(2)}) copy-start(bf16[272,128]{1,0:T(8,128)(2,1)} %get-tuple-element.33) | copy-start | bytes 208900
  3.2 11.0 %copy-start.25 = (bf16[272,128]{1,0:T(8,128)(2,1)S(1)}, bf16[272,128]{1,0:T(8,128)(2,1)}, u32[]{:S(2)}) copy-start(bf16[272,128]{1,0:T(8,128)(2,1)} %get-tuple-element.34) | copy-start | bytes 208900
  3.3 13.9 %copy-start.24 = (bf16[272,128]{1,0:T(8,128)(2,1)S(1)}, bf16[272,128]{1,0:T(8,128)(2,1)}, u32[]{:S(2)}) copy-start(bf16[272,128]{1,0:T(8,128)(2,1)} %get-tuple-element.35) | copy-start | bytes 208900
  3.3 18.1 %copy-start.23 = (bf16[272,128]{1,0:T(8,128)(2,1)S(1)}, bf16[272,128]{1,0:T(8,128)(2,1)}, u32[]{:S(2)}) copy-start(bf16[272,128]{1,0:T(8,128)(2,1)} %get-tuple-element.36) | copy-start | bytes 208900
  3.3 27.2 %copy-start.22 = (bf16[272,128]{1,0:T(8,128)(2,1)S(1)}, bf16[272,128]{1,0:T(8,128)(2,1)}, u32[]{:S(2)}) copy-start(bf16[272,128]{1,0:T(8,128)(2,1)} %get-tuple-element.37) | copy-start | bytes 208900
  3.3 51.6 %all-to-all-start = ((bf16[8,512,128]{2,1,0:T(8,128)(2,1)}), bf16[8,512,128]{2,1,0:T(8,128)(2,1)S(1)}, u32[]{:S(2)}, u32[]{:S(2)}) async-start(bf16[8,512,128]{2,1,0:T(8,128)(2,1)} %get-tuple-element.39), calls=%async_computation | async-start | bytes 2097152 | tf_op jit(solution)/shard_map/all_to_all | solution.py:549
  10.7 10.6 %collective-permute-start = (bf16[272,128]{1,0:T(8,128)(2,1)S(1)}, bf16[272,128]{1,0:T(8,128)(2,1)S(1)}, u32[]{:S(2)}, u32[]{:S(2)}) collective-permute-start(bf16[272,128]{1,0:T(8,128)(2,1)S(1)} %copy-done.28), channel_id=1, source_target_pairs={{0,4},{4,0},{8,12},{12,8},{16,20},{20,16},{24,28},{28,24},{1,5},{5... | collective-permute-start | bytes 208904 | tf_op jit(solution)/shard_map/ppermute | solution.py:544
  12.7 17.7 %collective-permute-start.1 = (bf16[272,128]{1,0:T(8,128)(2,1)S(1)}, bf16[272,128]{1,0:T(8,128)(2,1)S(1)}, u32[]{:S(2)}, u32[]{:S(2)}) collective-permute-start(bf16[272,128]{1,0:T(8,128)(2,1)S(1)} %copy-done.27), channel_id=1, source_target_pairs={{0,8},{4,12},{8,0},{12,4},{16,24},{20,28},{24,16},{28,20},{1,9},{5... | collective-permute-start | bytes 208904 | tf_op jit(solution)/shard_map/ppermute | solution.py:544
  14.2 21.9 %collective-permute-start.2 = (bf16[272,128]{1,0:T(8,128)(2,1)S(1)}, bf16[272,128]{1,0:T(8,128)(2,1)S(1)}, u32[]{:S(2)}, u32[]{:S(2)}) collective-permute-start(bf16[272,128]{1,0:T(8,128)(2,1)S(1)} %copy-done.26), channel_id=1, source_target_pairs={{0,12},{4,8},{8,4},{12,0},{16,28},{20,24},{24,20},{28,16},{1,13},{... | collective-permute-start | bytes 208904 | tf_op jit(solution)/shard_map/ppermute | solution.py:544
  14.3 31.0 %collective-permute-start.3 = (bf16[272,128]{1,0:T(8,128)(2,1)S(1)}, bf16[272,128]{1,0:T(8,128)(2,1)S(1)}, u32[]{:S(2)}, u32[]{:S(2)}) collective-permute-start(bf16[272,128]{1,0:T(8,128)(2,1)S(1)} %copy-done.25), channel_id=1, source_target_pairs={{0,16},{4,20},{8,24},{12,28},{16,0},{20,4},{24,8},{28,12},{1,17},{... | collective-permute-start | bytes 208904 | tf_op jit(solution)/shard_map/ppermute | solution.py:544
  17.1 30.2 %collective-permute-start.4 = (bf16[272,128]{1,0:T(8,128)(2,1)S(1)}, bf16[272,128]{1,0:T(8,128)(2,1)S(1)}, u32[]{:S(2)}, u32[]{:S(2)}) collective-permute-start(bf16[272,128]{1,0:T(8,128)(2,1)S(1)} %copy-done.24), channel_id=1, source_target_pairs={{0,20},{4,16},{8,28},{12,24},{16,4},{20,0},{24,12},{28,8},{1,21},{... | collective-permute-start | bytes 208904 | tf_op jit(solution)/shard_map/ppermute | solution.py:544
  21.3 14.7 %copy-start.15 = (bf16[272,128]{1,0:T(8,128)(2,1)}, bf16[272,128]{1,0:T(8,128)(2,1)S(1)}, u32[]{:S(2)}) copy-start(bf16[272,128]{1,0:T(8,128)(2,1)S(1)} %collective-permute-done.refs_1_.refs_3_) | copy-start | bytes 208900
  21.3 26.0 %collective-permute-start.5 = (bf16[272,128]{1,0:T(8,128)(2,1)S(1)}, bf16[272,128]{1,0:T(8,128)(2,1)S(1)}, u32[]{:S(2)}, u32[]{:S(2)}) collective-permute-start(bf16[272,128]{1,0:T(8,128)(2,1)S(1)} %copy-done.23), channel_id=1, source_target_pairs={{0,24},{4,28},{8,16},{12,20},{16,8},{20,12},{24,0},{28,4},{1,25},{... | collective-permute-start | bytes 208904 | tf_op jit(solution)/shard_map/ppermute | solution.py:544
  30.5 16.8 %collective-permute-start.6 = (bf16[272,128]{1,0:T(8,128)(2,1)S(1)}, bf16[272,128]{1,0:T(8,128)(2,1)S(1)}, u32[]{:S(2)}, u32[]{:S(2)}) collective-permute-start(bf16[272,128]{1,0:T(8,128)(2,1)S(1)} %copy-done.22), channel_id=1, source_target_pairs={{0,28},{4,24},{8,20},{12,16},{16,12},{20,8},{24,4},{28,0},{1,29},{... | collective-permute-start | bytes 208904 | tf_op jit(solution)/shard_map/ppermute | solution.py:544
  36.1 14.5 %copy-start.4 = (f32[128,512]{1,0:T(8,128)}, f32[128,512]{1,0:T(8,128)S(1)}, u32[]{:S(2)}) copy-start(f32[128,512]{1,0:T(8,128)S(1)} %slice_bitcast_fusion.refs_0_) | copy-start | bytes 786436
  36.1 11.2 %copy-start.17 = (bf16[272,128]{1,0:T(8,128)(2,1)}, bf16[272,128]{1,0:T(8,128)(2,1)S(1)}, u32[]{:S(2)}) copy-start(bf16[272,128]{1,0:T(8,128)(2,1)S(1)} %collective-permute-done.2.refs_3_.refs_5_) | copy-start | bytes 208900
  36.1 15.0 %collective-permute-start.13 = (f32[128,512]{1,0:T(8,128)S(1)}, f32[128,512]{1,0:T(8,128)S(1)}, u32[]{:S(2)}, u32[]{:S(2)}) collective-permute-start(f32[128,512]{1,0:T(8,128)S(1)} %slice_bitcast_fusion.refs_0_), channel_id=1, source_target_pairs={{0,2},{1,3},{2,0},{3,1},{4,6},{5,7},{6,4},{7,5},{8,10},{9,11},{10,... | collective-permute-start | bytes 786440 | tf_op jit(solution)/shard_map/ppermute | solution.py:553
  50.6 1.7 %collective-permute-start.10 = (f32[512,128]{1,0:T(8,128)}, f32[512,128]{1,0:T(8,128)S(1)}, u32[]{:S(2)}, u32[]{:S(2)}) collective-permute-start(f32[512,128]{1,0:T(8,128)} %get-tuple-element.44), channel_id=1, source_target_pairs={{0,1},{1,0},{2,3},{3,2},{4,5},{5,4},{6,7},{7,6},{8,9},{9,8},{10,11... | collective-permute-start | bytes 786440 | tf_op jit(solution)/shard_map/ppermute | solution.py:559
  50.6 11.3 %collective-permute-start.12 = (f32[128,512]{1,0:T(8,128)S(1)}, f32[128,512]{1,0:T(8,128)S(1)}, u32[]{:S(2)}, u32[]{:S(2)}) collective-permute-start(f32[128,512]{1,0:T(8,128)S(1)} %slice_bitcast_fusion.refs_0_), channel_id=1, source_target_pairs={{0,1},{1,0},{2,3},{3,2},{4,5},{5,4},{6,7},{7,6},{8,9},{9,8},{10,11... | collective-permute-start | bytes 786440 | tf_op jit(solution)/shard_map/ppermute | solution.py:554
  51.1 10.8 %collective-permute-start.14 = (f32[128,512]{1,0:T(8,128)S(1)}, f32[128,512]{1,0:T(8,128)S(1)}, u32[]{:S(2)}, u32[]{:S(2)}) collective-permute-start(f32[128,512]{1,0:T(8,128)S(1)} %collective-permute-done.13.refs_2_), channel_id=1, source_target_pairs={{0,1},{1,0},{2,3},{3,2},{4,5},{5,4},{6,7},{7,6},{8,9},{9,8},{10,11... | collective-permute-start | bytes 786440 | tf_op jit(solution)/shard_map/ppermute | solution.py:555
  53.3 8.0 %copy-start.3 = (f32[512,128]{1,0:T(8,128)}, f32[512,128]{1,0:T(8,128)S(1)}, u32[]{:S(2)}) copy-start(f32[512,128]{1,0:T(8,128)S(1)} %add.10.own_ref) | copy-start | bytes 786436
  53.3 8.6 %collective-permute-start.11 = (f32[512,128]{1,0:T(8,128)S(1)}, f32[512,128]{1,0:T(8,128)S(1)}, u32[]{:S(2)}, u32[]{:S(2)}) collective-permute-start(f32[512,128]{1,0:T(8,128)S(1)} %add.10.own_ref), channel_id=1, source_target_pairs={{0,2},{1,3},{2,0},{3,1},{4,6},{5,7},{6,4},{7,5},{8,10},{9,11},{10,... | collective-permute-start | bytes 786440 | tf_op jit(solution)/shard_map/ppermute | solution.py:561
  61.3 14.1 %collective-permute-start.16 = (f32[6,128,128]{2,1,0:T(8,128)}, f32[6,128,128]{2,1,0:T(8,128)S(1)}, u32[]{:S(2)}, u32[]{:S(2)}) collective-permute-start(f32[6,128,128]{2,1,0:T(8,128)} %get-tuple-element.51), channel_id=1, source_target_pairs={{0,1},{1,0},{2,3},{3,2},{4,5},{5,4},{6,7},{7,6},{8,9},{9,8},{10,11... | collective-permute-start | bytes 1179656 | tf_op jit(solution)/shard_map/ppermute | solution.py:571
  61.4 13.5 %copy-start.6 = (f32[6,128,128]{2,1,0:T(8,128)S(1)}, f32[6,128,128]{2,1,0:T(8,128)}, u32[]{:S(2)}) copy-start(f32[6,128,128]{2,1,0:T(8,128)} %get-tuple-element.49) | copy-start | bytes 1179652
  61.4 13.6 %copy-start.5 = (f32[6,128,128]{2,1,0:T(8,128)S(1)}, f32[6,128,128]{2,1,0:T(8,128)}, u32[]{:S(2)}) copy-start(f32[6,128,128]{2,1,0:T(8,128)} %get-tuple-element.41) | copy-start | bytes 1179652
  61.4 14.0 %copy-start.2 = (f32[6,128,128]{2,1,0:T(8,128)S(1)}, f32[6,128,128]{2,1,0:T(8,128)}, u32[]{:S(2)}) copy-start(f32[6,128,128]{2,1,0:T(8,128)} %get-tuple-element.50) | copy-start | bytes 1179652
  61.4 14.6 %collective-permute-start.8 = (f32[6,128,128]{2,1,0:T(8,128)}, f32[6,128,128]{2,1,0:T(8,128)S(1)}, u32[]{:S(2)}, u32[]{:S(2)}) collective-permute-start(f32[6,128,128]{2,1,0:T(8,128)} %get-tuple-element.43), channel_id=1, source_target_pairs={{0,1},{1,0},{2,3},{3,2},{4,5},{5,4},{6,7},{7,6},{8,9},{9,8},{10,11... | collective-permute-start | bytes 1179656 | tf_op jit(solution)/shard_map/ppermute | solution.py:571
  74.9 15.5 %collective-permute-start.15 = (f32[6,128,128]{2,1,0:T(8,128)S(1)}, f32[6,128,128]{2,1,0:T(8,128)S(1)}, u32[]{:S(2)}, u32[]{:S(2)}) collective-permute-start(f32[6,128,128]{2,1,0:T(8,128)S(1)} %copy-done.6), channel_id=1, source_target_pairs={{0,1},{1,0},{2,3},{3,2},{4,5},{5,4},{6,7},{7,6},{8,9},{9,8},{10,11... | collective-permute-start | bytes 1179656 | tf_op jit(solution)/shard_map/ppermute | solution.py:574
  75.0 20.2 %collective-permute-start.7 = (f32[6,128,128]{2,1,0:T(8,128)S(1)}, f32[6,128,128]{2,1,0:T(8,128)S(1)}, u32[]{:S(2)}, u32[]{:S(2)}) collective-permute-start(f32[6,128,128]{2,1,0:T(8,128)S(1)} %copy-done.5), channel_id=1, source_target_pairs={{0,1},{1,0},{2,3},{3,2},{4,5},{5,4},{6,7},{7,6},{8,9},{9,8},{10,11... | collective-permute-start | bytes 1179656 | tf_op jit(solution)/shard_map/ppermute | solution.py:574
  75.5 14.9 %collective-permute-start.17 = (f32[6,128,128]{2,1,0:T(8,128)S(1)}, f32[6,128,128]{2,1,0:T(8,128)S(1)}, u32[]{:S(2)}, u32[]{:S(2)}) collective-permute-start(f32[6,128,128]{2,1,0:T(8,128)S(1)} %add.11), channel_id=1, source_target_pairs={{0,2},{1,3},{2,0},{3,1},{4,6},{5,7},{6,4},{7,5},{8,10},{9,11},{10,... | collective-permute-start | bytes 1179656 | tf_op jit(solution)/shard_map/ppermute | solution.py:572
  76.5 18.7 %collective-permute-start.9 = (f32[6,128,128]{2,1,0:T(8,128)S(1)}, f32[6,128,128]{2,1,0:T(8,128)S(1)}, u32[]{:S(2)}, u32[]{:S(2)}) collective-permute-start(f32[6,128,128]{2,1,0:T(8,128)S(1)} %add.9), channel_id=1, source_target_pairs={{0,2},{1,3},{2,0},{3,1},{4,6},{5,7},{6,4},{7,5},{8,10},{9,11},{10,... | collective-permute-start | bytes 1179656 | tf_op jit(solution)/shard_map/ppermute | solution.py:572
  (16 other events, 26.7 us)

commit v2 on v1

--- a/solution.py
+++ b/solution.py
@@ -22,6 +22,14 @@
             body(index)
     else:
         lax.fori_loop(0, count, lambda index, carry: (body(index), carry)[1], 0)
+
+
+def limit(mib):
+    return pltpu.CompilerParams(vmem_limit_bytes=mib * 1024 * 1024)
+
+
+def near_core(*arrays):
+    return [pltpu.with_memory_space_constraint(array, pltpu.VMEM) for array in arrays]
 
 
 def spaces(count, space):
@@ -127,7 +135,7 @@
     head_rows = SLOTS * rows + CODE_ROWS
     dtype = desc_panel.dtype
     if direct:
-        heads = [jax.ShapeDtypeStruct((head_rows, width), dtype)] * leaves
+        heads = [pltpu.VMEM((head_rows, width), dtype)] * leaves
     else:
         heads = [jax.ShapeDtypeStruct((leaves, head_rows, width), dtype)]
     tails = jax.ShapeDtypeStruct((leaves, SLOTS * (block_count - 1) * rows, width), dtype)
@@ -139,6 +147,7 @@
     return pl.pallas_call(
         body,
         name="pack",
+        compiler_params=limit(12 if direct else 32),
         out_shape=heads + [tails],
         in_specs=spaces(3, pltpu.SMEM) + spaces(1, pltpu.VMEM),
         out_specs=spaces(len(heads), pltpu.VMEM) + spaces(1, pl.ANY),
@@ -207,8 +216,9 @@
     return pl.pallas_call(
         body,
         name="diagonal",
+        compiler_params=limit(12 if len(heads) > 1 else 40),
         out_shape=[
-            jax.ShapeDtypeStruct((cb * rows, rows), jnp.float32),
+            pltpu.VMEM((cb * rows, rows), jnp.float32),
             jax.ShapeDtypeStruct((leaves, rows), jnp.int32),
         ],
         in_specs=spaces(len(heads), pltpu.VMEM),
@@ -218,13 +228,13 @@
             pltpu.VMEM((rows, group * SLOTS * rows), heads[0].dtype),
         ],
         cost_estimate=pl.CostEstimate(flops=2000000000, bytes_accessed=1000000, transcendentals=0),
-    )(*heads)
-
-
-def below_kernel(cb, blk_count, per, leaves, count, codes, tails_hbm, *refs):
+    )(*(near_core(*heads) if len(heads) > 1 else heads))
+
+
+def below_kernel(cb, blk_count, per, leaves, count, codes, tails, *refs):
     heads = refs[:count]
     outs = refs[count:count + blk_count * HALVES]
-    acc, products, tails, sems = refs[count + blk_count * HALVES:]
+    acc, products = refs[count + blk_count * HALVES:]
     direct = count > 1
     me_leaf = lax.axis_index("leaf")
     me_blk = lax.axis_index("blk")
@@ -234,30 +244,19 @@
     extra = tail_rows // rows
     blocks = blk_count * cb * per
 
-    def source(index):
-        return jnp.bitwise_xor(me_leaf, index) if direct else index
-
-    def fetch(index, slot):
-        return pltpu.make_async_copy(tails_hbm.at[source(index)], tails.at[slot], sems.at[slot])
+    for first in range(0, blocks, cb):
+        acc[pl.ds(first, cb)] = jnp.zeros((cb, rows, rows), jnp.float32)
 
     def step(base):
         for offset in range(group):
-            fetch(base + offset, offset).start()
-
-        @pl.when(base == 0)
-        def _():
-            for first in range(0, blocks, cb):
-                acc[pl.ds(first, cb)] = jnp.zeros((cb, rows, rows), jnp.float32)
-
-        for offset in range(group):
             index = base + offset
-            fetch(index, offset).wait()
+            source = jnp.bitwise_xor(me_leaf, index) if direct else index
             for slot in range(SLOTS):
                 if direct:
                     head = heads[index][pl.ds(slot * rows, rows)]
                 else:
                     head = heads[0][index, pl.ds(slot * rows, rows)]
-                tail = tails[offset, pl.ds(slot * tail_rows, tail_rows)]
+                tail = tails[source, pl.ds(slot * tail_rows, tail_rows)]
                 products[offset * SLOTS + slot] = lax.dot_general(
                     tail, head, (((1,), (1,)), ((), ())), preferred_element_type=jnp.float32
                 )
@@ -291,17 +290,16 @@
     return pl.pallas_call(
         body,
         name="below",
-        out_shape=[jax.ShapeDtypeStruct((cb * per // HALVES, rows, rows), jnp.float32)] * outs,
-        in_specs=spaces(1, pltpu.SMEM) + spaces(1, pl.ANY) + spaces(len(heads), pltpu.VMEM),
+        compiler_params=limit(16 if len(heads) > 1 else 56),
+        out_shape=[pltpu.VMEM((cb * per // HALVES, rows, rows), jnp.float32)] * outs,
+        in_specs=spaces(1, pltpu.SMEM) + spaces(1 + len(heads), pltpu.VMEM),
         out_specs=spaces(outs, pltpu.VMEM),
         scratch_shapes=[
             pltpu.VMEM((blocks + 1, rows, rows), jnp.float32),
             pltpu.VMEM((group * SLOTS, tails.shape[1] // SLOTS, rows), jnp.float32),
-            pltpu.VMEM((group,) + tails.shape[1:], tails.dtype),
-            pltpu.SemaphoreType.DMA((group,)),
         ],
         cost_estimate=pl.CostEstimate(flops=2000000000, bytes_accessed=4000000, transcendentals=0),
-    )(codes, tails, *heads)
+    )(codes, *(near_core(tails, *heads) if len(heads) > 1 else [tails, *heads]))
 
 
 def factor_block(work, rows):
@@ -316,31 +314,39 @@
         def panel(index, carry):
             base = pl.multiple_of(top + index * PANEL, PANEL)
             strip = work[pl.ds(base, PANEL), :]
+            raw = work[top:, :rows]
             picks = [(lane == base + k) for k in range(PANEL)]
             corner = [
                 jnp.sum(jnp.where(picks[k], strip[:, :rows], 0.0), axis=1, keepdims=True)
                 for k in range(PANEL)
             ]
-            scales = []
+            factor = jnp.zeros((PANEL, 2 * rows), jnp.float32)
             for k in range(PANEL):
                 scale = lax.rsqrt(corner[k][k:k + 1])
-                scales.append(scale)
-                row = strip[k:k + 1] * scale
-                low = jnp.where(sub > k, corner[k] * scale, 0.0)
-                strip = jnp.where(sub == k, row, strip - low * row)
-                for m in range(k, PANEL):
-                    entry = corner[m][k:k + 1] * scale
-                    corner[m] = jnp.where(sub == k, entry, corner[m] - low * entry)
-            full = work[pl.ds(top, rows - top), :rows]
-            work[pl.ds(base, PANEL), :] = strip
-            rest = lax.broadcasted_iota(jnp.int32, (rows - top, 1), 0) + top >= base + PANEL
-            total = jnp.zeros((rows - top, 2 * rows), jnp.float32)
-            for k in reversed(range(PANEL)):
-                solved = strip[k:k + 1] * scales[k]
-                strip = strip - jnp.where(sub < k, corner[k], 0.0) * solved
-                column = jnp.sum(jnp.where(picks[k], full, 0.0), axis=1, keepdims=True)
-                total = total + jnp.where(rest, column, 0.0) * solved
-            work[pl.ds(top, rows - top), :] -= total
+                inverse = scale * scale
+                row = strip[k:k + 1]
+                factor = jnp.where(sub == k, row * scale, factor)
+                scaled = row * inverse
+                strip = jnp.where(sub == k, scaled, strip - corner[k] * scaled)
+                for m in range(k + 1, PANEL):
+                    entry = corner[m][k:k + 1]
+                    corner[m] = jnp.where(
+                        sub == k, entry * inverse, corner[m] - (corner[k] * entry) * inverse
+                    )
+            work[pl.ds(base, PANEL), :] = factor
+            for start, stop, masked in ((top, top + size, True), (top + size, rows, False)):
+                if start == stop:
+                    continue
+                full = work[start:stop, :]
+                row_id = lax.broadcasted_iota(jnp.int32, (stop - start, 1), 0) + start
+                for k in range(PANEL):
+                    column = jnp.sum(
+                        jnp.where(picks[k], raw[start - top:stop - top], 0.0), axis=1, keepdims=True
+                    )
+                    if masked:
+                        column = jnp.where(row_id >= base + PANEL, column, 0.0)
+                    full = full - column * strip[k:k + 1]
+                work[start:stop, :] = full
             return carry
 
         lax.fori_loop(0, size // PANEL, panel, 0)
@@ -393,15 +399,16 @@
     return pl.pallas_call(
         body,
         name="factor_first",
+        compiler_params=limit(12),
         out_shape=[
-            jax.ShapeDtypeStruct((cb, rows, cb * rows), jnp.float32),
-            jax.ShapeDtypeStruct((cb, rows, rows), jnp.float32),
+            pltpu.VMEM((cb, rows, cb * rows), jnp.float32),
+            pltpu.VMEM((cb, rows, rows), jnp.float32),
         ],
         in_specs=spaces(2 + blk_count, pltpu.VMEM),
         out_specs=spaces(2, pltpu.VMEM),
         scratch_shapes=[pltpu.VMEM((rows, 2 * rows), jnp.float32)],
         cost_estimate=pl.CostEstimate(flops=10000000000, bytes_accessed=2000000, transcendentals=0),
-    )(own_sum, other_sum, *strips)
+    )(*near_core(own_sum, other_sum), strips[0], *near_core(*strips[1:]))
 
 
 def last_factor(schur_in, inverses_in, cb, rows):
@@ -438,9 +445,10 @@
     return pl.pallas_call(
         body,
         name="factor_last",
+        compiler_params=limit(12),
         out_shape=[
-            jax.ShapeDtypeStruct((width, width), jnp.float32),
-            jax.ShapeDtypeStruct((rows, width), jnp.float32),
+            pltpu.VMEM((width, width), jnp.float32),
+            pltpu.VMEM((rows, width), jnp.float32),
         ],
         in_specs=spaces(2, pltpu.VMEM),
         out_specs=spaces(2, pltpu.VMEM),
@@ -450,7 +458,7 @@
             pltpu.VMEM((rows, 2 * rows), jnp.float32),
         ],
         cost_estimate=pl.CostEstimate(flops=12000000000, bytes_accessed=2000000, transcendentals=0),
-    )(schur_in, inverses_in)
+    )(*near_core(schur_in, inverses_in))
 
 
 def solve_dot(left, right):
@@ -488,14 +496,15 @@
     return pl.pallas_call(
         body,
         name="solve_left",
+        compiler_params=limit(16),
         out_shape=[
             jax.ShapeDtypeStruct((per + 1, rows, width), jnp.float32),
-            jax.ShapeDtypeStruct((per * rows, half), jnp.float32),
+            pltpu.VMEM((per * rows, half), jnp.float32),
         ],
         in_specs=spaces(3 + len(updates), pltpu.VMEM),
         out_specs=spaces(2, pltpu.VMEM),
         cost_estimate=pl.CostEstimate(flops=2000000000, bytes_accessed=5000000, transcendentals=0),
-    )(panel, *updates, whole, lower)
+    )(panel, *near_core(*updates, whole, lower))
 
 
 def solve_right(panel, updates, whole, carried, out, cb, per, rows):
@@ -517,13 +526,14 @@
     return pl.pallas_call(
         body,
         name="solve_right",
+        compiler_params=limit(16),
         out_shape=jax.ShapeDtypeStruct((per + 1, rows, width), jnp.float32),
         in_specs=spaces(3 + len(updates), pltpu.VMEM) + spaces(1, pl.ANY),
         out_specs=pl.BlockSpec(memory_space=pl.ANY),
         scratch_shapes=[pltpu.VMEM((per, rows, half), jnp.float32), pltpu.SemaphoreType.DMA(())],
         input_output_aliases={3 + len(updates): 0},
         cost_estimate=pl.CostEstimate(flops=2000000000, bytes_accessed=5000000, transcendentals=0),
-    )(panel, *updates, whole, carried, out)
+    )(panel, *near_core(*updates, whole, carried), out)
 
 
 def shards(desc_panel, row_map, anc_order, anc_below, anc_panel):
@@ -540,10 +550,11 @@
 
     *heads, tails = pack(desc_panel, row_map, anc_order, anc_below, cb, direct)
     if direct:
-        heads = [heads[0]] + [
-            lax.ppermute(heads[k], "leaf", [(i, i ^ k) for i in range(leaves)])
-            for k in range(1, leaves)
-        ]
+        received = [heads[0]]
+        for k in range(1, leaves):
+            swap = [(i, i ^ k) for i in range(leaves)]
+            received.append(lax.ppermute(heads[k], "leaf", swap))
+        heads = received
     else:
         heads = [lax.all_to_all(heads[0], "leaf", split_axis=0, concat_axis=0, tiled=True)]
     tails = lax.all_to_all(tails, "leaf", split_axis=0, concat_axis=0, tiled=True)

time: 99.9 us -> 92.1 us (0.922)
  Pallas kernels: 42.5 us -> 26.6 us
  waiting for transfers between devices: 19.9 us -> 26.4 us
  local copies, waits for them, and re-layouts: 6.25 us -> 8.5 us
    pallas_call x7, Pallas kernels: 42.5 us -> 26.6 us  [the longest x1 9.84 us: last_factor(): pl.pallas_call(body, name='factor_last', compiler_params=limit(12), out_s...]
    ppermute x2, waiting for transfers between devices: 0.01 us -> 5.66 us  [shards(): from_far.append(lax.ppermute(for_far[half] + passed, 'blk', far))]
    unnamed x58 -> x34, local copies, waits for them, and re-layouts: 5.29 us -> 8.48 us
  transfers between devices with their start and end apart: 19 -> 19, of which waited for: 5 -> 6; matrix products, arithmetic and copies ran while one was open for 2% -> 0% of each run, Pallas kernels for 36% -> 26%
where the time goes in v2:
time: 92.1 us; the launch traced here: 91.5 us
  starting transfers between devices  29.7 us (32%)
  Pallas kernels  26.6 us (29%)
  waiting for transfers between devices  26.4 us (29%)
  local copies, waits for them, and re-layouts  8.5 us (9%)
    ppermute x7, waiting for transfers between devices, shards(): received.append(lax.ppermute(heads[k], 'leaf', swap))  19.8 us
    ppermute x7, starting transfers between devices, shards(): received.append(lax.ppermute(heads[k], 'leaf', swap))  15.2 us
    pallas_call x1, Pallas kernels, last_factor(): pl.pallas_call(body, name='factor_last', compiler_params=limit(12), out_s...  9.84 us
    pallas_call x1, Pallas kernels, first_factor(): pl.pallas_call(body, name='factor_first', compiler_params=limit(12), out_...  9.52 us
    unnamed x34, local copies, waits for them, and re-layouts  8.48 us
    all_to_all x1, starting transfers between devices, shards(): lax.all_to_all(tails, 'leaf', split_axis=0, concat_axis=0, tiled=True)  7.42 us
    ppermute x2, waiting for transfers between devices, shards(): from_far.append(lax.ppermute(for_far[half] + passed, 'blk', far))  5.66 us
    ppermute x2, starting transfers between devices, shards(): from_far.append(lax.ppermute(for_far[half] + passed, 'blk', far))  2.16 us
  transfers between devices with their start and end apart: 19, of which 6 were waited for; matrix products, arithmetic and copies ran while one was open for 0% of the time, Pallas kernels for 26%

profile of v2, /device:TPU:0, one launch (start us, length us, event | category | flops | bytes accessed | tf_op | source)
XLA Modules:
  0.0 91.5 jit_solution(12321834492710221081)
XLA Ops:
  0.7 1.1 %copy-done = bf16[8,384,128]{2,1,0:T(8,128)(2,1)S(1)} copy-done((bf16[8,384,128]{2,1,0:T(8,128)(2,1)S(1)}, bf16[8,384,128]{2,1,0:T(8,128)(2,1)}, u32[]{:S(2)}) %copy-start) | copy-done | bytes 786456
  1.8 0.7 copy-done.2
  3.2 1.9 %pack.1 = (bf16[272,128]{1,0:T(8,128)(2,1)S(1)}, bf16[272,128]{1,0:T(8,128)(2,1)S(1)}, bf16[272,128]{1,0:T(8,128)(2,1)S(1)}, bf16[272,128]{1,0:T(8,128)(2,1)S(1)...) custom-call(s32[3,8]{1,0:T(4,128)S(1)} %bitcast.9, ...), custom_call_target="tpu_custom_call" | custom-call | tf_op jit(solution)/shard_map/pack/pallas_call | solution.py:147
  5.1 7.4 %all-to-all-start = ((bf16[8,512,128]{2,1,0:T(8,128)(2,1)}), bf16[8,512,128]{2,1,0:T(8,128)(2,1)S(1)}, u32[]{:S(2)}, u32[]{:S(2)}) async-start(bf16[8,512,128]{2,1,0:T(8,128)(2,1)} %get-tuple-element.39), calls=%async_computation | async-start | bytes 2097152 | tf_op jit(solution)/shard_map/all_to_all | solution.py:560
  12.5 2.0 %collective-permute-start = (bf16[272,128]{1,0:T(8,128)(2,1)S(1)}, bf16[272,128]{1,0:T(8,128)(2,1)S(1)}, u32[]{:S(2)}, u32[]{:S(2)}) collective-permute-start(bf16[272,128]{1,0:T(8,128)(2,1)S(1)} %get-tuple-element.31), channel_id=1, source_target_pairs={{0,4},{4,0},{8,12},{12,8},{16,20},{20,16},{24,28},{28,24},{1,5},{5... | collective-permute-start | bytes 208904 | tf_op jit(solution)/shard_map/ppermute | solution.py:556
  14.5 1.5 %collective-permute-start.1 = (bf16[272,128]{1,0:T(8,128)(2,1)S(1)}, bf16[272,128]{1,0:T(8,128)(2,1)S(1)}, u32[]{:S(2)}, u32[]{:S(2)}) collective-permute-start(bf16[272,128]{1,0:T(8,128)(2,1)S(1)} %get-tuple-element.32), channel_id=1, source_target_pairs={{0,8},{4,12},{8,0},{12,4},{16,24},{20,28},{24,16},{28,20},{1,9},{5... | collective-permute-start | bytes 208904 | tf_op jit(solution)/shard_map/ppermute | solution.py:556
  16.0 2.9 %collective-permute-start.3 = (bf16[272,128]{1,0:T(8,128)(2,1)S(1)}, bf16[272,128]{1,0:T(8,128)(2,1)S(1)}, u32[]{:S(2)}, u32[]{:S(2)}) collective-permute-start(bf16[272,128]{1,0:T(8,128)(2,1)S(1)} %get-tuple-element.34), channel_id=1, source_target_pairs={{0,16},{4,20},{8,24},{12,28},{16,0},{20,4},{24,8},{28,12},{1,17},{... | collective-permute-start | bytes 208904 | tf_op jit(solution)/shard_map/ppermute | solution.py:556
  18.9 1.5 %collective-permute-start.4 = (bf16[272,128]{1,0:T(8,128)(2,1)S(1)}, bf16[272,128]{1,0:T(8,128)(2,1)S(1)}, u32[]{:S(2)}, u32[]{:S(2)}) collective-permute-start(bf16[272,128]{1,0:T(8,128)(2,1)S(1)} %get-tuple-element.35), channel_id=1, source_target_pairs={{0,20},{4,16},{8,28},{12,24},{16,4},{20,0},{24,12},{28,8},{1,21},{... | collective-permute-start | bytes 208904 | tf_op jit(solution)/shard_map/ppermute | solution.py:556
  20.3 2.7 %collective-permute-done.refs_1_.refs_3_ = bf16[272,128]{1,0:T(8,128)(2,1)S(1)} collective-permute-done((bf16[272,128]{1,0:T(8,128)(2,1)S(1)}, bf16[272,128]{1,0:T(8,128)(2,1)S(1)}, u32[]{:S(2)}, u32[]{:S(2)}) %collective-permute-start) | collective-permute-done | bytes 69664 | tf_op jit(solution)/shard_map/ppermute | solution.py:556
  23.1 2.7 %collective-permute-start.5 = (bf16[272,128]{1,0:T(8,128)(2,1)S(1)}, bf16[272,128]{1,0:T(8,128)(2,1)S(1)}, u32[]{:S(2)}, u32[]{:S(2)}) collective-permute-start(bf16[272,128]{1,0:T(8,128)(2,1)S(1)} %get-tuple-element.36), channel_id=1, source_target_pairs={{0,24},{4,28},{8,16},{12,20},{16,8},{20,12},{24,0},{28,4},{1,25},{... | collective-permute-start | bytes 208904 | tf_op jit(solution)/shard_map/ppermute | solution.py:556
  25.8 6.4 %collective-permute-done.1.refs_2_.refs_4_ = bf16[272,128]{1,0:T(8,128)(2,1)S(1)} collective-permute-done((bf16[272,128]{1,0:T(8,128)(2,1)S(1)}, bf16[272,128]{1,0:T(8,128)(2,1)S(1)}, u32[]{:S(2)}, u32[]{:S(2)}) %collective-permute-start.1) | collective-permute-done | bytes 69664 | tf_op jit(solution)/shard_map/ppermute | solution.py:556
  32.2 4.6 %collective-permute-start.6 = (bf16[272,128]{1,0:T(8,128)(2,1)S(1)}, bf16[272,128]{1,0:T(8,128)(2,1)S(1)}, u32[]{:S(2)}, u32[]{:S(2)}) collective-permute-start(bf16[272,128]{1,0:T(8,128)(2,1)S(1)} %get-tuple-element.37), channel_id=1, source_target_pairs={{0,28},{4,24},{8,20},{12,16},{16,12},{20,8},{24,4},{28,0},{1,29},{... | collective-permute-start | bytes 208904 | tf_op jit(solution)/shard_map/ppermute | solution.py:556
  36.9 1.6 %collective-permute-start.13 = (f32[128,512]{1,0:T(8,128)S(1)}, f32[128,512]{1,0:T(8,128)S(1)}, u32[]{:S(2)}, u32[]{:S(2)}) collective-permute-start(f32[128,512]{1,0:T(8,128)S(1)} %slice_bitcast_fusion.refs_0_), channel_id=1, source_target_pairs={{0,2},{1,3},{2,0},{3,1},{4,6},{5,7},{6,4},{7,5},{8,10},{9,11},{10,... | collective-permute-start | bytes 786440 | tf_op jit(solution)/shard_map/ppermute | solution.py:564
  38.5 8.6 %collective-permute-done.3.refs_4_.refs_6_ = bf16[272,128]{1,0:T(8,128)(2,1)S(1)} collective-permute-done((bf16[272,128]{1,0:T(8,128)(2,1)S(1)}, bf16[272,128]{1,0:T(8,128)(2,1)S(1)}, u32[]{:S(2)}, u32[]{:S(2)}) %collective-permute-start.3) | collective-permute-done | bytes 69664 | tf_op jit(solution)/shard_map/ppermute | solution.py:556
  47.1 2.0 %collective-permute-done.4.refs_5_.refs_7_ = bf16[272,128]{1,0:T(8,128)(2,1)S(1)} collective-permute-done((bf16[272,128]{1,0:T(8,128)(2,1)S(1)}, bf16[272,128]{1,0:T(8,128)(2,1)S(1)}, u32[]{:S(2)}, u32[]{:S(2)}) %collective-permute-start.4) | collective-permute-done | bytes 69664 | tf_op jit(solution)/shard_map/ppermute | solution.py:556
  49.1 0.8 diagonal.1
  50.6 0.9 %collective-permute-done.10 = f32[512,128]{1,0:T(8,128)S(1)} collective-permute-done((f32[512,128]{1,0:T(8,128)S(1)}, f32[512,128]{1,0:T(8,128)S(1)}, u32[]{:S(2)}, u32[]{:S(2)}) %collective-permute-start.10) | collective-permute-done | bytes 262176 | tf_op jit(solution)/shard_map/ppermute | solution.py:570
  51.6 1.6 %collective-permute-start.11 = (f32[512,128]{1,0:T(8,128)S(1)}, f32[512,128]{1,0:T(8,128)}, u32[]{:S(2)}, u32[]{:S(2)}) collective-permute-start(f32[512,128]{1,0:T(8,128)S(1)} %add.10.own_ref), channel_id=1, source_target_pairs={{0,2},{1,3},{2,0},{3,1},{4,6},{5,7},{6,4},{7,5},{8,10},{9,11},{10,... | collective-permute-start | bytes 786440 | tf_op jit(solution)/shard_map/ppermute | solution.py:572
  53.2 0.9 copy-done.6
  54.0 0.9 copy-done.8
  54.9 0.9 copy-done.10
  55.8 0.9 copy-done.12
  56.7 0.9 copy-done.14
  57.6 0.9 copy-done.16
  58.5 1.4 %below.1 = (f32[6,128,128]{2,1,0:T(8,128)S(1)}, f32[6,128,128]{2,1,0:T(8,128)S(1)}, f32[6,128,128]{2,1,0:T(8,128)S(1)}, f32[6,128,128]{2,1,0:T(8,128)S(1)}, f32[...) custom-call(s32[8,128]{1,0:T(8,128)S(1)} %get-tuple-element.38.refs_, ...), custom_call_target="tpu_custom_call" | custom-call | flops 2000000000 | bytes 4000000 | tf_op jit(solution)/shard_map/below/pallas_call | solution.py:290
  60.5 9.5 %factor_first.1 = (f32[4,128,512]{2,1,0:T(8,128)S(1)}, f32[4,128,128]{2,1,0:T(8,128)S(1)}) custom-call(f32[512,128]{1,0:T(8,128)S(1)} %add.10.own_ref, f32[512,128]{1,0:T(8,128)} %collective-permute-done.11.other_ref, f32[128,512]{1,0:T(8,128)S(1)} %slice_bitcast_fusion.refs_0_, f32[128,512]{1,0:T(8,128)S(1)} %collective-permute-done.12.refs_1_, ...), custom_call_target="tpu_custom_call" | custom-call | flops 10000000000 | bytes 2000000 | tf_op jit(solution)/shard_map/factor_first/pallas_call | solution.py:399
  70.6 1.2 %collective-permute-start.17 = (f32[6,128,128]{2,1,0:T(8,128)S(1)}, f32[6,128,128]{2,1,0:T(8,128)S(1)}, u32[]{:S(2)}, u32[]{:S(2)}) collective-permute-start(f32[6,128,128]{2,1,0:T(8,128)S(1)} %add.11), channel_id=1, source_target_pairs={{0,2},{1,3},{2,0},{3,1},{4,6},{5,7},{6,4},{7,5},{8,10},{9,11},{10,... | collective-permute-start | bytes 1179656 | tf_op jit(solution)/shard_map/ppermute | solution.py:583
  71.9 1.0 %collective-permute-start.9 = (f32[6,128,128]{2,1,0:T(8,128)S(1)}, f32[6,128,128]{2,1,0:T(8,128)S(1)}, u32[]{:S(2)}, u32[]{:S(2)}) collective-permute-start(f32[6,128,128]{2,1,0:T(8,128)S(1)} %add.9), channel_id=1, source_target_pairs={{0,2},{1,3},{2,0},{3,1},{4,6},{5,7},{6,4},{7,5},{8,10},{9,11},{10,... | collective-permute-start | bytes 1179656 | tf_op jit(solution)/shard_map/ppermute | solution.py:583
  72.8 9.8 %factor_last.1 = (f32[512,512]{1,0:T(8,128)S(1)}, f32[128,512]{1,0:T(8,128)S(1)}) custom-call(f32[4,128,512]{2,1,0:T(8,128)S(1)} %get-tuple-element.45.schur_ref, f32[4,128,128]{2,1,0:T(8,128)S(1)} %get-tuple-element.46.inverses_ref), custom_call_target="tpu_custom_call" | custom-call | flops 12000000000 | bytes 2000000 | tf_op jit(solution)/shard_map/factor_last/pallas_call | solution.py:445
  82.7 1.8 %solve_left.1 = (f32[4,128,512]{2,1,0:T(8,128)}, f32[384,256]{1,0:T(8,128)S(1)}) custom-call(f32[4,128,512]{2,1,0:T(8,128)S(1)} %bitcast.7, f32[6,128,128]{2,1,0:T(8,128)S(1)} %get-tuple-element.48.refs_0_, f32[6,128,128]{2,1,0:T(8,128)S(1)} %collective-permute-done.15.refs_1_, f32[6,128,128]{2,1,0:T(8,128)S(1)} %collective-permute-done.17.refs_2_, ...), custom_call_target="tpu_custom_call" | custom-call | flops 2000000000 | bytes 5000000 | tf_op jit(solution)/shard_map/solve_left/pallas_call | solution.py:496
  84.6 5.7 %collective-permute-done.9.refs_2_ = f32[6,128,128]{2,1,0:T(8,128)S(1)} collective-permute-done((f32[6,128,128]{2,1,0:T(8,128)S(1)}, f32[6,128,128]{2,1,0:T(8,128)S(1)}, u32[]{:S(2)}, u32[]{:S(2)}) %collective-permute-start.9) | collective-permute-done | bytes 393248 | tf_op jit(solution)/shard_map/ppermute | solution.py:583
  90.2 1.3 %solve_right.1 = f32[4,128,512]{2,1,0:T(8,128)} custom-call(f32[4,128,512]{2,1,0:T(8,128)S(1)} %bitcast.8, f32[6,128,128]{2,1,0:T(8,128)S(1)} %get-tuple-element.40.refs_0_, f32[6,128,128]{2,1,0:T(8,128)S(1)} %collective-permute-done.7.refs_1_, f32[6,128,128]{2,1,0:T(8,128)S(1)} %collective-permute-done.9.refs_2_, ...), custom_call_target="tpu_custom_call", output_to_operand_aliasing={{}: (6, {})} | custom-call | flops 2000000000 | bytes 5000000 | tf_op jit(solution)/shard_map/solve_right/pallas_call | solution.py:526
  (51 shorter events, 3.4 us)
Async XLA Ops:
  0.7 1.1 %copy-start = (bf16[8,384,128]{2,1,0:T(8,128)(2,1)S(1)}, bf16[8,384,128]{2,1,0:T(8,128)(2,1)}, u32[]{:S(2)}) copy-start(bf16[8,384,128]{2,1,0:T(8,128)(2,1)} %refs_3_.1) | copy-start | bytes 2359300
  5.0 31.8 %copy-start.1 = (f32[1,4,1,128,512]{4,3,2,1,0:T(8,128)S(1)}, f32[1,4,1,128,512]{4,3,2,1,0:T(8,128)}, u32[]{:S(2)}) copy-start(f32[1,4,1,128,512]{4,3,2,1,0:T(8,128)} %param.9) | copy-start | bytes 3145732
  5.1 48.1 %all-to-all-start = ((bf16[8,512,128]{2,1,0:T(8,128)(2,1)}), bf16[8,512,128]{2,1,0:T(8,128)(2,1)S(1)}, u32[]{:S(2)}, u32[]{:S(2)}) async-start(bf16[8,512,128]{2,1,0:T(8,128)(2,1)} %get-tuple-element.39), calls=%async_computation | async-start | bytes 2097152 | tf_op jit(solution)/shard_map/all_to_all | solution.py:560
  12.5 10.6 %collective-permute-start = (bf16[272,128]{1,0:T(8,128)(2,1)S(1)}, bf16[272,128]{1,0:T(8,128)(2,1)S(1)}, u32[]{:S(2)}, u32[]{:S(2)}) collective-permute-start(bf16[272,128]{1,0:T(8,128)(2,1)S(1)} %get-tuple-element.31), channel_id=1, source_target_pairs={{0,4},{4,0},{8,12},{12,8},{16,20},{20,16},{24,28},{28,24},{1,5},{5... | collective-permute-start | bytes 208904 | tf_op jit(solution)/shard_map/ppermute | solution.py:556
  14.5 17.7 %collective-permute-start.1 = (bf16[272,128]{1,0:T(8,128)(2,1)S(1)}, bf16[272,128]{1,0:T(8,128)(2,1)S(1)}, u32[]{:S(2)}, u32[]{:S(2)}) collective-permute-start(bf16[272,128]{1,0:T(8,128)(2,1)S(1)} %get-tuple-element.32), channel_id=1, source_target_pairs={{0,8},{4,12},{8,0},{12,4},{16,24},{20,28},{24,16},{28,20},{1,9},{5... | collective-permute-start | bytes 208904 | tf_op jit(solution)/shard_map/ppermute | solution.py:556
  16.0 20.9 %collective-permute-start.2 = (bf16[272,128]{1,0:T(8,128)(2,1)S(1)}, bf16[272,128]{1,0:T(8,128)(2,1)S(1)}, u32[]{:S(2)}, u32[]{:S(2)}) collective-permute-start(bf16[272,128]{1,0:T(8,128)(2,1)S(1)} %get-tuple-element.33), channel_id=1, source_target_pairs={{0,12},{4,8},{8,4},{12,0},{16,28},{20,24},{24,20},{28,16},{1,13},{... | collective-permute-start | bytes 208904 | tf_op jit(solution)/shard_map/ppermute | solution.py:556
  16.0 31.1 %collective-permute-start.3 = (bf16[272,128]{1,0:T(8,128)(2,1)S(1)}, bf16[272,128]{1,0:T(8,128)(2,1)S(1)}, u32[]{:S(2)}, u32[]{:S(2)}) collective-permute-start(bf16[272,128]{1,0:T(8,128)(2,1)S(1)} %get-tuple-element.34), channel_id=1, source_target_pairs={{0,16},{4,20},{8,24},{12,28},{16,0},{20,4},{24,8},{28,12},{1,17},{... | collective-permute-start | bytes 208904 | tf_op jit(solution)/shard_map/ppermute | solution.py:556
  18.9 30.2 %collective-permute-start.4 = (bf16[272,128]{1,0:T(8,128)(2,1)S(1)}, bf16[272,128]{1,0:T(8,128)(2,1)S(1)}, u32[]{:S(2)}, u32[]{:S(2)}) collective-permute-start(bf16[272,128]{1,0:T(8,128)(2,1)S(1)} %get-tuple-element.35), channel_id=1, source_target_pairs={{0,20},{4,16},{8,28},{12,24},{16,4},{20,0},{24,12},{28,8},{1,21},{... | collective-permute-start | bytes 208904 | tf_op jit(solution)/shard_map/ppermute | solution.py:556
  23.1 26.0 %collective-permute-start.5 = (bf16[272,128]{1,0:T(8,128)(2,1)S(1)}, bf16[272,128]{1,0:T(8,128)(2,1)S(1)}, u32[]{:S(2)}, u32[]{:S(2)}) collective-permute-start(bf16[272,128]{1,0:T(8,128)(2,1)S(1)} %get-tuple-element.36), channel_id=1, source_target_pairs={{0,24},{4,28},{8,16},{12,20},{16,8},{20,12},{24,0},{28,4},{1,25},{... | collective-permute-start | bytes 208904 | tf_op jit(solution)/shard_map/ppermute | solution.py:556
  32.2 16.8 %copy-start.5 = (bf16[272,128]{1,0:T(8,128)(2,1)}, bf16[272,128]{1,0:T(8,128)(2,1)S(1)}, u32[]{:S(2)}) copy-start(bf16[272,128]{1,0:T(8,128)(2,1)S(1)} %collective-permute-done.1.refs_2_.refs_4_) | copy-start | bytes 208900
  32.2 16.8 %collective-permute-start.6 = (bf16[272,128]{1,0:T(8,128)(2,1)S(1)}, bf16[272,128]{1,0:T(8,128)(2,1)S(1)}, u32[]{:S(2)}, u32[]{:S(2)}) collective-permute-start(bf16[272,128]{1,0:T(8,128)(2,1)S(1)} %get-tuple-element.37), channel_id=1, source_target_pairs={{0,28},{4,24},{8,20},{12,16},{16,12},{20,8},{24,4},{28,0},{1,29},{... | collective-permute-start | bytes 208904 | tf_op jit(solution)/shard_map/ppermute | solution.py:556
  36.9 13.0 %copy-start.7 = (bf16[272,128]{1,0:T(8,128)(2,1)}, bf16[272,128]{1,0:T(8,128)(2,1)S(1)}, u32[]{:S(2)}) copy-start(bf16[272,128]{1,0:T(8,128)(2,1)S(1)} %collective-permute-done.2.refs_3_.refs_5_) | copy-start | bytes 208900
  36.9 13.6 %collective-permute-start.13 = (f32[128,512]{1,0:T(8,128)S(1)}, f32[128,512]{1,0:T(8,128)S(1)}, u32[]{:S(2)}, u32[]{:S(2)}) collective-permute-start(f32[128,512]{1,0:T(8,128)S(1)} %slice_bitcast_fusion.refs_0_), channel_id=1, source_target_pairs={{0,2},{1,3},{2,0},{3,1},{4,6},{5,7},{6,4},{7,5},{8,10},{9,11},{10,... | collective-permute-start | bytes 786440 | tf_op jit(solution)/shard_map/ppermute | solution.py:564
  47.1 2.8 %copy-start.9 = (bf16[272,128]{1,0:T(8,128)(2,1)}, bf16[272,128]{1,0:T(8,128)(2,1)S(1)}, u32[]{:S(2)}) copy-start(bf16[272,128]{1,0:T(8,128)(2,1)S(1)} %collective-permute-done.3.refs_4_.refs_6_) | copy-start | bytes 208900
  49.1 0.9 copy-start.13
  49.1 0.9 copy-start.15
  49.9 1.6 %collective-permute-start.10 = (f32[512,128]{1,0:T(8,128)S(1)}, f32[512,128]{1,0:T(8,128)S(1)}, u32[]{:S(2)}, u32[]{:S(2)}) collective-permute-start(f32[512,128]{1,0:T(8,128)S(1)} %get-tuple-element.44), channel_id=1, source_target_pairs={{0,1},{1,0},{2,3},{3,2},{4,5},{5,4},{6,7},{7,6},{8,9},{9,8},{10,11... | collective-permute-start | bytes 786440 | tf_op jit(solution)/shard_map/ppermute | solution.py:570
  50.0 10.5 %collective-permute-start.12 = (f32[128,512]{1,0:T(8,128)S(1)}, f32[128,512]{1,0:T(8,128)S(1)}, u32[]{:S(2)}, u32[]{:S(2)}) collective-permute-start(f32[128,512]{1,0:T(8,128)S(1)} %slice_bitcast_fusion.refs_0_), channel_id=1, source_target_pairs={{0,1},{1,0},{2,3},{3,2},{4,5},{5,4},{6,7},{7,6},{8,9},{9,8},{10,11... | collective-permute-start | bytes 786440 | tf_op jit(solution)/shard_map/ppermute | solution.py:565
  50.5 10.0 %collective-permute-start.14 = (f32[128,512]{1,0:T(8,128)S(1)}, f32[128,512]{1,0:T(8,128)S(1)}, u32[]{:S(2)}, u32[]{:S(2)}) collective-permute-start(f32[128,512]{1,0:T(8,128)S(1)} %collective-permute-done.13.refs_2_), channel_id=1, source_target_pairs={{0,1},{1,0},{2,3},{3,2},{4,5},{5,4},{6,7},{7,6},{8,9},{9,8},{10,11... | collective-permute-start | bytes 786440 | tf_op jit(solution)/shard_map/ppermute | solution.py:566
  51.6 8.9 %collective-permute-start.11 = (f32[512,128]{1,0:T(8,128)S(1)}, f32[512,128]{1,0:T(8,128)}, u32[]{:S(2)}, u32[]{:S(2)}) collective-permute-start(f32[512,128]{1,0:T(8,128)S(1)} %add.10.own_ref), channel_id=1, source_target_pairs={{0,2},{1,3},{2,0},{3,1},{4,6},{5,7},{6,4},{7,5},{8,10},{9,11},{10,... | collective-permute-start | bytes 786440 | tf_op jit(solution)/shard_map/ppermute | solution.py:572
  53.2 0.9 copy-start.6
  54.0 0.9 copy-start.8
  54.9 0.9 copy-start.10
  55.8 0.9 copy-start.12
  56.7 0.9 copy-start.14
  57.6 0.9 copy-start.16
  59.9 10.7 %collective-permute-start.16 = (f32[6,128,128]{2,1,0:T(8,128)S(1)}, f32[6,128,128]{2,1,0:T(8,128)S(1)}, u32[]{:S(2)}, u32[]{:S(2)}) collective-permute-start(f32[6,128,128]{2,1,0:T(8,128)S(1)} %get-tuple-element.51), channel_id=1, source_target_pairs={{0,1},{1,0},{2,3},{3,2},{4,5},{5,4},{6,7},{7,6},{8,9},{9,8},{10,11... | collective-permute-start | bytes 1179656 | tf_op jit(solution)/shard_map/ppermute | solution.py:582
  60.0 11.9 %collective-permute-start.8 = (f32[6,128,128]{2,1,0:T(8,128)S(1)}, f32[6,128,128]{2,1,0:T(8,128)S(1)}, u32[]{:S(2)}, u32[]{:S(2)}) collective-permute-start(f32[6,128,128]{2,1,0:T(8,128)S(1)} %get-tuple-element.43), channel_id=1, source_target_pairs={{0,1},{1,0},{2,3},{3,2},{4,5},{5,4},{6,7},{7,6},{8,9},{9,8},{10,11... | collective-permute-start | bytes 1179656 | tf_op jit(solution)/shard_map/ppermute | solution.py:582
  70.0 12.7 %collective-permute-start.15 = (f32[6,128,128]{2,1,0:T(8,128)S(1)}, f32[6,128,128]{2,1,0:T(8,128)S(1)}, u32[]{:S(2)}, u32[]{:S(2)}) collective-permute-start(f32[6,128,128]{2,1,0:T(8,128)S(1)} %get-tuple-element.49), channel_id=1, source_target_pairs={{0,1},{1,0},{2,3},{3,2},{4,5},{5,4},{6,7},{7,6},{8,9},{9,8},{10,11... | collective-permute-start | bytes 1179656 | tf_op jit(solution)/shard_map/ppermute | solution.py:585
  70.2 14.4 %collective-permute-start.7 = (f32[6,128,128]{2,1,0:T(8,128)S(1)}, f32[6,128,128]{2,1,0:T(8,128)S(1)}, u32[]{:S(2)}, u32[]{:S(2)}) collective-permute-start(f32[6,128,128]{2,1,0:T(8,128)S(1)} %get-tuple-element.41), channel_id=1, source_target_pairs={{0,1},{1,0},{2,3},{3,2},{4,5},{5,4},{6,7},{7,6},{8,9},{9,8},{10,11... | collective-permute-start | bytes 1179656 | tf_op jit(solution)/shard_map/ppermute | solution.py:585
  70.6 12.1 %collective-permute-start.17 = (f32[6,128,128]{2,1,0:T(8,128)S(1)}, f32[6,128,128]{2,1,0:T(8,128)S(1)}, u32[]{:S(2)}, u32[]{:S(2)}) collective-permute-start(f32[6,128,128]{2,1,0:T(8,128)S(1)} %add.11), channel_id=1, source_target_pairs={{0,2},{1,3},{2,0},{3,1},{4,6},{5,7},{6,4},{7,5},{8,10},{9,11},{10,... | collective-permute-start | bytes 1179656 | tf_op jit(solution)/shard_map/ppermute | solution.py:583
  71.9 18.3 %collective-permute-start.9 = (f32[6,128,128]{2,1,0:T(8,128)S(1)}, f32[6,128,128]{2,1,0:T(8,128)S(1)}, u32[]{:S(2)}, u32[]{:S(2)}) collective-permute-start(f32[6,128,128]{2,1,0:T(8,128)S(1)} %add.9), channel_id=1, source_target_pairs={{0,2},{1,3},{2,0},{3,1},{4,6},{5,7},{6,4},{7,5},{8,10},{9,11},{10,... | collective-permute-start | bytes 1179656 | tf_op jit(solution)/shard_map/ppermute | solution.py:583
  (4 other events, 2.9 us)

commit v3 on v2

--- a/solution.py
+++ b/solution.py
@@ -36,19 +36,25 @@
     return [pl.BlockSpec(memory_space=space)] * count
 
 
-def pack_kernel(cb, nb, direct, row_map, anc_order, anc_below, panel, *refs):
+def pack_kernel(cb, nb, direct, row_map, anc_order, anc_below, panel_hbm, anc_hbm, *refs):
     leaves = anc_order.shape[0]
     block_count, desc_count = row_map.shape
-    rows = panel.shape[1] // block_count
-    outs = refs[: leaves if direct else 1]
-    tail_out, inverse, used, chosen, codes, tail_sem = refs[len(outs):]
+    rows = panel_hbm.shape[1] // block_count
+    tail_rows = (block_count - 1) * rows
+    count = leaves if direct else 1
+    heads, tails = refs[:count], refs[count:2 * count]
+    strip, inverse, used, chosen, codes, panel, panel_sem, strip_sem = refs[2 * count:]
     me = lax.axis_index("leaf")
+    panel_copy = pltpu.make_async_copy(panel_hbm, panel, panel_sem)
+    panel_copy.start()
+    strip_copy = pltpu.make_async_copy(anc_hbm.at[0], strip, strip_sem)
+    strip_copy.start()
 
     def clear(leaf):
         inverse[anc_order[leaf]] = leaf
         used[leaf] = 0
         for slot in range(SLOTS):
-            chosen[leaf * SLOTS + slot] = -1
+            chosen[leaf * SLOTS + slot] = 0
             codes[(leaf * SLOTS + slot) * CODES] = cb
             for r in range(1, CODES):
                 codes[(leaf * SLOTS + slot) * CODES + r] = nb
@@ -71,74 +77,39 @@
             codes[place * CODES + r] = found
 
     repeat(desc_count, assign)
-
-    def dest(index):
-        return jnp.bitwise_xor(me, index) if direct else index
-
-    def tail_copy(index, slot):
-        leaf = dest(index)
-        desc = chosen[leaf * SLOTS + slot]
-        tail_rows = (block_count - 1) * rows
-        return desc, pltpu.make_async_copy(
-            panel.at[jnp.maximum(desc, 0), pl.ds(rows, tail_rows)],
-            tail_out.at[leaf, pl.ds(slot * tail_rows, tail_rows)],
-            tail_sem.at[index, slot],
-        )
-
-    def start(index):
-        for slot in range(SLOTS):
-            desc, copy = tail_copy(index, slot)
-
-            @pl.when(desc >= 0)
-            def _():
-                copy.start()
-
-    repeat(leaves, start)
-
-    def write_head(index):
-        leaf = dest(index)
+    panel_copy.wait()
+
+    def write(index):
+        leaf = jnp.bitwise_xor(me, index) if direct else index
+        head = heads[index] if direct else heads[0].at[index]
+        tail = tails[index] if direct else tails[0].at[index]
         row = lax.broadcasted_iota(jnp.int32, (CODE_ROWS, 128), 0)
         values = jnp.zeros((CODE_ROWS, 128), jnp.int32)
         for entry in range(SLOTS * CODES):
             values = jnp.where(row == entry, codes[leaf * SLOTS * CODES + entry], values)
-        values = values.astype(jnp.float32).astype(panel.dtype)
+        head[pl.ds(SLOTS * rows, CODE_ROWS)] = values.astype(jnp.float32).astype(panel.dtype)
         for slot in range(SLOTS):
-            desc = jnp.maximum(chosen[leaf * SLOTS + slot], 0)
-            block = panel[desc, pl.ds(0, rows)]
-            if direct:
-                outs[index][pl.ds(slot * rows, rows)] = block
-            else:
-                outs[0][index, pl.ds(slot * rows, rows)] = block
-        if direct:
-            outs[index][pl.ds(SLOTS * rows, CODE_ROWS)] = values
-        else:
-            outs[0][index, pl.ds(SLOTS * rows, CODE_ROWS)] = values
-
-    repeat(leaves, write_head)
-
-    def finish(index):
-        for slot in range(SLOTS):
-            desc, copy = tail_copy(index, slot)
-
-            @pl.when(desc >= 0)
-            def _():
-                copy.wait()
-
-    repeat(leaves, finish)
-
-
-def pack(desc_panel, row_map, anc_order, anc_below, cb, direct):
+            desc = chosen[leaf * SLOTS + slot]
+            head[pl.ds(slot * rows, rows)] = panel[desc, pl.ds(0, rows)]
+            tail[pl.ds(slot * tail_rows, tail_rows)] = panel[desc, pl.ds(rows, tail_rows)]
+
+    repeat(leaves, write)
+    strip_copy.wait()
+
+
+def pack(desc_panel, row_map, anc_order, anc_below, anc, cb, direct):
     leaves = anc_order.shape[0]
     block_count = row_map.shape[1]
     rows = desc_panel.shape[1] // block_count
     width = desc_panel.shape[2]
-    head_rows = SLOTS * rows + CODE_ROWS
+    head = (SLOTS * rows + CODE_ROWS, width)
+    tail = (SLOTS * (block_count - 1) * rows, width)
     dtype = desc_panel.dtype
     if direct:
-        heads = [pltpu.VMEM((head_rows, width), dtype)] * leaves
+        outs = [pltpu.VMEM(head, dtype)] * leaves + [pltpu.VMEM(tail, dtype)] * leaves
     else:
-        heads = [jax.ShapeDtypeStruct((leaves, head_rows, width), dtype)]
-    tails = jax.ShapeDtypeStruct((leaves, SLOTS * (block_count - 1) * rows, width), dtype)
+        outs = [jax.ShapeDtypeStruct((leaves,) + shape, dtype) for shape in (head, tail)]
+    outs.append(pltpu.VMEM(anc.shape[1:], anc.dtype))
     nb = anc_below.shape[1]
 
     def body(*refs):
@@ -147,18 +118,25 @@
     return pl.pallas_call(
         body,
         name="pack",
-        compiler_params=limit(12 if direct else 32),
-        out_shape=heads + [tails],
-        in_specs=spaces(3, pltpu.SMEM) + spaces(1, pltpu.VMEM),
-        out_specs=spaces(len(heads), pltpu.VMEM) + spaces(1, pl.ANY),
+        compiler_params=limit(12 if direct else 40),
+        out_shape=outs,
+        in_specs=spaces(3, pltpu.SMEM) + spaces(2, pl.ANY),
+        out_specs=spaces(len(outs), pltpu.VMEM),
         scratch_shapes=[
             pltpu.SMEM((leaves,), jnp.int32),
             pltpu.SMEM((leaves,), jnp.int32),
             pltpu.SMEM((leaves * SLOTS,), jnp.int32),
             pltpu.SMEM((leaves * SLOTS * CODES,), jnp.int32),
-            pltpu.SemaphoreType.DMA((leaves, SLOTS)),
-        ],
-    )(row_map.T, anc_order, anc_below, desc_panel)
+            pltpu.VMEM(desc_panel.shape, dtype),
+            pltpu.SemaphoreType.DMA(()),
+            pltpu.SemaphoreType.DMA(()),
+        ],
+    )(
+        *(
+            pltpu.with_memory_space_constraint(array, pltpu.HBM)
+            for array in (row_map.T, anc_order, anc_below, desc_panel, anc)
+        )
+    )
 
 
 def diagonal_kernel(cb, leaves, *refs):
@@ -231,16 +209,16 @@
     )(*(near_core(*heads) if len(heads) > 1 else heads))
 
 
-def below_kernel(cb, blk_count, per, leaves, count, codes, tails, *refs):
+def below_kernel(cb, blk_count, per, leaves, count, codes, *refs):
+    tails, refs = refs[:count], refs[count:]
     heads = refs[:count]
     outs = refs[count:count + blk_count * HALVES]
     acc, products = refs[count + blk_count * HALVES:]
     direct = count > 1
-    me_leaf = lax.axis_index("leaf")
     me_blk = lax.axis_index("blk")
     rows = acc.shape[1]
     group = min(leaves, 8)
-    tail_rows = tails.shape[1] // SLOTS
+    tail_rows = tails[0].shape[-2] // SLOTS
     extra = tail_rows // rows
     blocks = blk_count * cb * per
 
@@ -250,13 +228,13 @@
     def step(base):
         for offset in range(group):
             index = base + offset
-            source = jnp.bitwise_xor(me_leaf, index) if direct else index
             for slot in range(SLOTS):
                 if direct:
                     head = heads[index][pl.ds(slot * rows, rows)]
+                    tail = tails[index][pl.ds(slot * tail_rows, tail_rows)]
                 else:
                     head = heads[0][index, pl.ds(slot * rows, rows)]
-                tail = tails[source, pl.ds(slot * tail_rows, tail_rows)]
+                    tail = tails[0][index, pl.ds(slot * tail_rows, tail_rows)]
                 products[offset * SLOTS + slot] = lax.dot_general(
                     tail, head, (((1,), (1,)), ((), ())), preferred_element_type=jnp.float32
                 )
@@ -292,14 +270,14 @@
         name="below",
         compiler_params=limit(16 if len(heads) > 1 else 56),
         out_shape=[pltpu.VMEM((cb * per // HALVES, rows, rows), jnp.float32)] * outs,
-        in_specs=spaces(1, pltpu.SMEM) + spaces(1 + len(heads), pltpu.VMEM),
+        in_specs=spaces(1, pltpu.SMEM) + spaces(2 * len(heads), pltpu.VMEM),
         out_specs=spaces(outs, pltpu.VMEM),
         scratch_shapes=[
             pltpu.VMEM((blocks + 1, rows, rows), jnp.float32),
-            pltpu.VMEM((group * SLOTS, tails.shape[1] // SLOTS, rows), jnp.float32),
+            pltpu.VMEM((group * SLOTS, tails[0].shape[-2] // SLOTS, rows), jnp.float32),
         ],
         cost_estimate=pl.CostEstimate(flops=2000000000, bytes_accessed=4000000, transcendentals=0),
-    )(codes, *(near_core(tails, *heads) if len(heads) > 1 else [tails, *heads]))
+    )(codes, *(near_core(*tails, *heads) if len(heads) > 1 else [*tails, *heads]))
 
 
 def factor_block(work, rows):
@@ -352,7 +330,7 @@
         lax.fori_loop(0, size // PANEL, panel, 0)
 
 
-def eliminate(schur, inverses, work, block, cb, rows):
+def eliminate(schur, inverse_ref, work, block, cb, rows):
     eye = lax.broadcasted_iota(jnp.int32, (rows, rows), 0) == lax.broadcasted_iota(
         jnp.int32, (rows, rows), 1
     )
@@ -365,7 +343,7 @@
     factor_block(work, rows)
     schur[block, :, here:here + rows] = jnp.where(upper, work[:, :rows], 0.0)
     inverse = work[:, rows:]
-    inverses[block] = inverse
+    inverse_ref[...] = inverse
     if block + 1 < cb:
         after = here + rows
         strip = lax.dot_general(
@@ -381,12 +359,16 @@
             )
 
 
+def kept_inverse(schur, block, cb, rows):
+    return schur.at[cb - 1, :, block * rows:(block + 1) * rows]
+
+
 def first_factor(own_sum, other_sum, strips, cb, rows):
     blk_count = len(strips)
 
     def body(own_ref, other_ref, *refs):
         strip_refs = refs[:blk_count]
-        schur, inverses, work = refs[blk_count:]
+        schur, work = refs[blk_count:]
         me = lax.axis_index("blk")
         for x in range(blk_count):
             schur[jnp.bitwise_xor(me, x)] = strip_refs[x][...]
@@ -394,7 +376,7 @@
             part = slice(c * rows, (c + 1) * rows)
             schur[c, :, part] -= own_ref[part] + other_ref[part]
         for block in range(cb // SPLIT):
-            eliminate(schur, inverses, work, block, cb, rows)
+            eliminate(schur, kept_inverse(schur, block, cb, rows), work, block, cb, rows)
 
     return pl.pallas_call(
         body,
@@ -402,25 +384,24 @@
         compiler_params=limit(12),
         out_shape=[
             pltpu.VMEM((cb, rows, cb * rows), jnp.float32),
-            pltpu.VMEM((cb, rows, rows), jnp.float32),
         ],
         in_specs=spaces(2 + blk_count, pltpu.VMEM),
-        out_specs=spaces(2, pltpu.VMEM),
+        out_specs=spaces(1, pltpu.VMEM),
         scratch_shapes=[pltpu.VMEM((rows, 2 * rows), jnp.float32)],
         cost_estimate=pl.CostEstimate(flops=10000000000, bytes_accessed=2000000, transcendentals=0),
-    )(*near_core(own_sum, other_sum), strips[0], *near_core(*strips[1:]))
-
-
-def last_factor(schur_in, inverses_in, cb, rows):
+    )(*near_core(own_sum, other_sum, *strips))[0]
+
+
+def last_factor(schur_in, cb, rows):
     width = cb * rows
 
-    def body(schur_ref, inverses_ref, whole, lower, schur, inverses, work):
+    def body(schur_ref, whole, lower, schur, inverses, work):
         me = lax.axis_index("blk")
         schur[...] = schur_ref[...]
         for block in range(cb // SPLIT):
-            inverses[block] = inverses_ref[block]
+            inverses[block] = kept_inverse(schur_ref, block, cb, rows)[...]
         for block in range(cb // SPLIT, cb):
-            eliminate(schur, inverses, work, block, cb, rows)
+            eliminate(schur, inverses.at[block], work, block, cb, rows)
         for k in range(cb):
             piece = jnp.where(k <= me, schur[k, :, pl.ds(pl.multiple_of(me * rows, rows), rows)], 0.0)
             lower[:, k * rows:(k + 1) * rows] = piece.T
@@ -450,7 +431,7 @@
             pltpu.VMEM((width, width), jnp.float32),
             pltpu.VMEM((rows, width), jnp.float32),
         ],
-        in_specs=spaces(2, pltpu.VMEM),
+        in_specs=spaces(1, pltpu.VMEM),
         out_specs=spaces(2, pltpu.VMEM),
         scratch_shapes=[
             pltpu.VMEM((cb, rows, width), jnp.float32),
@@ -458,7 +439,7 @@
             pltpu.VMEM((rows, 2 * rows), jnp.float32),
         ],
         cost_estimate=pl.CostEstimate(flops=12000000000, bytes_accessed=2000000, transcendentals=0),
-    )(*near_core(schur_in, inverses_in))
+    )(*near_core(schur_in))
 
 
 def solve_dot(left, right):
@@ -548,19 +529,22 @@
     near = [(i, i ^ 1) for i in range(blk_count)]
     far = [(i, i ^ 2) for i in range(blk_count)]
 
-    *heads, tails = pack(desc_panel, row_map, anc_order, anc_below, cb, direct)
-    if direct:
-        received = [heads[0]]
+    panel = anc_panel.reshape(per + 1, rows, width)
+    *packed, strip = pack(desc_panel, row_map, anc_order, anc_below, panel, cb, direct)
+    count = len(packed) // 2
+    heads, tails = packed[:count], packed[count:]
+
+    def exchange(arrays):
+        if not direct:
+            return [lax.all_to_all(arrays[0], "leaf", split_axis=0, concat_axis=0, tiled=True)]
+        received = [arrays[0]]
         for k in range(1, leaves):
             swap = [(i, i ^ k) for i in range(leaves)]
-            received.append(lax.ppermute(heads[k], "leaf", swap))
-        heads = received
-    else:
-        heads = [lax.all_to_all(heads[0], "leaf", split_axis=0, concat_axis=0, tiled=True)]
-    tails = lax.all_to_all(tails, "leaf", split_axis=0, concat_axis=0, tiled=True)
-
-    panel = anc_panel.reshape(per + 1, rows, width)
-    strip = panel[0]
+            received.append(lax.ppermute(arrays[k], "leaf", swap))
+        return received
+
+    heads = exchange(heads)
+    tails = exchange(tails)
     strip_far = lax.ppermute(strip, "blk", far)
     strip_near = lax.ppermute(strip, "blk", near)
     strip_both = lax.ppermute(strip_far, "blk", near)
@@ -570,7 +554,7 @@
     diagonal_near = lax.ppermute(diagonal, "blk", near)
     diagonal = diagonal + diagonal_near
     diagonal_far = lax.ppermute(diagonal, "blk", far)
-    schur, inverses = first_factor(diagonal, diagonal_far, strips, cb, rows)
+    schur = first_factor(diagonal, diagonal_far, strips, cb, rows)
 
     partials = below_update(heads, tails, codes, cb, blk_count, per, leaves, rows)
     kept, for_near, for_far, for_both = (
@@ -583,7 +567,7 @@
         from_far.append(lax.ppermute(for_far[half] + passed, "blk", far))
     for half in range(HALVES):
         from_near.append(lax.ppermute(for_near[half], "blk", near))
-    whole, lower = last_factor(schur, inverses, cb, rows)
+    whole, lower = last_factor(schur, cb, rows)
     updates = [[kept[half], from_near[half], from_far[half]] for half in range(HALVES)]
     out, carried = solve_left(panel, updates[0], whole, lower, cb, per, rows)
     out = solve_right(panel, updates[1], whole, carried, out, cb, per, rows)

time: 92.1 us -> 78.3 us (0.85)
  the two profiles are of different devices: /device:TPU:0 before, /device:TPU:8 now
where the time goes in v3:
time: 78.3 us; the launch traced here: 78.1 us
  waiting for transfers between devices  26.1 us (33%)
  starting transfers between devices  25.9 us (33%)
  Pallas kernels  25.8 us (33%)
    ppermute x14, waiting for transfers between devices, exchange(): received.append(lax.ppermute(arrays[k], 'leaf', swap))  21.2 us
    ppermute x14, starting transfers between devices, exchange(): received.append(lax.ppermute(arrays[k], 'leaf', swap))  19 us
    pallas_call x1, Pallas kernels, last_factor(): pl.pallas_call(body, name='factor_last', compiler_params=limit(12), out_s...  9.84 us
    pallas_call x1, Pallas kernels, first_factor(): pl.pallas_call(body, name='factor_first', compiler_params=limit(12), out_...  8.59 us
    ppermute x1, waiting for transfers between devices, shards(): diagonal_far = lax.ppermute(diagonal, 'blk', far)  4.87 us
    ppermute x2, starting transfers between devices, shards(): from_far.append(lax.ppermute(for_far[half] + passed, 'blk', far))  2.09 us
    pallas_call x1, Pallas kernels, pack(): pl.pallas_call(body, name='pack', compiler_params=limit(12 if direct else...  2.04 us
    pallas_call x1, Pallas kernels, solve_left(): pl.pallas_call(body, name='solve_left', compiler_params=limit(16), out_sh...  1.85 us
  transfers between devices with their start and end apart: 25, of which 8 were waited for; matrix products, arithmetic and copies ran while one was open for 0% of the time, Pallas kernels for 29%

profile of v3, /device:TPU:8, one launch (start us, length us, event | category | flops | bytes accessed | tf_op | source)
XLA Modules:
  0.0 78.1 jit_solution(17312546594191246841)
XLA Ops:
  0.0 2.0 %pack.1 = (bf16[272,128]{1,0:T(8,128)(2,1)S(1)}, bf16[272,128]{1,0:T(8,128)(2,1)S(1)}, bf16[272,128]{1,0:T(8,128)(2,1)S(1)}, bf16[272,128]{1,0:T(8,128)(2,1)S(1)...) custom-call(s32[3,8]{1,0:T(4,128)} %bitcast.8, ...), custom_call_target="tpu_custom_call" | custom-call | tf_op jit(solution)/shard_map/pack/pallas_call | solution.py:118
  2.0 1.6 %collective-permute-start = (bf16[272,128]{1,0:T(8,128)(2,1)S(1)}, bf16[272,128]{1,0:T(8,128)(2,1)S(1)}, u32[]{:S(2)}, u32[]{:S(2)}) collective-permute-start(bf16[272,128]{1,0:T(8,128)(2,1)S(1)} %get-tuple-element.37), channel_id=1, source_target_pairs={{0,4},{4,0},{8,12},{12,8},{16,20},{20,16},{24,28},{28,24},{1,5},{5... | collective-permute-start | bytes 208904 | tf_op jit(solution)/shard_map/ppermute | solution.py:543
  3.6 0.4 collective-permute-start.1
  4.1 1.5 %collective-permute-start.2 = (bf16[272,128]{1,0:T(8,128)(2,1)S(1)}, bf16[272,128]{1,0:T(8,128)(2,1)S(1)}, u32[]{:S(2)}, u32[]{:S(2)}) collective-permute-start(bf16[272,128]{1,0:T(8,128)(2,1)S(1)} %get-tuple-element.39), channel_id=1, source_target_pairs={{0,12},{4,8},{8,4},{12,0},{16,28},{20,24},{24,20},{28,16},{1,13},{... | collective-permute-start | bytes 208904 | tf_op jit(solution)/shard_map/ppermute | solution.py:543
  5.6 2.6 %collective-permute-start.3 = (bf16[272,128]{1,0:T(8,128)(2,1)S(1)}, bf16[272,128]{1,0:T(8,128)(2,1)S(1)}, u32[]{:S(2)}, u32[]{:S(2)}) collective-permute-start(bf16[272,128]{1,0:T(8,128)(2,1)S(1)} %get-tuple-element.40), channel_id=1, source_target_pairs={{0,16},{4,20},{8,24},{12,28},{16,0},{20,4},{24,8},{28,12},{1,17},{... | collective-permute-start | bytes 208904 | tf_op jit(solution)/shard_map/ppermute | solution.py:543
  8.2 1.5 %collective-permute-start.7 = (bf16[512,128]{1,0:T(8,128)(2,1)S(1)}, bf16[512,128]{1,0:T(8,128)(2,1)S(1)}, u32[]{:S(2)}, u32[]{:S(2)}) collective-permute-start(bf16[512,128]{1,0:T(8,128)(2,1)S(1)} %get-tuple-element.46), channel_id=1, source_target_pairs={{0,4},{4,0},{8,12},{12,8},{16,20},{20,16},{24,28},{28,24},{1,5},{5... | collective-permute-start | bytes 393224 | tf_op jit(solution)/shard_map/ppermute | solution.py:543
  9.7 0.5 collective-permute-start.8
  10.1 0.8 collective-permute-start.4
  10.9 2.2 %collective-permute-start.5 = (bf16[272,128]{1,0:T(8,128)(2,1)S(1)}, bf16[272,128]{1,0:T(8,128)(2,1)S(1)}, u32[]{:S(2)}, u32[]{:S(2)}) collective-permute-start(bf16[272,128]{1,0:T(8,128)(2,1)S(1)} %get-tuple-element.42), channel_id=1, source_target_pairs={{0,24},{4,28},{8,16},{12,20},{16,8},{20,12},{24,0},{28,4},{1,25},{... | collective-permute-start | bytes 208904 | tf_op jit(solution)/shard_map/ppermute | solution.py:543
  13.2 1.0 %collective-permute-start.6 = (bf16[272,128]{1,0:T(8,128)(2,1)S(1)}, bf16[272,128]{1,0:T(8,128)(2,1)S(1)}, u32[]{:S(2)}, u32[]{:S(2)}) collective-permute-start(bf16[272,128]{1,0:T(8,128)(2,1)S(1)} %get-tuple-element.43), channel_id=1, source_target_pairs={{0,28},{4,24},{8,20},{12,16},{16,12},{20,8},{24,4},{28,0},{1,29},{... | collective-permute-start | bytes 208904 | tf_op jit(solution)/shard_map/ppermute | solution.py:543
  14.2 3.6 %collective-permute-done.4.refs_5_.refs_14_ = bf16[272,128]{1,0:T(8,128)(2,1)S(1)} collective-permute-done((bf16[272,128]{1,0:T(8,128)(2,1)S(1)}, bf16[272,128]{1,0:T(8,128)(2,1)S(1)}, u32[]{:S(2)}, u32[]{:S(2)}) %collective-permute-start.4) | collective-permute-done | bytes 69664 | tf_op jit(solution)/shard_map/ppermute | solution.py:543
  17.7 3.8 %collective-permute-start.9 = (bf16[512,128]{1,0:T(8,128)(2,1)S(1)}, bf16[512,128]{1,0:T(8,128)(2,1)S(1)}, u32[]{:S(2)}, u32[]{:S(2)}) collective-permute-start(bf16[512,128]{1,0:T(8,128)(2,1)S(1)} %get-tuple-element.48), channel_id=1, source_target_pairs={{0,12},{4,8},{8,4},{12,0},{16,28},{20,24},{24,20},{28,16},{1,13},{... | collective-permute-start | bytes 393224 | tf_op jit(solution)/shard_map/ppermute | solution.py:543
  21.6 0.7 collective-permute-done.5.refs_6_.refs_15_
  22.2 2.8 %collective-permute-done.6.refs_7_.refs_16_ = bf16[272,128]{1,0:T(8,128)(2,1)S(1)} collective-permute-done((bf16[272,128]{1,0:T(8,128)(2,1)S(1)}, bf16[272,128]{1,0:T(8,128)(2,1)S(1)}, u32[]{:S(2)}, u32[]{:S(2)}) %collective-permute-start.6) | collective-permute-done | bytes 69664 | tf_op jit(solution)/shard_map/ppermute | solution.py:543
  25.4 2.7 %collective-permute-start.13 = (bf16[512,128]{1,0:T(8,128)(2,1)S(1)}, bf16[512,128]{1,0:T(8,128)(2,1)S(1)}, u32[]{:S(2)}, u32[]{:S(2)}) collective-permute-start(bf16[512,128]{1,0:T(8,128)(2,1)S(1)} %get-tuple-element.52), channel_id=1, source_target_pairs={{0,28},{4,24},{8,20},{12,16},{16,12},{20,8},{24,4},{28,0},{1,29},{... | collective-permute-start | bytes 393224 | tf_op jit(solution)/shard_map/ppermute | solution.py:543
  28.1 0.8 %diagonal.1 = (f32[512,128]{1,0:T(8,128)S(1)}, s32[8,128]{1,0:T(8,128)S(1)}) custom-call(bf16[272,128]{1,0:T(8,128)(2,1)S(1)} %get-tuple-element.36.refs_0_.refs_9_, bf16[272,128]{1,0:T(8,128)(2,1)S(1)} %collective-permute-done.refs_1_.refs_10_, bf16[272,128]{1,0:T(8,128)(2,1)S(1)} %collective-permute-done.1.refs_2_.refs_11_, ...), custom_call_target="tpu_custom_call" | custom-call | flops 2000000000 | bytes 1000000 | tf_op jit(solution)/shard_map/diagonal/pallas_call | solution.py:194
  28.9 1.6 %collective-permute-start.20 = (f32[128,512]{1,0:T(8,128)S(1)}, f32[128,512]{1,0:T(8,128)S(1)}, u32[]{:S(2)}, u32[]{:S(2)}) collective-permute-start(f32[128,512]{1,0:T(8,128)S(1)} %get-tuple-element.58.refs_0_), channel_id=1, source_target_pairs={{0,2},{1,3},{2,0},{3,1},{4,6},{5,7},{6,4},{7,5},{8,10},{9,11},{10,... | collective-permute-start | bytes 786440 | tf_op jit(solution)/shard_map/ppermute | solution.py:548
  30.5 5.0 %collective-permute-done.10.refs_5_ = bf16[512,128]{1,0:T(8,128)(2,1)S(1)} collective-permute-done((bf16[512,128]{1,0:T(8,128)(2,1)S(1)}, bf16[512,128]{1,0:T(8,128)(2,1)S(1)}, u32[]{:S(2)}, u32[]{:S(2)}) %collective-permute-start.10) | collective-permute-done | bytes 131104 | tf_op jit(solution)/shard_map/ppermute | solution.py:543
  35.5 2.8 %collective-permute-done.11.refs_6_ = bf16[512,128]{1,0:T(8,128)(2,1)S(1)} collective-permute-done((bf16[512,128]{1,0:T(8,128)(2,1)S(1)}, bf16[512,128]{1,0:T(8,128)(2,1)S(1)}, u32[]{:S(2)}, u32[]{:S(2)}) %collective-permute-start.11) | collective-permute-done | bytes 131104 | tf_op jit(solution)/shard_map/ppermute | solution.py:543
  38.3 3.7 %collective-permute-done.12.refs_7_ = bf16[512,128]{1,0:T(8,128)(2,1)S(1)} collective-permute-done((bf16[512,128]{1,0:T(8,128)(2,1)S(1)}, bf16[512,128]{1,0:T(8,128)(2,1)S(1)}, u32[]{:S(2)}, u32[]{:S(2)}) %collective-permute-start.12) | collective-permute-done | bytes 131104 | tf_op jit(solution)/shard_map/ppermute | solution.py:543
  42.0 2.6 %collective-permute-done.13.refs_8_ = bf16[512,128]{1,0:T(8,128)(2,1)S(1)} collective-permute-done((bf16[512,128]{1,0:T(8,128)(2,1)S(1)}, bf16[512,128]{1,0:T(8,128)(2,1)S(1)}, u32[]{:S(2)}, u32[]{:S(2)}) %collective-permute-start.13) | collective-permute-done | bytes 131104 | tf_op jit(solution)/shard_map/ppermute | solution.py:543
  44.6 1.4 %below.1 = (f32[6,128,128]{2,1,0:T(8,128)S(1)}, f32[6,128,128]{2,1,0:T(8,128)S(1)}, f32[6,128,128]{2,1,0:T(8,128)S(1)}, f32[6,128,128]{2,1,0:T(8,128)S(1)}, f32[...) custom-call(s32[8,128]{1,0:T(8,128)S(1)} %get-tuple-element.44.refs_, ...), custom_call_target="tpu_custom_call" | custom-call | flops 2000000000 | bytes 4000000 | tf_op jit(solution)/shard_map/below/pallas_call | solution.py:268
  46.1 0.5 collective-permute-start.23
  47.2 1.6 %collective-permute-start.18 = (f32[512,128]{1,0:T(8,128)S(1)}, f32[512,128]{1,0:T(8,128)S(1)}, u32[]{:S(2)}, u32[]{:S(2)}) collective-permute-start(f32[512,128]{1,0:T(8,128)S(1)} %add.10.own_ref), channel_id=1, source_target_pairs={{0,2},{1,3},{2,0},{3,1},{4,6},{5,7},{6,4},{7,5},{8,10},{9,11},{10,... | collective-permute-start | bytes 786440 | tf_op jit(solution)/shard_map/ppermute | solution.py:556
  48.8 0.6 collective-permute-start.22
  49.5 0.8 %collective-permute-start.16 = (f32[6,128,128]{2,1,0:T(8,128)S(1)}, f32[6,128,128]{2,1,0:T(8,128)S(1)}, u32[]{:S(2)}, u32[]{:S(2)}) collective-permute-start(f32[6,128,128]{2,1,0:T(8,128)S(1)} %add.9), channel_id=1, source_target_pairs={{0,2},{1,3},{2,0},{3,1},{4,6},{5,7},{6,4},{7,5},{8,10},{9,11},{10,... | collective-permute-start | bytes 1179656 | tf_op jit(solution)/shard_map/ppermute | solution.py:567
  50.3 1.3 %collective-permute-start.24 = (f32[6,128,128]{2,1,0:T(8,128)S(1)}, f32[6,128,128]{2,1,0:T(8,128)S(1)}, u32[]{:S(2)}, u32[]{:S(2)}) collective-permute-start(f32[6,128,128]{2,1,0:T(8,128)S(1)} %add.11), channel_id=1, source_target_pairs={{0,2},{1,3},{2,0},{3,1},{4,6},{5,7},{6,4},{7,5},{8,10},{9,11},{10,... | collective-permute-start | bytes 1179656 | tf_op jit(solution)/shard_map/ppermute | solution.py:567
  51.6 4.9 %collective-permute-done.18.other_ref = f32[512,128]{1,0:T(8,128)S(1)} collective-permute-done((f32[512,128]{1,0:T(8,128)S(1)}, f32[512,128]{1,0:T(8,128)S(1)}, u32[]{:S(2)}, u32[]{:S(2)}) %collective-permute-start.18) | collective-permute-done | bytes 262176 | tf_op jit(solution)/shard_map/ppermute | solution.py:556
  56.4 8.6 %factor_first.1.schur_ref = f32[4,128,512]{2,1,0:T(8,128)S(1)} custom-call(f32[512,128]{1,0:T(8,128)S(1)} %add.10.own_ref, f32[512,128]{1,0:T(8,128)S(1)} %collective-permute-done.18.other_ref, f32[128,512]{1,0:T(8,128)S(1)} %get-tuple-element.58.refs_0_, f32[128,512]{1,0:T(8,128)S(1)} %collective-permute-done.19.refs_1_, ...), custom_call_target="tpu_custom_call" | custom-call | flops 10000000000 | bytes 2000000 | tf_op jit(solution)/shard_map/factor_first/pallas_call | solution.py:381
  65.0 9.8 %factor_last.1 = (f32[512,512]{1,0:T(8,128)S(1)}, f32[128,512]{1,0:T(8,128)S(1)}) custom-call(f32[4,128,512]{2,1,0:T(8,128)S(1)} %factor_first.1.schur_ref), custom_call_target="tpu_custom_call" | custom-call | flops 12000000000 | bytes 2000000 | tf_op jit(solution)/shard_map/factor_last/pallas_call | solution.py:426
  74.9 1.9 %solve_left.1 = (f32[4,128,512]{2,1,0:T(8,128)}, f32[384,256]{1,0:T(8,128)S(1)}) custom-call(f32[4,128,512]{2,1,0:T(8,128)S(1)} %bitcast.6, f32[6,128,128]{2,1,0:T(8,128)S(1)} %get-tuple-element.60.refs_0_, f32[6,128,128]{2,1,0:T(8,128)S(1)} %collective-permute-done.22.refs_1_, f32[6,128,128]{2,1,0:T(8,128)S(1)} %collective-permute-done.24.refs_2_, ...), custom_call_target="tpu_custom_call" | custom-call | flops 2000000000 | bytes 5000000 | tf_op jit(solution)/shard_map/solve_left/pallas_call | solution.py:477
  76.8 1.3 %solve_right.1 = f32[4,128,512]{2,1,0:T(8,128)} custom-call(f32[4,128,512]{2,1,0:T(8,128)S(1)} %bitcast.7, f32[6,128,128]{2,1,0:T(8,128)S(1)} %get-tuple-element.53.refs_0_, f32[6,128,128]{2,1,0:T(8,128)S(1)} %collective-permute-done.14.refs_1_, f32[6,128,128]{2,1,0:T(8,128)S(1)} %collective-permute-done.16.refs_2_, ...), custom_call_target="tpu_custom_call", output_to_operand_aliasing={{}: (6, {})} | custom-call | flops 2000000000 | bytes 5000000 | tf_op jit(solution)/shard_map/solve_right/pallas_call | solution.py:507
  (30 shorter events, 1.1 us)
Async XLA Ops:
  2.0 7.6 %collective-permute-start = (bf16[272,128]{1,0:T(8,128)(2,1)S(1)}, bf16[272,128]{1,0:T(8,128)(2,1)S(1)}, u32[]{:S(2)}, u32[]{:S(2)}) collective-permute-start(bf16[272,128]{1,0:T(8,128)(2,1)S(1)} %get-tuple-element.37), channel_id=1, source_target_pairs={{0,4},{4,0},{8,12},{12,8},{16,20},{20,16},{24,28},{28,24},{1,5},{5... | collective-permute-start | bytes 208904 | tf_op jit(solution)/shard_map/ppermute | solution.py:543
  3.6 6.5 %collective-permute-start.1 = (bf16[272,128]{1,0:T(8,128)(2,1)S(1)}, bf16[272,128]{1,0:T(8,128)(2,1)S(1)}, u32[]{:S(2)}, u32[]{:S(2)}) collective-permute-start(bf16[272,128]{1,0:T(8,128)(2,1)S(1)} %get-tuple-element.38), channel_id=1, source_target_pairs={{0,8},{4,12},{8,0},{12,4},{16,24},{20,28},{24,16},{28,20},{1,9},{5... | collective-permute-start | bytes 208904 | tf_op jit(solution)/shard_map/ppermute | solution.py:543
  4.1 6.9 %collective-permute-start.2 = (bf16[272,128]{1,0:T(8,128)(2,1)S(1)}, bf16[272,128]{1,0:T(8,128)(2,1)S(1)}, u32[]{:S(2)}, u32[]{:S(2)}) collective-permute-start(bf16[272,128]{1,0:T(8,128)(2,1)S(1)} %get-tuple-element.39), channel_id=1, source_target_pairs={{0,12},{4,8},{8,4},{12,0},{16,28},{20,24},{24,20},{28,16},{1,13},{... | collective-permute-start | bytes 208904 | tf_op jit(solution)/shard_map/ppermute | solution.py:543
  5.6 7.6 %collective-permute-start.3 = (bf16[272,128]{1,0:T(8,128)(2,1)S(1)}, bf16[272,128]{1,0:T(8,128)(2,1)S(1)}, u32[]{:S(2)}, u32[]{:S(2)}) collective-permute-start(bf16[272,128]{1,0:T(8,128)(2,1)S(1)} %get-tuple-element.40), channel_id=1, source_target_pairs={{0,16},{4,20},{8,24},{12,28},{16,0},{20,4},{24,8},{28,12},{1,17},{... | collective-permute-start | bytes 208904 | tf_op jit(solution)/shard_map/ppermute | solution.py:543
  8.2 16.9 %collective-permute-start.7 = (bf16[512,128]{1,0:T(8,128)(2,1)S(1)}, bf16[512,128]{1,0:T(8,128)(2,1)S(1)}, u32[]{:S(2)}, u32[]{:S(2)}) collective-permute-start(bf16[512,128]{1,0:T(8,128)(2,1)S(1)} %get-tuple-element.46), channel_id=1, source_target_pairs={{0,4},{4,0},{8,12},{12,8},{16,20},{20,16},{24,28},{28,24},{1,5},{5... | collective-permute-start | bytes 393224 | tf_op jit(solution)/shard_map/ppermute | solution.py:543
  9.7 15.7 %collective-permute-start.8 = (bf16[512,128]{1,0:T(8,128)(2,1)S(1)}, bf16[512,128]{1,0:T(8,128)(2,1)S(1)}, u32[]{:S(2)}, u32[]{:S(2)}) collective-permute-start(bf16[512,128]{1,0:T(8,128)(2,1)S(1)} %get-tuple-element.47), channel_id=1, source_target_pairs={{0,8},{4,12},{8,0},{12,4},{16,24},{20,28},{24,16},{28,20},{1,9},{5... | collective-permute-start | bytes 393224 | tf_op jit(solution)/shard_map/ppermute | solution.py:543
  10.1 7.6 %collective-permute-start.4 = (bf16[272,128]{1,0:T(8,128)(2,1)S(1)}, bf16[272,128]{1,0:T(8,128)(2,1)S(1)}, u32[]{:S(2)}, u32[]{:S(2)}) collective-permute-start(bf16[272,128]{1,0:T(8,128)(2,1)S(1)} %get-tuple-element.41), channel_id=1, source_target_pairs={{0,20},{4,16},{8,28},{12,24},{16,4},{20,0},{24,12},{28,8},{1,21},{... | collective-permute-start | bytes 208904 | tf_op jit(solution)/shard_map/ppermute | solution.py:543
  10.9 11.3 %collective-permute-start.5 = (bf16[272,128]{1,0:T(8,128)(2,1)S(1)}, bf16[272,128]{1,0:T(8,128)(2,1)S(1)}, u32[]{:S(2)}, u32[]{:S(2)}) collective-permute-start(bf16[272,128]{1,0:T(8,128)(2,1)S(1)} %get-tuple-element.42), channel_id=1, source_target_pairs={{0,24},{4,28},{8,16},{12,20},{16,8},{20,12},{24,0},{28,4},{1,25},{... | collective-permute-start | bytes 208904 | tf_op jit(solution)/shard_map/ppermute | solution.py:543
  13.2 11.9 %collective-permute-start.6 = (bf16[272,128]{1,0:T(8,128)(2,1)S(1)}, bf16[272,128]{1,0:T(8,128)(2,1)S(1)}, u32[]{:S(2)}, u32[]{:S(2)}) collective-permute-start(bf16[272,128]{1,0:T(8,128)(2,1)S(1)} %get-tuple-element.43), channel_id=1, source_target_pairs={{0,28},{4,24},{8,20},{12,16},{16,12},{20,8},{24,4},{28,0},{1,29},{... | collective-permute-start | bytes 208904 | tf_op jit(solution)/shard_map/ppermute | solution.py:543
  17.7 11.2 %collective-permute-start.9 = (bf16[512,128]{1,0:T(8,128)(2,1)S(1)}, bf16[512,128]{1,0:T(8,128)(2,1)S(1)}, u32[]{:S(2)}, u32[]{:S(2)}) collective-permute-start(bf16[512,128]{1,0:T(8,128)(2,1)S(1)} %get-tuple-element.48), channel_id=1, source_target_pairs={{0,12},{4,8},{8,4},{12,0},{16,28},{20,24},{24,20},{28,16},{1,13},{... | collective-permute-start | bytes 393224 | tf_op jit(solution)/shard_map/ppermute | solution.py:543
  22.2 13.3 %collective-permute-start.10 = (bf16[512,128]{1,0:T(8,128)(2,1)S(1)}, bf16[512,128]{1,0:T(8,128)(2,1)S(1)}, u32[]{:S(2)}, u32[]{:S(2)}) collective-permute-start(bf16[512,128]{1,0:T(8,128)(2,1)S(1)} %get-tuple-element.49), channel_id=1, source_target_pairs={{0,16},{4,20},{8,24},{12,28},{16,0},{20,4},{24,8},{28,12},{1,17},{... | collective-permute-start | bytes 393224 | tf_op jit(solution)/shard_map/ppermute | solution.py:543
  25.0 13.3 %collective-permute-start.11 = (bf16[512,128]{1,0:T(8,128)(2,1)S(1)}, bf16[512,128]{1,0:T(8,128)(2,1)S(1)}, u32[]{:S(2)}, u32[]{:S(2)}) collective-permute-start(bf16[512,128]{1,0:T(8,128)(2,1)S(1)} %get-tuple-element.50), channel_id=1, source_target_pairs={{0,20},{4,16},{8,28},{12,24},{16,4},{20,0},{24,12},{28,8},{1,21},{... | collective-permute-start | bytes 393224 | tf_op jit(solution)/shard_map/ppermute | solution.py:543
  25.1 17.0 %collective-permute-start.12 = (bf16[512,128]{1,0:T(8,128)(2,1)S(1)}, bf16[512,128]{1,0:T(8,128)(2,1)S(1)}, u32[]{:S(2)}, u32[]{:S(2)}) collective-permute-start(bf16[512,128]{1,0:T(8,128)(2,1)S(1)} %get-tuple-element.51), channel_id=1, source_target_pairs={{0,24},{4,28},{8,16},{12,20},{16,8},{20,12},{24,0},{28,4},{1,25},{... | collective-permute-start | bytes 393224 | tf_op jit(solution)/shard_map/ppermute | solution.py:543
  25.4 19.3 %collective-permute-start.13 = (bf16[512,128]{1,0:T(8,128)(2,1)S(1)}, bf16[512,128]{1,0:T(8,128)(2,1)S(1)}, u32[]{:S(2)}, u32[]{:S(2)}) collective-permute-start(bf16[512,128]{1,0:T(8,128)(2,1)S(1)} %get-tuple-element.52), channel_id=1, source_target_pairs={{0,28},{4,24},{8,20},{12,16},{16,12},{20,8},{24,4},{28,0},{1,29},{... | collective-permute-start | bytes 393224 | tf_op jit(solution)/shard_map/ppermute | solution.py:543
  28.9 17.8 %collective-permute-start.20 = (f32[128,512]{1,0:T(8,128)S(1)}, f32[128,512]{1,0:T(8,128)S(1)}, u32[]{:S(2)}, u32[]{:S(2)}) collective-permute-start(f32[128,512]{1,0:T(8,128)S(1)} %get-tuple-element.58.refs_0_), channel_id=1, source_target_pairs={{0,2},{1,3},{2,0},{3,1},{4,6},{5,7},{6,4},{7,5},{8,10},{9,11},{10,... | collective-permute-start | bytes 786440 | tf_op jit(solution)/shard_map/ppermute | solution.py:548
  35.5 11.6 %collective-permute-start.17 = (f32[512,128]{1,0:T(8,128)S(1)}, f32[512,128]{1,0:T(8,128)S(1)}, u32[]{:S(2)}, u32[]{:S(2)}) collective-permute-start(f32[512,128]{1,0:T(8,128)S(1)} %get-tuple-element.57), channel_id=1, source_target_pairs={{0,1},{1,0},{2,3},{3,2},{4,5},{5,4},{6,7},{7,6},{8,9},{9,8},{10,11... | collective-permute-start | bytes 786440 | tf_op jit(solution)/shard_map/ppermute | solution.py:554
  46.1 2.7 %collective-permute-start.15 = (f32[6,128,128]{2,1,0:T(8,128)S(1)}, f32[6,128,128]{2,1,0:T(8,128)S(1)}, u32[]{:S(2)}, u32[]{:S(2)}) collective-permute-start(f32[6,128,128]{2,1,0:T(8,128)S(1)} %get-tuple-element.56), channel_id=1, source_target_pairs={{0,1},{1,0},{2,3},{3,2},{4,5},{5,4},{6,7},{7,6},{8,9},{9,8},{10,11... | collective-permute-start | bytes 1179656 | tf_op jit(solution)/shard_map/ppermute | solution.py:566
  46.1 2.7 %collective-permute-start.23 = (f32[6,128,128]{2,1,0:T(8,128)S(1)}, f32[6,128,128]{2,1,0:T(8,128)S(1)}, u32[]{:S(2)}, u32[]{:S(2)}) collective-permute-start(f32[6,128,128]{2,1,0:T(8,128)S(1)} %get-tuple-element.63), channel_id=1, source_target_pairs={{0,1},{1,0},{2,3},{3,2},{4,5},{5,4},{6,7},{7,6},{8,9},{9,8},{10,11... | collective-permute-start | bytes 1179656 | tf_op jit(solution)/shard_map/ppermute | solution.py:566
  46.6 2.8 %collective-permute-start.19 = (f32[128,512]{1,0:T(8,128)S(1)}, f32[128,512]{1,0:T(8,128)S(1)}, u32[]{:S(2)}, u32[]{:S(2)}) collective-permute-start(f32[128,512]{1,0:T(8,128)S(1)} %get-tuple-element.58.refs_0_), channel_id=1, source_target_pairs={{0,1},{1,0},{2,3},{3,2},{4,5},{5,4},{6,7},{7,6},{8,9},{9,8},{10,11... | collective-permute-start | bytes 786440 | tf_op jit(solution)/shard_map/ppermute | solution.py:549
  46.7 3.6 %collective-permute-start.21 = (f32[128,512]{1,0:T(8,128)S(1)}, f32[128,512]{1,0:T(8,128)S(1)}, u32[]{:S(2)}, u32[]{:S(2)}) collective-permute-start(f32[128,512]{1,0:T(8,128)S(1)} %collective-permute-done.20.refs_2_), channel_id=1, source_target_pairs={{0,1},{1,0},{2,3},{3,2},{4,5},{5,4},{6,7},{7,6},{8,9},{9,8},{10,11... | collective-permute-start | bytes 786440 | tf_op jit(solution)/shard_map/ppermute | solution.py:550
  47.2 9.2 %collective-permute-start.18 = (f32[512,128]{1,0:T(8,128)S(1)}, f32[512,128]{1,0:T(8,128)S(1)}, u32[]{:S(2)}, u32[]{:S(2)}) collective-permute-start(f32[512,128]{1,0:T(8,128)S(1)} %add.10.own_ref), channel_id=1, source_target_pairs={{0,2},{1,3},{2,0},{3,1},{4,6},{5,7},{6,4},{7,5},{8,10},{9,11},{10,... | collective-permute-start | bytes 786440 | tf_op jit(solution)/shard_map/ppermute | solution.py:556
  48.8 28.0 %collective-permute-start.14 = (f32[6,128,128]{2,1,0:T(8,128)S(1)}, f32[6,128,128]{2,1,0:T(8,128)S(1)}, u32[]{:S(2)}, u32[]{:S(2)}) collective-permute-start(f32[6,128,128]{2,1,0:T(8,128)S(1)} %get-tuple-element.54), channel_id=1, source_target_pairs={{0,1},{1,0},{2,3},{3,2},{4,5},{5,4},{6,7},{7,6},{8,9},{9,8},{10,11... | collective-permute-start | bytes 1179656 | tf_op jit(solution)/shard_map/ppermute | solution.py:569
  48.8 26.1 %collective-permute-start.22 = (f32[6,128,128]{2,1,0:T(8,128)S(1)}, f32[6,128,128]{2,1,0:T(8,128)S(1)}, u32[]{:S(2)}, u32[]{:S(2)}) collective-permute-start(f32[6,128,128]{2,1,0:T(8,128)S(1)} %get-tuple-element.61), channel_id=1, source_target_pairs={{0,1},{1,0},{2,3},{3,2},{4,5},{5,4},{6,7},{7,6},{8,9},{9,8},{10,11... | collective-permute-start | bytes 1179656 | tf_op jit(solution)/shard_map/ppermute | solution.py:569
  49.5 27.3 %collective-permute-start.16 = (f32[6,128,128]{2,1,0:T(8,128)S(1)}, f32[6,128,128]{2,1,0:T(8,128)S(1)}, u32[]{:S(2)}, u32[]{:S(2)}) collective-permute-start(f32[6,128,128]{2,1,0:T(8,128)S(1)} %add.9), channel_id=1, source_target_pairs={{0,2},{1,3},{2,0},{3,1},{4,6},{5,7},{6,4},{7,5},{8,10},{9,11},{10,... | collective-permute-start | bytes 1179656 | tf_op jit(solution)/shard_map/ppermute | solution.py:567
  50.3 24.6 %collective-permute-start.24 = (f32[6,128,128]{2,1,0:T(8,128)S(1)}, f32[6,128,128]{2,1,0:T(8,128)S(1)}, u32[]{:S(2)}, u32[]{:S(2)}) collective-permute-start(f32[6,128,128]{2,1,0:T(8,128)S(1)} %add.11), channel_id=1, source_target_pairs={{0,2},{1,3},{2,0},{3,1},{4,6},{5,7},{6,4},{7,5},{8,10},{9,11},{10,... | collective-permute-start | bytes 1179656 | tf_op jit(solution)/shard_map/ppermute | solution.py:567
  65.0 9.9 %copy-start = (f32[1,4,1,128,512]{4,3,2,1,0:T(8,128)S(1)}, f32[1,4,1,128,512]{4,3,2,1,0:T(8,128)}, u32[]{:S(2)}) copy-start(f32[1,4,1,128,512]{4,3,2,1,0:T(8,128)} %param.9) | copy-start | bytes 3145732

commit v4 on v3

--- a/solution.py
+++ b/solution.py
@@ -8,10 +8,13 @@
 
 SLOTS = 2
 CODES = 4
-CODE_ROWS = 16
+CODE_ROWS = 8
 PANEL = 8
 SPLIT = 2
 HALVES = 2
+SCALE_ROWS = 16
+BITS = 23.0
+LOG2E = 1.4426950408889634
 DIRECT = 8
 HIGHEST = lax.Precision.HIGHEST
 
@@ -442,6 +445,50 @@
     )(*near_core(schur_in))
 
 
+def pack_sums(first, second):
+    count, rows, width = first.shape
+    pairs = count // 2
+
+    def body(first_ref, second_ref, out):
+        row = lax.broadcasted_iota(jnp.int32, (SCALE_ROWS, width), 0)
+        scales = jnp.zeros((SCALE_ROWS, width), jnp.int32)
+        lows = []
+        for j in range(count):
+            value = first_ref[j] + second_ref[j]
+            peak = jnp.maximum(jnp.max(jnp.abs(value), axis=0, keepdims=True), 1e-30)
+            power = jnp.floor(jnp.log(peak) * LOG2E + 1e-3) + 1.0
+            scales = jnp.where(row == j, power.astype(jnp.int32), scales)
+            whole = jnp.floor(value * jnp.exp2(BITS - power) + 0.5).astype(jnp.int32)
+            high = lax.shift_right_arithmetic(whole, 8)
+            lows.append(whole - high * 256)
+            out[j * rows:(j + 1) * rows] = high.astype(jnp.int16)
+        for j in range(pairs):
+            low = lows[j] + lows[j + pairs] * 256 - 32768
+            out[(count + j) * rows:(count + j + 1) * rows] = low.astype(jnp.int16)
+        out[(count + pairs) * rows:] = scales.astype(jnp.int16)
+
+    return pl.pallas_call(
+        body,
+        name="pack_sums",
+        compiler_params=limit(8),
+        out_shape=pltpu.VMEM(((count + pairs) * rows + SCALE_ROWS, width), jnp.int16),
+        in_specs=spaces(2, pltpu.VMEM),
+        out_specs=pl.BlockSpec(memory_space=pltpu.VMEM),
+    )(*near_core(first, second))
+
+
+def unpack_sums(ref, index, count, rows):
+    pairs = count // 2
+    high = ref[index * rows:(index + 1) * rows].astype(jnp.int32)
+    at = (count + index % pairs) * rows
+    low = ref[at:at + rows].astype(jnp.int32) + 32768
+    upper = lax.shift_right_logical(low, 8)
+    low = upper if index >= pairs else low - upper * 256
+    scales = ref[(count + pairs) * rows:].astype(jnp.float32)
+    scale = jnp.exp2(scales[index:index + 1] - BITS)
+    return (high * 256 + low).astype(jnp.float32) * scale
+
+
 def solve_dot(left, right):
     return lax.dot_general(
         left, right, (((1,), (1,)), ((), ())),
@@ -454,9 +501,9 @@
     for c in range(cb // HALVES):
         column = (half * (cb // HALVES) + c) * rows
         block = slice(c * per, (c + 1) * per)
-        update = update_refs[0][block]
-        for ref in update_refs[1:]:
-            update = update + ref[block]
+        count = (cb // HALVES) * per
+        coded = [unpack_sums(update_refs[2], index, count, rows)[None] for index in range(c * per, (c + 1) * per)]
+        update = update_refs[0][block] + update_refs[1][block] + jnp.concatenate(coded, axis=0)
         original = panel_ref[1:, :, column:column + rows]
         parts.append((original - update).reshape(per * rows, rows))
     return jnp.concatenate(parts, axis=1)
@@ -564,7 +611,7 @@
     from_far = []
     for half in range(HALVES):
         passed = lax.ppermute(for_both[half], "blk", near)
-        from_far.append(lax.ppermute(for_far[half] + passed, "blk", far))
+        from_far.append(lax.ppermute(pack_sums(for_far[half], passed), "blk", far))
     for half in range(HALVES):
         from_near.append(lax.ppermute(for_near[half], "blk", near))
     whole, lower = last_factor(schur, cb, rows)

time: 78.3 us -> 78.1 us (level)
  transfers between devices with their start and end apart: 25 -> 25, of which waited for: 8 -> 8; matrix products, arithmetic and copies ran while one was open for 0% -> 0% of each run, Pallas kernels for 29% -> 30%
where the time goes in v4:
time: 78.1 us; the launch traced here: 77.9 us
  Pallas kernels  26.4 us (34%)
  starting transfers between devices  25.9 us (33%)
  waiting for transfers between devices  25.5 us (33%)
    ppermute x14, waiting for transfers between devices, exchange(): received.append(lax.ppermute(arrays[k], 'leaf', swap))  20.9 us
    ppermute x14, starting transfers between devices, exchange(): received.append(lax.ppermute(arrays[k], 'leaf', swap))  19 us
    pallas_call x1, Pallas kernels, last_factor(): pl.pallas_call(body, name='factor_last', compiler_params=limit(12), out_s...  9.84 us
    pallas_call x1, Pallas kernels, first_factor(): pl.pallas_call(body, name='factor_first', compiler_params=limit(12), out_...  8.58 us
    ppermute x1, waiting for transfers between devices, shards(): diagonal_far = lax.ppermute(diagonal, 'blk', far)  4.52 us
    ppermute x2, starting transfers between devices, shards(): from_far.append(lax.ppermute(pack_sums(for_far[half], passed), 'blk', far))  2.09 us
    pallas_call x1, Pallas kernels, pack(): pl.pallas_call(body, name='pack', compiler_params=limit(12 if direct else...  2.04 us
    pallas_call x1, Pallas kernels, solve_left(): pl.pallas_call(body, name='solve_left', compiler_params=limit(16), out_sh...  1.94 us
  transfers between devices with their start and end apart: 25, of which 8 were waited for; matrix products, arithmetic and copies ran while one was open for 0% of the time, Pallas kernels for 30%

profile of v4, /device:TPU:8, one launch (start us, length us, event | category | flops | bytes accessed | tf_op | source)
XLA Modules:
  0.0 77.9 jit_solution(14240501716638107248)
XLA Ops:
  0.0 2.0 %pack.1 = (bf16[264,128]{1,0:T(8,128)(2,1)S(1)}, bf16[264,128]{1,0:T(8,128)(2,1)S(1)}, bf16[264,128]{1,0:T(8,128)(2,1)S(1)}, bf16[264,128]{1,0:T(8,128)(2,1)S(1)...) custom-call(s32[3,8]{1,0:T(4,128)} %bitcast.8, ...), custom_call_target="tpu_custom_call" | custom-call | tf_op jit(solution)/shard_map/pack/pallas_call | solution.py:121
  2.0 1.6 %collective-permute-start = (bf16[264,128]{1,0:T(8,128)(2,1)S(1)}, bf16[264,128]{1,0:T(8,128)(2,1)S(1)}, u32[]{:S(2)}, u32[]{:S(2)}) collective-permute-start(bf16[264,128]{1,0:T(8,128)(2,1)S(1)} %get-tuple-element.37), channel_id=1, source_target_pairs={{0,4},{4,0},{8,12},{12,8},{16,20},{20,16},{24,28},{28,24},{1,5},{5... | collective-permute-start | bytes 202760 | tf_op jit(solution)/shard_map/ppermute | solution.py:590
  3.6 0.4 collective-permute-start.1
  4.1 1.5 %collective-permute-start.2 = (bf16[264,128]{1,0:T(8,128)(2,1)S(1)}, bf16[264,128]{1,0:T(8,128)(2,1)S(1)}, u32[]{:S(2)}, u32[]{:S(2)}) collective-permute-start(bf16[264,128]{1,0:T(8,128)(2,1)S(1)} %get-tuple-element.39), channel_id=1, source_target_pairs={{0,12},{4,8},{8,4},{12,0},{16,28},{20,24},{24,20},{28,16},{1,13},{... | collective-permute-start | bytes 202760 | tf_op jit(solution)/shard_map/ppermute | solution.py:590
  5.6 2.6 %collective-permute-start.3 = (bf16[264,128]{1,0:T(8,128)(2,1)S(1)}, bf16[264,128]{1,0:T(8,128)(2,1)S(1)}, u32[]{:S(2)}, u32[]{:S(2)}) collective-permute-start(bf16[264,128]{1,0:T(8,128)(2,1)S(1)} %get-tuple-element.40), channel_id=1, source_target_pairs={{0,16},{4,20},{8,24},{12,28},{16,0},{20,4},{24,8},{28,12},{1,17},{... | collective-permute-start | bytes 202760 | tf_op jit(solution)/shard_map/ppermute | solution.py:590
  8.2 1.5 %collective-permute-start.7 = (bf16[512,128]{1,0:T(8,128)(2,1)S(1)}, bf16[512,128]{1,0:T(8,128)(2,1)S(1)}, u32[]{:S(2)}, u32[]{:S(2)}) collective-permute-start(bf16[512,128]{1,0:T(8,128)(2,1)S(1)} %get-tuple-element.46), channel_id=1, source_target_pairs={{0,4},{4,0},{8,12},{12,8},{16,20},{20,16},{24,28},{28,24},{1,5},{5... | collective-permute-start | bytes 393224 | tf_op jit(solution)/shard_map/ppermute | solution.py:590
  9.7 0.5 collective-permute-start.8
  10.1 0.7 collective-permute-start.4
  10.9 2.3 %collective-permute-start.5 = (bf16[264,128]{1,0:T(8,128)(2,1)S(1)}, bf16[264,128]{1,0:T(8,128)(2,1)S(1)}, u32[]{:S(2)}, u32[]{:S(2)}) collective-permute-start(bf16[264,128]{1,0:T(8,128)(2,1)S(1)} %get-tuple-element.42), channel_id=1, source_target_pairs={{0,24},{4,28},{8,16},{12,20},{16,8},{20,12},{24,0},{28,4},{1,25},{... | collective-permute-start | bytes 202760 | tf_op jit(solution)/shard_map/ppermute | solution.py:590
  13.2 1.0 %collective-permute-start.6 = (bf16[264,128]{1,0:T(8,128)(2,1)S(1)}, bf16[264,128]{1,0:T(8,128)(2,1)S(1)}, u32[]{:S(2)}, u32[]{:S(2)}) collective-permute-start(bf16[264,128]{1,0:T(8,128)(2,1)S(1)} %get-tuple-element.43), channel_id=1, source_target_pairs={{0,28},{4,24},{8,20},{12,16},{16,12},{20,8},{24,4},{28,0},{1,29},{... | collective-permute-start | bytes 202760 | tf_op jit(solution)/shard_map/ppermute | solution.py:590
  14.2 3.4 %collective-permute-done.4.refs_5_.refs_14_ = bf16[264,128]{1,0:T(8,128)(2,1)S(1)} collective-permute-done((bf16[264,128]{1,0:T(8,128)(2,1)S(1)}, bf16[264,128]{1,0:T(8,128)(2,1)S(1)}, u32[]{:S(2)}, u32[]{:S(2)}) %collective-permute-start.4) | collective-permute-done | bytes 67616 | tf_op jit(solution)/shard_map/ppermute | solution.py:590
  17.6 3.8 %collective-permute-start.9 = (bf16[512,128]{1,0:T(8,128)(2,1)S(1)}, bf16[512,128]{1,0:T(8,128)(2,1)S(1)}, u32[]{:S(2)}, u32[]{:S(2)}) collective-permute-start(bf16[512,128]{1,0:T(8,128)(2,1)S(1)} %get-tuple-element.48), channel_id=1, source_target_pairs={{0,12},{4,8},{8,4},{12,0},{16,28},{20,24},{24,20},{28,16},{1,13},{... | collective-permute-start | bytes 393224 | tf_op jit(solution)/shard_map/ppermute | solution.py:590
  21.4 0.6 collective-permute-done.5.refs_6_.refs_15_
  21.9 2.8 %collective-permute-done.6.refs_7_.refs_16_ = bf16[264,128]{1,0:T(8,128)(2,1)S(1)} collective-permute-done((bf16[264,128]{1,0:T(8,128)(2,1)S(1)}, bf16[264,128]{1,0:T(8,128)(2,1)S(1)}, u32[]{:S(2)}, u32[]{:S(2)}) %collective-permute-start.6) | collective-permute-done | bytes 67616 | tf_op jit(solution)/shard_map/ppermute | solution.py:590
  25.2 2.6 %collective-permute-start.13 = (bf16[512,128]{1,0:T(8,128)(2,1)S(1)}, bf16[512,128]{1,0:T(8,128)(2,1)S(1)}, u32[]{:S(2)}, u32[]{:S(2)}) collective-permute-start(bf16[512,128]{1,0:T(8,128)(2,1)S(1)} %get-tuple-element.52), channel_id=1, source_target_pairs={{0,28},{4,24},{8,20},{12,16},{16,12},{20,8},{24,4},{28,0},{1,29},{... | collective-permute-start | bytes 393224 | tf_op jit(solution)/shard_map/ppermute | solution.py:590
  27.8 0.8 %diagonal.1 = (f32[512,128]{1,0:T(8,128)S(1)}, s32[8,128]{1,0:T(8,128)S(1)}) custom-call(bf16[264,128]{1,0:T(8,128)(2,1)S(1)} %get-tuple-element.36.refs_0_.refs_9_, bf16[264,128]{1,0:T(8,128)(2,1)S(1)} %collective-permute-done.refs_1_.refs_10_, bf16[264,128]{1,0:T(8,128)(2,1)S(1)} %collective-permute-done.1.refs_2_.refs_11_, ...), custom_call_target="tpu_custom_call" | custom-call | flops 2000000000 | bytes 1000000 | tf_op jit(solution)/shard_map/diagonal/pallas_call | solution.py:197
  28.6 1.6 %collective-permute-start.20 = (f32[128,512]{1,0:T(8,128)S(1)}, f32[128,512]{1,0:T(8,128)S(1)}, u32[]{:S(2)}, u32[]{:S(2)}) collective-permute-start(f32[128,512]{1,0:T(8,128)S(1)} %get-tuple-element.58.refs_0_), channel_id=1, source_target_pairs={{0,2},{1,3},{2,0},{3,1},{4,6},{5,7},{6,4},{7,5},{8,10},{9,11},{10,... | collective-permute-start | bytes 786440 | tf_op jit(solution)/shard_map/ppermute | solution.py:595
  30.2 5.0 %collective-permute-done.10.refs_5_ = bf16[512,128]{1,0:T(8,128)(2,1)S(1)} collective-permute-done((bf16[512,128]{1,0:T(8,128)(2,1)S(1)}, bf16[512,128]{1,0:T(8,128)(2,1)S(1)}, u32[]{:S(2)}, u32[]{:S(2)}) %collective-permute-start.10) | collective-permute-done | bytes 131104 | tf_op jit(solution)/shard_map/ppermute | solution.py:590
  35.2 2.8 %collective-permute-done.11.refs_6_ = bf16[512,128]{1,0:T(8,128)(2,1)S(1)} collective-permute-done((bf16[512,128]{1,0:T(8,128)(2,1)S(1)}, bf16[512,128]{1,0:T(8,128)(2,1)S(1)}, u32[]{:S(2)}, u32[]{:S(2)}) %collective-permute-start.11) | collective-permute-done | bytes 131104 | tf_op jit(solution)/shard_map/ppermute | solution.py:590
  38.1 3.7 %collective-permute-done.12.refs_7_ = bf16[512,128]{1,0:T(8,128)(2,1)S(1)} collective-permute-done((bf16[512,128]{1,0:T(8,128)(2,1)S(1)}, bf16[512,128]{1,0:T(8,128)(2,1)S(1)}, u32[]{:S(2)}, u32[]{:S(2)}) %collective-permute-start.12) | collective-permute-done | bytes 131104 | tf_op jit(solution)/shard_map/ppermute | solution.py:590
  41.8 2.5 %collective-permute-done.13.refs_8_ = bf16[512,128]{1,0:T(8,128)(2,1)S(1)} collective-permute-done((bf16[512,128]{1,0:T(8,128)(2,1)S(1)}, bf16[512,128]{1,0:T(8,128)(2,1)S(1)}, u32[]{:S(2)}, u32[]{:S(2)}) %collective-permute-start.13) | collective-permute-done | bytes 131104 | tf_op jit(solution)/shard_map/ppermute | solution.py:590
  44.3 1.4 %below.1 = (f32[6,128,128]{2,1,0:T(8,128)S(1)}, f32[6,128,128]{2,1,0:T(8,128)S(1)}, f32[6,128,128]{2,1,0:T(8,128)S(1)}, f32[6,128,128]{2,1,0:T(8,128)S(1)}, f32[...) custom-call(s32[8,128]{1,0:T(8,128)S(1)} %get-tuple-element.44.refs_, ...), custom_call_target="tpu_custom_call" | custom-call | flops 2000000000 | bytes 4000000 | tf_op jit(solution)/shard_map/below/pallas_call | solution.py:271
  45.8 0.5 collective-permute-start.23
  46.9 1.6 %collective-permute-start.18 = (f32[512,128]{1,0:T(8,128)S(1)}, f32[512,128]{1,0:T(8,128)S(1)}, u32[]{:S(2)}, u32[]{:S(2)}) collective-permute-start(f32[512,128]{1,0:T(8,128)S(1)} %add.3.own_ref), channel_id=1, source_target_pairs={{0,2},{1,3},{2,0},{3,1},{4,6},{5,7},{6,4},{7,5},{8,10},{9,11},{10,... | collective-permute-start | bytes 786440 | tf_op jit(solution)/shard_map/ppermute | solution.py:603
  48.7 0.6 collective-permute-start.22
  49.5 0.7 collective-permute-start.16
  50.2 1.4 %collective-permute-start.24 = (s16[1168,128]{1,0:T(8,128)(2,1)S(1)}, s16[1168,128]{1,0:T(8,128)(2,1)S(1)}, u32[]{:S(2)}, u32[]{:S(2)}) collective-permute-start(s16[1168,128]{1,0:T(8,128)(2,1)S(1)} %pack_sums.3), channel_id=1, source_target_pairs={{0,2},{1,3},{2,0},{3,1},{4,6},{5,7},{6,4},{7,5},{8,10},{9,11},{10,... | collective-permute-start | bytes 897032 | tf_op jit(solution)/shard_map/ppermute | solution.py:614
  51.6 4.5 %collective-permute-done.18.other_ref = f32[512,128]{1,0:T(8,128)S(1)} collective-permute-done((f32[512,128]{1,0:T(8,128)S(1)}, f32[512,128]{1,0:T(8,128)S(1)}, u32[]{:S(2)}, u32[]{:S(2)}) %collective-permute-start.18) | collective-permute-done | bytes 262176 | tf_op jit(solution)/shard_map/ppermute | solution.py:603
  56.1 8.6 %factor_first.1.schur_ref = f32[4,128,512]{2,1,0:T(8,128)S(1)} custom-call(f32[512,128]{1,0:T(8,128)S(1)} %add.3.own_ref, f32[512,128]{1,0:T(8,128)S(1)} %collective-permute-done.18.other_ref, f32[128,512]{1,0:T(8,128)S(1)} %get-tuple-element.58.refs_0_, f32[128,512]{1,0:T(8,128)S(1)} %collective-permute-done.19.refs_1_, ...), custom_call_target="tpu_custom_call" | custom-call | flops 10000000000 | bytes 2000000 | tf_op jit(solution)/shard_map/factor_first/pallas_call | solution.py:384
  64.7 9.8 %factor_last.1 = (f32[512,512]{1,0:T(8,128)S(1)}, f32[128,512]{1,0:T(8,128)S(1)}) custom-call(f32[4,128,512]{2,1,0:T(8,128)S(1)} %factor_first.1.schur_ref), custom_call_target="tpu_custom_call" | custom-call | flops 12000000000 | bytes 2000000 | tf_op jit(solution)/shard_map/factor_last/pallas_call | solution.py:429
  74.6 1.9 %solve_left.1 = (f32[4,128,512]{2,1,0:T(8,128)}, f32[384,256]{1,0:T(8,128)S(1)}) custom-call(f32[4,128,512]{2,1,0:T(8,128)S(1)} %bitcast.6, f32[6,128,128]{2,1,0:T(8,128)S(1)} %get-tuple-element.60.refs_0_, f32[6,128,128]{2,1,0:T(8,128)S(1)} %collective-permute-done.22.refs_1_, s16[1168,128]{1,0:T(8,128)(2,1)S(1)} %collective-permute-done.24.refs_2_, ...), custom_call_target="tpu_custom_call" | custom-call | flops 2000000000 | bytes 5000000 | tf_op jit(solution)/shard_map/solve_left/pallas_call | solution.py:524
  76.6 1.4 %solve_right.1 = f32[4,128,512]{2,1,0:T(8,128)} custom-call(f32[4,128,512]{2,1,0:T(8,128)S(1)} %bitcast.7, f32[6,128,128]{2,1,0:T(8,128)S(1)} %get-tuple-element.53.refs_0_, f32[6,128,128]{2,1,0:T(8,128)S(1)} %collective-permute-done.14.refs_1_, s16[1168,128]{1,0:T(8,128)(2,1)S(1)} %collective-permute-done.16.refs_2_, ...), custom_call_target="tpu_custom_call", output_to_operand_aliasing={{}: (6, {})} | custom-call | flops 2000000000 | bytes 5000000 | tf_op jit(solution)/shard_map/solve_right/pallas_call | solution.py:554
  (30 shorter events, 1.5 us)
Async XLA Ops:
  2.0 7.6 %collective-permute-start = (bf16[264,128]{1,0:T(8,128)(2,1)S(1)}, bf16[264,128]{1,0:T(8,128)(2,1)S(1)}, u32[]{:S(2)}, u32[]{:S(2)}) collective-permute-start(bf16[264,128]{1,0:T(8,128)(2,1)S(1)} %get-tuple-element.37), channel_id=1, source_target_pairs={{0,4},{4,0},{8,12},{12,8},{16,20},{20,16},{24,28},{28,24},{1,5},{5... | collective-permute-start | bytes 202760 | tf_op jit(solution)/shard_map/ppermute | solution.py:590
  3.6 6.5 %collective-permute-start.1 = (bf16[264,128]{1,0:T(8,128)(2,1)S(1)}, bf16[264,128]{1,0:T(8,128)(2,1)S(1)}, u32[]{:S(2)}, u32[]{:S(2)}) collective-permute-start(bf16[264,128]{1,0:T(8,128)(2,1)S(1)} %get-tuple-element.38), channel_id=1, source_target_pairs={{0,8},{4,12},{8,0},{12,4},{16,24},{20,28},{24,16},{28,20},{1,9},{5... | collective-permute-start | bytes 202760 | tf_op jit(solution)/shard_map/ppermute | solution.py:590
  4.1 6.8 %collective-permute-start.2 = (bf16[264,128]{1,0:T(8,128)(2,1)S(1)}, bf16[264,128]{1,0:T(8,128)(2,1)S(1)}, u32[]{:S(2)}, u32[]{:S(2)}) collective-permute-start(bf16[264,128]{1,0:T(8,128)(2,1)S(1)} %get-tuple-element.39), channel_id=1, source_target_pairs={{0,12},{4,8},{8,4},{12,0},{16,28},{20,24},{24,20},{28,16},{1,13},{... | collective-permute-start | bytes 202760 | tf_op jit(solution)/shard_map/ppermute | solution.py:590
  5.6 7.6 %collective-permute-start.3 = (bf16[264,128]{1,0:T(8,128)(2,1)S(1)}, bf16[264,128]{1,0:T(8,128)(2,1)S(1)}, u32[]{:S(2)}, u32[]{:S(2)}) collective-permute-start(bf16[264,128]{1,0:T(8,128)(2,1)S(1)} %get-tuple-element.40), channel_id=1, source_target_pairs={{0,16},{4,20},{8,24},{12,28},{16,0},{20,4},{24,8},{28,12},{1,17},{... | collective-permute-start | bytes 202760 | tf_op jit(solution)/shard_map/ppermute | solution.py:590
  8.2 16.5 %collective-permute-start.7 = (bf16[512,128]{1,0:T(8,128)(2,1)S(1)}, bf16[512,128]{1,0:T(8,128)(2,1)S(1)}, u32[]{:S(2)}, u32[]{:S(2)}) collective-permute-start(bf16[512,128]{1,0:T(8,128)(2,1)S(1)} %get-tuple-element.46), channel_id=1, source_target_pairs={{0,4},{4,0},{8,12},{12,8},{16,20},{20,16},{24,28},{28,24},{1,5},{5... | collective-permute-start | bytes 393224 | tf_op jit(solution)/shard_map/ppermute | solution.py:590
  9.7 15.5 %collective-permute-start.8 = (bf16[512,128]{1,0:T(8,128)(2,1)S(1)}, bf16[512,128]{1,0:T(8,128)(2,1)S(1)}, u32[]{:S(2)}, u32[]{:S(2)}) collective-permute-start(bf16[512,128]{1,0:T(8,128)(2,1)S(1)} %get-tuple-element.47), channel_id=1, source_target_pairs={{0,8},{4,12},{8,0},{12,4},{16,24},{20,28},{24,16},{28,20},{1,9},{5... | collective-permute-start | bytes 393224 | tf_op jit(solution)/shard_map/ppermute | solution.py:590
  10.1 7.4 %collective-permute-start.4 = (bf16[264,128]{1,0:T(8,128)(2,1)S(1)}, bf16[264,128]{1,0:T(8,128)(2,1)S(1)}, u32[]{:S(2)}, u32[]{:S(2)}) collective-permute-start(bf16[264,128]{1,0:T(8,128)(2,1)S(1)} %get-tuple-element.41), channel_id=1, source_target_pairs={{0,20},{4,16},{8,28},{12,24},{16,4},{20,0},{24,12},{28,8},{1,21},{... | collective-permute-start | bytes 202760 | tf_op jit(solution)/shard_map/ppermute | solution.py:590
  10.9 11.1 %collective-permute-start.5 = (bf16[264,128]{1,0:T(8,128)(2,1)S(1)}, bf16[264,128]{1,0:T(8,128)(2,1)S(1)}, u32[]{:S(2)}, u32[]{:S(2)}) collective-permute-start(bf16[264,128]{1,0:T(8,128)(2,1)S(1)} %get-tuple-element.42), channel_id=1, source_target_pairs={{0,24},{4,28},{8,16},{12,20},{16,8},{20,12},{24,0},{28,4},{1,25},{... | collective-permute-start | bytes 202760 | tf_op jit(solution)/shard_map/ppermute | solution.py:590
  13.2 11.6 %collective-permute-start.6 = (bf16[264,128]{1,0:T(8,128)(2,1)S(1)}, bf16[264,128]{1,0:T(8,128)(2,1)S(1)}, u32[]{:S(2)}, u32[]{:S(2)}) collective-permute-start(bf16[264,128]{1,0:T(8,128)(2,1)S(1)} %get-tuple-element.43), channel_id=1, source_target_pairs={{0,28},{4,24},{8,20},{12,16},{16,12},{20,8},{24,4},{28,0},{1,29},{... | collective-permute-start | bytes 202760 | tf_op jit(solution)/shard_map/ppermute | solution.py:590
  17.6 11.0 %collective-permute-start.9 = (bf16[512,128]{1,0:T(8,128)(2,1)S(1)}, bf16[512,128]{1,0:T(8,128)(2,1)S(1)}, u32[]{:S(2)}, u32[]{:S(2)}) collective-permute-start(bf16[512,128]{1,0:T(8,128)(2,1)S(1)} %get-tuple-element.48), channel_id=1, source_target_pairs={{0,12},{4,8},{8,4},{12,0},{16,28},{20,24},{24,20},{28,16},{1,13},{... | collective-permute-start | bytes 393224 | tf_op jit(solution)/shard_map/ppermute | solution.py:590
  21.9 13.3 %collective-permute-start.10 = (bf16[512,128]{1,0:T(8,128)(2,1)S(1)}, bf16[512,128]{1,0:T(8,128)(2,1)S(1)}, u32[]{:S(2)}, u32[]{:S(2)}) collective-permute-start(bf16[512,128]{1,0:T(8,128)(2,1)S(1)} %get-tuple-element.49), channel_id=1, source_target_pairs={{0,16},{4,20},{8,24},{12,28},{16,0},{20,4},{24,8},{28,12},{1,17},{... | collective-permute-start | bytes 393224 | tf_op jit(solution)/shard_map/ppermute | solution.py:590
  24.7 13.3 %collective-permute-start.11 = (bf16[512,128]{1,0:T(8,128)(2,1)S(1)}, bf16[512,128]{1,0:T(8,128)(2,1)S(1)}, u32[]{:S(2)}, u32[]{:S(2)}) collective-permute-start(bf16[512,128]{1,0:T(8,128)(2,1)S(1)} %get-tuple-element.50), channel_id=1, source_target_pairs={{0,20},{4,16},{8,28},{12,24},{16,4},{20,0},{24,12},{28,8},{1,21},{... | collective-permute-start | bytes 393224 | tf_op jit(solution)/shard_map/ppermute | solution.py:590
  24.7 17.1 %collective-permute-start.12 = (bf16[512,128]{1,0:T(8,128)(2,1)S(1)}, bf16[512,128]{1,0:T(8,128)(2,1)S(1)}, u32[]{:S(2)}, u32[]{:S(2)}) collective-permute-start(bf16[512,128]{1,0:T(8,128)(2,1)S(1)} %get-tuple-element.51), channel_id=1, source_target_pairs={{0,24},{4,28},{8,16},{12,20},{16,8},{20,12},{24,0},{28,4},{1,25},{... | collective-permute-start | bytes 393224 | tf_op jit(solution)/shard_map/ppermute | solution.py:590
  25.2 19.2 %collective-permute-start.13 = (bf16[512,128]{1,0:T(8,128)(2,1)S(1)}, bf16[512,128]{1,0:T(8,128)(2,1)S(1)}, u32[]{:S(2)}, u32[]{:S(2)}) collective-permute-start(bf16[512,128]{1,0:T(8,128)(2,1)S(1)} %get-tuple-element.52), channel_id=1, source_target_pairs={{0,28},{4,24},{8,20},{12,16},{16,12},{20,8},{24,4},{28,0},{1,29},{... | collective-permute-start | bytes 393224 | tf_op jit(solution)/shard_map/ppermute | solution.py:590
  28.6 17.8 %collective-permute-start.20 = (f32[128,512]{1,0:T(8,128)S(1)}, f32[128,512]{1,0:T(8,128)S(1)}, u32[]{:S(2)}, u32[]{:S(2)}) collective-permute-start(f32[128,512]{1,0:T(8,128)S(1)} %get-tuple-element.58.refs_0_), channel_id=1, source_target_pairs={{0,2},{1,3},{2,0},{3,1},{4,6},{5,7},{6,4},{7,5},{8,10},{9,11},{10,... | collective-permute-start | bytes 786440 | tf_op jit(solution)/shard_map/ppermute | solution.py:595
  35.2 11.6 %collective-permute-start.17 = (f32[512,128]{1,0:T(8,128)S(1)}, f32[512,128]{1,0:T(8,128)S(1)}, u32[]{:S(2)}, u32[]{:S(2)}) collective-permute-start(f32[512,128]{1,0:T(8,128)S(1)} %get-tuple-element.57), channel_id=1, source_target_pairs={{0,1},{1,0},{2,3},{3,2},{4,5},{5,4},{6,7},{7,6},{8,9},{9,8},{10,11... | collective-permute-start | bytes 786440 | tf_op jit(solution)/shard_map/ppermute | solution.py:601
  45.7 2.7 %collective-permute-start.15 = (f32[6,128,128]{2,1,0:T(8,128)S(1)}, f32[6,128,128]{2,1,0:T(8,128)S(1)}, u32[]{:S(2)}, u32[]{:S(2)}) collective-permute-start(f32[6,128,128]{2,1,0:T(8,128)S(1)} %get-tuple-element.56), channel_id=1, source_target_pairs={{0,1},{1,0},{2,3},{3,2},{4,5},{5,4},{6,7},{7,6},{8,9},{9,8},{10,11... | collective-permute-start | bytes 1179656 | tf_op jit(solution)/shard_map/ppermute | solution.py:613
  45.8 2.9 %collective-permute-start.23 = (f32[6,128,128]{2,1,0:T(8,128)S(1)}, f32[6,128,128]{2,1,0:T(8,128)S(1)}, u32[]{:S(2)}, u32[]{:S(2)}) collective-permute-start(f32[6,128,128]{2,1,0:T(8,128)S(1)} %get-tuple-element.63), channel_id=1, source_target_pairs={{0,1},{1,0},{2,3},{3,2},{4,5},{5,4},{6,7},{7,6},{8,9},{9,8},{10,11... | collective-permute-start | bytes 1179656 | tf_op jit(solution)/shard_map/ppermute | solution.py:613
  46.3 3.2 %collective-permute-start.19 = (f32[128,512]{1,0:T(8,128)S(1)}, f32[128,512]{1,0:T(8,128)S(1)}, u32[]{:S(2)}, u32[]{:S(2)}) collective-permute-start(f32[128,512]{1,0:T(8,128)S(1)} %get-tuple-element.58.refs_0_), channel_id=1, source_target_pairs={{0,1},{1,0},{2,3},{3,2},{4,5},{5,4},{6,7},{7,6},{8,9},{9,8},{10,11... | collective-permute-start | bytes 786440 | tf_op jit(solution)/shard_map/ppermute | solution.py:596
  46.4 3.8 %collective-permute-start.21 = (f32[128,512]{1,0:T(8,128)S(1)}, f32[128,512]{1,0:T(8,128)S(1)}, u32[]{:S(2)}, u32[]{:S(2)}) collective-permute-start(f32[128,512]{1,0:T(8,128)S(1)} %collective-permute-done.20.refs_2_), channel_id=1, source_target_pairs={{0,1},{1,0},{2,3},{3,2},{4,5},{5,4},{6,7},{7,6},{8,9},{9,8},{10,11... | collective-permute-start | bytes 786440 | tf_op jit(solution)/shard_map/ppermute | solution.py:597
  46.9 9.2 %collective-permute-start.18 = (f32[512,128]{1,0:T(8,128)S(1)}, f32[512,128]{1,0:T(8,128)S(1)}, u32[]{:S(2)}, u32[]{:S(2)}) collective-permute-start(f32[512,128]{1,0:T(8,128)S(1)} %add.3.own_ref), channel_id=1, source_target_pairs={{0,2},{1,3},{2,0},{3,1},{4,6},{5,7},{6,4},{7,5},{8,10},{9,11},{10,... | collective-permute-start | bytes 786440 | tf_op jit(solution)/shard_map/ppermute | solution.py:603
  48.5 28.1 %collective-permute-start.14 = (f32[6,128,128]{2,1,0:T(8,128)S(1)}, f32[6,128,128]{2,1,0:T(8,128)S(1)}, u32[]{:S(2)}, u32[]{:S(2)}) collective-permute-start(f32[6,128,128]{2,1,0:T(8,128)S(1)} %get-tuple-element.54), channel_id=1, source_target_pairs={{0,1},{1,0},{2,3},{3,2},{4,5},{5,4},{6,7},{7,6},{8,9},{9,8},{10,11... | collective-permute-start | bytes 1179656 | tf_op jit(solution)/shard_map/ppermute | solution.py:616
  48.7 25.9 %collective-permute-start.22 = (f32[6,128,128]{2,1,0:T(8,128)S(1)}, f32[6,128,128]{2,1,0:T(8,128)S(1)}, u32[]{:S(2)}, u32[]{:S(2)}) collective-permute-start(f32[6,128,128]{2,1,0:T(8,128)S(1)} %get-tuple-element.61), channel_id=1, source_target_pairs={{0,1},{1,0},{2,3},{3,2},{4,5},{5,4},{6,7},{7,6},{8,9},{9,8},{10,11... | collective-permute-start | bytes 1179656 | tf_op jit(solution)/shard_map/ppermute | solution.py:616
  49.5 27.0 %collective-permute-start.16 = (s16[1168,128]{1,0:T(8,128)(2,1)S(1)}, s16[1168,128]{1,0:T(8,128)(2,1)S(1)}, u32[]{:S(2)}, u32[]{:S(2)}) collective-permute-start(s16[1168,128]{1,0:T(8,128)(2,1)S(1)} %pack_sums.2), channel_id=1, source_target_pairs={{0,2},{1,3},{2,0},{3,1},{4,6},{5,7},{6,4},{7,5},{8,10},{9,11},{10,... | collective-permute-start | bytes 897032 | tf_op jit(solution)/shard_map/ppermute | solution.py:614
  50.2 24.4 %collective-permute-start.24 = (s16[1168,128]{1,0:T(8,128)(2,1)S(1)}, s16[1168,128]{1,0:T(8,128)(2,1)S(1)}, u32[]{:S(2)}, u32[]{:S(2)}) collective-permute-start(s16[1168,128]{1,0:T(8,128)(2,1)S(1)} %pack_sums.3), channel_id=1, source_target_pairs={{0,2},{1,3},{2,0},{3,1},{4,6},{5,7},{6,4},{7,5},{8,10},{9,11},{10,... | collective-permute-start | bytes 897032 | tf_op jit(solution)/shard_map/ppermute | solution.py:614
  64.7 9.9 %copy-start = (f32[1,4,1,128,512]{4,3,2,1,0:T(8,128)S(1)}, f32[1,4,1,128,512]{4,3,2,1,0:T(8,128)}, u32[]{:S(2)}) copy-start(f32[1,4,1,128,512]{4,3,2,1,0:T(8,128)} %param.9) | copy-start | bytes 3145732

commit v5 on v4

--- a/solution.py
+++ b/solution.py
@@ -10,7 +10,6 @@
 CODES = 4
 CODE_ROWS = 8
 PANEL = 8
-SPLIT = 2
 HALVES = 2
 SCALE_ROWS = 16
 BITS = 23.0
@@ -333,53 +332,101 @@
         lax.fori_loop(0, size // PANEL, panel, 0)
 
 
-def eliminate(schur, inverse_ref, work, block, cb, rows):
-    eye = lax.broadcasted_iota(jnp.int32, (rows, rows), 0) == lax.broadcasted_iota(
-        jnp.int32, (rows, rows), 1
+def triangle(rows):
+    row = lax.broadcasted_iota(jnp.int32, (rows, rows), 0)
+    return row, lax.broadcasted_iota(jnp.int32, (rows, rows), 1)
+
+
+def fold_sums(first, second, cb, rows):
+    def body(first_ref, second_ref, total, folded):
+        row, col = triangle(rows)
+        line = lax.broadcasted_iota(jnp.int32, (PANEL, rows), 0)
+        marks = jnp.zeros((PANEL, rows), jnp.float32)
+        total[...] = first_ref[...] + second_ref[...]
+        for pair in range(cb // 2):
+            lower = total[2 * pair * rows:(2 * pair + 1) * rows]
+            upper = total[(2 * pair + 1) * rows:(2 * pair + 2) * rows]
+            folded[pair * rows:(pair + 1) * rows] = jnp.where(row >= col, lower, upper)
+            edge = jnp.sum(jnp.where(row == col, upper, 0.0), axis=0, keepdims=True)
+            marks = jnp.where(line == pair, edge, marks)
+        folded[cb // 2 * rows:] = marks
+
+    return pl.pallas_call(
+        body,
+        name="fold_sums",
+        compiler_params=limit(8),
+        out_shape=[
+            pltpu.VMEM((cb * rows, rows), jnp.float32),
+            pltpu.VMEM((cb // 2 * rows + PANEL, rows), jnp.float32),
+        ],
+        in_specs=spaces(2, pltpu.VMEM),
+        out_specs=spaces(2, pltpu.VMEM),
+    )(*near_core(first, second))
+
+
+def unfold_sums(folded, cb, rows):
+    row, col = triangle(rows)
+    blocks = []
+    for pair in range(cb // 2):
+        square = folded[pair * rows:(pair + 1) * rows]
+        edge = folded[cb // 2 * rows + pair:cb // 2 * rows + pair + 1]
+        lower = jnp.where(row > col, square, 0.0)
+        upper = jnp.where(row < col, square, 0.0)
+        blocks.append(lower + lower.T + jnp.where(row == col, square, 0.0))
+        blocks.append(upper + upper.T + jnp.where(row == col, edge, 0.0))
+    return blocks
+
+
+def small_dot(left, right, dims):
+    return lax.dot_general(
+        left, right, (dims, ((), ())), precision=HIGHEST, preferred_element_type=jnp.float32
     )
-    upper = lax.broadcasted_iota(jnp.int32, (rows, rows), 0) <= lax.broadcasted_iota(
-        jnp.int32, (rows, rows), 1
-    )
-    here = block * rows
-    work[:, :rows] = schur[block, :, here:here + rows]
-    work[:, rows:] = eye.astype(jnp.float32)
+
+
+def write_inverse(out, first, second, between, rows):
+    out[:rows, :rows] = first
+    out[:rows, rows:] = jnp.zeros_like(first)
+    out[rows:, rows:] = second
+    product = small_dot(between, first, ((0,), (0,)))
+    out[rows:, :rows] = -small_dot(second, product, ((1,), (0,)))
+
+
+def eliminate(block, work, rows):
+    row, col = triangle(rows)
+    work[:, :rows] = block
+    work[:, rows:] = (row == col).astype(jnp.float32)
     factor_block(work, rows)
-    schur[block, :, here:here + rows] = jnp.where(upper, work[:, :rows], 0.0)
-    inverse = work[:, rows:]
-    inverse_ref[...] = inverse
-    if block + 1 < cb:
-        after = here + rows
-        strip = lax.dot_general(
-            inverse, schur[block, :, after:], (((1,), (0,)), ((), ())),
-            precision=HIGHEST, preferred_element_type=jnp.float32,
-        )
-        schur[block, :, after:] = strip
-        for other in range(block + 1, cb):
-            offset = (other - block - 1) * rows
-            schur[other, :, other * rows:] -= lax.dot_general(
-                strip[:, offset:offset + rows], strip[:, offset:], (((0,), (0,)), ((), ())),
-                precision=HIGHEST, preferred_element_type=jnp.float32,
-            )
-
-
-def kept_inverse(schur, block, cb, rows):
-    return schur.at[cb - 1, :, block * rows:(block + 1) * rows]
+    return jnp.where(row <= col, work[:, :rows], 0.0), work[:, rows:]
 
 
 def first_factor(own_sum, other_sum, strips, cb, rows):
     blk_count = len(strips)
+    half = cb // HALVES
 
     def body(own_ref, other_ref, *refs):
         strip_refs = refs[:blk_count]
-        schur, work = refs[blk_count:]
+        schur, lead, inverses, work = refs[blk_count:]
         me = lax.axis_index("blk")
         for x in range(blk_count):
             schur[jnp.bitwise_xor(me, x)] = strip_refs[x][...]
+        others = unfold_sums(other_ref, cb, rows)
         for c in range(cb):
             part = slice(c * rows, (c + 1) * rows)
-            schur[c, :, part] -= own_ref[part] + other_ref[part]
-        for block in range(cb // SPLIT):
-            eliminate(schur, kept_inverse(schur, block, cb, rows), work, block, cb, rows)
+            schur[c, :, part] -= own_ref[part] + others[c]
+        for block in range(half):
+            here = block * rows
+            upper, inverse = eliminate(schur[block, :, here:here + rows], work, rows)
+            schur[block, :, here:here + rows] = upper
+            inverses[block] = inverse
+            after = here + rows
+            strip = small_dot(inverse, schur[block, :, after:], ((1,), (0,)))
+            schur[block, :, after:] = strip
+            for other in range(block + 1, cb):
+                offset = (other - block - 1) * rows
+                schur[other, :, other * rows:] -= small_dot(
+                    strip[:, offset:offset + rows], strip[:, offset:], ((0,), (0,))
+                )
+        write_inverse(lead, inverses[0], inverses[1], schur[0, :, rows:2 * rows], rows)
 
     return pl.pallas_call(
         body,
@@ -387,62 +434,71 @@
         compiler_params=limit(12),
         out_shape=[
             pltpu.VMEM((cb, rows, cb * rows), jnp.float32),
+            pltpu.VMEM((half * rows, half * rows), jnp.float32),
         ],
         in_specs=spaces(2 + blk_count, pltpu.VMEM),
-        out_specs=spaces(1, pltpu.VMEM),
-        scratch_shapes=[pltpu.VMEM((rows, 2 * rows), jnp.float32)],
-        cost_estimate=pl.CostEstimate(flops=10000000000, bytes_accessed=2000000, transcendentals=0),
-    )(*near_core(own_sum, other_sum, *strips))[0]
-
-
-def last_factor(schur_in, cb, rows):
-    width = cb * rows
-
-    def body(schur_ref, whole, lower, schur, inverses, work):
-        me = lax.axis_index("blk")
-        schur[...] = schur_ref[...]
-        for block in range(cb // SPLIT):
-            inverses[block] = kept_inverse(schur_ref, block, cb, rows)[...]
-        for block in range(cb // SPLIT, cb):
-            eliminate(schur, inverses.at[block], work, block, cb, rows)
-        for k in range(cb):
-            piece = jnp.where(k <= me, schur[k, :, pl.ds(pl.multiple_of(me * rows, rows), rows)], 0.0)
-            lower[:, k * rows:(k + 1) * rows] = piece.T
-        whole[...] = jnp.zeros_like(whole)
-        for i in range(cb):
-            whole[i * rows:(i + 1) * rows, i * rows:(i + 1) * rows] = inverses[i]
-            if i:
-                done = slice(0, i * rows)
-                total = jnp.zeros((rows, i * rows), jnp.float32)
-                for k in range(i):
-                    total = total + lax.dot_general(
-                        schur[k, :, i * rows:(i + 1) * rows],
-                        whole[k * rows:(k + 1) * rows, done],
-                        (((0,), (0,)), ((), ())),
-                        precision=HIGHEST, preferred_element_type=jnp.float32,
-                    )
-                whole[i * rows:(i + 1) * rows, done] = -lax.dot_general(
-                    inverses[i], total, (((1,), (0,)), ((), ())),
-                    precision=HIGHEST, preferred_element_type=jnp.float32,
-                )
-
-    return pl.pallas_call(
-        body,
-        name="factor_last",
-        compiler_params=limit(12),
-        out_shape=[
-            pltpu.VMEM((width, width), jnp.float32),
-            pltpu.VMEM((rows, width), jnp.float32),
-        ],
-        in_specs=spaces(1, pltpu.VMEM),
         out_specs=spaces(2, pltpu.VMEM),
         scratch_shapes=[
-            pltpu.VMEM((cb, rows, width), jnp.float32),
-            pltpu.VMEM((cb, rows, rows), jnp.float32),
+            pltpu.VMEM((half, rows, rows), jnp.float32),
             pltpu.VMEM((rows, 2 * rows), jnp.float32),
         ],
-        cost_estimate=pl.CostEstimate(flops=12000000000, bytes_accessed=2000000, transcendentals=0),
-    )(*near_core(schur_in))
+        cost_estimate=pl.CostEstimate(flops=10000000000, bytes_accessed=2000000, transcendentals=0),
+    )(*near_core(own_sum, other_sum, *strips))
+
+
+def middle_factor(schur, cb, rows):
+    def body(schur_ref, strip, corner, inverse_ref, work):
+        block = cb // HALVES
+        here = block * rows
+        upper, inverse = eliminate(schur_ref[block, :, here:here + rows], work, rows)
+        side = small_dot(inverse, schur_ref[block, :, here + rows:], ((1,), (0,)))
+        strip[:, :rows] = upper
+        strip[:, rows:] = side
+        inverse_ref[...] = inverse
+        corner[...] = schur_ref[cb - 1, :, here + rows:] - small_dot(side, side, ((0,), (0,)))
+
+    return pl.pallas_call(
+        body,
+        name="factor_middle",
+        compiler_params=limit(8),
+        out_shape=[
+            pltpu.VMEM((rows, 2 * rows), jnp.float32),
+            pltpu.VMEM((rows, rows), jnp.float32),
+            pltpu.VMEM((rows, rows), jnp.float32),
+        ],
+        in_specs=spaces(1, pltpu.VMEM),
+        out_specs=spaces(3, pltpu.VMEM),
+        scratch_shapes=[pltpu.VMEM((rows, 2 * rows), jnp.float32)],
+        cost_estimate=pl.CostEstimate(flops=5000000000, bytes_accessed=1000000, transcendentals=0),
+    )(*near_core(schur))
+
+
+def last_factor(schur, strip, corner, inverse, cb, rows):
+    half = cb // HALVES
+
+    def body(schur_ref, strip_ref, corner_ref, inverse_ref, trail, lower, work):
+        me = lax.axis_index("blk")
+        upper, last = eliminate(corner_ref[...], work, rows)
+        write_inverse(trail, inverse_ref[...], last, strip_ref[:, rows:], rows)
+        mine = pl.ds(pl.multiple_of(me * rows, rows), rows)
+        late = pl.ds(pl.multiple_of(jnp.maximum(me - half, 0) * rows, rows), rows)
+        pieces = [schur_ref[k, :, mine] for k in range(half)] + [strip_ref[:, late], upper]
+        for k in range(cb):
+            lower[:, k * rows:(k + 1) * rows] = jnp.where(k <= me, pieces[k], 0.0).T
+
+    return pl.pallas_call(
+        body,
+        name="factor_last",
+        compiler_params=limit(8),
+        out_shape=[
+            pltpu.VMEM((half * rows, half * rows), jnp.float32),
+            pltpu.VMEM((rows, cb * rows), jnp.float32),
+        ],
+        in_specs=spaces(4, pltpu.VMEM),
+        out_specs=spaces(2, pltpu.VMEM),
+        scratch_shapes=[pltpu.VMEM((rows, 2 * rows), jnp.float32)],
+        cost_estimate=pl.CostEstimate(flops=5000000000, bytes_accessed=1000000, transcendentals=0),
+    )(*near_core(schur, strip, corner, inverse))
 
 
 def pack_sums(first, second):
@@ -489,13 +545,6 @@
     return (high * 256 + low).astype(jnp.float32) * scale
 
 
-def solve_dot(left, right):
-    return lax.dot_general(
-        left, right, (((1,), (1,)), ((), ())),
-        precision=HIGHEST, preferred_element_type=jnp.float32,
-    )
-
-
 def remaining(panel_ref, update_refs, half, cb, per, rows):
     parts = []
     for c in range(cb // HALVES):
@@ -509,17 +558,19 @@
     return jnp.concatenate(parts, axis=1)
 
 
-def solve_left(panel, updates, whole, lower, cb, per, rows):
+def solve_left(panel, updates, lead, schur, lower, cb, per, rows):
     width = cb * rows
     half = width // HALVES
 
     def body(panel_ref, *refs):
         updates_ref = refs[:len(updates)]
-        whole_ref, lower_ref, out, carried = refs[len(updates):]
+        lead_ref, schur_ref, lower_ref, out, carried = refs[len(updates):]
         left = remaining(panel_ref, updates_ref, 0, cb, per, rows)
         out[0] = lower_ref[...]
-        out[1:, :, :half] = solve_dot(left, whole_ref[:half, :half]).reshape(per, rows, half)
-        carried[...] = solve_dot(left, whole_ref[half:, :half])
+        value = small_dot(left, lead_ref[...], ((1,), (1,)))
+        out[1:, :, :half] = value.reshape(per, rows, half)
+        across = schur_ref[:cb // HALVES, :, half:].reshape(half, half)
+        carried[...] = small_dot(value, across, ((1,), (0,)))
 
     return pl.pallas_call(
         body,
@@ -529,21 +580,21 @@
             jax.ShapeDtypeStruct((per + 1, rows, width), jnp.float32),
             pltpu.VMEM((per * rows, half), jnp.float32),
         ],
-        in_specs=spaces(3 + len(updates), pltpu.VMEM),
+        in_specs=spaces(4 + len(updates), pltpu.VMEM),
         out_specs=spaces(2, pltpu.VMEM),
         cost_estimate=pl.CostEstimate(flops=2000000000, bytes_accessed=5000000, transcendentals=0),
-    )(panel, *near_core(*updates, whole, lower))
-
-
-def solve_right(panel, updates, whole, carried, out, cb, per, rows):
+    )(panel, *near_core(*updates, lead, schur, lower))
+
+
+def solve_right(panel, updates, trail, carried, out, cb, per, rows):
     width = cb * rows
     half = width // HALVES
 
     def body(panel_ref, *refs):
         updates_ref = refs[:len(updates)]
-        whole_ref, carried_ref, _, result, stage, sem = refs[len(updates):]
-        left = remaining(panel_ref, updates_ref, 1, cb, per, rows)
-        value = carried_ref[...] + solve_dot(left, whole_ref[half:, half:])
+        trail_ref, carried_ref, _, result, stage, sem = refs[len(updates):]
+        left = remaining(panel_ref, updates_ref, 1, cb, per, rows) - carried_ref[...]
+        value = small_dot(left, trail_ref[...], ((1,), (1,)))
         stage[...] = value.reshape(per, rows, half)
         copy = pltpu.make_async_copy(
             stage, result.at[pl.ds(1, per), :, pl.ds(half, half)], sem
@@ -561,7 +612,7 @@
         scratch_shapes=[pltpu.VMEM((per, rows, half), jnp.float32), pltpu.SemaphoreType.DMA(())],
         input_output_aliases={3 + len(updates): 0},
         cost_estimate=pl.CostEstimate(flops=2000000000, bytes_accessed=5000000, transcendentals=0),
-    )(panel, *near_core(*updates, whole, carried), out)
+    )(panel, *near_core(*updates, trail, carried), out)
 
 
 def shards(desc_panel, row_map, anc_order, anc_below, anc_panel):
@@ -599,9 +650,9 @@
 
     diagonal, codes = diagonal_update(heads, cb, leaves, rows)
     diagonal_near = lax.ppermute(diagonal, "blk", near)
-    diagonal = diagonal + diagonal_near
-    diagonal_far = lax.ppermute(diagonal, "blk", far)
-    schur = first_factor(diagonal, diagonal_far, strips, cb, rows)
+    diagonal, folded = fold_sums(diagonal, diagonal_near, cb, rows)
+    folded = lax.ppermute(folded, "blk", far)
+    schur, lead = first_factor(diagonal, folded, strips, cb, rows)
 
     partials = below_update(heads, tails, codes, cb, blk_count, per, leaves, rows)
     kept, for_near, for_far, for_both = (
@@ -614,10 +665,11 @@
         from_far.append(lax.ppermute(pack_sums(for_far[half], passed), "blk", far))
     for half in range(HALVES):
         from_near.append(lax.ppermute(for_near[half], "blk", near))
-    whole, lower = last_factor(schur, cb, rows)
+    strip, corner, inverse = middle_factor(schur, cb, rows)
+    trail, lower = last_factor(schur, strip, corner, inverse, cb, rows)
     updates = [[kept[half], from_near[half], from_far[half]] for half in range(HALVES)]
-    out, carried = solve_left(panel, updates[0], whole, lower, cb, per, rows)
-    out = solve_right(panel, updates[1], whole, carried, out, cb, per, rows)
+    out, carried = solve_left(panel, updates[0], lead, schur, lower, cb, per, rows)
+    out = solve_right(panel, updates[1], trail, carried, out, cb, per, rows)
     return out.reshape(anc_panel.shape)
 
 

time: 78.1 us -> 79.5 us (1.018)
  waiting for transfers between devices: 25.5 us -> 28.2 us
  Pallas kernels: 26.4 us -> 25.4 us
    ppermute x2, waiting for transfers between devices: 0.01 us -> 3.78 us  [shards(): from_far.append(lax.ppermute(pack_sums(for_far[half], passed), 'blk', far))]
    pallas_call x1 -> x3, Pallas kernels: 9.84 us -> 8.03 us  [the longest x1 3.99 us: middle_factor(): pl.pallas_call(body, name='factor_middle', compiler_params=limit(8), out_...]
    ppermute x1, waiting for transfers between devices: 4.52 us -> 3.44 us  [shards(): folded = lax.ppermute(folded, 'blk', far)]
  transfers between devices with their start and end apart: 25 -> 25, of which waited for: 8 -> 9; matrix products, arithmetic and copies ran while one was open for 0% -> 0% of each run, Pallas kernels for 30% -> 28%
where the time goes in v5:
time: 79.5 us; the launch traced here: 79.3 us
  waiting for transfers between devices  28.2 us (35%)
  starting transfers between devices  25.6 us (32%)
  Pallas kernels  25.4 us (32%)
    ppermute x14, waiting for transfers between devices, exchange(): received.append(lax.ppermute(arrays[k], 'leaf', swap))  20.9 us
    ppermute x14, starting transfers between devices, exchange(): received.append(lax.ppermute(arrays[k], 'leaf', swap))  19 us
    pallas_call x1, Pallas kernels, first_factor(): pl.pallas_call(body, name='factor_first', compiler_params=limit(12), out_...  8.93 us
    pallas_call x1, Pallas kernels, middle_factor(): pl.pallas_call(body, name='factor_middle', compiler_params=limit(8), out_...  3.99 us
    pallas_call x1, Pallas kernels, last_factor(): pl.pallas_call(body, name='factor_last', compiler_params=limit(8), out_sh...  3.98 us
    ppermute x2, waiting for transfers between devices, shards(): from_far.append(lax.ppermute(pack_sums(for_far[half], passed), 'blk', far))  3.78 us
    ppermute x1, waiting for transfers between devices, shards(): folded = lax.ppermute(folded, 'blk', far)  3.44 us
    pallas_call x1, Pallas kernels, solve_left(): pl.pallas_call(body, name='solve_left', compiler_params=limit(16), out_sh...  2.42 us
  transfers between devices with their start and end apart: 25, of which 9 were waited for; matrix products, arithmetic and copies ran while one was open for 0% of the time, Pallas kernels for 28%

profile of v5, /device:TPU:8, one launch (start us, length us, event | category | flops | bytes accessed | tf_op | source)
XLA Modules:
  0.0 79.3 jit_solution(8428411754226031389)
XLA Ops:
  0.0 2.0 %pack.1 = (bf16[264,128]{1,0:T(8,128)(2,1)S(1)}, bf16[264,128]{1,0:T(8,128)(2,1)S(1)}, bf16[264,128]{1,0:T(8,128)(2,1)S(1)}, bf16[264,128]{1,0:T(8,128)(2,1)S(1)...) custom-call(s32[3,8]{1,0:T(4,128)} %bitcast.8, ...), custom_call_target="tpu_custom_call" | custom-call | tf_op jit(solution)/shard_map/pack/pallas_call | solution.py:120
  2.0 1.6 %collective-permute-start = (bf16[264,128]{1,0:T(8,128)(2,1)S(1)}, bf16[264,128]{1,0:T(8,128)(2,1)S(1)}, u32[]{:S(2)}, u32[]{:S(2)}) collective-permute-start(bf16[264,128]{1,0:T(8,128)(2,1)S(1)} %get-tuple-element.44), channel_id=1, source_target_pairs={{0,4},{4,0},{8,12},{12,8},{16,20},{20,16},{24,28},{28,24},{1,5},{5... | collective-permute-start | bytes 202760 | tf_op jit(solution)/shard_map/ppermute | solution.py:641
  4.1 1.5 %collective-permute-start.2 = (bf16[264,128]{1,0:T(8,128)(2,1)S(1)}, bf16[264,128]{1,0:T(8,128)(2,1)S(1)}, u32[]{:S(2)}, u32[]{:S(2)}) collective-permute-start(bf16[264,128]{1,0:T(8,128)(2,1)S(1)} %get-tuple-element.46), channel_id=1, source_target_pairs={{0,12},{4,8},{8,4},{12,0},{16,28},{20,24},{24,20},{28,16},{1,13},{... | collective-permute-start | bytes 202760 | tf_op jit(solution)/shard_map/ppermute | solution.py:641
  5.6 2.6 %collective-permute-start.3 = (bf16[264,128]{1,0:T(8,128)(2,1)S(1)}, bf16[264,128]{1,0:T(8,128)(2,1)S(1)}, u32[]{:S(2)}, u32[]{:S(2)}) collective-permute-start(bf16[264,128]{1,0:T(8,128)(2,1)S(1)} %get-tuple-element.47), channel_id=1, source_target_pairs={{0,16},{4,20},{8,24},{12,28},{16,0},{20,4},{24,8},{28,12},{1,17},{... | collective-permute-start | bytes 202760 | tf_op jit(solution)/shard_map/ppermute | solution.py:641
  8.2 1.5 %collective-permute-start.7 = (bf16[512,128]{1,0:T(8,128)(2,1)S(1)}, bf16[512,128]{1,0:T(8,128)(2,1)S(1)}, u32[]{:S(2)}, u32[]{:S(2)}) collective-permute-start(bf16[512,128]{1,0:T(8,128)(2,1)S(1)} %get-tuple-element.53), channel_id=1, source_target_pairs={{0,4},{4,0},{8,12},{12,8},{16,20},{20,16},{24,28},{28,24},{1,5},{5... | collective-permute-start | bytes 393224 | tf_op jit(solution)/shard_map/ppermute | solution.py:641
  9.7 0.5 collective-permute-start.8
  10.1 0.7 collective-permute-start.4
  10.9 2.3 %collective-permute-start.5 = (bf16[264,128]{1,0:T(8,128)(2,1)S(1)}, bf16[264,128]{1,0:T(8,128)(2,1)S(1)}, u32[]{:S(2)}, u32[]{:S(2)}) collective-permute-start(bf16[264,128]{1,0:T(8,128)(2,1)S(1)} %get-tuple-element.49), channel_id=1, source_target_pairs={{0,24},{4,28},{8,16},{12,20},{16,8},{20,12},{24,0},{28,4},{1,25},{... | collective-permute-start | bytes 202760 | tf_op jit(solution)/shard_map/ppermute | solution.py:641
  13.2 1.0 %collective-permute-start.6 = (bf16[264,128]{1,0:T(8,128)(2,1)S(1)}, bf16[264,128]{1,0:T(8,128)(2,1)S(1)}, u32[]{:S(2)}, u32[]{:S(2)}) collective-permute-start(bf16[264,128]{1,0:T(8,128)(2,1)S(1)} %get-tuple-element.50), channel_id=1, source_target_pairs={{0,28},{4,24},{8,20},{12,16},{16,12},{20,8},{24,4},{28,0},{1,29},{... | collective-permute-start | bytes 202760 | tf_op jit(solution)/shard_map/ppermute | solution.py:641
  14.2 3.4 %collective-permute-done.4.refs_5_.refs_14_ = bf16[264,128]{1,0:T(8,128)(2,1)S(1)} collective-permute-done((bf16[264,128]{1,0:T(8,128)(2,1)S(1)}, bf16[264,128]{1,0:T(8,128)(2,1)S(1)}, u32[]{:S(2)}, u32[]{:S(2)}) %collective-permute-start.4) | collective-permute-done | bytes 67616 | tf_op jit(solution)/shard_map/ppermute | solution.py:641
  17.6 3.8 %collective-permute-start.9 = (bf16[512,128]{1,0:T(8,128)(2,1)S(1)}, bf16[512,128]{1,0:T(8,128)(2,1)S(1)}, u32[]{:S(2)}, u32[]{:S(2)}) collective-permute-start(bf16[512,128]{1,0:T(8,128)(2,1)S(1)} %get-tuple-element.55), channel_id=1, source_target_pairs={{0,12},{4,8},{8,4},{12,0},{16,28},{20,24},{24,20},{28,16},{1,13},{... | collective-permute-start | bytes 393224 | tf_op jit(solution)/shard_map/ppermute | solution.py:641
  21.4 0.6 collective-permute-done.5.refs_6_.refs_15_
  21.9 2.8 %collective-permute-done.6.refs_7_.refs_16_ = bf16[264,128]{1,0:T(8,128)(2,1)S(1)} collective-permute-done((bf16[264,128]{1,0:T(8,128)(2,1)S(1)}, bf16[264,128]{1,0:T(8,128)(2,1)S(1)}, u32[]{:S(2)}, u32[]{:S(2)}) %collective-permute-start.6) | collective-permute-done | bytes 67616 | tf_op jit(solution)/shard_map/ppermute | solution.py:641
  25.2 2.6 %collective-permute-start.13 = (bf16[512,128]{1,0:T(8,128)(2,1)S(1)}, bf16[512,128]{1,0:T(8,128)(2,1)S(1)}, u32[]{:S(2)}, u32[]{:S(2)}) collective-permute-start(bf16[512,128]{1,0:T(8,128)(2,1)S(1)} %get-tuple-element.59), channel_id=1, source_target_pairs={{0,28},{4,24},{8,20},{12,16},{16,12},{20,8},{24,4},{28,0},{1,29},{... | collective-permute-start | bytes 393224 | tf_op jit(solution)/shard_map/ppermute | solution.py:641
  27.8 0.8 diagonal.1
  28.6 1.6 %collective-permute-start.20 = (f32[128,512]{1,0:T(8,128)S(1)}, f32[128,512]{1,0:T(8,128)S(1)}, u32[]{:S(2)}, u32[]{:S(2)}) collective-permute-start(f32[128,512]{1,0:T(8,128)S(1)} %get-tuple-element.67.refs_0_), channel_id=1, source_target_pairs={{0,2},{1,3},{2,0},{3,1},{4,6},{5,7},{6,4},{7,5},{8,10},{9,11},{10,... | collective-permute-start | bytes 786440 | tf_op jit(solution)/shard_map/ppermute | solution.py:646
  30.2 5.0 %collective-permute-done.10.refs_5_ = bf16[512,128]{1,0:T(8,128)(2,1)S(1)} collective-permute-done((bf16[512,128]{1,0:T(8,128)(2,1)S(1)}, bf16[512,128]{1,0:T(8,128)(2,1)S(1)}, u32[]{:S(2)}, u32[]{:S(2)}) %collective-permute-start.10) | collective-permute-done | bytes 131104 | tf_op jit(solution)/shard_map/ppermute | solution.py:641
  35.2 2.8 %collective-permute-done.11.refs_6_ = bf16[512,128]{1,0:T(8,128)(2,1)S(1)} collective-permute-done((bf16[512,128]{1,0:T(8,128)(2,1)S(1)}, bf16[512,128]{1,0:T(8,128)(2,1)S(1)}, u32[]{:S(2)}, u32[]{:S(2)}) %collective-permute-start.11) | collective-permute-done | bytes 131104 | tf_op jit(solution)/shard_map/ppermute | solution.py:641
  38.1 3.7 %collective-permute-done.12.refs_7_ = bf16[512,128]{1,0:T(8,128)(2,1)S(1)} collective-permute-done((bf16[512,128]{1,0:T(8,128)(2,1)S(1)}, bf16[512,128]{1,0:T(8,128)(2,1)S(1)}, u32[]{:S(2)}, u32[]{:S(2)}) %collective-permute-start.12) | collective-permute-done | bytes 131104 | tf_op jit(solution)/shard_map/ppermute | solution.py:641
  41.8 2.5 %collective-permute-done.13.refs_8_ = bf16[512,128]{1,0:T(8,128)(2,1)S(1)} collective-permute-done((bf16[512,128]{1,0:T(8,128)(2,1)S(1)}, bf16[512,128]{1,0:T(8,128)(2,1)S(1)}, u32[]{:S(2)}, u32[]{:S(2)}) %collective-permute-start.13) | collective-permute-done | bytes 131104 | tf_op jit(solution)/shard_map/ppermute | solution.py:641
  44.3 1.4 %below.1 = (f32[6,128,128]{2,1,0:T(8,128)S(1)}, f32[6,128,128]{2,1,0:T(8,128)S(1)}, f32[6,128,128]{2,1,0:T(8,128)S(1)}, f32[6,128,128]{2,1,0:T(8,128)S(1)}, f32[...) custom-call(s32[8,128]{1,0:T(8,128)S(1)} %get-tuple-element.51.refs_, ...), custom_call_target="tpu_custom_call" | custom-call | flops 2000000000 | bytes 4000000 | tf_op jit(solution)/shard_map/below/pallas_call | solution.py:270
  45.8 0.5 collective-permute-start.19
  46.5 1.6 %collective-permute-start.18 = (f32[264,128]{1,0:T(8,128)S(1)}, f32[264,128]{1,0:T(8,128)S(1)}, u32[]{:S(2)}, u32[]{:S(2)}) collective-permute-start(f32[264,128]{1,0:T(8,128)S(1)} %get-tuple-element.66), channel_id=1, source_target_pairs={{0,2},{1,3},{2,0},{3,1},{4,6},{5,7},{6,4},{7,5},{8,10},{9,11},{10,... | collective-permute-start | bytes 405512 | tf_op jit(solution)/shard_map/ppermute | solution.py:654
  49.0 3.4 %collective-permute-done.18.other_ref = f32[264,128]{1,0:T(8,128)S(1)} collective-permute-done((f32[264,128]{1,0:T(8,128)S(1)}, f32[264,128]{1,0:T(8,128)S(1)}, u32[]{:S(2)}, u32[]{:S(2)}) %collective-permute-start.18) | collective-permute-done | bytes 135200 | tf_op jit(solution)/shard_map/ppermute | solution.py:654
  52.4 1.5 %collective-permute-start.16 = (s16[1168,128]{1,0:T(8,128)(2,1)S(1)}, s16[1168,128]{1,0:T(8,128)(2,1)S(1)}, u32[]{:S(2)}, u32[]{:S(2)}) collective-permute-start(s16[1168,128]{1,0:T(8,128)(2,1)S(1)} %pack_sums.2), channel_id=1, source_target_pairs={{0,2},{1,3},{2,0},{3,1},{4,6},{5,7},{6,4},{7,5},{8,10},{9,11},{10,... | collective-permute-start | bytes 897032 | tf_op jit(solution)/shard_map/ppermute | solution.py:665
  54.0 8.9 %factor_first.1 = (f32[4,128,512]{2,1,0:T(8,128)S(1)}, f32[256,256]{1,0:T(8,128)S(1)}) custom-call(f32[512,128]{1,0:T(8,128)S(1)} %get-tuple-element.65.own_ref, f32[264,128]{1,0:T(8,128)S(1)} %collective-permute-done.18.other_ref, f32[128,512]{1,0:T(8,128)S(1)} %get-tuple-element.67.refs_0_, f32[128,512]{1,0:T(8,128)S(1)} %collective-permute-done.19.refs_1_, ...), custom_call_target="tpu_custom_call" | custom-call | flops 10000000000 | bytes 2000000 | tf_op jit(solution)/shard_map/factor_first/pallas_call | solution.py:431
  62.9 4.0 %factor_middle.1 = (f32[128,256]{1,0:T(8,128)S(1)}, f32[128,128]{1,0:T(8,128)S(1)}, f32[128,128]{1,0:T(8,128)S(1)}) custom-call(f32[4,128,512]{2,1,0:T(8,128)S(1)} %get-tuple-element.68.schur_ref.refs_4_), custom_call_target="tpu_custom_call" | custom-call | flops 5000000000 | bytes 1000000 | tf_op jit(solution)/shard_map/factor_middle/pallas_call | solution.py:460
  67.1 0.6 collective-permute-start.24
  67.7 4.0 %factor_last.1 = (f32[256,256]{1,0:T(8,128)S(1)}, f32[128,512]{1,0:T(8,128)S(1)}) custom-call(f32[4,128,512]{2,1,0:T(8,128)S(1)} %get-tuple-element.68.schur_ref.refs_4_, f32[128,256]{1,0:T(8,128)S(1)} %get-tuple-element.69.strip_ref, f32[128,128]{1,0:T(8,128)S(1)} %get-tuple-element.70.corner_ref, f32[128,128]{1,0:T(8,128)S(1)} %get-tuple-element.71.inverse_ref), custom_call_target="tpu_custom_call" | custom-call | flops 5000000000 | bytes 1000000 | tf_op jit(solution)/shard_map/factor_last/pallas_call | solution.py:489
  71.7 3.8 %collective-permute-done.24.refs_2_ = s16[1168,128]{1,0:T(8,128)(2,1)S(1)} collective-permute-done((s16[1168,128]{1,0:T(8,128)(2,1)S(1)}, s16[1168,128]{1,0:T(8,128)(2,1)S(1)}, u32[]{:S(2)}, u32[]{:S(2)}) %collective-permute-start.24) | collective-permute-done | bytes 299040 | tf_op jit(solution)/shard_map/ppermute | solution.py:665
  75.5 2.4 %solve_left.1 = (f32[4,128,512]{2,1,0:T(8,128)}, f32[384,256]{1,0:T(8,128)S(1)}) custom-call(f32[4,128,512]{2,1,0:T(8,128)S(1)} %bitcast.6, f32[6,128,128]{2,1,0:T(8,128)S(1)} %get-tuple-element.73.refs_0_, f32[6,128,128]{2,1,0:T(8,128)S(1)} %collective-permute-done.22.refs_1_, s16[1168,128]{1,0:T(8,128)(2,1)S(1)} %collective-permute-done.24.refs_2_, ...), custom_call_target="tpu_custom_call" | custom-call | flops 2000000000 | bytes 5000000 | tf_op jit(solution)/shard_map/solve_left/pallas_call | solution.py:575
  77.9 1.4 %solve_right.1 = f32[4,128,512]{2,1,0:T(8,128)} custom-call(f32[4,128,512]{2,1,0:T(8,128)S(1)} %bitcast.7, f32[6,128,128]{2,1,0:T(8,128)S(1)} %get-tuple-element.60.refs_0_, f32[6,128,128]{2,1,0:T(8,128)S(1)} %collective-permute-done.14.refs_1_, s16[1168,128]{1,0:T(8,128)(2,1)S(1)} %collective-permute-done.16.refs_2_, ...), custom_call_target="tpu_custom_call", output_to_operand_aliasing={{}: (6, {})} | custom-call | flops 2000000000 | bytes 5000000 | tf_op jit(solution)/shard_map/solve_right/pallas_call | solution.py:605
  (31 shorter events, 2.3 us)
Async XLA Ops:
  2.0 7.6 %collective-permute-start = (bf16[264,128]{1,0:T(8,128)(2,1)S(1)}, bf16[264,128]{1,0:T(8,128)(2,1)S(1)}, u32[]{:S(2)}, u32[]{:S(2)}) collective-permute-start(bf16[264,128]{1,0:T(8,128)(2,1)S(1)} %get-tuple-element.44), channel_id=1, source_target_pairs={{0,4},{4,0},{8,12},{12,8},{16,20},{20,16},{24,28},{28,24},{1,5},{5... | collective-permute-start | bytes 202760 | tf_op jit(solution)/shard_map/ppermute | solution.py:641
  3.6 6.5 %collective-permute-start.1 = (bf16[264,128]{1,0:T(8,128)(2,1)S(1)}, bf16[264,128]{1,0:T(8,128)(2,1)S(1)}, u32[]{:S(2)}, u32[]{:S(2)}) collective-permute-start(bf16[264,128]{1,0:T(8,128)(2,1)S(1)} %get-tuple-element.45), channel_id=1, source_target_pairs={{0,8},{4,12},{8,0},{12,4},{16,24},{20,28},{24,16},{28,20},{1,9},{5... | collective-permute-start | bytes 202760 | tf_op jit(solution)/shard_map/ppermute | solution.py:641
  4.1 6.8 %collective-permute-start.2 = (bf16[264,128]{1,0:T(8,128)(2,1)S(1)}, bf16[264,128]{1,0:T(8,128)(2,1)S(1)}, u32[]{:S(2)}, u32[]{:S(2)}) collective-permute-start(bf16[264,128]{1,0:T(8,128)(2,1)S(1)} %get-tuple-element.46), channel_id=1, source_target_pairs={{0,12},{4,8},{8,4},{12,0},{16,28},{20,24},{24,20},{28,16},{1,13},{... | collective-permute-start | bytes 202760 | tf_op jit(solution)/shard_map/ppermute | solution.py:641
  5.6 7.6 %collective-permute-start.3 = (bf16[264,128]{1,0:T(8,128)(2,1)S(1)}, bf16[264,128]{1,0:T(8,128)(2,1)S(1)}, u32[]{:S(2)}, u32[]{:S(2)}) collective-permute-start(bf16[264,128]{1,0:T(8,128)(2,1)S(1)} %get-tuple-element.47), channel_id=1, source_target_pairs={{0,16},{4,20},{8,24},{12,28},{16,0},{20,4},{24,8},{28,12},{1,17},{... | collective-permute-start | bytes 202760 | tf_op jit(solution)/shard_map/ppermute | solution.py:641
  8.2 16.5 %collective-permute-start.7 = (bf16[512,128]{1,0:T(8,128)(2,1)S(1)}, bf16[512,128]{1,0:T(8,128)(2,1)S(1)}, u32[]{:S(2)}, u32[]{:S(2)}) collective-permute-start(bf16[512,128]{1,0:T(8,128)(2,1)S(1)} %get-tuple-element.53), channel_id=1, source_target_pairs={{0,4},{4,0},{8,12},{12,8},{16,20},{20,16},{24,28},{28,24},{1,5},{5... | collective-permute-start | bytes 393224 | tf_op jit(solution)/shard_map/ppermute | solution.py:641
  9.7 15.5 %collective-permute-start.8 = (bf16[512,128]{1,0:T(8,128)(2,1)S(1)}, bf16[512,128]{1,0:T(8,128)(2,1)S(1)}, u32[]{:S(2)}, u32[]{:S(2)}) collective-permute-start(bf16[512,128]{1,0:T(8,128)(2,1)S(1)} %get-tuple-element.54), channel_id=1, source_target_pairs={{0,8},{4,12},{8,0},{12,4},{16,24},{20,28},{24,16},{28,20},{1,9},{5... | collective-permute-start | bytes 393224 | tf_op jit(solution)/shard_map/ppermute | solution.py:641
  10.1 7.4 %collective-permute-start.4 = (bf16[264,128]{1,0:T(8,128)(2,1)S(1)}, bf16[264,128]{1,0:T(8,128)(2,1)S(1)}, u32[]{:S(2)}, u32[]{:S(2)}) collective-permute-start(bf16[264,128]{1,0:T(8,128)(2,1)S(1)} %get-tuple-element.48), channel_id=1, source_target_pairs={{0,20},{4,16},{8,28},{12,24},{16,4},{20,0},{24,12},{28,8},{1,21},{... | collective-permute-start | bytes 202760 | tf_op jit(solution)/shard_map/ppermute | solution.py:641
  10.9 11.1 %collective-permute-start.5 = (bf16[264,128]{1,0:T(8,128)(2,1)S(1)}, bf16[264,128]{1,0:T(8,128)(2,1)S(1)}, u32[]{:S(2)}, u32[]{:S(2)}) collective-permute-start(bf16[264,128]{1,0:T(8,128)(2,1)S(1)} %get-tuple-element.49), channel_id=1, source_target_pairs={{0,24},{4,28},{8,16},{12,20},{16,8},{20,12},{24,0},{28,4},{1,25},{... | collective-permute-start | bytes 202760 | tf_op jit(solution)/shard_map/ppermute | solution.py:641
  13.2 11.6 %collective-permute-start.6 = (bf16[264,128]{1,0:T(8,128)(2,1)S(1)}, bf16[264,128]{1,0:T(8,128)(2,1)S(1)}, u32[]{:S(2)}, u32[]{:S(2)}) collective-permute-start(bf16[264,128]{1,0:T(8,128)(2,1)S(1)} %get-tuple-element.50), channel_id=1, source_target_pairs={{0,28},{4,24},{8,20},{12,16},{16,12},{20,8},{24,4},{28,0},{1,29},{... | collective-permute-start | bytes 202760 | tf_op jit(solution)/shard_map/ppermute | solution.py:641
  17.6 11.0 %collective-permute-start.9 = (bf16[512,128]{1,0:T(8,128)(2,1)S(1)}, bf16[512,128]{1,0:T(8,128)(2,1)S(1)}, u32[]{:S(2)}, u32[]{:S(2)}) collective-permute-start(bf16[512,128]{1,0:T(8,128)(2,1)S(1)} %get-tuple-element.55), channel_id=1, source_target_pairs={{0,12},{4,8},{8,4},{12,0},{16,28},{20,24},{24,20},{28,16},{1,13},{... | collective-permute-start | bytes 393224 | tf_op jit(solution)/shard_map/ppermute | solution.py:641
  21.9 13.3 %collective-permute-start.10 = (bf16[512,128]{1,0:T(8,128)(2,1)S(1)}, bf16[512,128]{1,0:T(8,128)(2,1)S(1)}, u32[]{:S(2)}, u32[]{:S(2)}) collective-permute-start(bf16[512,128]{1,0:T(8,128)(2,1)S(1)} %get-tuple-element.56), channel_id=1, source_target_pairs={{0,16},{4,20},{8,24},{12,28},{16,0},{20,4},{24,8},{28,12},{1,17},{... | collective-permute-start | bytes 393224 | tf_op jit(solution)/shard_map/ppermute | solution.py:641
  24.7 13.3 %collective-permute-start.11 = (bf16[512,128]{1,0:T(8,128)(2,1)S(1)}, bf16[512,128]{1,0:T(8,128)(2,1)S(1)}, u32[]{:S(2)}, u32[]{:S(2)}) collective-permute-start(bf16[512,128]{1,0:T(8,128)(2,1)S(1)} %get-tuple-element.57), channel_id=1, source_target_pairs={{0,20},{4,16},{8,28},{12,24},{16,4},{20,0},{24,12},{28,8},{1,21},{... | collective-permute-start | bytes 393224 | tf_op jit(solution)/shard_map/ppermute | solution.py:641
  24.7 17.1 %collective-permute-start.12 = (bf16[512,128]{1,0:T(8,128)(2,1)S(1)}, bf16[512,128]{1,0:T(8,128)(2,1)S(1)}, u32[]{:S(2)}, u32[]{:S(2)}) collective-permute-start(bf16[512,128]{1,0:T(8,128)(2,1)S(1)} %get-tuple-element.58), channel_id=1, source_target_pairs={{0,24},{4,28},{8,16},{12,20},{16,8},{20,12},{24,0},{28,4},{1,25},{... | collective-permute-start | bytes 393224 | tf_op jit(solution)/shard_map/ppermute | solution.py:641
  25.2 19.2 %collective-permute-start.13 = (bf16[512,128]{1,0:T(8,128)(2,1)S(1)}, bf16[512,128]{1,0:T(8,128)(2,1)S(1)}, u32[]{:S(2)}, u32[]{:S(2)}) collective-permute-start(bf16[512,128]{1,0:T(8,128)(2,1)S(1)} %get-tuple-element.59), channel_id=1, source_target_pairs={{0,28},{4,24},{8,20},{12,16},{16,12},{20,8},{24,4},{28,0},{1,29},{... | collective-permute-start | bytes 393224 | tf_op jit(solution)/shard_map/ppermute | solution.py:641
  28.6 17.7 %collective-permute-start.20 = (f32[128,512]{1,0:T(8,128)S(1)}, f32[128,512]{1,0:T(8,128)S(1)}, u32[]{:S(2)}, u32[]{:S(2)}) collective-permute-start(f32[128,512]{1,0:T(8,128)S(1)} %get-tuple-element.67.refs_0_), channel_id=1, source_target_pairs={{0,2},{1,3},{2,0},{3,1},{4,6},{5,7},{6,4},{7,5},{8,10},{9,11},{10,... | collective-permute-start | bytes 786440 | tf_op jit(solution)/shard_map/ppermute | solution.py:646
  35.2 11.2 %collective-permute-start.17 = (f32[512,128]{1,0:T(8,128)S(1)}, f32[512,128]{1,0:T(8,128)S(1)}, u32[]{:S(2)}, u32[]{:S(2)}) collective-permute-start(f32[512,128]{1,0:T(8,128)S(1)} %get-tuple-element.64.first_ref), channel_id=1, source_target_pairs={{0,1},{1,0},{2,3},{3,2},{4,5},{5,4},{6,7},{7,6},{8,9},{9,8},{10,11... | collective-permute-start | bytes 786440 | tf_op jit(solution)/shard_map/ppermute | solution.py:652
  45.7 2.5 %collective-permute-start.15 = (f32[6,128,128]{2,1,0:T(8,128)S(1)}, f32[6,128,128]{2,1,0:T(8,128)S(1)}, u32[]{:S(2)}, u32[]{:S(2)}) collective-permute-start(f32[6,128,128]{2,1,0:T(8,128)S(1)} %get-tuple-element.63), channel_id=1, source_target_pairs={{0,1},{1,0},{2,3},{3,2},{4,5},{5,4},{6,7},{7,6},{8,9},{9,8},{10,11... | collective-permute-start | bytes 1179656 | tf_op jit(solution)/shard_map/ppermute | solution.py:664
  45.8 3.0 %collective-permute-start.19 = (f32[128,512]{1,0:T(8,128)S(1)}, f32[128,512]{1,0:T(8,128)S(1)}, u32[]{:S(2)}, u32[]{:S(2)}) collective-permute-start(f32[128,512]{1,0:T(8,128)S(1)} %get-tuple-element.67.refs_0_), channel_id=1, source_target_pairs={{0,1},{1,0},{2,3},{3,2},{4,5},{5,4},{6,7},{7,6},{8,9},{9,8},{10,11... | collective-permute-start | bytes 786440 | tf_op jit(solution)/shard_map/ppermute | solution.py:647
  46.3 7.6 %collective-permute-start.21 = (f32[128,512]{1,0:T(8,128)S(1)}, f32[128,512]{1,0:T(8,128)S(1)}, u32[]{:S(2)}, u32[]{:S(2)}) collective-permute-start(f32[128,512]{1,0:T(8,128)S(1)} %collective-permute-done.20.refs_2_), channel_id=1, source_target_pairs={{0,1},{1,0},{2,3},{3,2},{4,5},{5,4},{6,7},{7,6},{8,9},{9,8},{10,11... | collective-permute-start | bytes 786440 | tf_op jit(solution)/shard_map/ppermute | solution.py:648
  46.5 6.0 %collective-permute-start.18 = (f32[264,128]{1,0:T(8,128)S(1)}, f32[264,128]{1,0:T(8,128)S(1)}, u32[]{:S(2)}, u32[]{:S(2)}) collective-permute-start(f32[264,128]{1,0:T(8,128)S(1)} %get-tuple-element.66), channel_id=1, source_target_pairs={{0,2},{1,3},{2,0},{3,1},{4,6},{5,7},{6,4},{7,5},{8,10},{9,11},{10,... | collective-permute-start | bytes 405512 | tf_op jit(solution)/shard_map/ppermute | solution.py:654
  48.0 29.9 %collective-permute-start.14 = (f32[6,128,128]{2,1,0:T(8,128)S(1)}, f32[6,128,128]{2,1,0:T(8,128)S(1)}, u32[]{:S(2)}, u32[]{:S(2)}) collective-permute-start(f32[6,128,128]{2,1,0:T(8,128)S(1)} %get-tuple-element.61), channel_id=1, source_target_pairs={{0,1},{1,0},{2,3},{3,2},{4,5},{5,4},{6,7},{7,6},{8,9},{9,8},{10,11... | collective-permute-start | bytes 1179656 | tf_op jit(solution)/shard_map/ppermute | solution.py:667
  48.2 23.5 %collective-permute-start.22 = (f32[6,128,128]{2,1,0:T(8,128)S(1)}, f32[6,128,128]{2,1,0:T(8,128)S(1)}, u32[]{:S(2)}, u32[]{:S(2)}) collective-permute-start(f32[6,128,128]{2,1,0:T(8,128)S(1)} %get-tuple-element.74), channel_id=1, source_target_pairs={{0,1},{1,0},{2,3},{3,2},{4,5},{5,4},{6,7},{7,6},{8,9},{9,8},{10,11... | collective-permute-start | bytes 1179656 | tf_op jit(solution)/shard_map/ppermute | solution.py:667
  48.8 18.1 %collective-permute-start.23 = (f32[6,128,128]{2,1,0:T(8,128)S(1)}, f32[6,128,128]{2,1,0:T(8,128)S(1)}, u32[]{:S(2)}, u32[]{:S(2)}) collective-permute-start(f32[6,128,128]{2,1,0:T(8,128)S(1)} %get-tuple-element.76), channel_id=1, source_target_pairs={{0,1},{1,0},{2,3},{3,2},{4,5},{5,4},{6,7},{7,6},{8,9},{9,8},{10,11... | collective-permute-start | bytes 1179656 | tf_op jit(solution)/shard_map/ppermute | solution.py:664
  52.4 25.5 %collective-permute-start.16 = (s16[1168,128]{1,0:T(8,128)(2,1)S(1)}, s16[1168,128]{1,0:T(8,128)(2,1)S(1)}, u32[]{:S(2)}, u32[]{:S(2)}) collective-permute-start(s16[1168,128]{1,0:T(8,128)(2,1)S(1)} %pack_sums.2), channel_id=1, source_target_pairs={{0,2},{1,3},{2,0},{3,1},{4,6},{5,7},{6,4},{7,5},{8,10},{9,11},{10,... | collective-permute-start | bytes 897032 | tf_op jit(solution)/shard_map/ppermute | solution.py:665
  67.1 8.4 %collective-permute-start.24 = (s16[1168,128]{1,0:T(8,128)(2,1)S(1)}, s16[1168,128]{1,0:T(8,128)(2,1)S(1)}, u32[]{:S(2)}, u32[]{:S(2)}) collective-permute-start(s16[1168,128]{1,0:T(8,128)(2,1)S(1)} %pack_sums.3), channel_id=1, source_target_pairs={{0,2},{1,3},{2,0},{3,1},{4,6},{5,7},{6,4},{7,5},{8,10},{9,11},{10,... | collective-permute-start | bytes 897032 | tf_op jit(solution)/shard_map/ppermute | solution.py:665
  67.7 7.8 %copy-start = (f32[1,4,1,128,512]{4,3,2,1,0:T(8,128)S(1)}, f32[1,4,1,128,512]{4,3,2,1,0:T(8,128)}, u32[]{:S(2)}) copy-start(f32[1,4,1,128,512]{4,3,2,1,0:T(8,128)} %param.9) | copy-start | bytes 3145732

commit v6 on v5

--- a/solution.py
+++ b/solution.py
@@ -38,7 +38,7 @@
     return [pl.BlockSpec(memory_space=space)] * count
 
 
-def pack_kernel(cb, nb, direct, row_map, anc_order, anc_below, panel_hbm, anc_hbm, *refs):
+def pack_kernel(cb, direct, row_map, anc_order, panel_hbm, anc_hbm, *refs):
     leaves = anc_order.shape[0]
     block_count, desc_count = row_map.shape
     rows = panel_hbm.shape[1] // block_count
@@ -59,7 +59,7 @@
             chosen[leaf * SLOTS + slot] = 0
             codes[(leaf * SLOTS + slot) * CODES] = cb
             for r in range(1, CODES):
-                codes[(leaf * SLOTS + slot) * CODES + r] = nb
+                codes[(leaf * SLOTS + slot) * CODES + r] = 0
 
     repeat(leaves, clear)
 
@@ -72,11 +72,7 @@
         chosen[place] = desc
         codes[place * CODES] = head - anc_order[leaf] * cb
         for r in range(1, block_count):
-            target = row_map[r, desc]
-            found = jnp.int32(nb)
-            for q in range(anc_below.shape[1]):
-                found = jnp.where(anc_below[leaf, q] == target, q, found)
-            codes[place * CODES + r] = found
+            codes[place * CODES + r] = row_map[r, desc] - leaves * cb
 
     repeat(desc_count, assign)
     panel_copy.wait()
@@ -99,7 +95,7 @@
     strip_copy.wait()
 
 
-def pack(desc_panel, row_map, anc_order, anc_below, anc, cb, direct):
+def pack(desc_panel, row_map, anc_order, anc, cb, direct):
     leaves = anc_order.shape[0]
     block_count = row_map.shape[1]
     rows = desc_panel.shape[1] // block_count
@@ -112,17 +108,16 @@
     else:
         outs = [jax.ShapeDtypeStruct((leaves,) + shape, dtype) for shape in (head, tail)]
     outs.append(pltpu.VMEM(anc.shape[1:], anc.dtype))
-    nb = anc_below.shape[1]
 
     def body(*refs):
-        pack_kernel(cb, nb, direct, *refs)
+        pack_kernel(cb, direct, *refs)
 
     return pl.pallas_call(
         body,
         name="pack",
         compiler_params=limit(12 if direct else 40),
         out_shape=outs,
-        in_specs=spaces(3, pltpu.SMEM) + spaces(2, pl.ANY),
+        in_specs=spaces(2, pltpu.SMEM) + spaces(2, pl.ANY),
         out_specs=spaces(len(outs), pltpu.VMEM),
         scratch_shapes=[
             pltpu.SMEM((leaves,), jnp.int32),
@@ -136,12 +131,12 @@
     )(
         *(
             pltpu.with_memory_space_constraint(array, pltpu.HBM)
-            for array in (row_map.T, anc_order, anc_below, desc_panel, anc)
+            for array in (row_map.T, anc_order, desc_panel, anc)
         )
     )
 
 
-def diagonal_kernel(cb, leaves, *refs):
+def diagonal_kernel(cb, leaves, anc_below, *refs):
     heads = refs[:-4]
     out, codes, left, right = refs[-4:]
     direct = len(heads) > 1
@@ -175,19 +170,32 @@
             left[...], right[...], (((1,), (1,)), ((), ())), preferred_element_type=jnp.float32
         )
 
+    def locate(first, size):
+        ids = codes[pl.ds(first, size)] + leaves * cb
+        found = jnp.zeros_like(ids)
+        me = lax.axis_index("leaf")
+        for q in range(anc_below.shape[1]):
+            found = jnp.where(ids == anc_below[me, q], q, found)
+        codes[pl.ds(first, size)] = jnp.where(
+            lax.rem(lane, CODES) == 0, codes[pl.ds(first, size)], found
+        )
+
     if leaves == group:
         out[...] = step(0).reshape(out.shape)
+        locate(0, group)
     else:
         out[...] = jnp.zeros_like(out)
 
         def accumulate(index, carry):
-            out[...] += step(index * group).reshape(out.shape)
+            first = pl.multiple_of(index * group, group)
+            out[...] += step(first).reshape(out.shape)
+            locate(first, group)
             return carry
 
         lax.fori_loop(0, leaves // group, accumulate, 0)
 
 
-def diagonal_update(heads, cb, leaves, rows):
+def diagonal_update(heads, anc_below, cb, leaves, rows):
     group = min(leaves, 8)
 
     def body(*refs):
@@ -201,31 +209,31 @@
             pltpu.VMEM((cb * rows, rows), jnp.float32),
             jax.ShapeDtypeStruct((leaves, rows), jnp.int32),
         ],
-        in_specs=spaces(len(heads), pltpu.VMEM),
+        in_specs=spaces(1, pltpu.SMEM) + spaces(len(heads), pltpu.VMEM),
         out_specs=spaces(2, pltpu.VMEM),
         scratch_shapes=[
             pltpu.VMEM((cb * rows, group * SLOTS * rows), heads[0].dtype),
             pltpu.VMEM((rows, group * SLOTS * rows), heads[0].dtype),
         ],
         cost_estimate=pl.CostEstimate(flops=2000000000, bytes_accessed=1000000, transcendentals=0),
-    )(*(near_core(*heads) if len(heads) > 1 else heads))
-
-
-def below_kernel(cb, blk_count, per, leaves, count, codes, *refs):
+    )(anc_below, *(near_core(*heads) if len(heads) > 1 else heads))
+
+
+def below_kernel(cb, blk_count, per, leaves, count, parts, codes, *refs):
     tails, refs = refs[:count], refs[count:]
     heads = refs[:count]
-    outs = refs[count:count + blk_count * HALVES]
-    acc, products = refs[count + blk_count * HALVES:]
+    outs = refs[count:count + len(parts)]
+    acc, products = refs[count + len(parts):]
     direct = count > 1
     me_blk = lax.axis_index("blk")
     rows = acc.shape[1]
     group = min(leaves, 8)
     tail_rows = tails[0].shape[-2] // SLOTS
     extra = tail_rows // rows
-    blocks = blk_count * cb * per
-
-    for first in range(0, blocks, cb):
-        acc[pl.ds(first, cb)] = jnp.zeros((cb, rows, rows), jnp.float32)
+    size = cb * per // HALVES
+    trash = len(parts) * size
+    for first in range(0, trash, size):
+        acc[pl.ds(first, size)] = jnp.zeros((size, rows, rows), jnp.float32)
 
     def step(base):
         for offset in range(group):
@@ -246,40 +254,42 @@
                 for r in range(extra):
                     position = codes[base + offset, slot * CODES + 1 + r]
                     relative = jnp.bitwise_xor(lax.rem(position, blk_count), me_blk)
-                    place = (relative * cb + column) * per + lax.div(position, blk_count)
-                    place = jnp.where(column < cb, place, blocks)
+                    part = relative * HALVES + lax.div(column * HALVES, cb)
+                    start = jnp.int32(-1)
+                    for at, (x, half) in enumerate(parts):
+                        start = jnp.where(part == x * HALVES + half, at * size, start)
+                    inside = lax.rem(column, cb // HALVES) * per + lax.div(position, blk_count)
+                    place = jnp.where((column < cb) & (start >= 0), start + inside, trash)
                     acc[place] += products[offset * SLOTS + slot, pl.ds(r * rows, rows)]
 
     if leaves == group:
         step(0)
     else:
         lax.fori_loop(0, leaves // group, lambda index, carry: (step(index * group), carry)[1], 0)
+    for at, out in enumerate(outs):
+        out[...] = acc[pl.ds(at * size, size)]
+
+
+def below_update(heads, tails, codes, parts, cb, blk_count, per, leaves, rows):
+    group = min(leaves, 8)
     size = cb * per // HALVES
-    for part, out in enumerate(outs):
-        out[...] = acc[pl.ds(part * size, size)]
-
-
-def below_update(heads, tails, codes, cb, blk_count, per, leaves, rows):
-    group = min(leaves, 8)
-    blocks = blk_count * cb * per
-    outs = blk_count * HALVES
 
     def body(*refs):
-        below_kernel(cb, blk_count, per, leaves, len(heads), *refs)
-
-    return pl.pallas_call(
-        body,
-        name="below",
+        below_kernel(cb, blk_count, per, leaves, len(heads), parts, *refs)
+
+    results = pl.pallas_call(
+        body,
         compiler_params=limit(16 if len(heads) > 1 else 56),
-        out_shape=[pltpu.VMEM((cb * per // HALVES, rows, rows), jnp.float32)] * outs,
+        out_shape=[pltpu.VMEM((size, rows, rows), jnp.float32)] * len(parts),
         in_specs=spaces(1, pltpu.SMEM) + spaces(2 * len(heads), pltpu.VMEM),
-        out_specs=spaces(outs, pltpu.VMEM),
+        out_specs=spaces(len(parts), pltpu.VMEM),
         scratch_shapes=[
-            pltpu.VMEM((blocks + 1, rows, rows), jnp.float32),
+            pltpu.VMEM((len(parts) * size + 1, rows, rows), jnp.float32),
             pltpu.VMEM((group * SLOTS, tails[0].shape[-2] // SLOTS, rows), jnp.float32),
         ],
         cost_estimate=pl.CostEstimate(flops=2000000000, bytes_accessed=4000000, transcendentals=0),
     )(codes, *(near_core(*tails, *heads) if len(heads) > 1 else [*tails, *heads]))
+    return dict(zip(parts, results))
 
 
 def factor_block(work, rows):
@@ -628,7 +638,7 @@
     far = [(i, i ^ 2) for i in range(blk_count)]
 
     panel = anc_panel.reshape(per + 1, rows, width)
-    *packed, strip = pack(desc_panel, row_map, anc_order, anc_below, panel, cb, direct)
+    *packed, strip = pack(desc_panel, row_map, anc_order, panel, cb, direct)
     count = len(packed) // 2
     heads, tails = packed[:count], packed[count:]
 
@@ -648,15 +658,20 @@
     strip_both = lax.ppermute(strip_far, "blk", near)
     strips = [strip, strip_near, strip_far, strip_both]
 
-    diagonal, codes = diagonal_update(heads, cb, leaves, rows)
+    diagonal, codes = diagonal_update(heads, anc_below, cb, leaves, rows)
     diagonal_near = lax.ppermute(diagonal, "blk", near)
     diagonal, folded = fold_sums(diagonal, diagonal_near, cb, rows)
     folded = lax.ppermute(folded, "blk", far)
     schur, lead = first_factor(diagonal, folded, strips, cb, rows)
 
-    partials = below_update(heads, tails, codes, cb, blk_count, per, leaves, rows)
+    every = [(x, half) for x in range(blk_count) for half in range(HALVES)]
+    urgent = [(2, 0), (3, 0)]
+    later = [part for part in every if part not in urgent]
+    sizes = (cb, blk_count, per, leaves, rows)
+    partials = below_update(heads, tails, codes, urgent, *sizes)
+    partials.update(below_update(heads, tails, codes, later, *sizes))
     kept, for_near, for_far, for_both = (
-        partials[HALVES * x:HALVES * (x + 1)] for x in range(blk_count)
+        [partials[x, half] for half in range(HALVES)] for x in range(blk_count)
     )
     from_near = []
     from_far = []

time: 79.5 us -> 76.7 us (0.965)
  waiting for transfers between devices: 28.2 us -> 23.7 us
  Pallas kernels: 25.4 us -> 27 us
    ppermute x2, waiting for transfers between devices: 3.78 us -> 1.35 us  [shards(): from_far.append(lax.ppermute(pack_sums(for_far[half], passed), 'blk', far))]
    ppermute x1, waiting for transfers between devices: 3.44 us -> 2.03 us  [shards(): folded = lax.ppermute(folded, 'blk', far)]
    pallas_call x1 -> x2, Pallas kernels: 1.4 us -> 2.46 us  [below_update(): pl.pallas_call(body, compiler_params=limit(16 if len(heads) > 1 else 56),...]
  transfers between devices with their start and end apart: 25 -> 25, of which waited for: 9 -> 9; matrix products, arithmetic and copies ran while one was open for 0% -> 0% of each run, Pallas kernels for 28% -> 31%
where the time goes in v6:
time: 76.7 us; the launch traced here: 76.6 us
  Pallas kernels  27 us (35%)
  starting transfers between devices  25.7 us (34%)
  waiting for transfers between devices  23.7 us (31%)
    ppermute x14, waiting for transfers between devices, exchange(): received.append(lax.ppermute(arrays[k], 'leaf', swap))  20.3 us
    ppermute x14, starting transfers between devices, exchange(): received.append(lax.ppermute(arrays[k], 'leaf', swap))  19 us
    pallas_call x1, Pallas kernels, first_factor(): pl.pallas_call(body, name='factor_first', compiler_params=limit(12), out_...  8.93 us
    pallas_call x1, Pallas kernels, middle_factor(): pl.pallas_call(body, name='factor_middle', compiler_params=limit(8), out_...  3.99 us
    pallas_call x1, Pallas kernels, last_factor(): pl.pallas_call(body, name='factor_last', compiler_params=limit(8), out_sh...  3.98 us
    pallas_call x2, Pallas kernels, below_update(): pl.pallas_call(body, compiler_params=limit(16 if len(heads) > 1 else 56),...  2.46 us
    pallas_call x1, Pallas kernels, solve_left(): pl.pallas_call(body, name='solve_left', compiler_params=limit(16), out_sh...  2.42 us
    ppermute x2, starting transfers between devices, shards(): from_far.append(lax.ppermute(pack_sums(for_far[half], passed), 'blk', far))  2.09 us
  transfers between devices with their start and end apart: 25, of which 9 were waited for; matrix products, arithmetic and copies ran while one was open for 0% of the time, Pallas kernels for 31%

profile of v6, /device:TPU:8, one launch (start us, length us, event | category | flops | bytes accessed | tf_op | source)
XLA Modules:
  0.0 76.6 jit_solution(15834222787499501222)
XLA Ops:
  0.0 2.0 %pack.1 = (bf16[264,128]{1,0:T(8,128)(2,1)S(1)}, bf16[264,128]{1,0:T(8,128)(2,1)S(1)}, bf16[264,128]{1,0:T(8,128)(2,1)S(1)}, bf16[264,128]{1,0:T(8,128)(2,1)S(1)...) custom-call(s32[3,8]{1,0:T(4,128)} %bitcast.8, ...), custom_call_target="tpu_custom_call" | custom-call | tf_op jit(solution)/shard_map/pack/pallas_call | solution.py:115
  2.0 1.6 %collective-permute-start = (bf16[264,128]{1,0:T(8,128)(2,1)S(1)}, bf16[264,128]{1,0:T(8,128)(2,1)S(1)}, u32[]{:S(2)}, u32[]{:S(2)}) collective-permute-start(bf16[264,128]{1,0:T(8,128)(2,1)S(1)} %get-tuple-element.44), channel_id=1, source_target_pairs={{0,4},{4,0},{8,12},{12,8},{16,20},{20,16},{24,28},{28,24},{1,5},{5... | collective-permute-start | bytes 202760 | tf_op jit(solution)/shard_map/ppermute | solution.py:651
  4.0 1.5 %collective-permute-start.2 = (bf16[264,128]{1,0:T(8,128)(2,1)S(1)}, bf16[264,128]{1,0:T(8,128)(2,1)S(1)}, u32[]{:S(2)}, u32[]{:S(2)}) collective-permute-start(bf16[264,128]{1,0:T(8,128)(2,1)S(1)} %get-tuple-element.46), channel_id=1, source_target_pairs={{0,12},{4,8},{8,4},{12,0},{16,28},{20,24},{24,20},{28,16},{1,13},{... | collective-permute-start | bytes 202760 | tf_op jit(solution)/shard_map/ppermute | solution.py:651
  5.5 2.6 %collective-permute-start.3 = (bf16[264,128]{1,0:T(8,128)(2,1)S(1)}, bf16[264,128]{1,0:T(8,128)(2,1)S(1)}, u32[]{:S(2)}, u32[]{:S(2)}) collective-permute-start(bf16[264,128]{1,0:T(8,128)(2,1)S(1)} %get-tuple-element.47), channel_id=1, source_target_pairs={{0,16},{4,20},{8,24},{12,28},{16,0},{20,4},{24,8},{28,12},{1,17},{... | collective-permute-start | bytes 202760 | tf_op jit(solution)/shard_map/ppermute | solution.py:651
  8.1 1.5 %collective-permute-start.7 = (bf16[512,128]{1,0:T(8,128)(2,1)S(1)}, bf16[512,128]{1,0:T(8,128)(2,1)S(1)}, u32[]{:S(2)}, u32[]{:S(2)}) collective-permute-start(bf16[512,128]{1,0:T(8,128)(2,1)S(1)} %get-tuple-element.53), channel_id=1, source_target_pairs={{0,4},{4,0},{8,12},{12,8},{16,20},{20,16},{24,28},{28,24},{1,5},{5... | collective-permute-start | bytes 393224 | tf_op jit(solution)/shard_map/ppermute | solution.py:651
  10.1 0.7 collective-permute-start.4
  10.8 2.3 %collective-permute-start.5 = (bf16[264,128]{1,0:T(8,128)(2,1)S(1)}, bf16[264,128]{1,0:T(8,128)(2,1)S(1)}, u32[]{:S(2)}, u32[]{:S(2)}) collective-permute-start(bf16[264,128]{1,0:T(8,128)(2,1)S(1)} %get-tuple-element.49), channel_id=1, source_target_pairs={{0,24},{4,28},{8,16},{12,20},{16,8},{20,12},{24,0},{28,4},{1,25},{... | collective-permute-start | bytes 202760 | tf_op jit(solution)/shard_map/ppermute | solution.py:651
  13.1 1.0 %collective-permute-start.6 = (bf16[264,128]{1,0:T(8,128)(2,1)S(1)}, bf16[264,128]{1,0:T(8,128)(2,1)S(1)}, u32[]{:S(2)}, u32[]{:S(2)}) collective-permute-start(bf16[264,128]{1,0:T(8,128)(2,1)S(1)} %get-tuple-element.50), channel_id=1, source_target_pairs={{0,28},{4,24},{8,20},{12,16},{16,12},{20,8},{24,4},{28,0},{1,29},{... | collective-permute-start | bytes 202760 | tf_op jit(solution)/shard_map/ppermute | solution.py:651
  14.1 3.4 %collective-permute-done.4.refs_6_.refs_14_ = bf16[264,128]{1,0:T(8,128)(2,1)S(1)} collective-permute-done((bf16[264,128]{1,0:T(8,128)(2,1)S(1)}, bf16[264,128]{1,0:T(8,128)(2,1)S(1)}, u32[]{:S(2)}, u32[]{:S(2)}) %collective-permute-start.4) | collective-permute-done | bytes 67616 | tf_op jit(solution)/shard_map/ppermute | solution.py:651
  17.5 3.8 %collective-permute-start.9 = (bf16[512,128]{1,0:T(8,128)(2,1)S(1)}, bf16[512,128]{1,0:T(8,128)(2,1)S(1)}, u32[]{:S(2)}, u32[]{:S(2)}) collective-permute-start(bf16[512,128]{1,0:T(8,128)(2,1)S(1)} %get-tuple-element.55), channel_id=1, source_target_pairs={{0,12},{4,8},{8,4},{12,0},{16,28},{20,24},{24,20},{28,16},{1,13},{... | collective-permute-start | bytes 393224 | tf_op jit(solution)/shard_map/ppermute | solution.py:651
  21.3 0.6 collective-permute-done.5.refs_7_.refs_15_
  21.9 2.8 %collective-permute-done.6.refs_8_.refs_16_ = bf16[264,128]{1,0:T(8,128)(2,1)S(1)} collective-permute-done((bf16[264,128]{1,0:T(8,128)(2,1)S(1)}, bf16[264,128]{1,0:T(8,128)(2,1)S(1)}, u32[]{:S(2)}, u32[]{:S(2)}) %collective-permute-start.6) | collective-permute-done | bytes 67616 | tf_op jit(solution)/shard_map/ppermute | solution.py:651
  25.1 2.6 %collective-permute-start.13 = (bf16[512,128]{1,0:T(8,128)(2,1)S(1)}, bf16[512,128]{1,0:T(8,128)(2,1)S(1)}, u32[]{:S(2)}, u32[]{:S(2)}) collective-permute-start(bf16[512,128]{1,0:T(8,128)(2,1)S(1)} %get-tuple-element.59), channel_id=1, source_target_pairs={{0,28},{4,24},{8,20},{12,16},{16,12},{20,8},{24,4},{28,0},{1,29},{... | collective-permute-start | bytes 393224 | tf_op jit(solution)/shard_map/ppermute | solution.py:651
  27.7 1.4 %diagonal.1 = (f32[512,128]{1,0:T(8,128)S(1)}, s32[8,128]{1,0:T(8,128)S(1)}) custom-call(s32[8,12]{1,0:T(8,128)S(1)} %copy-done.1, bf16[264,128]{1,0:T(8,128)(2,1)S(1)} %get-tuple-element.43.refs_1_.refs_9_, bf16[264,128]{1,0:T(8,128)(2,1)S(1)} %collective-permute-done.refs_2_.refs_10_, bf16[264,128]{1,0:T(8,128)(2,1)S(1)} %collective-permute-done.1.refs_3_.refs_11_, ...), custom_call_target="tpu_custom_call" | custom-call | flops 2000000000 | bytes 1000000 | tf_op jit(solution)/shard_map/diagonal/pallas_call | solution.py:204
  29.2 1.6 %collective-permute-start.20 = (f32[128,512]{1,0:T(8,128)S(1)}, f32[128,512]{1,0:T(8,128)S(1)}, u32[]{:S(2)}, u32[]{:S(2)}) collective-permute-start(f32[128,512]{1,0:T(8,128)S(1)} %get-tuple-element.67.refs_0_), channel_id=1, source_target_pairs={{0,2},{1,3},{2,0},{3,1},{4,6},{5,7},{6,4},{7,5},{8,10},{9,11},{10,... | collective-permute-start | bytes 786440 | tf_op jit(solution)/shard_map/ppermute | solution.py:656
  30.7 4.4 %collective-permute-done.10.refs_5_ = bf16[512,128]{1,0:T(8,128)(2,1)S(1)} collective-permute-done((bf16[512,128]{1,0:T(8,128)(2,1)S(1)}, bf16[512,128]{1,0:T(8,128)(2,1)S(1)}, u32[]{:S(2)}, u32[]{:S(2)}) %collective-permute-start.10) | collective-permute-done | bytes 131104 | tf_op jit(solution)/shard_map/ppermute | solution.py:651
  35.2 2.8 %collective-permute-done.11.refs_6_ = bf16[512,128]{1,0:T(8,128)(2,1)S(1)} collective-permute-done((bf16[512,128]{1,0:T(8,128)(2,1)S(1)}, bf16[512,128]{1,0:T(8,128)(2,1)S(1)}, u32[]{:S(2)}, u32[]{:S(2)}) %collective-permute-start.11) | collective-permute-done | bytes 131104 | tf_op jit(solution)/shard_map/ppermute | solution.py:651
  38.0 3.8 %collective-permute-done.12.refs_7_ = bf16[512,128]{1,0:T(8,128)(2,1)S(1)} collective-permute-done((bf16[512,128]{1,0:T(8,128)(2,1)S(1)}, bf16[512,128]{1,0:T(8,128)(2,1)S(1)}, u32[]{:S(2)}, u32[]{:S(2)}) %collective-permute-start.12) | collective-permute-done | bytes 131104 | tf_op jit(solution)/shard_map/ppermute | solution.py:651
  41.8 2.5 %collective-permute-done.13.refs_8_ = bf16[512,128]{1,0:T(8,128)(2,1)S(1)} collective-permute-done((bf16[512,128]{1,0:T(8,128)(2,1)S(1)}, bf16[512,128]{1,0:T(8,128)(2,1)S(1)}, u32[]{:S(2)}, u32[]{:S(2)}) %collective-permute-start.13) | collective-permute-done | bytes 131104 | tf_op jit(solution)/shard_map/ppermute | solution.py:651
  44.3 1.1 %shard_map.56 = (f32[6,128,128]{2,1,0:T(8,128)S(1)}, f32[6,128,128]{2,1,0:T(8,128)S(1)}) custom-call(s32[8,128]{1,0:T(8,128)S(1)} %get-tuple-element.51.refs_0_, bf16[512,128]{1,0:T(8,128)(2,1)S(1)} %get-tuple-element.52.refs_1_, bf16[512,128]{1,0:T(8,128)(2,1)S(1)} %collective-permute-done.7.refs_2_, bf16[512,128]{1,0:T(8,128)(2,1)S(1)} %collective-permute-done.8.refs_3_, ...), custom_call_target="tpu_custom_call" | custom-call | flops 2000000000 | bytes 4000000 | tf_op jit(solution)/shard_map/pallas_call | solution.py:280
  45.5 0.5 collective-permute-start.19
  46.1 1.6 %collective-permute-start.18 = (f32[264,128]{1,0:T(8,128)S(1)}, f32[264,128]{1,0:T(8,128)S(1)}, u32[]{:S(2)}, u32[]{:S(2)}) collective-permute-start(f32[264,128]{1,0:T(8,128)S(1)} %get-tuple-element.66), channel_id=1, source_target_pairs={{0,2},{1,3},{2,0},{3,1},{4,6},{5,7},{6,4},{7,5},{8,10},{9,11},{10,... | collective-permute-start | bytes 405512 | tf_op jit(solution)/shard_map/ppermute | solution.py:664
  47.7 1.3 %shard_map.55 = (f32[6,128,128]{2,1,0:T(8,128)S(1)}, f32[6,128,128]{2,1,0:T(8,128)S(1)}, f32[6,128,128]{2,1,0:T(8,128)S(1)}, f32[6,128,128]{2,1,0:T(8,128)S(1)},...) custom-call(s32[8,128]{1,0:T(8,128)S(1)} %get-tuple-element.51.refs_0_, ...), custom_call_target="tpu_custom_call" | custom-call | flops 2000000000 | bytes 4000000 | tf_op jit(solution)/shard_map/pallas_call | solution.py:280
  50.1 2.0 %collective-permute-done.18.other_ref = f32[264,128]{1,0:T(8,128)S(1)} collective-permute-done((f32[264,128]{1,0:T(8,128)S(1)}, f32[264,128]{1,0:T(8,128)S(1)}, u32[]{:S(2)}, u32[]{:S(2)}) %collective-permute-start.18) | collective-permute-done | bytes 135200 | tf_op jit(solution)/shard_map/ppermute | solution.py:664
  52.1 1.5 %collective-permute-start.24 = (s16[1168,128]{1,0:T(8,128)(2,1)S(1)}, s16[1168,128]{1,0:T(8,128)(2,1)S(1)}, u32[]{:S(2)}, u32[]{:S(2)}) collective-permute-start(s16[1168,128]{1,0:T(8,128)(2,1)S(1)} %pack_sums.3), channel_id=1, source_target_pairs={{0,2},{1,3},{2,0},{3,1},{4,6},{5,7},{6,4},{7,5},{8,10},{9,11},{10,... | collective-permute-start | bytes 897032 | tf_op jit(solution)/shard_map/ppermute | solution.py:680
  53.6 8.9 %factor_first.1 = (f32[4,128,512]{2,1,0:T(8,128)S(1)}, f32[256,256]{1,0:T(8,128)S(1)}) custom-call(f32[512,128]{1,0:T(8,128)S(1)} %get-tuple-element.65.own_ref, f32[264,128]{1,0:T(8,128)S(1)} %collective-permute-done.18.other_ref, f32[128,512]{1,0:T(8,128)S(1)} %get-tuple-element.67.refs_0_, f32[128,512]{1,0:T(8,128)S(1)} %collective-permute-done.19.refs_1_, ...), custom_call_target="tpu_custom_call" | custom-call | flops 10000000000 | bytes 2000000 | tf_op jit(solution)/shard_map/factor_first/pallas_call | solution.py:441
  62.6 4.0 %factor_middle.1 = (f32[128,256]{1,0:T(8,128)S(1)}, f32[128,128]{1,0:T(8,128)S(1)}, f32[128,128]{1,0:T(8,128)S(1)}) custom-call(f32[4,128,512]{2,1,0:T(8,128)S(1)} %get-tuple-element.68.schur_ref.refs_4_), custom_call_target="tpu_custom_call" | custom-call | flops 5000000000 | bytes 1000000 | tf_op jit(solution)/shard_map/factor_middle/pallas_call | solution.py:470
  66.8 0.6 collective-permute-start.16
  67.4 4.0 %factor_last.1 = (f32[256,256]{1,0:T(8,128)S(1)}, f32[128,512]{1,0:T(8,128)S(1)}) custom-call(f32[4,128,512]{2,1,0:T(8,128)S(1)} %get-tuple-element.68.schur_ref.refs_4_, f32[128,256]{1,0:T(8,128)S(1)} %get-tuple-element.69.strip_ref, f32[128,128]{1,0:T(8,128)S(1)} %get-tuple-element.70.corner_ref, f32[128,128]{1,0:T(8,128)S(1)} %get-tuple-element.71.inverse_ref), custom_call_target="tpu_custom_call" | custom-call | flops 5000000000 | bytes 1000000 | tf_op jit(solution)/shard_map/factor_last/pallas_call | solution.py:499
  71.4 2.4 %solve_left.1 = (f32[4,128,512]{2,1,0:T(8,128)}, f32[384,256]{1,0:T(8,128)S(1)}) custom-call(f32[4,128,512]{2,1,0:T(8,128)S(1)} %bitcast.6, f32[6,128,128]{2,1,0:T(8,128)S(1)} %get-tuple-element.73.refs_0_, f32[6,128,128]{2,1,0:T(8,128)S(1)} %collective-permute-done.22.refs_1_, s16[1168,128]{1,0:T(8,128)(2,1)S(1)} %collective-permute-done.24.refs_2_, ...), custom_call_target="tpu_custom_call" | custom-call | flops 2000000000 | bytes 5000000 | tf_op jit(solution)/shard_map/solve_left/pallas_call | solution.py:585
  73.8 1.3 %collective-permute-done.16.refs_2_ = s16[1168,128]{1,0:T(8,128)(2,1)S(1)} collective-permute-done((s16[1168,128]{1,0:T(8,128)(2,1)S(1)}, s16[1168,128]{1,0:T(8,128)(2,1)S(1)}, u32[]{:S(2)}, u32[]{:S(2)}) %collective-permute-start.16) | collective-permute-done | bytes 299040 | tf_op jit(solution)/shard_map/ppermute | solution.py:680
  75.2 1.4 %solve_right.1 = f32[4,128,512]{2,1,0:T(8,128)} custom-call(f32[4,128,512]{2,1,0:T(8,128)S(1)} %bitcast.7, f32[6,128,128]{2,1,0:T(8,128)S(1)} %get-tuple-element.60.refs_0_, f32[6,128,128]{2,1,0:T(8,128)S(1)} %collective-permute-done.14.refs_1_, s16[1168,128]{1,0:T(8,128)(2,1)S(1)} %collective-permute-done.16.refs_2_, ...), custom_call_target="tpu_custom_call", output_to_operand_aliasing={{}: (6, {})} | custom-call | flops 2000000000 | bytes 5000000 | tf_op jit(solution)/shard_map/solve_right/pallas_call | solution.py:615
  (34 shorter events, 2.8 us)
Async XLA Ops:
  2.0 7.6 %collective-permute-start = (bf16[264,128]{1,0:T(8,128)(2,1)S(1)}, bf16[264,128]{1,0:T(8,128)(2,1)S(1)}, u32[]{:S(2)}, u32[]{:S(2)}) collective-permute-start(bf16[264,128]{1,0:T(8,128)(2,1)S(1)} %get-tuple-element.44), channel_id=1, source_target_pairs={{0,4},{4,0},{8,12},{12,8},{16,20},{20,16},{24,28},{28,24},{1,5},{5... | collective-permute-start | bytes 202760 | tf_op jit(solution)/shard_map/ppermute | solution.py:651
  3.5 6.5 %collective-permute-start.1 = (bf16[264,128]{1,0:T(8,128)(2,1)S(1)}, bf16[264,128]{1,0:T(8,128)(2,1)S(1)}, u32[]{:S(2)}, u32[]{:S(2)}) collective-permute-start(bf16[264,128]{1,0:T(8,128)(2,1)S(1)} %get-tuple-element.45), channel_id=1, source_target_pairs={{0,8},{4,12},{8,0},{12,4},{16,24},{20,28},{24,16},{28,20},{1,9},{5... | collective-permute-start | bytes 202760 | tf_op jit(solution)/shard_map/ppermute | solution.py:651
  4.0 6.8 %collective-permute-start.2 = (bf16[264,128]{1,0:T(8,128)(2,1)S(1)}, bf16[264,128]{1,0:T(8,128)(2,1)S(1)}, u32[]{:S(2)}, u32[]{:S(2)}) collective-permute-start(bf16[264,128]{1,0:T(8,128)(2,1)S(1)} %get-tuple-element.46), channel_id=1, source_target_pairs={{0,12},{4,8},{8,4},{12,0},{16,28},{20,24},{24,20},{28,16},{1,13},{... | collective-permute-start | bytes 202760 | tf_op jit(solution)/shard_map/ppermute | solution.py:651
  5.5 7.6 %collective-permute-start.3 = (bf16[264,128]{1,0:T(8,128)(2,1)S(1)}, bf16[264,128]{1,0:T(8,128)(2,1)S(1)}, u32[]{:S(2)}, u32[]{:S(2)}) collective-permute-start(bf16[264,128]{1,0:T(8,128)(2,1)S(1)} %get-tuple-element.47), channel_id=1, source_target_pairs={{0,16},{4,20},{8,24},{12,28},{16,0},{20,4},{24,8},{28,12},{1,17},{... | collective-permute-start | bytes 202760 | tf_op jit(solution)/shard_map/ppermute | solution.py:651
  8.1 16.5 %collective-permute-start.7 = (bf16[512,128]{1,0:T(8,128)(2,1)S(1)}, bf16[512,128]{1,0:T(8,128)(2,1)S(1)}, u32[]{:S(2)}, u32[]{:S(2)}) collective-permute-start(bf16[512,128]{1,0:T(8,128)(2,1)S(1)} %get-tuple-element.53), channel_id=1, source_target_pairs={{0,4},{4,0},{8,12},{12,8},{16,20},{20,16},{24,28},{28,24},{1,5},{5... | collective-permute-start | bytes 393224 | tf_op jit(solution)/shard_map/ppermute | solution.py:651
  9.6 15.5 %collective-permute-start.8 = (bf16[512,128]{1,0:T(8,128)(2,1)S(1)}, bf16[512,128]{1,0:T(8,128)(2,1)S(1)}, u32[]{:S(2)}, u32[]{:S(2)}) collective-permute-start(bf16[512,128]{1,0:T(8,128)(2,1)S(1)} %get-tuple-element.54), channel_id=1, source_target_pairs={{0,8},{4,12},{8,0},{12,4},{16,24},{20,28},{24,16},{28,20},{1,9},{5... | collective-permute-start | bytes 393224 | tf_op jit(solution)/shard_map/ppermute | solution.py:651
  10.1 7.4 %collective-permute-start.4 = (bf16[264,128]{1,0:T(8,128)(2,1)S(1)}, bf16[264,128]{1,0:T(8,128)(2,1)S(1)}, u32[]{:S(2)}, u32[]{:S(2)}) collective-permute-start(bf16[264,128]{1,0:T(8,128)(2,1)S(1)} %get-tuple-element.48), channel_id=1, source_target_pairs={{0,20},{4,16},{8,28},{12,24},{16,4},{20,0},{24,12},{28,8},{1,21},{... | collective-permute-start | bytes 202760 | tf_op jit(solution)/shard_map/ppermute | solution.py:651
  10.8 11.1 %collective-permute-start.5 = (bf16[264,128]{1,0:T(8,128)(2,1)S(1)}, bf16[264,128]{1,0:T(8,128)(2,1)S(1)}, u32[]{:S(2)}, u32[]{:S(2)}) collective-permute-start(bf16[264,128]{1,0:T(8,128)(2,1)S(1)} %get-tuple-element.49), channel_id=1, source_target_pairs={{0,24},{4,28},{8,16},{12,20},{16,8},{20,12},{24,0},{28,4},{1,25},{... | collective-permute-start | bytes 202760 | tf_op jit(solution)/shard_map/ppermute | solution.py:651
  13.1 11.6 %collective-permute-start.6 = (bf16[264,128]{1,0:T(8,128)(2,1)S(1)}, bf16[264,128]{1,0:T(8,128)(2,1)S(1)}, u32[]{:S(2)}, u32[]{:S(2)}) collective-permute-start(bf16[264,128]{1,0:T(8,128)(2,1)S(1)} %get-tuple-element.50), channel_id=1, source_target_pairs={{0,28},{4,24},{8,20},{12,16},{16,12},{20,8},{24,4},{28,0},{1,29},{... | collective-permute-start | bytes 202760 | tf_op jit(solution)/shard_map/ppermute | solution.py:651
  17.5 11.6 %collective-permute-start.9 = (bf16[512,128]{1,0:T(8,128)(2,1)S(1)}, bf16[512,128]{1,0:T(8,128)(2,1)S(1)}, u32[]{:S(2)}, u32[]{:S(2)}) collective-permute-start(bf16[512,128]{1,0:T(8,128)(2,1)S(1)} %get-tuple-element.55), channel_id=1, source_target_pairs={{0,12},{4,8},{8,4},{12,0},{16,28},{20,24},{24,20},{28,16},{1,13},{... | collective-permute-start | bytes 393224 | tf_op jit(solution)/shard_map/ppermute | solution.py:651
  21.9 5.9 %copy-start.1 = (s32[8,12]{1,0:T(8,128)S(1)}, s32[8,12]{1,0:T(8,128)}, u32[]{:S(2)}) copy-start(s32[8,12]{1,0:T(8,128)} %refs_0_.1) | copy-start | bytes 1156
  21.9 13.3 %collective-permute-start.10 = (bf16[512,128]{1,0:T(8,128)(2,1)S(1)}, bf16[512,128]{1,0:T(8,128)(2,1)S(1)}, u32[]{:S(2)}, u32[]{:S(2)}) collective-permute-start(bf16[512,128]{1,0:T(8,128)(2,1)S(1)} %get-tuple-element.56), channel_id=1, source_target_pairs={{0,16},{4,20},{8,24},{12,28},{16,0},{20,4},{24,8},{28,12},{1,17},{... | collective-permute-start | bytes 393224 | tf_op jit(solution)/shard_map/ppermute | solution.py:651
  24.7 13.3 %collective-permute-start.11 = (bf16[512,128]{1,0:T(8,128)(2,1)S(1)}, bf16[512,128]{1,0:T(8,128)(2,1)S(1)}, u32[]{:S(2)}, u32[]{:S(2)}) collective-permute-start(bf16[512,128]{1,0:T(8,128)(2,1)S(1)} %get-tuple-element.57), channel_id=1, source_target_pairs={{0,20},{4,16},{8,28},{12,24},{16,4},{20,0},{24,12},{28,8},{1,21},{... | collective-permute-start | bytes 393224 | tf_op jit(solution)/shard_map/ppermute | solution.py:651
  24.7 17.1 %collective-permute-start.12 = (bf16[512,128]{1,0:T(8,128)(2,1)S(1)}, bf16[512,128]{1,0:T(8,128)(2,1)S(1)}, u32[]{:S(2)}, u32[]{:S(2)}) collective-permute-start(bf16[512,128]{1,0:T(8,128)(2,1)S(1)} %get-tuple-element.58), channel_id=1, source_target_pairs={{0,24},{4,28},{8,16},{12,20},{16,8},{20,12},{24,0},{28,4},{1,25},{... | collective-permute-start | bytes 393224 | tf_op jit(solution)/shard_map/ppermute | solution.py:651
  25.1 19.2 %collective-permute-start.13 = (bf16[512,128]{1,0:T(8,128)(2,1)S(1)}, bf16[512,128]{1,0:T(8,128)(2,1)S(1)}, u32[]{:S(2)}, u32[]{:S(2)}) collective-permute-start(bf16[512,128]{1,0:T(8,128)(2,1)S(1)} %get-tuple-element.59), channel_id=1, source_target_pairs={{0,28},{4,24},{8,20},{12,16},{16,12},{20,8},{24,4},{28,0},{1,29},{... | collective-permute-start | bytes 393224 | tf_op jit(solution)/shard_map/ppermute | solution.py:651
  29.2 16.8 %collective-permute-start.20 = (f32[128,512]{1,0:T(8,128)S(1)}, f32[128,512]{1,0:T(8,128)S(1)}, u32[]{:S(2)}, u32[]{:S(2)}) collective-permute-start(f32[128,512]{1,0:T(8,128)S(1)} %get-tuple-element.67.refs_0_), channel_id=1, source_target_pairs={{0,2},{1,3},{2,0},{3,1},{4,6},{5,7},{6,4},{7,5},{8,10},{9,11},{10,... | collective-permute-start | bytes 786440 | tf_op jit(solution)/shard_map/ppermute | solution.py:656
  35.2 10.9 %collective-permute-start.17 = (f32[512,128]{1,0:T(8,128)S(1)}, f32[512,128]{1,0:T(8,128)S(1)}, u32[]{:S(2)}, u32[]{:S(2)}) collective-permute-start(f32[512,128]{1,0:T(8,128)S(1)} %get-tuple-element.64.first_ref), channel_id=1, source_target_pairs={{0,1},{1,0},{2,3},{3,2},{4,5},{5,4},{6,7},{7,6},{8,9},{9,8},{10,11... | collective-permute-start | bytes 786440 | tf_op jit(solution)/shard_map/ppermute | solution.py:662
  45.4 3.9 %collective-permute-start.23 = (f32[6,128,128]{2,1,0:T(8,128)S(1)}, f32[6,128,128]{2,1,0:T(8,128)S(1)}, u32[]{:S(2)}, u32[]{:S(2)}) collective-permute-start(f32[6,128,128]{2,1,0:T(8,128)S(1)} %get-tuple-element.76), channel_id=1, source_target_pairs={{0,1},{1,0},{2,3},{3,2},{4,5},{5,4},{6,7},{7,6},{8,9},{9,8},{10,11... | collective-permute-start | bytes 1179656 | tf_op jit(solution)/shard_map/ppermute | solution.py:679
  45.5 4.4 %collective-permute-start.19 = (f32[128,512]{1,0:T(8,128)S(1)}, f32[128,512]{1,0:T(8,128)S(1)}, u32[]{:S(2)}, u32[]{:S(2)}) collective-permute-start(f32[128,512]{1,0:T(8,128)S(1)} %get-tuple-element.67.refs_0_), channel_id=1, source_target_pairs={{0,1},{1,0},{2,3},{3,2},{4,5},{5,4},{6,7},{7,6},{8,9},{9,8},{10,11... | collective-permute-start | bytes 786440 | tf_op jit(solution)/shard_map/ppermute | solution.py:657
  46.0 7.6 %collective-permute-start.21 = (f32[128,512]{1,0:T(8,128)S(1)}, f32[128,512]{1,0:T(8,128)S(1)}, u32[]{:S(2)}, u32[]{:S(2)}) collective-permute-start(f32[128,512]{1,0:T(8,128)S(1)} %collective-permute-done.20.refs_2_), channel_id=1, source_target_pairs={{0,1},{1,0},{2,3},{3,2},{4,5},{5,4},{6,7},{7,6},{8,9},{9,8},{10,11... | collective-permute-start | bytes 786440 | tf_op jit(solution)/shard_map/ppermute | solution.py:658
  46.1 6.0 %collective-permute-start.18 = (f32[264,128]{1,0:T(8,128)S(1)}, f32[264,128]{1,0:T(8,128)S(1)}, u32[]{:S(2)}, u32[]{:S(2)}) collective-permute-start(f32[264,128]{1,0:T(8,128)S(1)} %get-tuple-element.66), channel_id=1, source_target_pairs={{0,2},{1,3},{2,0},{3,1},{4,6},{5,7},{6,4},{7,5},{8,10},{9,11},{10,... | collective-permute-start | bytes 405512 | tf_op jit(solution)/shard_map/ppermute | solution.py:664
  49.0 24.8 %collective-permute-start.14 = (f32[6,128,128]{2,1,0:T(8,128)S(1)}, f32[6,128,128]{2,1,0:T(8,128)S(1)}, u32[]{:S(2)}, u32[]{:S(2)}) collective-permute-start(f32[6,128,128]{2,1,0:T(8,128)S(1)} %get-tuple-element.61), channel_id=1, source_target_pairs={{0,1},{1,0},{2,3},{3,2},{4,5},{5,4},{6,7},{7,6},{8,9},{9,8},{10,11... | collective-permute-start | bytes 1179656 | tf_op jit(solution)/shard_map/ppermute | solution.py:682
  49.3 17.3 %collective-permute-start.15 = (f32[6,128,128]{2,1,0:T(8,128)S(1)}, f32[6,128,128]{2,1,0:T(8,128)S(1)}, u32[]{:S(2)}, u32[]{:S(2)}) collective-permute-start(f32[6,128,128]{2,1,0:T(8,128)S(1)} %get-tuple-element.63), channel_id=1, source_target_pairs={{0,1},{1,0},{2,3},{3,2},{4,5},{5,4},{6,7},{7,6},{8,9},{9,8},{10,11... | collective-permute-start | bytes 1179656 | tf_op jit(solution)/shard_map/ppermute | solution.py:679
  49.9 21.5 %collective-permute-start.22 = (f32[6,128,128]{2,1,0:T(8,128)S(1)}, f32[6,128,128]{2,1,0:T(8,128)S(1)}, u32[]{:S(2)}, u32[]{:S(2)}) collective-permute-start(f32[6,128,128]{2,1,0:T(8,128)S(1)} %get-tuple-element.74), channel_id=1, source_target_pairs={{0,1},{1,0},{2,3},{3,2},{4,5},{5,4},{6,7},{7,6},{8,9},{9,8},{10,11... | collective-permute-start | bytes 1179656 | tf_op jit(solution)/shard_map/ppermute | solution.py:682
  52.1 19.3 %collective-permute-start.24 = (s16[1168,128]{1,0:T(8,128)(2,1)S(1)}, s16[1168,128]{1,0:T(8,128)(2,1)S(1)}, u32[]{:S(2)}, u32[]{:S(2)}) collective-permute-start(s16[1168,128]{1,0:T(8,128)(2,1)S(1)} %pack_sums.3), channel_id=1, source_target_pairs={{0,2},{1,3},{2,0},{3,1},{4,6},{5,7},{6,4},{7,5},{8,10},{9,11},{10,... | collective-permute-start | bytes 897032 | tf_op jit(solution)/shard_map/ppermute | solution.py:680
  66.8 8.4 %collective-permute-start.16 = (s16[1168,128]{1,0:T(8,128)(2,1)S(1)}, s16[1168,128]{1,0:T(8,128)(2,1)S(1)}, u32[]{:S(2)}, u32[]{:S(2)}) collective-permute-start(s16[1168,128]{1,0:T(8,128)(2,1)S(1)} %pack_sums.2), channel_id=1, source_target_pairs={{0,2},{1,3},{2,0},{3,1},{4,6},{5,7},{6,4},{7,5},{8,10},{9,11},{10,... | collective-permute-start | bytes 897032 | tf_op jit(solution)/shard_map/ppermute | solution.py:680
  67.4 4.0 %copy-start = (f32[1,4,1,128,512]{4,3,2,1,0:T(8,128)S(1)}, f32[1,4,1,128,512]{4,3,2,1,0:T(8,128)}, u32[]{:S(2)}) copy-start(f32[1,4,1,128,512]{4,3,2,1,0:T(8,128)} %param.9) | copy-start | bytes 3145732

commit v7 on v6

--- a/solution.py
+++ b/solution.py
@@ -38,19 +38,26 @@
     return [pl.BlockSpec(memory_space=space)] * count
 
 
-def pack_kernel(cb, direct, row_map, anc_order, panel_hbm, anc_hbm, *refs):
-    leaves = anc_order.shape[0]
-    block_count, desc_count = row_map.shape
+def pack_kernel(cb, direct, map_hbm, order_hbm, panel_hbm, anc_hbm, *refs):
+    leaves = order_hbm.shape[0]
+    block_count, desc_count = map_hbm.shape
     rows = panel_hbm.shape[1] // block_count
     tail_rows = (block_count - 1) * rows
     count = leaves if direct else 1
     heads, tails = refs[:count], refs[count:2 * count]
-    strip, inverse, used, chosen, codes, panel, panel_sem, strip_sem = refs[2 * count:]
+    strip, inverse, used, chosen, codes, row_map, anc_order, panel, sems = refs[2 * count:]
     me = lax.axis_index("leaf")
-    panel_copy = pltpu.make_async_copy(panel_hbm, panel, panel_sem)
-    panel_copy.start()
-    strip_copy = pltpu.make_async_copy(anc_hbm.at[0], strip, strip_sem)
-    strip_copy.start()
+    copies = [
+        pltpu.make_async_copy(source, target, sems.at[at])
+        for at, (source, target) in enumerate((
+            (map_hbm, row_map), (order_hbm, anc_order),
+            (panel_hbm, panel), (anc_hbm.at[0], strip),
+        ))
+    ]
+    for copy in copies:
+        copy.start()
+    copies[0].wait()
+    copies[1].wait()
 
     def clear(leaf):
         inverse[anc_order[leaf]] = leaf
@@ -75,7 +82,7 @@
             codes[place * CODES + r] = row_map[r, desc] - leaves * cb
 
     repeat(desc_count, assign)
-    panel_copy.wait()
+    copies[2].wait()
 
     def write(index):
         leaf = jnp.bitwise_xor(me, index) if direct else index
@@ -92,7 +99,7 @@
             tail[pl.ds(slot * tail_rows, tail_rows)] = panel[desc, pl.ds(rows, tail_rows)]
 
     repeat(leaves, write)
-    strip_copy.wait()
+    copies[3].wait()
 
 
 def pack(desc_panel, row_map, anc_order, anc, cb, direct):
@@ -117,16 +124,17 @@
         name="pack",
         compiler_params=limit(12 if direct else 40),
         out_shape=outs,
-        in_specs=spaces(2, pltpu.SMEM) + spaces(2, pl.ANY),
+        in_specs=spaces(4, pl.ANY),
         out_specs=spaces(len(outs), pltpu.VMEM),
         scratch_shapes=[
             pltpu.SMEM((leaves,), jnp.int32),
             pltpu.SMEM((leaves,), jnp.int32),
             pltpu.SMEM((leaves * SLOTS,), jnp.int32),
             pltpu.SMEM((leaves * SLOTS * CODES,), jnp.int32),
+            pltpu.SMEM(row_map.T.shape, jnp.int32),
+            pltpu.SMEM(anc_order.shape, jnp.int32),
             pltpu.VMEM(desc_panel.shape, dtype),
-            pltpu.SemaphoreType.DMA(()),
-            pltpu.SemaphoreType.DMA(()),
+            pltpu.SemaphoreType.DMA((4,)),
         ],
     )(
         *(
@@ -137,8 +145,8 @@
 
 
 def diagonal_kernel(cb, leaves, anc_below, *refs):
-    heads = refs[:-4]
-    out, codes, left, right = refs[-4:]
+    heads = refs[:-6]
+    out, codes_out, left, right, codes, code_sem = refs[-6:]
     direct = len(heads) > 1
     rows = out.shape[1]
     group = min(leaves, 8)
@@ -180,9 +188,13 @@
             lax.rem(lane, CODES) == 0, codes[pl.ds(first, size)], found
         )
 
+    code_copy = pltpu.make_async_copy(codes, codes_out, code_sem)
     if leaves == group:
-        out[...] = step(0).reshape(out.shape)
+        product = step(0)
         locate(0, group)
+        code_copy.start()
+        out[...] = product.reshape(out.shape)
+        code_copy.wait()
     else:
         out[...] = jnp.zeros_like(out)
 
@@ -193,6 +205,8 @@
             return carry
 
         lax.fori_loop(0, leaves // group, accumulate, 0)
+        code_copy.start()
+        code_copy.wait()
 
 
 def diagonal_update(heads, anc_below, cb, leaves, rows):
@@ -207,13 +221,15 @@
         compiler_params=limit(12 if len(heads) > 1 else 40),
         out_shape=[
             pltpu.VMEM((cb * rows, rows), jnp.float32),
-            jax.ShapeDtypeStruct((leaves, rows), jnp.int32),
+            pltpu.SMEM((leaves, rows), jnp.int32),
         ],
         in_specs=spaces(1, pltpu.SMEM) + spaces(len(heads), pltpu.VMEM),
-        out_specs=spaces(2, pltpu.VMEM),
+        out_specs=spaces(1, pltpu.VMEM) + spaces(1, pltpu.SMEM),
         scratch_shapes=[
             pltpu.VMEM((cb * rows, group * SLOTS * rows), heads[0].dtype),
             pltpu.VMEM((rows, group * SLOTS * rows), heads[0].dtype),
+            pltpu.VMEM((leaves, rows), jnp.int32),
+            pltpu.SemaphoreType.DMA(()),
         ],
         cost_estimate=pl.CostEstimate(flops=2000000000, bytes_accessed=1000000, transcendentals=0),
     )(anc_below, *(near_core(*heads) if len(heads) > 1 else heads))
@@ -288,7 +304,7 @@
             pltpu.VMEM((group * SLOTS, tails[0].shape[-2] // SLOTS, rows), jnp.float32),
         ],
         cost_estimate=pl.CostEstimate(flops=2000000000, bytes_accessed=4000000, transcendentals=0),
-    )(codes, *(near_core(*tails, *heads) if len(heads) > 1 else [*tails, *heads]))
+    )(pltpu.with_memory_space_constraint(codes, pltpu.SMEM), *(near_core(*tails, *heads) if len(heads) > 1 else [*tails, *heads]))
     return dict(zip(parts, results))
 
 

time: 76.7 us -> 75.4 us (0.983)
  Pallas kernels: 27 us -> 25.7 us
    pallas_call x2, Pallas kernels: 2.46 us -> 1.27 us  [below_update(): pl.pallas_call(body, compiler_params=limit(16 if len(heads) > 1 else 56),...]
where the time goes in v7:
time: 75.4 us; the launch traced here: 75.3 us
  Pallas kernels  25.7 us (34%)
  starting transfers between devices  25.7 us (34%)
  waiting for transfers between devices  23.8 us (32%)
    ppermute x14, waiting for transfers between devices, exchange(): received.append(lax.ppermute(arrays[k], 'leaf', swap))  19.8 us
    ppermute x14, starting transfers between devices, exchange(): received.append(lax.ppermute(arrays[k], 'leaf', swap))  19 us
    pallas_call x1, Pallas kernels, first_factor(): pl.pallas_call(body, name='factor_first', compiler_params=limit(12), out_...  8.94 us
    pallas_call x1, Pallas kernels, middle_factor(): pl.pallas_call(body, name='factor_middle', compiler_params=limit(8), out_...  3.99 us
    pallas_call x1, Pallas kernels, last_factor(): pl.pallas_call(body, name='factor_last', compiler_params=limit(8), out_sh...  3.98 us
    ppermute x1, waiting for transfers between devices, shards(): folded = lax.ppermute(folded, 'blk', far)  2.63 us
    pallas_call x1, Pallas kernels, solve_left(): pl.pallas_call(body, name='solve_left', compiler_params=limit(16), out_sh...  2.41 us
    ppermute x2, starting transfers between devices, shards(): from_far.append(lax.ppermute(pack_sums(for_far[half], passed), 'blk', far))  2.09 us
  transfers between devices with their start and end apart: 25, of which 9 were waited for; matrix products, arithmetic and copies ran while one was open for 0% of the time, Pallas kernels for 31%

profile of v7, /device:TPU:8, one launch (start us, length us, event | category | flops | bytes accessed | tf_op | source)
XLA Modules:
  0.0 75.3 jit_solution(5498457910526706339)
XLA Ops:
  0.0 1.3 %pack.1 = (bf16[264,128]{1,0:T(8,128)(2,1)S(1)}, bf16[264,128]{1,0:T(8,128)(2,1)S(1)}, bf16[264,128]{1,0:T(8,128)(2,1)S(1)}, bf16[264,128]{1,0:T(8,128)(2,1)S(1)...) custom-call(s32[3,8]{1,0:T(4,128)} %bitcast.8, ...), custom_call_target="tpu_custom_call" | custom-call | tf_op jit(solution)/shard_map/pack/pallas_call | solution.py:122
  1.3 1.6 %collective-permute-start = (bf16[264,128]{1,0:T(8,128)(2,1)S(1)}, bf16[264,128]{1,0:T(8,128)(2,1)S(1)}, u32[]{:S(2)}, u32[]{:S(2)}) collective-permute-start(bf16[264,128]{1,0:T(8,128)(2,1)S(1)} %get-tuple-element.44), channel_id=1, source_target_pairs={{0,4},{4,0},{8,12},{12,8},{16,20},{20,16},{24,28},{28,24},{1,5},{5... | collective-permute-start | bytes 202760 | tf_op jit(solution)/shard_map/ppermute | solution.py:667
  3.3 1.5 %collective-permute-start.2 = (bf16[264,128]{1,0:T(8,128)(2,1)S(1)}, bf16[264,128]{1,0:T(8,128)(2,1)S(1)}, u32[]{:S(2)}, u32[]{:S(2)}) collective-permute-start(bf16[264,128]{1,0:T(8,128)(2,1)S(1)} %get-tuple-element.46), channel_id=1, source_target_pairs={{0,12},{4,8},{8,4},{12,0},{16,28},{20,24},{24,20},{28,16},{1,13},{... | collective-permute-start | bytes 202760 | tf_op jit(solution)/shard_map/ppermute | solution.py:667
  4.9 2.6 %collective-permute-start.3 = (bf16[264,128]{1,0:T(8,128)(2,1)S(1)}, bf16[264,128]{1,0:T(8,128)(2,1)S(1)}, u32[]{:S(2)}, u32[]{:S(2)}) collective-permute-start(bf16[264,128]{1,0:T(8,128)(2,1)S(1)} %get-tuple-element.47), channel_id=1, source_target_pairs={{0,16},{4,20},{8,24},{12,28},{16,0},{20,4},{24,8},{28,12},{1,17},{... | collective-permute-start | bytes 202760 | tf_op jit(solution)/shard_map/ppermute | solution.py:667
  7.4 1.5 %collective-permute-start.7 = (bf16[512,128]{1,0:T(8,128)(2,1)S(1)}, bf16[512,128]{1,0:T(8,128)(2,1)S(1)}, u32[]{:S(2)}, u32[]{:S(2)}) collective-permute-start(bf16[512,128]{1,0:T(8,128)(2,1)S(1)} %get-tuple-element.53), channel_id=1, source_target_pairs={{0,4},{4,0},{8,12},{12,8},{16,20},{20,16},{24,28},{28,24},{1,5},{5... | collective-permute-start | bytes 393224 | tf_op jit(solution)/shard_map/ppermute | solution.py:667
  9.4 0.7 collective-permute-start.4
  10.1 2.3 %collective-permute-start.5 = (bf16[264,128]{1,0:T(8,128)(2,1)S(1)}, bf16[264,128]{1,0:T(8,128)(2,1)S(1)}, u32[]{:S(2)}, u32[]{:S(2)}) collective-permute-start(bf16[264,128]{1,0:T(8,128)(2,1)S(1)} %get-tuple-element.49), channel_id=1, source_target_pairs={{0,24},{4,28},{8,16},{12,20},{16,8},{20,12},{24,0},{28,4},{1,25},{... | collective-permute-start | bytes 202760 | tf_op jit(solution)/shard_map/ppermute | solution.py:667
  12.4 1.0 %collective-permute-start.6 = (bf16[264,128]{1,0:T(8,128)(2,1)S(1)}, bf16[264,128]{1,0:T(8,128)(2,1)S(1)}, u32[]{:S(2)}, u32[]{:S(2)}) collective-permute-start(bf16[264,128]{1,0:T(8,128)(2,1)S(1)} %get-tuple-element.50), channel_id=1, source_target_pairs={{0,28},{4,24},{8,20},{12,16},{16,12},{20,8},{24,4},{28,0},{1,29},{... | collective-permute-start | bytes 202760 | tf_op jit(solution)/shard_map/ppermute | solution.py:667
  13.4 3.4 %collective-permute-done.4.refs_6_.refs_14_ = bf16[264,128]{1,0:T(8,128)(2,1)S(1)} collective-permute-done((bf16[264,128]{1,0:T(8,128)(2,1)S(1)}, bf16[264,128]{1,0:T(8,128)(2,1)S(1)}, u32[]{:S(2)}, u32[]{:S(2)}) %collective-permute-start.4) | collective-permute-done | bytes 67616 | tf_op jit(solution)/shard_map/ppermute | solution.py:667
  16.8 3.8 %collective-permute-start.9 = (bf16[512,128]{1,0:T(8,128)(2,1)S(1)}, bf16[512,128]{1,0:T(8,128)(2,1)S(1)}, u32[]{:S(2)}, u32[]{:S(2)}) collective-permute-start(bf16[512,128]{1,0:T(8,128)(2,1)S(1)} %get-tuple-element.55), channel_id=1, source_target_pairs={{0,12},{4,8},{8,4},{12,0},{16,28},{20,24},{24,20},{28,16},{1,13},{... | collective-permute-start | bytes 393224 | tf_op jit(solution)/shard_map/ppermute | solution.py:667
  20.6 0.6 collective-permute-done.5.refs_7_.refs_15_
  21.2 2.8 %collective-permute-done.6.refs_8_.refs_16_ = bf16[264,128]{1,0:T(8,128)(2,1)S(1)} collective-permute-done((bf16[264,128]{1,0:T(8,128)(2,1)S(1)}, bf16[264,128]{1,0:T(8,128)(2,1)S(1)}, u32[]{:S(2)}, u32[]{:S(2)}) %collective-permute-start.6) | collective-permute-done | bytes 67616 | tf_op jit(solution)/shard_map/ppermute | solution.py:667
  24.4 2.6 %collective-permute-start.13 = (bf16[512,128]{1,0:T(8,128)(2,1)S(1)}, bf16[512,128]{1,0:T(8,128)(2,1)S(1)}, u32[]{:S(2)}, u32[]{:S(2)}) collective-permute-start(bf16[512,128]{1,0:T(8,128)(2,1)S(1)} %get-tuple-element.59), channel_id=1, source_target_pairs={{0,28},{4,24},{8,20},{12,16},{16,12},{20,8},{24,4},{28,0},{1,29},{... | collective-permute-start | bytes 393224 | tf_op jit(solution)/shard_map/ppermute | solution.py:667
  27.1 1.9 %diagonal.1 = (f32[512,128]{1,0:T(8,128)S(1)}, s32[8,128]{1,0:T(8,128)S(4)}) custom-call(s32[8,12]{1,0:T(8,128)S(1)} %copy-done.1, bf16[264,128]{1,0:T(8,128)(2,1)S(1)} %get-tuple-element.43.refs_1_.refs_9_, bf16[264,128]{1,0:T(8,128)(2,1)S(1)} %collective-permute-done.refs_2_.refs_10_, bf16[264,128]{1,0:T(8,128)(2,1)S(1)} %collective-permute-done.1.refs_3_.refs_11_, ...), custom_call_target="tpu_custom_call" | custom-call | flops 2000000000 | bytes 1000000 | tf_op jit(solution)/shard_map/diagonal/pallas_call | solution.py:218
  29.0 1.6 %collective-permute-start.20 = (f32[128,512]{1,0:T(8,128)S(1)}, f32[128,512]{1,0:T(8,128)S(1)}, u32[]{:S(2)}, u32[]{:S(2)}) collective-permute-start(f32[128,512]{1,0:T(8,128)S(1)} %get-tuple-element.67.refs_0_), channel_id=1, source_target_pairs={{0,2},{1,3},{2,0},{3,1},{4,6},{5,7},{6,4},{7,5},{8,10},{9,11},{10,... | collective-permute-start | bytes 786440 | tf_op jit(solution)/shard_map/ppermute | solution.py:672
  30.6 3.9 %collective-permute-done.10.refs_5_ = bf16[512,128]{1,0:T(8,128)(2,1)S(1)} collective-permute-done((bf16[512,128]{1,0:T(8,128)(2,1)S(1)}, bf16[512,128]{1,0:T(8,128)(2,1)S(1)}, u32[]{:S(2)}, u32[]{:S(2)}) %collective-permute-start.10) | collective-permute-done | bytes 131104 | tf_op jit(solution)/shard_map/ppermute | solution.py:667
  34.5 2.8 %collective-permute-done.11.refs_6_ = bf16[512,128]{1,0:T(8,128)(2,1)S(1)} collective-permute-done((bf16[512,128]{1,0:T(8,128)(2,1)S(1)}, bf16[512,128]{1,0:T(8,128)(2,1)S(1)}, u32[]{:S(2)}, u32[]{:S(2)}) %collective-permute-start.11) | collective-permute-done | bytes 131104 | tf_op jit(solution)/shard_map/ppermute | solution.py:667
  37.3 3.8 %collective-permute-done.12.refs_7_ = bf16[512,128]{1,0:T(8,128)(2,1)S(1)} collective-permute-done((bf16[512,128]{1,0:T(8,128)(2,1)S(1)}, bf16[512,128]{1,0:T(8,128)(2,1)S(1)}, u32[]{:S(2)}, u32[]{:S(2)}) %collective-permute-start.12) | collective-permute-done | bytes 131104 | tf_op jit(solution)/shard_map/ppermute | solution.py:667
  41.1 2.5 %collective-permute-done.13.refs_8_ = bf16[512,128]{1,0:T(8,128)(2,1)S(1)} collective-permute-done((bf16[512,128]{1,0:T(8,128)(2,1)S(1)}, bf16[512,128]{1,0:T(8,128)(2,1)S(1)}, u32[]{:S(2)}, u32[]{:S(2)}) %collective-permute-start.13) | collective-permute-done | bytes 131104 | tf_op jit(solution)/shard_map/ppermute | solution.py:667
  43.6 0.5 shard_map.56
  44.2 0.5 collective-permute-start.19
  44.8 1.6 %collective-permute-start.18 = (f32[264,128]{1,0:T(8,128)S(1)}, f32[264,128]{1,0:T(8,128)S(1)}, u32[]{:S(2)}, u32[]{:S(2)}) collective-permute-start(f32[264,128]{1,0:T(8,128)S(1)} %get-tuple-element.66), channel_id=1, source_target_pairs={{0,2},{1,3},{2,0},{3,1},{4,6},{5,7},{6,4},{7,5},{8,10},{9,11},{10,... | collective-permute-start | bytes 405512 | tf_op jit(solution)/shard_map/ppermute | solution.py:680
  46.4 0.7 shard_map.55
  48.2 2.6 %collective-permute-done.18.other_ref = f32[264,128]{1,0:T(8,128)S(1)} collective-permute-done((f32[264,128]{1,0:T(8,128)S(1)}, f32[264,128]{1,0:T(8,128)S(1)}, u32[]{:S(2)}, u32[]{:S(2)}) %collective-permute-start.18) | collective-permute-done | bytes 135200 | tf_op jit(solution)/shard_map/ppermute | solution.py:680
  50.8 1.5 %collective-permute-start.24 = (s16[1168,128]{1,0:T(8,128)(2,1)S(1)}, s16[1168,128]{1,0:T(8,128)(2,1)S(1)}, u32[]{:S(2)}, u32[]{:S(2)}) collective-permute-start(s16[1168,128]{1,0:T(8,128)(2,1)S(1)} %pack_sums.3), channel_id=1, source_target_pairs={{0,2},{1,3},{2,0},{3,1},{4,6},{5,7},{6,4},{7,5},{8,10},{9,11},{10,... | collective-permute-start | bytes 897032 | tf_op jit(solution)/shard_map/ppermute | solution.py:696
  52.4 8.9 %factor_first.1 = (f32[4,128,512]{2,1,0:T(8,128)S(1)}, f32[256,256]{1,0:T(8,128)S(1)}) custom-call(f32[512,128]{1,0:T(8,128)S(1)} %get-tuple-element.65.own_ref, f32[264,128]{1,0:T(8,128)S(1)} %collective-permute-done.18.other_ref, f32[128,512]{1,0:T(8,128)S(1)} %get-tuple-element.67.refs_0_, f32[128,512]{1,0:T(8,128)S(1)} %collective-permute-done.19.refs_1_, ...), custom_call_target="tpu_custom_call" | custom-call | flops 10000000000 | bytes 2000000 | tf_op jit(solution)/shard_map/factor_first/pallas_call | solution.py:457
  61.3 4.0 %factor_middle.1 = (f32[128,256]{1,0:T(8,128)S(1)}, f32[128,128]{1,0:T(8,128)S(1)}, f32[128,128]{1,0:T(8,128)S(1)}) custom-call(f32[4,128,512]{2,1,0:T(8,128)S(1)} %get-tuple-element.68.schur_ref.refs_4_), custom_call_target="tpu_custom_call" | custom-call | flops 5000000000 | bytes 1000000 | tf_op jit(solution)/shard_map/factor_middle/pallas_call | solution.py:486
  65.5 0.6 collective-permute-start.16
  66.1 4.0 %factor_last.1 = (f32[256,256]{1,0:T(8,128)S(1)}, f32[128,512]{1,0:T(8,128)S(1)}) custom-call(f32[4,128,512]{2,1,0:T(8,128)S(1)} %get-tuple-element.68.schur_ref.refs_4_, f32[128,256]{1,0:T(8,128)S(1)} %get-tuple-element.69.strip_ref, f32[128,128]{1,0:T(8,128)S(1)} %get-tuple-element.70.corner_ref, f32[128,128]{1,0:T(8,128)S(1)} %get-tuple-element.71.inverse_ref), custom_call_target="tpu_custom_call" | custom-call | flops 5000000000 | bytes 1000000 | tf_op jit(solution)/shard_map/factor_last/pallas_call | solution.py:515
  70.1 2.4 %solve_left.1 = (f32[4,128,512]{2,1,0:T(8,128)}, f32[384,256]{1,0:T(8,128)S(1)}) custom-call(f32[4,128,512]{2,1,0:T(8,128)S(1)} %bitcast.6, f32[6,128,128]{2,1,0:T(8,128)S(1)} %get-tuple-element.73.refs_0_, f32[6,128,128]{2,1,0:T(8,128)S(1)} %collective-permute-done.22.refs_1_, s16[1168,128]{1,0:T(8,128)(2,1)S(1)} %collective-permute-done.24.refs_2_, ...), custom_call_target="tpu_custom_call" | custom-call | flops 2000000000 | bytes 5000000 | tf_op jit(solution)/shard_map/solve_left/pallas_call | solution.py:601
  72.6 1.3 %collective-permute-done.16.refs_2_ = s16[1168,128]{1,0:T(8,128)(2,1)S(1)} collective-permute-done((s16[1168,128]{1,0:T(8,128)(2,1)S(1)}, s16[1168,128]{1,0:T(8,128)(2,1)S(1)}, u32[]{:S(2)}, u32[]{:S(2)}) %collective-permute-start.16) | collective-permute-done | bytes 299040 | tf_op jit(solution)/shard_map/ppermute | solution.py:696
  73.9 1.4 %solve_right.1 = f32[4,128,512]{2,1,0:T(8,128)} custom-call(f32[4,128,512]{2,1,0:T(8,128)S(1)} %bitcast.7, f32[6,128,128]{2,1,0:T(8,128)S(1)} %get-tuple-element.60.refs_0_, f32[6,128,128]{2,1,0:T(8,128)S(1)} %collective-permute-done.14.refs_1_, s16[1168,128]{1,0:T(8,128)(2,1)S(1)} %collective-permute-done.16.refs_2_, ...), custom_call_target="tpu_custom_call", output_to_operand_aliasing={{}: (6, {})} | custom-call | flops 2000000000 | bytes 5000000 | tf_op jit(solution)/shard_map/solve_right/pallas_call | solution.py:631
  (34 shorter events, 2.8 us)
Async XLA Ops:
  1.3 7.6 %collective-permute-start = (bf16[264,128]{1,0:T(8,128)(2,1)S(1)}, bf16[264,128]{1,0:T(8,128)(2,1)S(1)}, u32[]{:S(2)}, u32[]{:S(2)}) collective-permute-start(bf16[264,128]{1,0:T(8,128)(2,1)S(1)} %get-tuple-element.44), channel_id=1, source_target_pairs={{0,4},{4,0},{8,12},{12,8},{16,20},{20,16},{24,28},{28,24},{1,5},{5... | collective-permute-start | bytes 202760 | tf_op jit(solution)/shard_map/ppermute | solution.py:667
  2.9 6.5 %collective-permute-start.1 = (bf16[264,128]{1,0:T(8,128)(2,1)S(1)}, bf16[264,128]{1,0:T(8,128)(2,1)S(1)}, u32[]{:S(2)}, u32[]{:S(2)}) collective-permute-start(bf16[264,128]{1,0:T(8,128)(2,1)S(1)} %get-tuple-element.45), channel_id=1, source_target_pairs={{0,8},{4,12},{8,0},{12,4},{16,24},{20,28},{24,16},{28,20},{1,9},{5... | collective-permute-start | bytes 202760 | tf_op jit(solution)/shard_map/ppermute | solution.py:667
  3.3 6.8 %collective-permute-start.2 = (bf16[264,128]{1,0:T(8,128)(2,1)S(1)}, bf16[264,128]{1,0:T(8,128)(2,1)S(1)}, u32[]{:S(2)}, u32[]{:S(2)}) collective-permute-start(bf16[264,128]{1,0:T(8,128)(2,1)S(1)} %get-tuple-element.46), channel_id=1, source_target_pairs={{0,12},{4,8},{8,4},{12,0},{16,28},{20,24},{24,20},{28,16},{1,13},{... | collective-permute-start | bytes 202760 | tf_op jit(solution)/shard_map/ppermute | solution.py:667
  4.9 7.6 %collective-permute-start.3 = (bf16[264,128]{1,0:T(8,128)(2,1)S(1)}, bf16[264,128]{1,0:T(8,128)(2,1)S(1)}, u32[]{:S(2)}, u32[]{:S(2)}) collective-permute-start(bf16[264,128]{1,0:T(8,128)(2,1)S(1)} %get-tuple-element.47), channel_id=1, source_target_pairs={{0,16},{4,20},{8,24},{12,28},{16,0},{20,4},{24,8},{28,12},{1,17},{... | collective-permute-start | bytes 202760 | tf_op jit(solution)/shard_map/ppermute | solution.py:667
  7.4 16.5 %collective-permute-start.7 = (bf16[512,128]{1,0:T(8,128)(2,1)S(1)}, bf16[512,128]{1,0:T(8,128)(2,1)S(1)}, u32[]{:S(2)}, u32[]{:S(2)}) collective-permute-start(bf16[512,128]{1,0:T(8,128)(2,1)S(1)} %get-tuple-element.53), channel_id=1, source_target_pairs={{0,4},{4,0},{8,12},{12,8},{16,20},{20,16},{24,28},{28,24},{1,5},{5... | collective-permute-start | bytes 393224 | tf_op jit(solution)/shard_map/ppermute | solution.py:667
  8.9 15.5 %collective-permute-start.8 = (bf16[512,128]{1,0:T(8,128)(2,1)S(1)}, bf16[512,128]{1,0:T(8,128)(2,1)S(1)}, u32[]{:S(2)}, u32[]{:S(2)}) collective-permute-start(bf16[512,128]{1,0:T(8,128)(2,1)S(1)} %get-tuple-element.54), channel_id=1, source_target_pairs={{0,8},{4,12},{8,0},{12,4},{16,24},{20,28},{24,16},{28,20},{1,9},{5... | collective-permute-start | bytes 393224 | tf_op jit(solution)/shard_map/ppermute | solution.py:667
  9.4 7.4 %collective-permute-start.4 = (bf16[264,128]{1,0:T(8,128)(2,1)S(1)}, bf16[264,128]{1,0:T(8,128)(2,1)S(1)}, u32[]{:S(2)}, u32[]{:S(2)}) collective-permute-start(bf16[264,128]{1,0:T(8,128)(2,1)S(1)} %get-tuple-element.48), channel_id=1, source_target_pairs={{0,20},{4,16},{8,28},{12,24},{16,4},{20,0},{24,12},{28,8},{1,21},{... | collective-permute-start | bytes 202760 | tf_op jit(solution)/shard_map/ppermute | solution.py:667
  10.1 11.1 %collective-permute-start.5 = (bf16[264,128]{1,0:T(8,128)(2,1)S(1)}, bf16[264,128]{1,0:T(8,128)(2,1)S(1)}, u32[]{:S(2)}, u32[]{:S(2)}) collective-permute-start(bf16[264,128]{1,0:T(8,128)(2,1)S(1)} %get-tuple-element.49), channel_id=1, source_target_pairs={{0,24},{4,28},{8,16},{12,20},{16,8},{20,12},{24,0},{28,4},{1,25},{... | collective-permute-start | bytes 202760 | tf_op jit(solution)/shard_map/ppermute | solution.py:667
  12.4 11.6 %collective-permute-start.6 = (bf16[264,128]{1,0:T(8,128)(2,1)S(1)}, bf16[264,128]{1,0:T(8,128)(2,1)S(1)}, u32[]{:S(2)}, u32[]{:S(2)}) collective-permute-start(bf16[264,128]{1,0:T(8,128)(2,1)S(1)} %get-tuple-element.50), channel_id=1, source_target_pairs={{0,28},{4,24},{8,20},{12,16},{16,12},{20,8},{24,4},{28,0},{1,29},{... | collective-permute-start | bytes 202760 | tf_op jit(solution)/shard_map/ppermute | solution.py:667
  16.8 12.2 %collective-permute-start.9 = (bf16[512,128]{1,0:T(8,128)(2,1)S(1)}, bf16[512,128]{1,0:T(8,128)(2,1)S(1)}, u32[]{:S(2)}, u32[]{:S(2)}) collective-permute-start(bf16[512,128]{1,0:T(8,128)(2,1)S(1)} %get-tuple-element.55), channel_id=1, source_target_pairs={{0,12},{4,8},{8,4},{12,0},{16,28},{20,24},{24,20},{28,16},{1,13},{... | collective-permute-start | bytes 393224 | tf_op jit(solution)/shard_map/ppermute | solution.py:667
  21.2 5.9 %copy-start.1 = (s32[8,12]{1,0:T(8,128)S(1)}, s32[8,12]{1,0:T(8,128)}, u32[]{:S(2)}) copy-start(s32[8,12]{1,0:T(8,128)} %refs_0_.1) | copy-start | bytes 1156
  21.2 13.3 %collective-permute-start.10 = (bf16[512,128]{1,0:T(8,128)(2,1)S(1)}, bf16[512,128]{1,0:T(8,128)(2,1)S(1)}, u32[]{:S(2)}, u32[]{:S(2)}) collective-permute-start(bf16[512,128]{1,0:T(8,128)(2,1)S(1)} %get-tuple-element.56), channel_id=1, source_target_pairs={{0,16},{4,20},{8,24},{12,28},{16,0},{20,4},{24,8},{28,12},{1,17},{... | collective-permute-start | bytes 393224 | tf_op jit(solution)/shard_map/ppermute | solution.py:667
  24.0 13.3 %collective-permute-start.11 = (bf16[512,128]{1,0:T(8,128)(2,1)S(1)}, bf16[512,128]{1,0:T(8,128)(2,1)S(1)}, u32[]{:S(2)}, u32[]{:S(2)}) collective-permute-start(bf16[512,128]{1,0:T(8,128)(2,1)S(1)} %get-tuple-element.57), channel_id=1, source_target_pairs={{0,20},{4,16},{8,28},{12,24},{16,4},{20,0},{24,12},{28,8},{1,21},{... | collective-permute-start | bytes 393224 | tf_op jit(solution)/shard_map/ppermute | solution.py:667
  24.0 17.1 %collective-permute-start.12 = (bf16[512,128]{1,0:T(8,128)(2,1)S(1)}, bf16[512,128]{1,0:T(8,128)(2,1)S(1)}, u32[]{:S(2)}, u32[]{:S(2)}) collective-permute-start(bf16[512,128]{1,0:T(8,128)(2,1)S(1)} %get-tuple-element.58), channel_id=1, source_target_pairs={{0,24},{4,28},{8,16},{12,20},{16,8},{20,12},{24,0},{28,4},{1,25},{... | collective-permute-start | bytes 393224 | tf_op jit(solution)/shard_map/ppermute | solution.py:667
  24.4 19.2 %collective-permute-start.13 = (bf16[512,128]{1,0:T(8,128)(2,1)S(1)}, bf16[512,128]{1,0:T(8,128)(2,1)S(1)}, u32[]{:S(2)}, u32[]{:S(2)}) collective-permute-start(bf16[512,128]{1,0:T(8,128)(2,1)S(1)} %get-tuple-element.59), channel_id=1, source_target_pairs={{0,28},{4,24},{8,20},{12,16},{16,12},{20,8},{24,4},{28,0},{1,29},{... | collective-permute-start | bytes 393224 | tf_op jit(solution)/shard_map/ppermute | solution.py:667
  29.0 15.7 %collective-permute-start.20 = (f32[128,512]{1,0:T(8,128)S(1)}, f32[128,512]{1,0:T(8,128)S(1)}, u32[]{:S(2)}, u32[]{:S(2)}) collective-permute-start(f32[128,512]{1,0:T(8,128)S(1)} %get-tuple-element.67.refs_0_), channel_id=1, source_target_pairs={{0,2},{1,3},{2,0},{3,1},{4,6},{5,7},{6,4},{7,5},{8,10},{9,11},{10,... | collective-permute-start | bytes 786440 | tf_op jit(solution)/shard_map/ppermute | solution.py:672
  34.5 10.3 %collective-permute-start.17 = (f32[512,128]{1,0:T(8,128)S(1)}, f32[512,128]{1,0:T(8,128)S(1)}, u32[]{:S(2)}, u32[]{:S(2)}) collective-permute-start(f32[512,128]{1,0:T(8,128)S(1)} %get-tuple-element.64.first_ref), channel_id=1, source_target_pairs={{0,1},{1,0},{2,3},{3,2},{4,5},{5,4},{6,7},{7,6},{8,9},{9,8},{10,11... | collective-permute-start | bytes 786440 | tf_op jit(solution)/shard_map/ppermute | solution.py:678
  44.1 3.3 %collective-permute-start.23 = (f32[6,128,128]{2,1,0:T(8,128)S(1)}, f32[6,128,128]{2,1,0:T(8,128)S(1)}, u32[]{:S(2)}, u32[]{:S(2)}) collective-permute-start(f32[6,128,128]{2,1,0:T(8,128)S(1)} %get-tuple-element.76), channel_id=1, source_target_pairs={{0,1},{1,0},{2,3},{3,2},{4,5},{5,4},{6,7},{7,6},{8,9},{9,8},{10,11... | collective-permute-start | bytes 1179656 | tf_op jit(solution)/shard_map/ppermute | solution.py:695
  44.2 3.8 %collective-permute-start.19 = (f32[128,512]{1,0:T(8,128)S(1)}, f32[128,512]{1,0:T(8,128)S(1)}, u32[]{:S(2)}, u32[]{:S(2)}) collective-permute-start(f32[128,512]{1,0:T(8,128)S(1)} %get-tuple-element.67.refs_0_), channel_id=1, source_target_pairs={{0,1},{1,0},{2,3},{3,2},{4,5},{5,4},{6,7},{7,6},{8,9},{9,8},{10,11... | collective-permute-start | bytes 786440 | tf_op jit(solution)/shard_map/ppermute | solution.py:673
  44.7 7.6 %collective-permute-start.21 = (f32[128,512]{1,0:T(8,128)S(1)}, f32[128,512]{1,0:T(8,128)S(1)}, u32[]{:S(2)}, u32[]{:S(2)}) collective-permute-start(f32[128,512]{1,0:T(8,128)S(1)} %collective-permute-done.20.refs_2_), channel_id=1, source_target_pairs={{0,1},{1,0},{2,3},{3,2},{4,5},{5,4},{6,7},{7,6},{8,9},{9,8},{10,11... | collective-permute-start | bytes 786440 | tf_op jit(solution)/shard_map/ppermute | solution.py:674
  44.8 6.0 %collective-permute-start.18 = (f32[264,128]{1,0:T(8,128)S(1)}, f32[264,128]{1,0:T(8,128)S(1)}, u32[]{:S(2)}, u32[]{:S(2)}) collective-permute-start(f32[264,128]{1,0:T(8,128)S(1)} %get-tuple-element.66), channel_id=1, source_target_pairs={{0,2},{1,3},{2,0},{3,1},{4,6},{5,7},{6,4},{7,5},{8,10},{9,11},{10,... | collective-permute-start | bytes 405512 | tf_op jit(solution)/shard_map/ppermute | solution.py:680
  47.2 25.4 %collective-permute-start.14 = (f32[6,128,128]{2,1,0:T(8,128)S(1)}, f32[6,128,128]{2,1,0:T(8,128)S(1)}, u32[]{:S(2)}, u32[]{:S(2)}) collective-permute-start(f32[6,128,128]{2,1,0:T(8,128)S(1)} %get-tuple-element.61), channel_id=1, source_target_pairs={{0,1},{1,0},{2,3},{3,2},{4,5},{5,4},{6,7},{7,6},{8,9},{9,8},{10,11... | collective-permute-start | bytes 1179656 | tf_op jit(solution)/shard_map/ppermute | solution.py:698
  47.4 17.9 %collective-permute-start.15 = (f32[6,128,128]{2,1,0:T(8,128)S(1)}, f32[6,128,128]{2,1,0:T(8,128)S(1)}, u32[]{:S(2)}, u32[]{:S(2)}) collective-permute-start(f32[6,128,128]{2,1,0:T(8,128)S(1)} %get-tuple-element.63), channel_id=1, source_target_pairs={{0,1},{1,0},{2,3},{3,2},{4,5},{5,4},{6,7},{7,6},{8,9},{9,8},{10,11... | collective-permute-start | bytes 1179656 | tf_op jit(solution)/shard_map/ppermute | solution.py:695
  48.0 22.1 %collective-permute-start.22 = (f32[6,128,128]{2,1,0:T(8,128)S(1)}, f32[6,128,128]{2,1,0:T(8,128)S(1)}, u32[]{:S(2)}, u32[]{:S(2)}) collective-permute-start(f32[6,128,128]{2,1,0:T(8,128)S(1)} %get-tuple-element.74), channel_id=1, source_target_pairs={{0,1},{1,0},{2,3},{3,2},{4,5},{5,4},{6,7},{7,6},{8,9},{9,8},{10,11... | collective-permute-start | bytes 1179656 | tf_op jit(solution)/shard_map/ppermute | solution.py:698
  50.8 19.3 %collective-permute-start.24 = (s16[1168,128]{1,0:T(8,128)(2,1)S(1)}, s16[1168,128]{1,0:T(8,128)(2,1)S(1)}, u32[]{:S(2)}, u32[]{:S(2)}) collective-permute-start(s16[1168,128]{1,0:T(8,128)(2,1)S(1)} %pack_sums.3), channel_id=1, source_target_pairs={{0,2},{1,3},{2,0},{3,1},{4,6},{5,7},{6,4},{7,5},{8,10},{9,11},{10,... | collective-permute-start | bytes 897032 | tf_op jit(solution)/shard_map/ppermute | solution.py:696
  65.5 8.4 %collective-permute-start.16 = (s16[1168,128]{1,0:T(8,128)(2,1)S(1)}, s16[1168,128]{1,0:T(8,128)(2,1)S(1)}, u32[]{:S(2)}, u32[]{:S(2)}) collective-permute-start(s16[1168,128]{1,0:T(8,128)(2,1)S(1)} %pack_sums.2), channel_id=1, source_target_pairs={{0,2},{1,3},{2,0},{3,1},{4,6},{5,7},{6,4},{7,5},{8,10},{9,11},{10,... | collective-permute-start | bytes 897032 | tf_op jit(solution)/shard_map/ppermute | solution.py:696
  66.1 4.0 %copy-start = (f32[1,4,1,128,512]{4,3,2,1,0:T(8,128)S(1)}, f32[1,4,1,128,512]{4,3,2,1,0:T(8,128)}, u32[]{:S(2)}) copy-start(f32[1,4,1,128,512]{4,3,2,1,0:T(8,128)} %param.9) | copy-start | bytes 3145732

commit v8 on v7

--- a/solution.py
+++ b/solution.py
@@ -12,7 +12,9 @@
 PANEL = 8
 HALVES = 2
 SCALE_ROWS = 16
-BITS = 23.0
+BITS = 20.0
+LOW_BITS = 5
+LOWS = 3
 LOG2E = 1.4426950408889634
 DIRECT = 8
 HIGHEST = lax.Precision.HIGHEST
@@ -529,7 +531,8 @@
 
 def pack_sums(first, second):
     count, rows, width = first.shape
-    pairs = count // 2
+    groups = -(-count // LOWS)
+    base = 2**LOW_BITS
 
     def body(first_ref, second_ref, out):
         row = lax.broadcasted_iota(jnp.int32, (SCALE_ROWS, width), 0)
@@ -541,34 +544,36 @@
             power = jnp.floor(jnp.log(peak) * LOG2E + 1e-3) + 1.0
             scales = jnp.where(row == j, power.astype(jnp.int32), scales)
             whole = jnp.floor(value * jnp.exp2(BITS - power) + 0.5).astype(jnp.int32)
-            high = lax.shift_right_arithmetic(whole, 8)
-            lows.append(whole - high * 256)
+            high = lax.shift_right_arithmetic(whole, LOW_BITS)
+            lows.append(whole - high * base)
             out[j * rows:(j + 1) * rows] = high.astype(jnp.int16)
-        for j in range(pairs):
-            low = lows[j] + lows[j + pairs] * 256 - 32768
-            out[(count + j) * rows:(count + j + 1) * rows] = low.astype(jnp.int16)
-        out[(count + pairs) * rows:] = scales.astype(jnp.int16)
+        for group in range(groups):
+            low = jnp.zeros((rows, width), jnp.int32)
+            for j in reversed(range(group, count, groups)):
+                low = low * base + lows[j]
+            out[(count + group) * rows:(count + group + 1) * rows] = low.astype(jnp.int16)
+        out[(count + groups) * rows:] = scales.astype(jnp.int16)
 
     return pl.pallas_call(
         body,
         name="pack_sums",
         compiler_params=limit(8),
-        out_shape=pltpu.VMEM(((count + pairs) * rows + SCALE_ROWS, width), jnp.int16),
+        out_shape=pltpu.VMEM(((count + groups) * rows + SCALE_ROWS, width), jnp.int16),
         in_specs=spaces(2, pltpu.VMEM),
         out_specs=pl.BlockSpec(memory_space=pltpu.VMEM),
     )(*near_core(first, second))
 
 
 def unpack_sums(ref, index, count, rows):
-    pairs = count // 2
+    groups = -(-count // LOWS)
+    base = 2**LOW_BITS
     high = ref[index * rows:(index + 1) * rows].astype(jnp.int32)
-    at = (count + index % pairs) * rows
-    low = ref[at:at + rows].astype(jnp.int32) + 32768
-    upper = lax.shift_right_logical(low, 8)
-    low = upper if index >= pairs else low - upper * 256
-    scales = ref[(count + pairs) * rows:].astype(jnp.float32)
+    at = (count + index % groups) * rows
+    low = ref[at:at + rows].astype(jnp.int32)
+    low = lax.shift_right_logical(low, LOW_BITS * (index // groups)) & (base - 1)
+    scales = ref[(count + groups) * rows:].astype(jnp.float32)
     scale = jnp.exp2(scales[index:index + 1] - BITS)
-    return (high * 256 + low).astype(jnp.float32) * scale
+    return (high * base + low).astype(jnp.float32) * scale
 
 
 def remaining(panel_ref, update_refs, half, cb, per, rows):

time: 75.4 us -> 74.7 us (level)
  no operation moved by 1% of the time
where the time goes in v8:
time: 74.7 us; the launch traced here: 74.6 us
  Pallas kernels  25.7 us (34%)
  starting transfers between devices  25.7 us (34%)
  waiting for transfers between devices  23.1 us (31%)
    ppermute x14, waiting for transfers between devices, exchange(): received.append(lax.ppermute(arrays[k], 'leaf', swap))  19.8 us
    ppermute x14, starting transfers between devices, exchange(): received.append(lax.ppermute(arrays[k], 'leaf', swap))  19 us
    pallas_call x1, Pallas kernels, first_factor(): pl.pallas_call(body, name='factor_first', compiler_params=limit(12), out_...  8.93 us
    pallas_call x1, Pallas kernels, middle_factor(): pl.pallas_call(body, name='factor_middle', compiler_params=limit(8), out_...  3.99 us
    pallas_call x1, Pallas kernels, last_factor(): pl.pallas_call(body, name='factor_last', compiler_params=limit(8), out_sh...  3.98 us
    ppermute x1, waiting for transfers between devices, shards(): folded = lax.ppermute(folded, 'blk', far)  2.63 us
    pallas_call x1, Pallas kernels, solve_left(): pl.pallas_call(body, name='solve_left', compiler_params=limit(16), out_sh...  2.41 us
    ppermute x2, starting transfers between devices, shards(): from_far.append(lax.ppermute(pack_sums(for_far[half], passed), 'blk', far))  2.09 us
  transfers between devices with their start and end apart: 25, of which 9 were waited for; matrix products, arithmetic and copies ran while one was open for 0% of the time, Pallas kernels for 31%

profile of v8, /device:TPU:8, one launch (start us, length us, event | category | flops | bytes accessed | tf_op | source)
XLA Modules:
  0.0 74.6 jit_solution(3897858722555002686)
XLA Ops:
  0.0 1.3 %pack.1 = (bf16[264,128]{1,0:T(8,128)(2,1)S(1)}, bf16[264,128]{1,0:T(8,128)(2,1)S(1)}, bf16[264,128]{1,0:T(8,128)(2,1)S(1)}, bf16[264,128]{1,0:T(8,128)(2,1)S(1)...) custom-call(s32[3,8]{1,0:T(4,128)} %bitcast.8, ...), custom_call_target="tpu_custom_call" | custom-call | tf_op jit(solution)/shard_map/pack/pallas_call | solution.py:124
  1.3 1.6 %collective-permute-start = (bf16[264,128]{1,0:T(8,128)(2,1)S(1)}, bf16[264,128]{1,0:T(8,128)(2,1)S(1)}, u32[]{:S(2)}, u32[]{:S(2)}) collective-permute-start(bf16[264,128]{1,0:T(8,128)(2,1)S(1)} %get-tuple-element.44), channel_id=1, source_target_pairs={{0,4},{4,0},{8,12},{12,8},{16,20},{20,16},{24,28},{28,24},{1,5},{5... | collective-permute-start | bytes 202760 | tf_op jit(solution)/shard_map/ppermute | solution.py:672
  3.3 1.5 %collective-permute-start.2 = (bf16[264,128]{1,0:T(8,128)(2,1)S(1)}, bf16[264,128]{1,0:T(8,128)(2,1)S(1)}, u32[]{:S(2)}, u32[]{:S(2)}) collective-permute-start(bf16[264,128]{1,0:T(8,128)(2,1)S(1)} %get-tuple-element.46), channel_id=1, source_target_pairs={{0,12},{4,8},{8,4},{12,0},{16,28},{20,24},{24,20},{28,16},{1,13},{... | collective-permute-start | bytes 202760 | tf_op jit(solution)/shard_map/ppermute | solution.py:672
  4.9 2.6 %collective-permute-start.3 = (bf16[264,128]{1,0:T(8,128)(2,1)S(1)}, bf16[264,128]{1,0:T(8,128)(2,1)S(1)}, u32[]{:S(2)}, u32[]{:S(2)}) collective-permute-start(bf16[264,128]{1,0:T(8,128)(2,1)S(1)} %get-tuple-element.47), channel_id=1, source_target_pairs={{0,16},{4,20},{8,24},{12,28},{16,0},{20,4},{24,8},{28,12},{1,17},{... | collective-permute-start | bytes 202760 | tf_op jit(solution)/shard_map/ppermute | solution.py:672
  7.4 1.5 %collective-permute-start.7 = (bf16[512,128]{1,0:T(8,128)(2,1)S(1)}, bf16[512,128]{1,0:T(8,128)(2,1)S(1)}, u32[]{:S(2)}, u32[]{:S(2)}) collective-permute-start(bf16[512,128]{1,0:T(8,128)(2,1)S(1)} %get-tuple-element.53), channel_id=1, source_target_pairs={{0,4},{4,0},{8,12},{12,8},{16,20},{20,16},{24,28},{28,24},{1,5},{5... | collective-permute-start | bytes 393224 | tf_op jit(solution)/shard_map/ppermute | solution.py:672
  9.4 0.7 collective-permute-start.4
  10.1 2.3 %collective-permute-start.5 = (bf16[264,128]{1,0:T(8,128)(2,1)S(1)}, bf16[264,128]{1,0:T(8,128)(2,1)S(1)}, u32[]{:S(2)}, u32[]{:S(2)}) collective-permute-start(bf16[264,128]{1,0:T(8,128)(2,1)S(1)} %get-tuple-element.49), channel_id=1, source_target_pairs={{0,24},{4,28},{8,16},{12,20},{16,8},{20,12},{24,0},{28,4},{1,25},{... | collective-permute-start | bytes 202760 | tf_op jit(solution)/shard_map/ppermute | solution.py:672
  12.4 1.0 %collective-permute-start.6 = (bf16[264,128]{1,0:T(8,128)(2,1)S(1)}, bf16[264,128]{1,0:T(8,128)(2,1)S(1)}, u32[]{:S(2)}, u32[]{:S(2)}) collective-permute-start(bf16[264,128]{1,0:T(8,128)(2,1)S(1)} %get-tuple-element.50), channel_id=1, source_target_pairs={{0,28},{4,24},{8,20},{12,16},{16,12},{20,8},{24,4},{28,0},{1,29},{... | collective-permute-start | bytes 202760 | tf_op jit(solution)/shard_map/ppermute | solution.py:672
  13.4 3.4 %collective-permute-done.4.refs_6_.refs_14_ = bf16[264,128]{1,0:T(8,128)(2,1)S(1)} collective-permute-done((bf16[264,128]{1,0:T(8,128)(2,1)S(1)}, bf16[264,128]{1,0:T(8,128)(2,1)S(1)}, u32[]{:S(2)}, u32[]{:S(2)}) %collective-permute-start.4) | collective-permute-done | bytes 67616 | tf_op jit(solution)/shard_map/ppermute | solution.py:672
  16.8 3.8 %collective-permute-start.9 = (bf16[512,128]{1,0:T(8,128)(2,1)S(1)}, bf16[512,128]{1,0:T(8,128)(2,1)S(1)}, u32[]{:S(2)}, u32[]{:S(2)}) collective-permute-start(bf16[512,128]{1,0:T(8,128)(2,1)S(1)} %get-tuple-element.55), channel_id=1, source_target_pairs={{0,12},{4,8},{8,4},{12,0},{16,28},{20,24},{24,20},{28,16},{1,13},{... | collective-permute-start | bytes 393224 | tf_op jit(solution)/shard_map/ppermute | solution.py:672
  20.6 0.6 collective-permute-done.5.refs_7_.refs_15_
  21.2 2.8 %collective-permute-done.6.refs_8_.refs_16_ = bf16[264,128]{1,0:T(8,128)(2,1)S(1)} collective-permute-done((bf16[264,128]{1,0:T(8,128)(2,1)S(1)}, bf16[264,128]{1,0:T(8,128)(2,1)S(1)}, u32[]{:S(2)}, u32[]{:S(2)}) %collective-permute-start.6) | collective-permute-done | bytes 67616 | tf_op jit(solution)/shard_map/ppermute | solution.py:672
  24.4 2.6 %collective-permute-start.13 = (bf16[512,128]{1,0:T(8,128)(2,1)S(1)}, bf16[512,128]{1,0:T(8,128)(2,1)S(1)}, u32[]{:S(2)}, u32[]{:S(2)}) collective-permute-start(bf16[512,128]{1,0:T(8,128)(2,1)S(1)} %get-tuple-element.59), channel_id=1, source_target_pairs={{0,28},{4,24},{8,20},{12,16},{16,12},{20,8},{24,4},{28,0},{1,29},{... | collective-permute-start | bytes 393224 | tf_op jit(solution)/shard_map/ppermute | solution.py:672
  27.1 1.9 %diagonal.1 = (f32[512,128]{1,0:T(8,128)S(1)}, s32[8,128]{1,0:T(8,128)S(4)}) custom-call(s32[8,12]{1,0:T(8,128)S(1)} %copy-done.1, bf16[264,128]{1,0:T(8,128)(2,1)S(1)} %get-tuple-element.43.refs_1_.refs_9_, bf16[264,128]{1,0:T(8,128)(2,1)S(1)} %collective-permute-done.refs_2_.refs_10_, bf16[264,128]{1,0:T(8,128)(2,1)S(1)} %collective-permute-done.1.refs_3_.refs_11_, ...), custom_call_target="tpu_custom_call" | custom-call | flops 2000000000 | bytes 1000000 | tf_op jit(solution)/shard_map/diagonal/pallas_call | solution.py:220
  29.0 1.6 %collective-permute-start.20 = (f32[128,512]{1,0:T(8,128)S(1)}, f32[128,512]{1,0:T(8,128)S(1)}, u32[]{:S(2)}, u32[]{:S(2)}) collective-permute-start(f32[128,512]{1,0:T(8,128)S(1)} %get-tuple-element.67.refs_0_), channel_id=1, source_target_pairs={{0,2},{1,3},{2,0},{3,1},{4,6},{5,7},{6,4},{7,5},{8,10},{9,11},{10,... | collective-permute-start | bytes 786440 | tf_op jit(solution)/shard_map/ppermute | solution.py:677
  30.6 3.9 %collective-permute-done.10.refs_5_ = bf16[512,128]{1,0:T(8,128)(2,1)S(1)} collective-permute-done((bf16[512,128]{1,0:T(8,128)(2,1)S(1)}, bf16[512,128]{1,0:T(8,128)(2,1)S(1)}, u32[]{:S(2)}, u32[]{:S(2)}) %collective-permute-start.10) | collective-permute-done | bytes 131104 | tf_op jit(solution)/shard_map/ppermute | solution.py:672
  34.5 2.8 %collective-permute-done.11.refs_6_ = bf16[512,128]{1,0:T(8,128)(2,1)S(1)} collective-permute-done((bf16[512,128]{1,0:T(8,128)(2,1)S(1)}, bf16[512,128]{1,0:T(8,128)(2,1)S(1)}, u32[]{:S(2)}, u32[]{:S(2)}) %collective-permute-start.11) | collective-permute-done | bytes 131104 | tf_op jit(solution)/shard_map/ppermute | solution.py:672
  37.3 3.8 %collective-permute-done.12.refs_7_ = bf16[512,128]{1,0:T(8,128)(2,1)S(1)} collective-permute-done((bf16[512,128]{1,0:T(8,128)(2,1)S(1)}, bf16[512,128]{1,0:T(8,128)(2,1)S(1)}, u32[]{:S(2)}, u32[]{:S(2)}) %collective-permute-start.12) | collective-permute-done | bytes 131104 | tf_op jit(solution)/shard_map/ppermute | solution.py:672
  41.1 2.5 %collective-permute-done.13.refs_8_ = bf16[512,128]{1,0:T(8,128)(2,1)S(1)} collective-permute-done((bf16[512,128]{1,0:T(8,128)(2,1)S(1)}, bf16[512,128]{1,0:T(8,128)(2,1)S(1)}, u32[]{:S(2)}, u32[]{:S(2)}) %collective-permute-start.13) | collective-permute-done | bytes 131104 | tf_op jit(solution)/shard_map/ppermute | solution.py:672
  43.6 0.5 shard_map.56
  44.2 0.5 collective-permute-start.19
  44.9 1.6 %collective-permute-start.18 = (f32[264,128]{1,0:T(8,128)S(1)}, f32[264,128]{1,0:T(8,128)S(1)}, u32[]{:S(2)}, u32[]{:S(2)}) collective-permute-start(f32[264,128]{1,0:T(8,128)S(1)} %get-tuple-element.66), channel_id=1, source_target_pairs={{0,2},{1,3},{2,0},{3,1},{4,6},{5,7},{6,4},{7,5},{8,10},{9,11},{10,... | collective-permute-start | bytes 405512 | tf_op jit(solution)/shard_map/ppermute | solution.py:685
  46.4 0.7 shard_map.55
  48.2 2.6 %collective-permute-done.18.other_ref = f32[264,128]{1,0:T(8,128)S(1)} collective-permute-done((f32[264,128]{1,0:T(8,128)S(1)}, f32[264,128]{1,0:T(8,128)S(1)}, u32[]{:S(2)}, u32[]{:S(2)}) %collective-permute-start.18) | collective-permute-done | bytes 135200 | tf_op jit(solution)/shard_map/ppermute | solution.py:685
  50.8 1.5 %collective-permute-start.24 = (s16[1040,128]{1,0:T(8,128)(2,1)S(1)}, s16[1040,128]{1,0:T(8,128)(2,1)S(1)}, u32[]{:S(2)}, u32[]{:S(2)}) collective-permute-start(s16[1040,128]{1,0:T(8,128)(2,1)S(1)} %pack_sums.3), channel_id=1, source_target_pairs={{0,2},{1,3},{2,0},{3,1},{4,6},{5,7},{6,4},{7,5},{8,10},{9,11},{10,... | collective-permute-start | bytes 798728 | tf_op jit(solution)/shard_map/ppermute | solution.py:701
  52.4 8.9 %factor_first.1 = (f32[4,128,512]{2,1,0:T(8,128)S(1)}, f32[256,256]{1,0:T(8,128)S(1)}) custom-call(f32[512,128]{1,0:T(8,128)S(1)} %get-tuple-element.65.own_ref, f32[264,128]{1,0:T(8,128)S(1)} %collective-permute-done.18.other_ref, f32[128,512]{1,0:T(8,128)S(1)} %get-tuple-element.67.refs_0_, f32[128,512]{1,0:T(8,128)S(1)} %collective-permute-done.19.refs_1_, ...), custom_call_target="tpu_custom_call" | custom-call | flops 10000000000 | bytes 2000000 | tf_op jit(solution)/shard_map/factor_first/pallas_call | solution.py:459
  61.3 4.0 %factor_middle.1 = (f32[128,256]{1,0:T(8,128)S(1)}, f32[128,128]{1,0:T(8,128)S(1)}, f32[128,128]{1,0:T(8,128)S(1)}) custom-call(f32[4,128,512]{2,1,0:T(8,128)S(1)} %get-tuple-element.68.schur_ref.refs_4_), custom_call_target="tpu_custom_call" | custom-call | flops 5000000000 | bytes 1000000 | tf_op jit(solution)/shard_map/factor_middle/pallas_call | solution.py:488
  65.5 0.6 collective-permute-start.16
  66.1 4.0 %factor_last.1 = (f32[256,256]{1,0:T(8,128)S(1)}, f32[128,512]{1,0:T(8,128)S(1)}) custom-call(f32[4,128,512]{2,1,0:T(8,128)S(1)} %get-tuple-element.68.schur_ref.refs_4_, f32[128,256]{1,0:T(8,128)S(1)} %get-tuple-element.69.strip_ref, f32[128,128]{1,0:T(8,128)S(1)} %get-tuple-element.70.corner_ref, f32[128,128]{1,0:T(8,128)S(1)} %get-tuple-element.71.inverse_ref), custom_call_target="tpu_custom_call" | custom-call | flops 5000000000 | bytes 1000000 | tf_op jit(solution)/shard_map/factor_last/pallas_call | solution.py:517
  70.1 2.4 %solve_left.1 = (f32[4,128,512]{2,1,0:T(8,128)}, f32[384,256]{1,0:T(8,128)S(1)}) custom-call(f32[4,128,512]{2,1,0:T(8,128)S(1)} %bitcast.6, f32[6,128,128]{2,1,0:T(8,128)S(1)} %get-tuple-element.73.refs_0_, f32[6,128,128]{2,1,0:T(8,128)S(1)} %collective-permute-done.22.refs_1_, s16[1040,128]{1,0:T(8,128)(2,1)S(1)} %collective-permute-done.24.refs_2_, ...), custom_call_target="tpu_custom_call" | custom-call | flops 2000000000 | bytes 5000000 | tf_op jit(solution)/shard_map/solve_left/pallas_call | solution.py:606
  72.5 0.6 collective-permute-done.16.refs_2_
  73.2 1.4 %solve_right.1 = f32[4,128,512]{2,1,0:T(8,128)} custom-call(f32[4,128,512]{2,1,0:T(8,128)S(1)} %bitcast.7, f32[6,128,128]{2,1,0:T(8,128)S(1)} %get-tuple-element.60.refs_0_, f32[6,128,128]{2,1,0:T(8,128)S(1)} %collective-permute-done.14.refs_1_, s16[1040,128]{1,0:T(8,128)(2,1)S(1)} %collective-permute-done.16.refs_2_, ...), custom_call_target="tpu_custom_call", output_to_operand_aliasing={{}: (6, {})} | custom-call | flops 2000000000 | bytes 5000000 | tf_op jit(solution)/shard_map/solve_right/pallas_call | solution.py:636
  (34 shorter events, 2.8 us)
Async XLA Ops:
  1.3 7.6 %collective-permute-start = (bf16[264,128]{1,0:T(8,128)(2,1)S(1)}, bf16[264,128]{1,0:T(8,128)(2,1)S(1)}, u32[]{:S(2)}, u32[]{:S(2)}) collective-permute-start(bf16[264,128]{1,0:T(8,128)(2,1)S(1)} %get-tuple-element.44), channel_id=1, source_target_pairs={{0,4},{4,0},{8,12},{12,8},{16,20},{20,16},{24,28},{28,24},{1,5},{5... | collective-permute-start | bytes 202760 | tf_op jit(solution)/shard_map/ppermute | solution.py:672
  2.9 6.5 %collective-permute-start.1 = (bf16[264,128]{1,0:T(8,128)(2,1)S(1)}, bf16[264,128]{1,0:T(8,128)(2,1)S(1)}, u32[]{:S(2)}, u32[]{:S(2)}) collective-permute-start(bf16[264,128]{1,0:T(8,128)(2,1)S(1)} %get-tuple-element.45), channel_id=1, source_target_pairs={{0,8},{4,12},{8,0},{12,4},{16,24},{20,28},{24,16},{28,20},{1,9},{5... | collective-permute-start | bytes 202760 | tf_op jit(solution)/shard_map/ppermute | solution.py:672
  3.3 6.8 %collective-permute-start.2 = (bf16[264,128]{1,0:T(8,128)(2,1)S(1)}, bf16[264,128]{1,0:T(8,128)(2,1)S(1)}, u32[]{:S(2)}, u32[]{:S(2)}) collective-permute-start(bf16[264,128]{1,0:T(8,128)(2,1)S(1)} %get-tuple-element.46), channel_id=1, source_target_pairs={{0,12},{4,8},{8,4},{12,0},{16,28},{20,24},{24,20},{28,16},{1,13},{... | collective-permute-start | bytes 202760 | tf_op jit(solution)/shard_map/ppermute | solution.py:672
  4.9 7.6 %collective-permute-start.3 = (bf16[264,128]{1,0:T(8,128)(2,1)S(1)}, bf16[264,128]{1,0:T(8,128)(2,1)S(1)}, u32[]{:S(2)}, u32[]{:S(2)}) collective-permute-start(bf16[264,128]{1,0:T(8,128)(2,1)S(1)} %get-tuple-element.47), channel_id=1, source_target_pairs={{0,16},{4,20},{8,24},{12,28},{16,0},{20,4},{24,8},{28,12},{1,17},{... | collective-permute-start | bytes 202760 | tf_op jit(solution)/shard_map/ppermute | solution.py:672
  7.4 16.5 %collective-permute-start.7 = (bf16[512,128]{1,0:T(8,128)(2,1)S(1)}, bf16[512,128]{1,0:T(8,128)(2,1)S(1)}, u32[]{:S(2)}, u32[]{:S(2)}) collective-permute-start(bf16[512,128]{1,0:T(8,128)(2,1)S(1)} %get-tuple-element.53), channel_id=1, source_target_pairs={{0,4},{4,0},{8,12},{12,8},{16,20},{20,16},{24,28},{28,24},{1,5},{5... | collective-permute-start | bytes 393224 | tf_op jit(solution)/shard_map/ppermute | solution.py:672
  8.9 15.5 %collective-permute-start.8 = (bf16[512,128]{1,0:T(8,128)(2,1)S(1)}, bf16[512,128]{1,0:T(8,128)(2,1)S(1)}, u32[]{:S(2)}, u32[]{:S(2)}) collective-permute-start(bf16[512,128]{1,0:T(8,128)(2,1)S(1)} %get-tuple-element.54), channel_id=1, source_target_pairs={{0,8},{4,12},{8,0},{12,4},{16,24},{20,28},{24,16},{28,20},{1,9},{5... | collective-permute-start | bytes 393224 | tf_op jit(solution)/shard_map/ppermute | solution.py:672
  9.4 7.4 %collective-permute-start.4 = (bf16[264,128]{1,0:T(8,128)(2,1)S(1)}, bf16[264,128]{1,0:T(8,128)(2,1)S(1)}, u32[]{:S(2)}, u32[]{:S(2)}) collective-permute-start(bf16[264,128]{1,0:T(8,128)(2,1)S(1)} %get-tuple-element.48), channel_id=1, source_target_pairs={{0,20},{4,16},{8,28},{12,24},{16,4},{20,0},{24,12},{28,8},{1,21},{... | collective-permute-start | bytes 202760 | tf_op jit(solution)/shard_map/ppermute | solution.py:672
  10.1 11.1 %collective-permute-start.5 = (bf16[264,128]{1,0:T(8,128)(2,1)S(1)}, bf16[264,128]{1,0:T(8,128)(2,1)S(1)}, u32[]{:S(2)}, u32[]{:S(2)}) collective-permute-start(bf16[264,128]{1,0:T(8,128)(2,1)S(1)} %get-tuple-element.49), channel_id=1, source_target_pairs={{0,24},{4,28},{8,16},{12,20},{16,8},{20,12},{24,0},{28,4},{1,25},{... | collective-permute-start | bytes 202760 | tf_op jit(solution)/shard_map/ppermute | solution.py:672
  12.4 11.6 %collective-permute-start.6 = (bf16[264,128]{1,0:T(8,128)(2,1)S(1)}, bf16[264,128]{1,0:T(8,128)(2,1)S(1)}, u32[]{:S(2)}, u32[]{:S(2)}) collective-permute-start(bf16[264,128]{1,0:T(8,128)(2,1)S(1)} %get-tuple-element.50), channel_id=1, source_target_pairs={{0,28},{4,24},{8,20},{12,16},{16,12},{20,8},{24,4},{28,0},{1,29},{... | collective-permute-start | bytes 202760 | tf_op jit(solution)/shard_map/ppermute | solution.py:672
  16.8 12.2 %collective-permute-start.9 = (bf16[512,128]{1,0:T(8,128)(2,1)S(1)}, bf16[512,128]{1,0:T(8,128)(2,1)S(1)}, u32[]{:S(2)}, u32[]{:S(2)}) collective-permute-start(bf16[512,128]{1,0:T(8,128)(2,1)S(1)} %get-tuple-element.55), channel_id=1, source_target_pairs={{0,12},{4,8},{8,4},{12,0},{16,28},{20,24},{24,20},{28,16},{1,13},{... | collective-permute-start | bytes 393224 | tf_op jit(solution)/shard_map/ppermute | solution.py:672
  21.2 5.9 %copy-start.1 = (s32[8,12]{1,0:T(8,128)S(1)}, s32[8,12]{1,0:T(8,128)}, u32[]{:S(2)}) copy-start(s32[8,12]{1,0:T(8,128)} %refs_0_.1) | copy-start | bytes 1156
  21.2 13.3 %collective-permute-start.10 = (bf16[512,128]{1,0:T(8,128)(2,1)S(1)}, bf16[512,128]{1,0:T(8,128)(2,1)S(1)}, u32[]{:S(2)}, u32[]{:S(2)}) collective-permute-start(bf16[512,128]{1,0:T(8,128)(2,1)S(1)} %get-tuple-element.56), channel_id=1, source_target_pairs={{0,16},{4,20},{8,24},{12,28},{16,0},{20,4},{24,8},{28,12},{1,17},{... | collective-permute-start | bytes 393224 | tf_op jit(solution)/shard_map/ppermute | solution.py:672
  24.0 13.3 %collective-permute-start.11 = (bf16[512,128]{1,0:T(8,128)(2,1)S(1)}, bf16[512,128]{1,0:T(8,128)(2,1)S(1)}, u32[]{:S(2)}, u32[]{:S(2)}) collective-permute-start(bf16[512,128]{1,0:T(8,128)(2,1)S(1)} %get-tuple-element.57), channel_id=1, source_target_pairs={{0,20},{4,16},{8,28},{12,24},{16,4},{20,0},{24,12},{28,8},{1,21},{... | collective-permute-start | bytes 393224 | tf_op jit(solution)/shard_map/ppermute | solution.py:672
  24.0 17.1 %collective-permute-start.12 = (bf16[512,128]{1,0:T(8,128)(2,1)S(1)}, bf16[512,128]{1,0:T(8,128)(2,1)S(1)}, u32[]{:S(2)}, u32[]{:S(2)}) collective-permute-start(bf16[512,128]{1,0:T(8,128)(2,1)S(1)} %get-tuple-element.58), channel_id=1, source_target_pairs={{0,24},{4,28},{8,16},{12,20},{16,8},{20,12},{24,0},{28,4},{1,25},{... | collective-permute-start | bytes 393224 | tf_op jit(solution)/shard_map/ppermute | solution.py:672
  24.4 19.2 %collective-permute-start.13 = (bf16[512,128]{1,0:T(8,128)(2,1)S(1)}, bf16[512,128]{1,0:T(8,128)(2,1)S(1)}, u32[]{:S(2)}, u32[]{:S(2)}) collective-permute-start(bf16[512,128]{1,0:T(8,128)(2,1)S(1)} %get-tuple-element.59), channel_id=1, source_target_pairs={{0,28},{4,24},{8,20},{12,16},{16,12},{20,8},{24,4},{28,0},{1,29},{... | collective-permute-start | bytes 393224 | tf_op jit(solution)/shard_map/ppermute | solution.py:672
  29.0 15.7 %collective-permute-start.20 = (f32[128,512]{1,0:T(8,128)S(1)}, f32[128,512]{1,0:T(8,128)S(1)}, u32[]{:S(2)}, u32[]{:S(2)}) collective-permute-start(f32[128,512]{1,0:T(8,128)S(1)} %get-tuple-element.67.refs_0_), channel_id=1, source_target_pairs={{0,2},{1,3},{2,0},{3,1},{4,6},{5,7},{6,4},{7,5},{8,10},{9,11},{10,... | collective-permute-start | bytes 786440 | tf_op jit(solution)/shard_map/ppermute | solution.py:677
  34.5 10.3 %collective-permute-start.17 = (f32[512,128]{1,0:T(8,128)S(1)}, f32[512,128]{1,0:T(8,128)S(1)}, u32[]{:S(2)}, u32[]{:S(2)}) collective-permute-start(f32[512,128]{1,0:T(8,128)S(1)} %get-tuple-element.64.first_ref), channel_id=1, source_target_pairs={{0,1},{1,0},{2,3},{3,2},{4,5},{5,4},{6,7},{7,6},{8,9},{9,8},{10,11... | collective-permute-start | bytes 786440 | tf_op jit(solution)/shard_map/ppermute | solution.py:683
  44.1 3.3 %collective-permute-start.23 = (f32[6,128,128]{2,1,0:T(8,128)S(1)}, f32[6,128,128]{2,1,0:T(8,128)S(1)}, u32[]{:S(2)}, u32[]{:S(2)}) collective-permute-start(f32[6,128,128]{2,1,0:T(8,128)S(1)} %get-tuple-element.76), channel_id=1, source_target_pairs={{0,1},{1,0},{2,3},{3,2},{4,5},{5,4},{6,7},{7,6},{8,9},{9,8},{10,11... | collective-permute-start | bytes 1179656 | tf_op jit(solution)/shard_map/ppermute | solution.py:700
  44.2 3.8 %collective-permute-start.19 = (f32[128,512]{1,0:T(8,128)S(1)}, f32[128,512]{1,0:T(8,128)S(1)}, u32[]{:S(2)}, u32[]{:S(2)}) collective-permute-start(f32[128,512]{1,0:T(8,128)S(1)} %get-tuple-element.67.refs_0_), channel_id=1, source_target_pairs={{0,1},{1,0},{2,3},{3,2},{4,5},{5,4},{6,7},{7,6},{8,9},{9,8},{10,11... | collective-permute-start | bytes 786440 | tf_op jit(solution)/shard_map/ppermute | solution.py:678
  44.7 7.6 %collective-permute-start.21 = (f32[128,512]{1,0:T(8,128)S(1)}, f32[128,512]{1,0:T(8,128)S(1)}, u32[]{:S(2)}, u32[]{:S(2)}) collective-permute-start(f32[128,512]{1,0:T(8,128)S(1)} %collective-permute-done.20.refs_2_), channel_id=1, source_target_pairs={{0,1},{1,0},{2,3},{3,2},{4,5},{5,4},{6,7},{7,6},{8,9},{9,8},{10,11... | collective-permute-start | bytes 786440 | tf_op jit(solution)/shard_map/ppermute | solution.py:679
  44.9 6.0 %collective-permute-start.18 = (f32[264,128]{1,0:T(8,128)S(1)}, f32[264,128]{1,0:T(8,128)S(1)}, u32[]{:S(2)}, u32[]{:S(2)}) collective-permute-start(f32[264,128]{1,0:T(8,128)S(1)} %get-tuple-element.66), channel_id=1, source_target_pairs={{0,2},{1,3},{2,0},{3,1},{4,6},{5,7},{6,4},{7,5},{8,10},{9,11},{10,... | collective-permute-start | bytes 405512 | tf_op jit(solution)/shard_map/ppermute | solution.py:685
  47.2 25.4 %collective-permute-start.14 = (f32[6,128,128]{2,1,0:T(8,128)S(1)}, f32[6,128,128]{2,1,0:T(8,128)S(1)}, u32[]{:S(2)}, u32[]{:S(2)}) collective-permute-start(f32[6,128,128]{2,1,0:T(8,128)S(1)} %get-tuple-element.61), channel_id=1, source_target_pairs={{0,1},{1,0},{2,3},{3,2},{4,5},{5,4},{6,7},{7,6},{8,9},{9,8},{10,11... | collective-permute-start | bytes 1179656 | tf_op jit(solution)/shard_map/ppermute | solution.py:703
  47.4 17.9 %collective-permute-start.15 = (f32[6,128,128]{2,1,0:T(8,128)S(1)}, f32[6,128,128]{2,1,0:T(8,128)S(1)}, u32[]{:S(2)}, u32[]{:S(2)}) collective-permute-start(f32[6,128,128]{2,1,0:T(8,128)S(1)} %get-tuple-element.63), channel_id=1, source_target_pairs={{0,1},{1,0},{2,3},{3,2},{4,5},{5,4},{6,7},{7,6},{8,9},{9,8},{10,11... | collective-permute-start | bytes 1179656 | tf_op jit(solution)/shard_map/ppermute | solution.py:700
  48.0 22.1 %collective-permute-start.22 = (f32[6,128,128]{2,1,0:T(8,128)S(1)}, f32[6,128,128]{2,1,0:T(8,128)S(1)}, u32[]{:S(2)}, u32[]{:S(2)}) collective-permute-start(f32[6,128,128]{2,1,0:T(8,128)S(1)} %get-tuple-element.74), channel_id=1, source_target_pairs={{0,1},{1,0},{2,3},{3,2},{4,5},{5,4},{6,7},{7,6},{8,9},{9,8},{10,11... | collective-permute-start | bytes 1179656 | tf_op jit(solution)/shard_map/ppermute | solution.py:703
  50.8 19.3 %collective-permute-start.24 = (s16[1040,128]{1,0:T(8,128)(2,1)S(1)}, s16[1040,128]{1,0:T(8,128)(2,1)S(1)}, u32[]{:S(2)}, u32[]{:S(2)}) collective-permute-start(s16[1040,128]{1,0:T(8,128)(2,1)S(1)} %pack_sums.3), channel_id=1, source_target_pairs={{0,2},{1,3},{2,0},{3,1},{4,6},{5,7},{6,4},{7,5},{8,10},{9,11},{10,... | collective-permute-start | bytes 798728 | tf_op jit(solution)/shard_map/ppermute | solution.py:701
  65.5 7.7 %collective-permute-start.16 = (s16[1040,128]{1,0:T(8,128)(2,1)S(1)}, s16[1040,128]{1,0:T(8,128)(2,1)S(1)}, u32[]{:S(2)}, u32[]{:S(2)}) collective-permute-start(s16[1040,128]{1,0:T(8,128)(2,1)S(1)} %pack_sums.2), channel_id=1, source_target_pairs={{0,2},{1,3},{2,0},{3,1},{4,6},{5,7},{6,4},{7,5},{8,10},{9,11},{10,... | collective-permute-start | bytes 798728 | tf_op jit(solution)/shard_map/ppermute | solution.py:701
  66.1 4.0 %copy-start = (f32[1,4,1,128,512]{4,3,2,1,0:T(8,128)S(1)}, f32[1,4,1,128,512]{4,3,2,1,0:T(8,128)}, u32[]{:S(2)}) copy-start(f32[1,4,1,128,512]{4,3,2,1,0:T(8,128)} %param.9) | copy-start | bytes 3145732

commit v9 on v8

--- a/solution.py
+++ b/solution.py
@@ -12,9 +12,9 @@
 PANEL = 8
 HALVES = 2
 SCALE_ROWS = 16
-BITS = 20.0
-LOW_BITS = 5
-LOWS = 3
+BITS = 19.0
+LOW_BITS = 4
+LOWS = 4
 LOG2E = 1.4426950408889634
 DIRECT = 8
 HIGHEST = lax.Precision.HIGHEST
@@ -531,7 +531,8 @@
 
 def pack_sums(first, second):
     count, rows, width = first.shape
-    groups = -(-count // LOWS)
+    groups = -(-2 * count // LOWS)
+    part = rows // 2
     base = 2**LOW_BITS
 
     def body(first_ref, second_ref, out):
@@ -545,105 +546,127 @@
             scales = jnp.where(row == j, power.astype(jnp.int32), scales)
             whole = jnp.floor(value * jnp.exp2(BITS - power) + 0.5).astype(jnp.int32)
             high = lax.shift_right_arithmetic(whole, LOW_BITS)
-            lows.append(whole - high * base)
+            low = whole - high * base
+            lows.extend((low[:part], low[part:]))
             out[j * rows:(j + 1) * rows] = high.astype(jnp.int16)
         for group in range(groups):
-            low = jnp.zeros((rows, width), jnp.int32)
-            for j in reversed(range(group, count, groups)):
+            low = jnp.zeros((part, width), jnp.int32)
+            for j in reversed(range(group, 2 * count, groups)):
                 low = low * base + lows[j]
-            out[(count + group) * rows:(count + group + 1) * rows] = low.astype(jnp.int16)
-        out[(count + groups) * rows:] = scales.astype(jnp.int16)
+            at = count * rows + group * part
+            out[at:at + part] = (low - 32768).astype(jnp.int16)
+        out[count * rows + groups * part:] = scales.astype(jnp.int16)
 
     return pl.pallas_call(
         body,
         name="pack_sums",
         compiler_params=limit(8),
-        out_shape=pltpu.VMEM(((count + groups) * rows + SCALE_ROWS, width), jnp.int16),
+        out_shape=pltpu.VMEM((count * rows + groups * part + SCALE_ROWS, width), jnp.int16),
         in_specs=spaces(2, pltpu.VMEM),
         out_specs=pl.BlockSpec(memory_space=pltpu.VMEM),
     )(*near_core(first, second))
 
 
 def unpack_sums(ref, index, count, rows):
-    groups = -(-count // LOWS)
+    groups = -(-2 * count // LOWS)
+    part = rows // 2
     base = 2**LOW_BITS
     high = ref[index * rows:(index + 1) * rows].astype(jnp.int32)
-    at = (count + index % groups) * rows
-    low = ref[at:at + rows].astype(jnp.int32)
-    low = lax.shift_right_logical(low, LOW_BITS * (index // groups)) & (base - 1)
-    scales = ref[(count + groups) * rows:].astype(jnp.float32)
+    lows = []
+    for j in (2 * index, 2 * index + 1):
+        at = count * rows + j % groups * part
+        low = ref[at:at + part].astype(jnp.int32) + 32768
+        lows.append(lax.shift_right_logical(low, LOW_BITS * (j // groups)) & (base - 1))
+    scales = ref[count * rows + groups * part:].astype(jnp.float32)
     scale = jnp.exp2(scales[index:index + 1] - BITS)
-    return (high * base + low).astype(jnp.float32) * scale
-
-
-def remaining(panel_ref, update_refs, half, cb, per, rows):
-    parts = []
-    for c in range(cb // HALVES):
-        column = (half * (cb // HALVES) + c) * rows
-        block = slice(c * per, (c + 1) * per)
-        count = (cb // HALVES) * per
-        coded = [unpack_sums(update_refs[2], index, count, rows)[None] for index in range(c * per, (c + 1) * per)]
-        update = update_refs[0][block] + update_refs[1][block] + jnp.concatenate(coded, axis=0)
-        original = panel_ref[1:, :, column:column + rows]
-        parts.append((original - update).reshape(per * rows, rows))
+    return (high * base + jnp.concatenate(lows, axis=0)).astype(jnp.float32) * scale
+
+
+def original(panel_ref, half, column_blocks, per, rows):
+    first = half * column_blocks
+    parts = [
+        panel_ref[1:, :, (first + c) * rows:(first + c + 1) * rows].reshape(per * rows, rows)
+        for c in range(column_blocks)
+    ]
     return jnp.concatenate(parts, axis=1)
 
 
-def solve_left(panel, updates, lead, schur, lower, cb, per, rows):
+def side_by_side(blocks, per):
+    columns = [
+        jnp.concatenate(blocks[first:first + per], axis=0)
+        for first in range(0, len(blocks), per)
+    ]
+    return jnp.concatenate(columns, axis=1)
+
+
+def local_sums(first_ref, second_ref, per):
+    return side_by_side([first_ref[j] + second_ref[j] for j in range(first_ref.shape[0])], per)
+
+
+def far_sums(ref, count, per, rows):
+    return side_by_side([unpack_sums(ref, j, count, rows) for j in range(count)], per)
+
+
+def solve_left(panel, local, coded, later, lead, schur, cb, per, rows):
     width = cb * rows
     half = width // HALVES
-
-    def body(panel_ref, *refs):
-        updates_ref = refs[:len(updates)]
-        lead_ref, schur_ref, lower_ref, out, carried = refs[len(updates):]
-        left = remaining(panel_ref, updates_ref, 0, cb, per, rows)
-        out[0] = lower_ref[...]
+    columns = cb // HALVES
+
+    def body(panel_ref, kept, near, far, kept_later, near_later, lead_ref, schur_ref, solved,
+             carried):
+        left = original(panel_ref, 0, columns, per, rows) - local_sums(kept, near, per)
+        left = left - far_sums(far, columns * per, per, rows)
         value = small_dot(left, lead_ref[...], ((1,), (1,)))
-        out[1:, :, :half] = value.reshape(per, rows, half)
-        across = schur_ref[:cb // HALVES, :, half:].reshape(half, half)
-        carried[...] = small_dot(value, across, ((1,), (0,)))
+        solved[...] = value.reshape(per, rows, half)
+        across = schur_ref[:columns, :, half:].reshape(half, half)
+        right = original(panel_ref, 1, columns, per, rows)
+        right = right - local_sums(kept_later, near_later, per)
+        carried[...] = right - small_dot(value, across, ((1,), (0,)))
 
     return pl.pallas_call(
         body,
         name="solve_left",
         compiler_params=limit(16),
         out_shape=[
-            jax.ShapeDtypeStruct((per + 1, rows, width), jnp.float32),
+            pltpu.VMEM((per, rows, half), jnp.float32),
             pltpu.VMEM((per * rows, half), jnp.float32),
         ],
-        in_specs=spaces(4 + len(updates), pltpu.VMEM),
+        in_specs=spaces(8, pltpu.VMEM),
         out_specs=spaces(2, pltpu.VMEM),
         cost_estimate=pl.CostEstimate(flops=2000000000, bytes_accessed=5000000, transcendentals=0),
-    )(panel, *near_core(*updates, lead, schur, lower))
-
-
-def solve_right(panel, updates, trail, carried, out, cb, per, rows):
+    )(panel, *near_core(*local, coded, *later, lead, schur))
+
+
+def solve_right(coded, trail, carried, solved, lower, cb, per, rows):
     width = cb * rows
     half = width // HALVES
 
-    def body(panel_ref, *refs):
-        updates_ref = refs[:len(updates)]
-        trail_ref, carried_ref, _, result, stage, sem = refs[len(updates):]
-        left = remaining(panel_ref, updates_ref, 1, cb, per, rows) - carried_ref[...]
+    def body(far, trail_ref, carried_ref, solved_ref, lower_ref, result, stage, sems):
+        below = result.at[pl.ds(1, per)]
+        copies = [
+            pltpu.make_async_copy(lower_ref, result.at[0], sems.at[0]),
+            pltpu.make_async_copy(solved_ref, below.at[:, :, pl.ds(0, half)], sems.at[1]),
+            pltpu.make_async_copy(stage, below.at[:, :, pl.ds(half, half)], sems.at[2]),
+        ]
+        copies[0].start()
+        copies[1].start()
+        left = carried_ref[...] - far_sums(far, cb // HALVES * per, per, rows)
         value = small_dot(left, trail_ref[...], ((1,), (1,)))
         stage[...] = value.reshape(per, rows, half)
-        copy = pltpu.make_async_copy(
-            stage, result.at[pl.ds(1, per), :, pl.ds(half, half)], sem
-        )
-        copy.start()
-        copy.wait()
+        copies[2].start()
+        for copy in copies:
+            copy.wait()
 
     return pl.pallas_call(
         body,
         name="solve_right",
         compiler_params=limit(16),
         out_shape=jax.ShapeDtypeStruct((per + 1, rows, width), jnp.float32),
-        in_specs=spaces(3 + len(updates), pltpu.VMEM) + spaces(1, pl.ANY),
+        in_specs=spaces(5, pltpu.VMEM),
         out_specs=pl.BlockSpec(memory_space=pl.ANY),
-        scratch_shapes=[pltpu.VMEM((per, rows, half), jnp.float32), pltpu.SemaphoreType.DMA(())],
-        input_output_aliases={3 + len(updates): 0},
+        scratch_shapes=[pltpu.VMEM((per, rows, half), jnp.float32), pltpu.SemaphoreType.DMA((3,))],
         cost_estimate=pl.CostEstimate(flops=2000000000, bytes_accessed=5000000, transcendentals=0),
-    )(panel, *near_core(*updates, trail, carried), out)
+    )(*near_core(coded, trail, carried, solved, lower))
 
 
 def shards(desc_panel, row_map, anc_order, anc_below, anc_panel):
@@ -703,9 +726,11 @@
         from_near.append(lax.ppermute(for_near[half], "blk", near))
     strip, corner, inverse = middle_factor(schur, cb, rows)
     trail, lower = last_factor(schur, strip, corner, inverse, cb, rows)
-    updates = [[kept[half], from_near[half], from_far[half]] for half in range(HALVES)]
-    out, carried = solve_left(panel, updates[0], lead, schur, lower, cb, per, rows)
-    out = solve_right(panel, updates[1], trail, carried, out, cb, per, rows)
+    local = [[kept[half], from_near[half]] for half in range(HALVES)]
+    solved, carried = solve_left(
+        panel, local[0], from_far[0], local[1], lead, schur, cb, per, rows
+    )
+    out = solve_right(from_far[1], trail, carried, solved, lower, cb, per, rows)
     return out.reshape(anc_panel.shape)
 
 

time: 74.7 us -> 77.3 us (1.035)
  the two profiles are of different devices: /device:TPU:8 before, /device:TPU:0 now
where the time goes in v9:
time: 77.3 us; the launch traced here: 77.1 us
  starting transfers between devices  37.4 us (48%)
  Pallas kernels  24.8 us (32%)
  waiting for transfers between devices  14.7 us (19%)
    ppermute x14, starting transfers between devices, exchange(): received.append(lax.ppermute(arrays[k], 'leaf', swap))  30.8 us
    ppermute x14, waiting for transfers between devices, exchange(): received.append(lax.ppermute(arrays[k], 'leaf', swap))  10.9 us
    pallas_call x1, Pallas kernels, first_factor(): pl.pallas_call(body, name='factor_first', compiler_params=limit(12), out_...  8.93 us
    pallas_call x1, Pallas kernels, middle_factor(): pl.pallas_call(body, name='factor_middle', compiler_params=limit(8), out_...  3.99 us
    pallas_call x1, Pallas kernels, last_factor(): pl.pallas_call(body, name='factor_last', compiler_params=limit(8), out_sh...  3.98 us
    ppermute x1, waiting for transfers between devices, shards(): folded = lax.ppermute(folded, 'blk', far)  2.74 us
    ppermute x2, starting transfers between devices, shards(): from_far.append(lax.ppermute(pack_sums(for_far[half], passed), 'blk', far))  2.09 us
    pallas_call x1, Pallas kernels, diagonal_update(): pl.pallas_call(body, name='diagonal', compiler_params=limit(12 if len(hea...  1.94 us
  transfers between devices with their start and end apart: 25, of which 7 were waited for; matrix products, arithmetic and copies ran while one was open for 0% of the time, Pallas kernels for 29%

profile of v9, /device:TPU:0, one launch (start us, length us, event | category | flops | bytes accessed | tf_op | source)
XLA Modules:
  0.0 77.1 jit_solution(828457191990408948)
XLA Ops:
  0.0 1.3 %pack.1 = (bf16[264,128]{1,0:T(8,128)(2,1)S(1)}, bf16[264,128]{1,0:T(8,128)(2,1)S(1)}, bf16[264,128]{1,0:T(8,128)(2,1)S(1)}, bf16[264,128]{1,0:T(8,128)(2,1)S(1)...) custom-call(s32[3,8]{1,0:T(4,128)} %bitcast.7, ...), custom_call_target="tpu_custom_call" | custom-call | tf_op jit(solution)/shard_map/pack/pallas_call | solution.py:124
  1.3 3.0 %collective-permute-start = (bf16[264,128]{1,0:T(8,128)(2,1)S(1)}, bf16[264,128]{1,0:T(8,128)(2,1)S(1)}, u32[]{:S(2)}, u32[]{:S(2)}) collective-permute-start(bf16[264,128]{1,0:T(8,128)(2,1)S(1)} %get-tuple-element.44), channel_id=1, source_target_pairs={{0,4},{4,0},{8,12},{12,8},{16,20},{20,16},{24,28},{28,24},{1,5},{5... | collective-permute-start | bytes 202760 | tf_op jit(solution)/shard_map/ppermute | solution.py:695
  4.3 1.6 %collective-permute-start.1 = (bf16[264,128]{1,0:T(8,128)(2,1)S(1)}, bf16[264,128]{1,0:T(8,128)(2,1)S(1)}, u32[]{:S(2)}, u32[]{:S(2)}) collective-permute-start(bf16[264,128]{1,0:T(8,128)(2,1)S(1)} %get-tuple-element.45), channel_id=1, source_target_pairs={{0,8},{4,12},{8,0},{12,4},{16,24},{20,28},{24,16},{28,20},{1,9},{5... | collective-permute-start | bytes 202760 | tf_op jit(solution)/shard_map/ppermute | solution.py:695
  5.9 3.0 %collective-permute-start.3 = (bf16[264,128]{1,0:T(8,128)(2,1)S(1)}, bf16[264,128]{1,0:T(8,128)(2,1)S(1)}, u32[]{:S(2)}, u32[]{:S(2)}) collective-permute-start(bf16[264,128]{1,0:T(8,128)(2,1)S(1)} %get-tuple-element.47), channel_id=1, source_target_pairs={{0,16},{4,20},{8,24},{12,28},{16,0},{20,4},{24,8},{28,12},{1,17},{... | collective-permute-start | bytes 202760 | tf_op jit(solution)/shard_map/ppermute | solution.py:695
  8.9 3.8 %collective-permute-start.11 = (bf16[512,128]{1,0:T(8,128)(2,1)S(1)}, bf16[512,128]{1,0:T(8,128)(2,1)S(1)}, u32[]{:S(2)}, u32[]{:S(2)}) collective-permute-start(bf16[512,128]{1,0:T(8,128)(2,1)S(1)} %get-tuple-element.57), channel_id=1, source_target_pairs={{0,20},{4,16},{8,28},{12,24},{16,4},{20,0},{24,12},{28,8},{1,21},{... | collective-permute-start | bytes 393224 | tf_op jit(solution)/shard_map/ppermute | solution.py:695
  12.9 3.8 %collective-permute-start.5 = (bf16[264,128]{1,0:T(8,128)(2,1)S(1)}, bf16[264,128]{1,0:T(8,128)(2,1)S(1)}, u32[]{:S(2)}, u32[]{:S(2)}) collective-permute-start(bf16[264,128]{1,0:T(8,128)(2,1)S(1)} %get-tuple-element.49), channel_id=1, source_target_pairs={{0,24},{4,28},{8,16},{12,20},{16,8},{20,12},{24,0},{28,4},{1,25},{... | collective-permute-start | bytes 202760 | tf_op jit(solution)/shard_map/ppermute | solution.py:695
  16.7 8.2 %collective-permute-start.6 = (bf16[264,128]{1,0:T(8,128)(2,1)S(1)}, bf16[264,128]{1,0:T(8,128)(2,1)S(1)}, u32[]{:S(2)}, u32[]{:S(2)}) collective-permute-start(bf16[264,128]{1,0:T(8,128)(2,1)S(1)} %get-tuple-element.50), channel_id=1, source_target_pairs={{0,28},{4,24},{8,20},{12,16},{16,12},{20,8},{24,4},{28,0},{1,29},{... | collective-permute-start | bytes 202760 | tf_op jit(solution)/shard_map/ppermute | solution.py:695
  24.8 6.5 %collective-permute-done.4.refs_6_.refs_14_ = bf16[264,128]{1,0:T(8,128)(2,1)S(1)} collective-permute-done((bf16[264,128]{1,0:T(8,128)(2,1)S(1)}, bf16[264,128]{1,0:T(8,128)(2,1)S(1)}, u32[]{:S(2)}, u32[]{:S(2)}) %collective-permute-start.4) | collective-permute-done | bytes 67616 | tf_op jit(solution)/shard_map/ppermute | solution.py:695
  31.3 2.0 %collective-permute-start.12 = (bf16[512,128]{1,0:T(8,128)(2,1)S(1)}, bf16[512,128]{1,0:T(8,128)(2,1)S(1)}, u32[]{:S(2)}, u32[]{:S(2)}) collective-permute-start(bf16[512,128]{1,0:T(8,128)(2,1)S(1)} %get-tuple-element.58), channel_id=1, source_target_pairs={{0,24},{4,28},{8,16},{12,20},{16,8},{20,12},{24,0},{28,4},{1,25},{... | collective-permute-start | bytes 393224 | tf_op jit(solution)/shard_map/ppermute | solution.py:695
  33.4 1.8 %collective-permute-start.13 = (bf16[512,128]{1,0:T(8,128)(2,1)S(1)}, bf16[512,128]{1,0:T(8,128)(2,1)S(1)}, u32[]{:S(2)}, u32[]{:S(2)}) collective-permute-start(bf16[512,128]{1,0:T(8,128)(2,1)S(1)} %get-tuple-element.59), channel_id=1, source_target_pairs={{0,28},{4,24},{8,20},{12,16},{16,12},{20,8},{24,4},{28,0},{1,29},{... | collective-permute-start | bytes 393224 | tf_op jit(solution)/shard_map/ppermute | solution.py:695
  35.1 1.5 %collective-permute-start.7 = (bf16[512,128]{1,0:T(8,128)(2,1)S(1)}, bf16[512,128]{1,0:T(8,128)(2,1)S(1)}, u32[]{:S(2)}, u32[]{:S(2)}) collective-permute-start(bf16[512,128]{1,0:T(8,128)(2,1)S(1)} %get-tuple-element.53), channel_id=1, source_target_pairs={{0,4},{4,0},{8,12},{12,8},{16,20},{20,16},{24,28},{28,24},{1,5},{5... | collective-permute-start | bytes 393224 | tf_op jit(solution)/shard_map/ppermute | solution.py:695
  36.6 2.0 %collective-permute-start.9 = (bf16[512,128]{1,0:T(8,128)(2,1)S(1)}, bf16[512,128]{1,0:T(8,128)(2,1)S(1)}, u32[]{:S(2)}, u32[]{:S(2)}) collective-permute-start(bf16[512,128]{1,0:T(8,128)(2,1)S(1)} %get-tuple-element.55), channel_id=1, source_target_pairs={{0,12},{4,8},{8,4},{12,0},{16,28},{20,24},{24,20},{28,16},{1,13},{... | collective-permute-start | bytes 393224 | tf_op jit(solution)/shard_map/ppermute | solution.py:695
  38.6 1.9 %diagonal.1 = (f32[512,128]{1,0:T(8,128)S(1)}, s32[8,128]{1,0:T(8,128)S(4)}) custom-call(s32[8,12]{1,0:T(8,128)S(1)} %copy-done.1, bf16[264,128]{1,0:T(8,128)(2,1)S(1)} %get-tuple-element.43.refs_1_.refs_9_, bf16[264,128]{1,0:T(8,128)(2,1)S(1)} %collective-permute-done.refs_2_.refs_10_, bf16[264,128]{1,0:T(8,128)(2,1)S(1)} %collective-permute-done.1.refs_3_.refs_11_, ...), custom_call_target="tpu_custom_call" | custom-call | flops 2000000000 | bytes 1000000 | tf_op jit(solution)/shard_map/diagonal/pallas_call | solution.py:220
  40.6 1.6 %collective-permute-start.19 = (f32[128,512]{1,0:T(8,128)S(1)}, f32[128,512]{1,0:T(8,128)S(1)}, u32[]{:S(2)}, u32[]{:S(2)}) collective-permute-start(f32[128,512]{1,0:T(8,128)S(1)} %get-tuple-element.65.refs_0_), channel_id=1, source_target_pairs={{0,2},{1,3},{2,0},{3,1},{4,6},{5,7},{6,4},{7,5},{8,10},{9,11},{10,... | collective-permute-start | bytes 786440 | tf_op jit(solution)/shard_map/ppermute | solution.py:700
  42.2 0.2 collective-permute-done.13.refs_8_
  42.5 1.5 %collective-permute-done.8.refs_3_ = bf16[512,128]{1,0:T(8,128)(2,1)S(1)} collective-permute-done((bf16[512,128]{1,0:T(8,128)(2,1)S(1)}, bf16[512,128]{1,0:T(8,128)(2,1)S(1)}, u32[]{:S(2)}, u32[]{:S(2)}) %collective-permute-start.8) | collective-permute-done | bytes 131104 | tf_op jit(solution)/shard_map/ppermute | solution.py:695
  44.0 2.6 %collective-permute-done.9.refs_4_ = bf16[512,128]{1,0:T(8,128)(2,1)S(1)} collective-permute-done((bf16[512,128]{1,0:T(8,128)(2,1)S(1)}, bf16[512,128]{1,0:T(8,128)(2,1)S(1)}, u32[]{:S(2)}, u32[]{:S(2)}) %collective-permute-start.9) | collective-permute-done | bytes 131104 | tf_op jit(solution)/shard_map/ppermute | solution.py:695
  46.6 0.5 shard_map.56
  47.2 0.5 collective-permute-start.18
  47.9 1.5 %collective-permute-start.17 = (f32[264,128]{1,0:T(8,128)S(1)}, f32[264,128]{1,0:T(8,128)S(1)}, u32[]{:S(2)}, u32[]{:S(2)}) collective-permute-start(f32[264,128]{1,0:T(8,128)S(1)} %get-tuple-element.64), channel_id=1, source_target_pairs={{0,2},{1,3},{2,0},{3,1},{4,6},{5,7},{6,4},{7,5},{8,10},{9,11},{10,... | collective-permute-start | bytes 405512 | tf_op jit(solution)/shard_map/ppermute | solution.py:708
  49.3 0.7 shard_map.55
  50.3 0.4 collective-permute-start.24
  51.1 2.7 %collective-permute-done.17.other_ref = f32[264,128]{1,0:T(8,128)S(1)} collective-permute-done((f32[264,128]{1,0:T(8,128)S(1)}, f32[264,128]{1,0:T(8,128)S(1)}, u32[]{:S(2)}, u32[]{:S(2)}) %collective-permute-start.17) | collective-permute-done | bytes 135200 | tf_op jit(solution)/shard_map/ppermute | solution.py:708
  53.8 1.4 %collective-permute-start.23 = (s16[976,128]{1,0:T(8,128)(2,1)S(1)}, s16[976,128]{1,0:T(8,128)(2,1)S(1)}, u32[]{:S(2)}, u32[]{:S(2)}) collective-permute-start(s16[976,128]{1,0:T(8,128)(2,1)S(1)} %pack_sums.3), channel_id=1, source_target_pairs={{0,2},{1,3},{2,0},{3,1},{4,6},{5,7},{6,4},{7,5},{8,10},{9,11},{10,... | collective-permute-start | bytes 749576 | tf_op jit(solution)/shard_map/ppermute | solution.py:724
  55.3 8.9 %factor_first.1 = (f32[4,128,512]{2,1,0:T(8,128)S(1)}, f32[256,256]{1,0:T(8,128)S(1)}) custom-call(f32[512,128]{1,0:T(8,128)S(1)} %get-tuple-element.63.own_ref, f32[264,128]{1,0:T(8,128)S(1)} %collective-permute-done.17.other_ref, f32[128,512]{1,0:T(8,128)S(1)} %get-tuple-element.65.refs_0_, f32[128,512]{1,0:T(8,128)S(1)} %collective-permute-done.18.refs_1_, ...), custom_call_target="tpu_custom_call" | custom-call | flops 10000000000 | bytes 2000000 | tf_op jit(solution)/shard_map/factor_first/pallas_call | solution.py:459
  64.2 4.0 %factor_middle.1 = (f32[128,256]{1,0:T(8,128)S(1)}, f32[128,128]{1,0:T(8,128)S(1)}, f32[128,128]{1,0:T(8,128)S(1)}) custom-call(f32[4,128,512]{2,1,0:T(8,128)S(1)} %get-tuple-element.66.schur_ref), custom_call_target="tpu_custom_call" | custom-call | flops 5000000000 | bytes 1000000 | tf_op jit(solution)/shard_map/factor_middle/pallas_call | solution.py:488
  68.2 0.2 pack_sums.2
  68.4 0.7 collective-permute-start.15
  69.1 4.0 %factor_last.1 = (f32[256,256]{1,0:T(8,128)S(1)}, f32[128,512]{1,0:T(8,128)S(1)}) custom-call(f32[4,128,512]{2,1,0:T(8,128)S(1)} %get-tuple-element.66.schur_ref, f32[128,256]{1,0:T(8,128)S(1)} %get-tuple-element.67.strip_ref, f32[128,128]{1,0:T(8,128)S(1)} %get-tuple-element.68.corner_ref, f32[128,128]{1,0:T(8,128)S(1)} %get-tuple-element.69.inverse_ref), custom_call_target="tpu_custom_call" | custom-call | flops 5000000000 | bytes 1000000 | tf_op jit(solution)/shard_map/factor_last/pallas_call | solution.py:517
  73.1 1.5 %solve_left.1 = (f32[3,128,256]{2,1,0:T(8,128)S(1)}, f32[384,256]{1,0:T(8,128)S(1)}) custom-call(f32[4,128,512]{2,1,0:T(8,128)S(1)} %bitcast.6, f32[6,128,128]{2,1,0:T(8,128)S(1)} %get-tuple-element.71.kept, f32[6,128,128]{2,1,0:T(8,128)S(1)} %collective-permute-done.21.near, s16[976,128]{1,0:T(8,128)(2,1)S(1)} %collective-permute-done.23.far, ...), custom_call_target="tpu_custom_call" | custom-call | flops 2000000000 | bytes 5000000 | tf_op jit(solution)/shard_map/solve_left/pallas_call | solution.py:626
  74.7 1.1 %collective-permute-done.15.far = s16[976,128]{1,0:T(8,128)(2,1)S(1)} collective-permute-done((s16[976,128]{1,0:T(8,128)(2,1)S(1)}, s16[976,128]{1,0:T(8,128)(2,1)S(1)}, u32[]{:S(2)}, u32[]{:S(2)}) %collective-permute-start.15) | collective-permute-done | bytes 249888 | tf_op jit(solution)/shard_map/ppermute | solution.py:724
  75.8 1.3 %solve_right.1 = f32[4,128,512]{2,1,0:T(8,128)} custom-call(s16[976,128]{1,0:T(8,128)(2,1)S(1)} %collective-permute-done.15.far, f32[256,256]{1,0:T(8,128)S(1)} %get-tuple-element.70.trail_ref, f32[384,256]{1,0:T(8,128)S(1)} %get-tuple-element.78.carried_ref, f32[3,128,256]{2,1,0:T(8,128)S(1)} %get-tuple-element.79.solved_ref, ...), custom_call_target="tpu_custom_call" | custom-call | flops 2000000000 | bytes 5000000 | tf_op jit(solution)/shard_map/solve_right/pallas_call | solution.py:660
  (34 shorter events, 1.1 us)
Async XLA Ops:
  1.3 7.6 %collective-permute-start = (bf16[264,128]{1,0:T(8,128)(2,1)S(1)}, bf16[264,128]{1,0:T(8,128)(2,1)S(1)}, u32[]{:S(2)}, u32[]{:S(2)}) collective-permute-start(bf16[264,128]{1,0:T(8,128)(2,1)S(1)} %get-tuple-element.44), channel_id=1, source_target_pairs={{0,4},{4,0},{8,12},{12,8},{16,20},{20,16},{24,28},{28,24},{1,5},{5... | collective-permute-start | bytes 202760 | tf_op jit(solution)/shard_map/ppermute | solution.py:695
  4.3 8.4 %collective-permute-start.1 = (bf16[264,128]{1,0:T(8,128)(2,1)S(1)}, bf16[264,128]{1,0:T(8,128)(2,1)S(1)}, u32[]{:S(2)}, u32[]{:S(2)}) collective-permute-start(bf16[264,128]{1,0:T(8,128)(2,1)S(1)} %get-tuple-element.45), channel_id=1, source_target_pairs={{0,8},{4,12},{8,0},{12,4},{16,24},{20,28},{24,16},{28,20},{1,9},{5... | collective-permute-start | bytes 202760 | tf_op jit(solution)/shard_map/ppermute | solution.py:695
  5.9 6.9 %collective-permute-start.2 = (bf16[264,128]{1,0:T(8,128)(2,1)S(1)}, bf16[264,128]{1,0:T(8,128)(2,1)S(1)}, u32[]{:S(2)}, u32[]{:S(2)}) collective-permute-start(bf16[264,128]{1,0:T(8,128)(2,1)S(1)} %get-tuple-element.46), channel_id=1, source_target_pairs={{0,12},{4,8},{8,4},{12,0},{16,28},{20,24},{24,20},{28,16},{1,13},{... | collective-permute-start | bytes 202760 | tf_op jit(solution)/shard_map/ppermute | solution.py:695
  5.9 10.8 %collective-permute-start.3 = (bf16[264,128]{1,0:T(8,128)(2,1)S(1)}, bf16[264,128]{1,0:T(8,128)(2,1)S(1)}, u32[]{:S(2)}, u32[]{:S(2)}) collective-permute-start(bf16[264,128]{1,0:T(8,128)(2,1)S(1)} %get-tuple-element.47), channel_id=1, source_target_pairs={{0,16},{4,20},{8,24},{12,28},{16,0},{20,4},{24,8},{28,12},{1,17},{... | collective-permute-start | bytes 202760 | tf_op jit(solution)/shard_map/ppermute | solution.py:695
  8.9 27.7 %collective-permute-start.10 = (bf16[512,128]{1,0:T(8,128)(2,1)S(1)}, bf16[512,128]{1,0:T(8,128)(2,1)S(1)}, u32[]{:S(2)}, u32[]{:S(2)}) collective-permute-start(bf16[512,128]{1,0:T(8,128)(2,1)S(1)} %get-tuple-element.56), channel_id=1, source_target_pairs={{0,16},{4,20},{8,24},{12,28},{16,0},{20,4},{24,8},{28,12},{1,17},{... | collective-permute-start | bytes 393224 | tf_op jit(solution)/shard_map/ppermute | solution.py:695
  8.9 27.7 %collective-permute-start.11 = (bf16[512,128]{1,0:T(8,128)(2,1)S(1)}, bf16[512,128]{1,0:T(8,128)(2,1)S(1)}, u32[]{:S(2)}, u32[]{:S(2)}) collective-permute-start(bf16[512,128]{1,0:T(8,128)(2,1)S(1)} %get-tuple-element.57), channel_id=1, source_target_pairs={{0,20},{4,16},{8,28},{12,24},{16,4},{20,0},{24,12},{28,8},{1,21},{... | collective-permute-start | bytes 393224 | tf_op jit(solution)/shard_map/ppermute | solution.py:695
  12.8 18.5 %collective-permute-start.4 = (bf16[264,128]{1,0:T(8,128)(2,1)S(1)}, bf16[264,128]{1,0:T(8,128)(2,1)S(1)}, u32[]{:S(2)}, u32[]{:S(2)}) collective-permute-start(bf16[264,128]{1,0:T(8,128)(2,1)S(1)} %get-tuple-element.48), channel_id=1, source_target_pairs={{0,20},{4,16},{8,28},{12,24},{16,4},{20,0},{24,12},{28,8},{1,21},{... | collective-permute-start | bytes 202760 | tf_op jit(solution)/shard_map/ppermute | solution.py:695
  12.9 20.5 %collective-permute-start.5 = (bf16[264,128]{1,0:T(8,128)(2,1)S(1)}, bf16[264,128]{1,0:T(8,128)(2,1)S(1)}, u32[]{:S(2)}, u32[]{:S(2)}) collective-permute-start(bf16[264,128]{1,0:T(8,128)(2,1)S(1)} %get-tuple-element.49), channel_id=1, source_target_pairs={{0,24},{4,28},{8,16},{12,20},{16,8},{20,12},{24,0},{28,4},{1,25},{... | collective-permute-start | bytes 202760 | tf_op jit(solution)/shard_map/ppermute | solution.py:695
  16.7 18.5 %collective-permute-start.6 = (bf16[264,128]{1,0:T(8,128)(2,1)S(1)}, bf16[264,128]{1,0:T(8,128)(2,1)S(1)}, u32[]{:S(2)}, u32[]{:S(2)}) collective-permute-start(bf16[264,128]{1,0:T(8,128)(2,1)S(1)} %get-tuple-element.50), channel_id=1, source_target_pairs={{0,28},{4,24},{8,20},{12,16},{16,12},{20,8},{24,4},{28,0},{1,29},{... | collective-permute-start | bytes 202760 | tf_op jit(solution)/shard_map/ppermute | solution.py:695
  31.3 9.3 %collective-permute-start.12 = (bf16[512,128]{1,0:T(8,128)(2,1)S(1)}, bf16[512,128]{1,0:T(8,128)(2,1)S(1)}, u32[]{:S(2)}, u32[]{:S(2)}) collective-permute-start(bf16[512,128]{1,0:T(8,128)(2,1)S(1)} %get-tuple-element.58), channel_id=1, source_target_pairs={{0,24},{4,28},{8,16},{12,20},{16,8},{20,12},{24,0},{28,4},{1,25},{... | collective-permute-start | bytes 393224 | tf_op jit(solution)/shard_map/ppermute | solution.py:695
  33.4 5.3 %copy-start.1 = (s32[8,12]{1,0:T(8,128)S(1)}, s32[8,12]{1,0:T(8,128)}, u32[]{:S(2)}) copy-start(s32[8,12]{1,0:T(8,128)} %refs_0_.1) | copy-start | bytes 1156
  33.4 9.1 %collective-permute-start.13 = (bf16[512,128]{1,0:T(8,128)(2,1)S(1)}, bf16[512,128]{1,0:T(8,128)(2,1)S(1)}, u32[]{:S(2)}, u32[]{:S(2)}) collective-permute-start(bf16[512,128]{1,0:T(8,128)(2,1)S(1)} %get-tuple-element.59), channel_id=1, source_target_pairs={{0,28},{4,24},{8,20},{12,16},{16,12},{20,8},{24,4},{28,0},{1,29},{... | collective-permute-start | bytes 393224 | tf_op jit(solution)/shard_map/ppermute | solution.py:695
  35.1 7.3 %collective-permute-start.7 = (bf16[512,128]{1,0:T(8,128)(2,1)S(1)}, bf16[512,128]{1,0:T(8,128)(2,1)S(1)}, u32[]{:S(2)}, u32[]{:S(2)}) collective-permute-start(bf16[512,128]{1,0:T(8,128)(2,1)S(1)} %get-tuple-element.53), channel_id=1, source_target_pairs={{0,4},{4,0},{8,12},{12,8},{16,20},{20,16},{24,28},{28,24},{1,5},{5... | collective-permute-start | bytes 393224 | tf_op jit(solution)/shard_map/ppermute | solution.py:695
  36.6 7.3 %collective-permute-start.8 = (bf16[512,128]{1,0:T(8,128)(2,1)S(1)}, bf16[512,128]{1,0:T(8,128)(2,1)S(1)}, u32[]{:S(2)}, u32[]{:S(2)}) collective-permute-start(bf16[512,128]{1,0:T(8,128)(2,1)S(1)} %get-tuple-element.54), channel_id=1, source_target_pairs={{0,8},{4,12},{8,0},{12,4},{16,24},{20,28},{24,16},{28,20},{1,9},{5... | collective-permute-start | bytes 393224 | tf_op jit(solution)/shard_map/ppermute | solution.py:695
  36.6 10.0 %collective-permute-start.9 = (bf16[512,128]{1,0:T(8,128)(2,1)S(1)}, bf16[512,128]{1,0:T(8,128)(2,1)S(1)}, u32[]{:S(2)}, u32[]{:S(2)}) collective-permute-start(bf16[512,128]{1,0:T(8,128)(2,1)S(1)} %get-tuple-element.55), channel_id=1, source_target_pairs={{0,12},{4,8},{8,4},{12,0},{16,28},{20,24},{24,20},{28,16},{1,13},{... | collective-permute-start | bytes 393224 | tf_op jit(solution)/shard_map/ppermute | solution.py:695
  40.6 7.1 %collective-permute-start.19 = (f32[128,512]{1,0:T(8,128)S(1)}, f32[128,512]{1,0:T(8,128)S(1)}, u32[]{:S(2)}, u32[]{:S(2)}) collective-permute-start(f32[128,512]{1,0:T(8,128)S(1)} %get-tuple-element.65.refs_0_), channel_id=1, source_target_pairs={{0,2},{1,3},{2,0},{3,1},{4,6},{5,7},{6,4},{7,5},{8,10},{9,11},{10,... | collective-permute-start | bytes 786440 | tf_op jit(solution)/shard_map/ppermute | solution.py:700
  42.4 5.4 %collective-permute-start.16 = (f32[512,128]{1,0:T(8,128)S(1)}, f32[512,128]{1,0:T(8,128)S(1)}, u32[]{:S(2)}, u32[]{:S(2)}) collective-permute-start(f32[512,128]{1,0:T(8,128)S(1)} %get-tuple-element.62.first_ref), channel_id=1, source_target_pairs={{0,1},{1,0},{2,3},{3,2},{4,5},{5,4},{6,7},{7,6},{8,9},{9,8},{10,11... | collective-permute-start | bytes 786440 | tf_op jit(solution)/shard_map/ppermute | solution.py:706
  47.1 3.2 %collective-permute-start.22 = (f32[6,128,128]{2,1,0:T(8,128)S(1)}, f32[6,128,128]{2,1,0:T(8,128)S(1)}, u32[]{:S(2)}, u32[]{:S(2)}) collective-permute-start(f32[6,128,128]{2,1,0:T(8,128)S(1)} %get-tuple-element.74), channel_id=1, source_target_pairs={{0,1},{1,0},{2,3},{3,2},{4,5},{5,4},{6,7},{7,6},{8,9},{9,8},{10,11... | collective-permute-start | bytes 1179656 | tf_op jit(solution)/shard_map/ppermute | solution.py:723
  47.2 3.7 %collective-permute-start.18 = (f32[128,512]{1,0:T(8,128)S(1)}, f32[128,512]{1,0:T(8,128)S(1)}, u32[]{:S(2)}, u32[]{:S(2)}) collective-permute-start(f32[128,512]{1,0:T(8,128)S(1)} %get-tuple-element.65.refs_0_), channel_id=1, source_target_pairs={{0,1},{1,0},{2,3},{3,2},{4,5},{5,4},{6,7},{7,6},{8,9},{9,8},{10,11... | collective-permute-start | bytes 786440 | tf_op jit(solution)/shard_map/ppermute | solution.py:701
  47.7 7.6 %collective-permute-start.20 = (f32[128,512]{1,0:T(8,128)S(1)}, f32[128,512]{1,0:T(8,128)S(1)}, u32[]{:S(2)}, u32[]{:S(2)}) collective-permute-start(f32[128,512]{1,0:T(8,128)S(1)} %collective-permute-done.19.refs_2_), channel_id=1, source_target_pairs={{0,1},{1,0},{2,3},{3,2},{4,5},{5,4},{6,7},{7,6},{8,9},{9,8},{10,11... | collective-permute-start | bytes 786440 | tf_op jit(solution)/shard_map/ppermute | solution.py:702
  47.9 6.0 %collective-permute-start.17 = (f32[264,128]{1,0:T(8,128)S(1)}, f32[264,128]{1,0:T(8,128)S(1)}, u32[]{:S(2)}, u32[]{:S(2)}) collective-permute-start(f32[264,128]{1,0:T(8,128)S(1)} %get-tuple-element.64), channel_id=1, source_target_pairs={{0,2},{1,3},{2,0},{3,1},{4,6},{5,7},{6,4},{7,5},{8,10},{9,11},{10,... | collective-permute-start | bytes 405512 | tf_op jit(solution)/shard_map/ppermute | solution.py:708
  50.1 23.0 %collective-permute-start.21 = (f32[6,128,128]{2,1,0:T(8,128)S(1)}, f32[6,128,128]{2,1,0:T(8,128)S(1)}, u32[]{:S(2)}, u32[]{:S(2)}) collective-permute-start(f32[6,128,128]{2,1,0:T(8,128)S(1)} %get-tuple-element.72), channel_id=1, source_target_pairs={{0,1},{1,0},{2,3},{3,2},{4,5},{5,4},{6,7},{7,6},{8,9},{9,8},{10,11... | collective-permute-start | bytes 1179656 | tf_op jit(solution)/shard_map/ppermute | solution.py:726
  50.3 22.8 %collective-permute-start.24 = (f32[6,128,128]{2,1,0:T(8,128)S(1)}, f32[6,128,128]{2,1,0:T(8,128)S(1)}, u32[]{:S(2)}, u32[]{:S(2)}) collective-permute-start(f32[6,128,128]{2,1,0:T(8,128)S(1)} %get-tuple-element.76), channel_id=1, source_target_pairs={{0,1},{1,0},{2,3},{3,2},{4,5},{5,4},{6,7},{7,6},{8,9},{9,8},{10,11... | collective-permute-start | bytes 1179656 | tf_op jit(solution)/shard_map/ppermute | solution.py:726
  50.9 17.3 %collective-permute-start.14 = (f32[6,128,128]{2,1,0:T(8,128)S(1)}, f32[6,128,128]{2,1,0:T(8,128)S(1)}, u32[]{:S(2)}, u32[]{:S(2)}) collective-permute-start(f32[6,128,128]{2,1,0:T(8,128)S(1)} %get-tuple-element.61), channel_id=1, source_target_pairs={{0,1},{1,0},{2,3},{3,2},{4,5},{5,4},{6,7},{7,6},{8,9},{9,8},{10,11... | collective-permute-start | bytes 1179656 | tf_op jit(solution)/shard_map/ppermute | solution.py:723
  53.8 19.3 %collective-permute-start.23 = (s16[976,128]{1,0:T(8,128)(2,1)S(1)}, s16[976,128]{1,0:T(8,128)(2,1)S(1)}, u32[]{:S(2)}, u32[]{:S(2)}) collective-permute-start(s16[976,128]{1,0:T(8,128)(2,1)S(1)} %pack_sums.3), channel_id=1, source_target_pairs={{0,2},{1,3},{2,0},{3,1},{4,6},{5,7},{6,4},{7,5},{8,10},{9,11},{10,... | collective-permute-start | bytes 749576 | tf_op jit(solution)/shard_map/ppermute | solution.py:724
  68.4 7.3 %collective-permute-start.15 = (s16[976,128]{1,0:T(8,128)(2,1)S(1)}, s16[976,128]{1,0:T(8,128)(2,1)S(1)}, u32[]{:S(2)}, u32[]{:S(2)}) collective-permute-start(s16[976,128]{1,0:T(8,128)(2,1)S(1)} %pack_sums.2), channel_id=1, source_target_pairs={{0,2},{1,3},{2,0},{3,1},{4,6},{5,7},{6,4},{7,5},{8,10},{9,11},{10,... | collective-permute-start | bytes 749576 | tf_op jit(solution)/shard_map/ppermute | solution.py:724
  69.1 4.0 %copy-start = (f32[1,4,1,128,512]{4,3,2,1,0:T(8,128)S(1)}, f32[1,4,1,128,512]{4,3,2,1,0:T(8,128)}, u32[]{:S(2)}) copy-start(f32[1,4,1,128,512]{4,3,2,1,0:T(8,128)} %param.9) | copy-start | bytes 3145732
